TPU v7x, 32 devices: a whole 2x2x4 slice. The times are simulated.
32 devices in a mesh: fsdp: 4 (over z), context: 4 (over y, x), tensor: 2 (over core).
Axes of the slice: x: 2, y: 2, z: 4, core: 2. Of those that a mesh axis runs over, the one named last changes fastest.
Arguments:
- hidden: bfloat16 [4, 512, 1024], P('fsdp', 'context'), may hold values from -6 to 6
- segments: int32 [4, 512], P('fsdp', 'context'), may hold values from 0 to 3, never falling along the last dimension, each value on 1 to 256 neighbouring positions
- w_query: bfloat16 [1024, 2048], P(('fsdp', 'context'), 'tensor'), may hold values from -0.1875 to 0.1875
- key_projection: bfloat16 [1024, 1024], P(('fsdp', 'context'), 'tensor'), may hold values from -0.1875 to 0.1875
- value_projection: bfloat16 [1024, 1024], P(('fsdp', 'context'), 'tensor'), may hold values from -0.1875 to 0.1875
- w_out: bfloat16 [2048, 1024], P('tensor', ('fsdp', 'context')), may hold values from -0.5 to 0.5
- w_gate: bfloat16 [1024, 3072], P(('fsdp', 'context'), 'tensor'), may hold values from -0.1875 to 0.1875
- w_up: bfloat16 [1024, 3072], P(('fsdp', 'context'), 'tensor'), may hold values from -0.1875 to 0.1875
- w_down: bfloat16 [3072, 1024], P('tensor', ('fsdp', 'context')), may hold values from -0.109375 to 0.109375
- gain_attn: bfloat16 [1024], P(('fsdp', 'context')), may hold values from 0.5 to 1.5
- gain_ffn: bfloat16 [1024], P(('fsdp', 'context')), may hold values from 0.5 to 1.5
- query_norm_gain: bfloat16 [128], P(('fsdp', 'context')), may hold values from 0.5 to 1.5
- gain_key: bfloat16 [128], P(('fsdp', 'context')), may hold values from 0.5 to 1.5
- cotangent: bfloat16 [4, 512, 1024], P('fsdp', 'context'), may hold values from -6 to 6
Outputs:
- output: bfloat16 [4, 512, 1024], P('fsdp', 'context')
- grad_hidden: bfloat16 [4, 512, 1024], P('fsdp', 'context')
- grad_w_query: float32 [1024, 2048], P(('fsdp', 'context'), 'tensor')
- grad_w_key: float32 [1024, 1024], P(('fsdp', 'context'), 'tensor')
- grad_w_value: float32 [1024, 1024], P(('fsdp', 'context'), 'tensor')
- grad_w_out: float32 [2048, 1024], P('tensor', ('fsdp', 'context'))
- grad_w_gate: float32 [1024, 3072], P(('fsdp', 'context'), 'tensor')
- grad_w_up: float32 [1024, 3072], P(('fsdp', 'context'), 'tensor')
- grad_w_down: float32 [3072, 1024], P('tensor', ('fsdp', 'context'))
- grad_gain_attn: float32 [1024], P(('fsdp', 'context'))
- grad_gain_ffn: float32 [1024], P(('fsdp', 'context'))
- grad_gain_query: float32 [128], P(('fsdp', 'context'))
- grad_gain_key: float32 [128], P(('fsdp', 'context'))
Inputs may be any that keep to these rules, and one draw needn't show every extreme that they name: `segments`: within each sequence the document numbers start at 0 and never fall along the positions; each document holds at most 256 tokens, and one holds exactly 256.
All inputs are finite; a program needn't handle non-finite values.
Results may differ from a plain program's by a relative error of at most 0.023.
Values may be sent and summed in bfloat16 or wider, within the bound.
No kernel may reach another device: no remote copies, remote signals or barrier semaphores. Data moves between devices by JAX's collectives and lax.ppermute only.
A program may use at most 128 MiB of HBM per device.

v0:
```python
import jax
import jax.numpy as jnp
from jax import lax
from jax.sharding import PartitionSpec as P

HEAD_SIZE = 128


epsilon = 1e-06
theta_base = 1000000.0


def scale_rows(values, gain):
    factor = lax.rsqrt(jnp.mean(values * values, axis=-1, keepdims=True) + epsilon)
    return (values * factor * gain, factor)


def scale_back(values, factor, gain, upstream):
    normed = values * factor
    weighted = upstream * gain
    inward = factor * (weighted - normed * jnp.mean(weighted * normed, axis=-1, keepdims=True))
    return (inward, upstream * normed)


def rotary_apply(values, cosine_table, sine_table):
    half_width = values.shape[-1] // 2
    first_half = values[..., :half_width]
    second_half = values[..., half_width:]
    cosine_table = cosine_table[:, None, :]
    sine_table = sine_table[:, None, :]
    return jnp.concatenate(
        [
            first_half * cosine_table - second_half * sine_table,
            second_half * cosine_table + first_half * sine_table,
        ],
        axis=-1,
    )


def contract_rows(left, right):
    return lax.dot_general(
        left, right, (((0,), (0,)), ((), ())), preferred_element_type=jnp.float32
    )


def contract_cols(left, right):
    return lax.dot_general(
        left, right, (((1,), (1,)), ((), ())), preferred_element_type=jnp.float32
    )


def gather_weights(
    w_query,
    key_projection,
    value_projection,
    w_out,
    w_gate,
    w_up,
    w_down,
    gain_attn,
    gain_ffn,
    query_norm_gain,
    gain_key,
):
    return (
        lax.all_gather(w_query, ("fsdp", "context"), axis=0, tiled=True),
        lax.all_gather(key_projection, ("fsdp", "context"), axis=0, tiled=True),
        lax.all_gather(value_projection, ("fsdp", "context"), axis=0, tiled=True),
        lax.all_gather(w_out, ("fsdp", "context"), axis=1, tiled=True),
        lax.all_gather(w_gate, ("fsdp", "context"), axis=0, tiled=True),
        lax.all_gather(w_up, ("fsdp", "context"), axis=0, tiled=True),
        lax.all_gather(w_down, ("fsdp", "context"), axis=1, tiled=True),
        lax.all_gather(gain_attn, ("fsdp", "context"), axis=0, tiled=True),
        lax.all_gather(gain_ffn, ("fsdp", "context"), axis=0, tiled=True),
        lax.all_gather(query_norm_gain, ("fsdp", "context"), axis=0, tiled=True),
        lax.all_gather(gain_key, ("fsdp", "context"), axis=0, tiled=True),
    )


def forward_pass(x_rows, seg_rows, query_pos, cosine_table, sine_table, weights):
    (
        w_query,
        key_projection,
        value_projection,
        w_out,
        w_gate,
        w_up,
        w_down,
        gain_attn,
        gain_ffn,
        query_norm_gain,
        gain_key,
    ) = weights
    tokens = x_rows.shape[0]
    kv_local = key_projection.shape[1] // HEAD_SIZE
    q_local = w_query.shape[1] // HEAD_SIZE
    query_group = q_local // kv_local
    scale = HEAD_SIZE ** (-0.5)
    h_norm, factor_one = scale_rows(x_rows, gain_attn.astype(jnp.float32))
    hidden_lowered = h_norm.astype(jnp.bfloat16)
    query_unrotated = jnp.dot(hidden_lowered, w_query, preferred_element_type=jnp.float32).reshape(
        tokens, q_local, HEAD_SIZE
    )
    key_unrotated = jnp.dot(
        hidden_lowered, key_projection, preferred_element_type=jnp.float32
    ).reshape(tokens, kv_local, HEAD_SIZE)
    value_lowered = jnp.dot(
        hidden_lowered, value_projection, preferred_element_type=jnp.float32
    ).astype(jnp.bfloat16)
    query_norm, query_factor = scale_rows(query_unrotated, query_norm_gain.astype(jnp.float32))
    key_norm, key_factor = scale_rows(key_unrotated, gain_key.astype(jnp.float32))
    query_lowered = (
        rotary_apply(query_norm, cosine_table, sine_table)
        .astype(jnp.bfloat16)
        .reshape(tokens, kv_local, query_group, HEAD_SIZE)
    )
    key_low = (
        rotary_apply(key_norm, cosine_table, sine_table)
        .astype(jnp.bfloat16)
        .reshape(tokens, kv_local * HEAD_SIZE)
    )

    def attend_block(carry, key_block, value_block, key_seg, key_start):
        block_rows = key_block.shape[0]
        needed = (key_start <= query_pos[-1]) & (key_seg[-1] >= seg_rows[0])

        def attend_compute(state):
            numer, totals = state
            key_pos = key_start + jnp.arange(block_rows, dtype=jnp.int32)
            allowed = (seg_rows[:, None] == key_seg[None, :]) & (
                query_pos[:, None] >= key_pos[None, :]
            )
            scores = (
                jnp.einsum(
                    "qgrh,kgh->grqk",
                    query_lowered,
                    key_block.reshape(block_rows, kv_local, HEAD_SIZE),
                    preferred_element_type=jnp.float32,
                )
                * scale
            )
            expo = jnp.where(allowed, jnp.exp(scores), 0.0)
            partial_sum = jnp.einsum(
                "grqk,kgh->qgrh",
                expo.astype(jnp.bfloat16),
                value_block.reshape(block_rows, kv_local, HEAD_SIZE),
                preferred_element_type=jnp.float32,
            )
            return (numer + partial_sum, totals + jnp.sum(expo, axis=-1))

        return lax.cond(needed, attend_compute, lambda state: state, carry)

    initial = (
        jnp.zeros((tokens, kv_local, query_group, HEAD_SIZE), jnp.float32),
        jnp.zeros((kv_local, query_group, tokens), jnp.float32),
    )
    key_rows = lax.all_gather(key_low, "context", axis=0, tiled=True)
    value_rows = lax.all_gather(value_lowered, "context", axis=0, tiled=True)
    seg_piece = lax.all_gather(seg_rows, "context", axis=0, tiled=True)
    count = key_rows.shape[0]
    block_rows = min(count, tokens)

    def advance(block_index, state):
        offset = block_index * block_rows
        return attend_block(
            state,
            lax.dynamic_slice_in_dim(key_rows, offset, block_rows, 0),
            lax.dynamic_slice_in_dim(value_rows, offset, block_rows, 0),
            lax.dynamic_slice_in_dim(seg_piece, offset, block_rows, 0),
            offset,
        )

    numer, totals = lax.fori_loop(0, count // block_rows, advance, initial)
    attn_raw = numer / jnp.transpose(totals, (2, 0, 1))[..., None]
    attn_low = attn_raw.astype(jnp.bfloat16).reshape(tokens, q_local * HEAD_SIZE)
    branch = lax.psum(
        jnp.dot(attn_low, w_out, preferred_element_type=jnp.float32).astype(jnp.bfloat16), "tensor"
    ).astype(jnp.float32)
    x_mid = x_rows + branch
    h_two, factor_two = scale_rows(x_mid, gain_ffn.astype(jnp.float32))
    h_two_low = h_two.astype(jnp.bfloat16)
    gate = jnp.dot(h_two_low, w_gate, preferred_element_type=jnp.float32)
    up_proj = jnp.dot(h_two_low, w_up, preferred_element_type=jnp.float32)
    units_low = (jax.nn.silu(gate) * up_proj).astype(jnp.bfloat16)
    ffn_out = lax.psum(
        jnp.dot(units_low, w_down, preferred_element_type=jnp.float32).astype(jnp.bfloat16),
        "tensor",
    ).astype(jnp.float32)
    result = x_mid + ffn_out
    return (
        result,
        factor_one,
        hidden_lowered,
        query_unrotated,
        query_factor,
        key_unrotated,
        key_factor,
        query_lowered,
        key_low,
        value_lowered,
        attn_raw,
        attn_low,
        totals,
        x_mid,
        factor_two,
        h_two_low,
        gate,
        up_proj,
        units_low,
    )


def local(
    hidden,
    segments,
    w_query,
    key_projection,
    value_projection,
    w_out,
    w_gate,
    w_up,
    w_down,
    gain_attn,
    gain_ffn,
    query_norm_gain,
    gain_key,
    cotangent,
):
    tokens = hidden.shape[1]
    width = hidden.shape[2]
    x_rows = hidden.reshape(tokens, width).astype(jnp.float32)
    seg_rows = segments.reshape(tokens)
    query_pos = lax.axis_index("context") * tokens + jnp.arange(tokens, dtype=jnp.int32)
    half_width = HEAD_SIZE // 2
    freq = theta_base ** (-(jnp.arange(half_width, dtype=jnp.float32) * 2.0 / HEAD_SIZE))
    angle = query_pos.astype(jnp.float32)[:, None] * freq[None, :]
    cosine_table = jnp.cos(angle)
    sine_table = jnp.sin(angle)
    weights = gather_weights(
        w_query,
        key_projection,
        value_projection,
        w_out,
        w_gate,
        w_up,
        w_down,
        gain_attn,
        gain_ffn,
        query_norm_gain,
        gain_key,
    )
    saved = forward_pass(x_rows, seg_rows, query_pos, cosine_table, sine_table, weights)
    out_rows = saved[0]
    weights = gather_weights(
        w_query,
        key_projection,
        value_projection,
        w_out,
        w_gate,
        w_up,
        w_down,
        gain_attn,
        gain_ffn,
        query_norm_gain,
        gain_key,
    )
    saved = forward_pass(x_rows, seg_rows, query_pos, cosine_table, sine_table, weights)
    (
        result,
        factor_one,
        hidden_lowered,
        query_unrotated,
        query_factor,
        key_unrotated,
        key_factor,
        query_lowered,
        key_low,
        value_lowered,
        attn_raw,
        attn_low,
        totals,
        x_mid,
        factor_two,
        h_two_low,
        gate,
        up_proj,
        units_low,
    ) = saved
    (
        full_query,
        full_key,
        full_value,
        full_out,
        full_gate,
        full_up,
        full_down,
        full_gain_attn,
        full_gain_ffn,
        full_gain_query,
        full_gain_key,
    ) = weights
    kv_local = full_key.shape[1] // HEAD_SIZE
    q_local = full_query.shape[1] // HEAD_SIZE
    query_group = q_local // kv_local
    kv_width = kv_local * HEAD_SIZE
    scale = HEAD_SIZE ** (-0.5)
    grad_out = cotangent.reshape(tokens, width)
    grad_down = contract_rows(units_low, grad_out)
    grad_units = contract_cols(grad_out, full_down)
    sigmoid_gate = jax.nn.sigmoid(gate)
    grad_gate_low = (
        grad_units * up_proj * sigmoid_gate * (1.0 + gate * (1.0 - sigmoid_gate))
    ).astype(jnp.bfloat16)
    grad_up_low = (grad_units * gate * sigmoid_gate).astype(jnp.bfloat16)
    grad_gate = contract_rows(h_two_low, grad_gate_low)
    grad_up = contract_rows(h_two_low, grad_up_low)
    grad_h_two = lax.psum(
        (contract_cols(grad_gate_low, full_gate) + contract_cols(grad_up_low, full_up)).astype(
            jnp.bfloat16
        ),
        "tensor",
    ).astype(jnp.float32)
    mid_inward, mid_gain_rows = scale_back(
        x_mid, factor_two, full_gain_ffn.astype(jnp.float32), grad_h_two
    )
    grad_gain_ffn = jnp.sum(mid_gain_rows, axis=0)
    grad_mid = grad_out.astype(jnp.float32) + mid_inward
    grad_mid_low = grad_mid.astype(jnp.bfloat16)
    grad_wout = contract_rows(attn_low, grad_mid_low)
    grad_attn = contract_cols(grad_mid_low, full_out).reshape(
        tokens, kv_local, query_group, HEAD_SIZE
    )
    totals_rows = jnp.transpose(totals, (2, 0, 1))[..., None]
    grad_scaled = (grad_attn / totals_rows).astype(jnp.bfloat16)
    delta = jnp.sum(grad_attn * attn_raw, axis=-1)
    grad_totals = -jnp.transpose(delta, (1, 2, 0)) / totals

    def back_block(grad_query_acc, inputs):
        key_block, value_block, key_seg, block_index = inputs
        key_start = block_index * tokens
        needed = (key_start <= query_pos[-1]) & (key_seg[-1] >= seg_rows[0])

        def back_compute(accum):
            key_pos = key_start + jnp.arange(tokens, dtype=jnp.int32)
            allowed = (seg_rows[:, None] == key_seg[None, :]) & (
                query_pos[:, None] >= key_pos[None, :]
            )
            key_heads = key_block.reshape(tokens, kv_local, HEAD_SIZE)
            value_heads = value_block.reshape(tokens, kv_local, HEAD_SIZE)
            scores = (
                jnp.einsum(
                    "qgrh,kgh->grqk", query_lowered, key_heads, preferred_element_type=jnp.float32
                )
                * scale
            )
            expo = jnp.where(allowed, jnp.exp(scores), 0.0)
            grad_value = jnp.einsum(
                "grqk,qgrh->kgh",
                expo.astype(jnp.bfloat16),
                grad_scaled,
                preferred_element_type=jnp.float32,
            )
            grad_expo = (
                jnp.einsum(
                    "qgrh,kgh->grqk", grad_scaled, value_heads, preferred_element_type=jnp.float32
                )
                + grad_totals[..., None]
            )
            grad_scores = (expo * grad_expo).astype(jnp.bfloat16)
            accum = (
                accum
                + jnp.einsum(
                    "grqk,kgh->qgrh", grad_scores, key_heads, preferred_element_type=jnp.float32
                )
                * scale
            )
            grad_key = (
                jnp.einsum(
                    "grqk,qgrh->kgh", grad_scores, query_lowered, preferred_element_type=jnp.float32
                )
                * scale
            )
            return (
                accum,
                jnp.concatenate(
                    [grad_key.reshape(tokens, kv_width), grad_value.reshape(tokens, kv_width)],
                    axis=1,
                ),
            )

        def skip_block(accum):
            return (accum, jnp.zeros((tokens, 2 * kv_width), jnp.float32))

        return lax.cond(needed, back_compute, skip_block, grad_query_acc)

    key_all, value_all, seg_all = (
        lax.all_gather(key_low, "context", axis=0, tiled=True),
        lax.all_gather(value_lowered, "context", axis=0, tiled=True),
        lax.all_gather(seg_rows, "context", axis=0, tiled=True),
    )
    blocks = key_all.shape[0] // tokens
    grad_query_rot, kv_terms = lax.scan(
        back_block,
        jnp.zeros((tokens, kv_local, query_group, HEAD_SIZE), jnp.float32),
        (
            key_all.reshape(blocks, tokens, kv_width),
            value_all.reshape(blocks, tokens, kv_width),
            seg_all.reshape(blocks, tokens),
            jnp.arange(blocks, dtype=jnp.int32),
        ),
    )
    kv_grad = lax.psum_scatter(
        kv_terms.reshape(blocks * tokens, 2 * kv_width).astype(jnp.bfloat16),
        "context",
        scatter_dimension=0,
        tiled=True,
    ).astype(jnp.float32)
    grad_value_low = kv_grad[:, kv_width:].astype(jnp.bfloat16)
    grad_key_norm = rotary_apply(
        kv_grad[:, :kv_width].reshape(tokens, kv_local, HEAD_SIZE), cosine_table, -sine_table
    )
    grad_query_norm = rotary_apply(
        grad_query_rot.reshape(tokens, q_local, HEAD_SIZE), cosine_table, -sine_table
    )
    query_inward, query_gain_rows = scale_back(
        query_unrotated, query_factor, full_gain_query.astype(jnp.float32), grad_query_norm
    )
    key_inward, key_gain_rows = scale_back(
        key_unrotated, key_factor, full_gain_key.astype(jnp.float32), grad_key_norm
    )
    grad_query_low = query_inward.astype(jnp.bfloat16).reshape(tokens, q_local * HEAD_SIZE)
    grad_key_low = key_inward.astype(jnp.bfloat16).reshape(tokens, kv_width)
    grad_wquery = contract_rows(hidden_lowered, grad_query_low)
    grad_wkey = contract_rows(hidden_lowered, grad_key_low)
    grad_wvalue = contract_rows(hidden_lowered, grad_value_low)
    grad_h_part = (
        contract_cols(grad_query_low, full_query)
        + contract_cols(grad_key_low, full_key)
        + contract_cols(grad_value_low, full_value)
    )
    grad_h, grad_gain_query, grad_gain_key = (
        lax.psum(grad_h_part.astype(jnp.bfloat16), "tensor").astype(jnp.float32),
        lax.psum(jnp.sum(query_gain_rows, axis=(0, 1)).astype(jnp.bfloat16), "tensor").astype(
            jnp.float32
        ),
        lax.psum(jnp.sum(key_gain_rows, axis=(0, 1)).astype(jnp.bfloat16), "tensor").astype(
            jnp.float32
        ),
    )
    first_inward, first_gain_rows = scale_back(
        x_rows, factor_one, full_gain_attn.astype(jnp.float32), grad_h
    )
    grad_gain_attn = jnp.sum(first_gain_rows, axis=0)
    grad_input = (grad_mid + first_inward).astype(jnp.bfloat16)
    all_shards = (
        lax.psum_scatter(grad_wquery, ("fsdp", "context"), scatter_dimension=0, tiled=True),
        lax.psum_scatter(grad_wkey, ("fsdp", "context"), scatter_dimension=0, tiled=True),
        lax.psum_scatter(grad_wvalue, ("fsdp", "context"), scatter_dimension=0, tiled=True),
        lax.psum_scatter(grad_wout, ("fsdp", "context"), scatter_dimension=1, tiled=True),
        lax.psum_scatter(grad_gate, ("fsdp", "context"), scatter_dimension=0, tiled=True),
        lax.psum_scatter(grad_up, ("fsdp", "context"), scatter_dimension=0, tiled=True),
        lax.psum_scatter(grad_down, ("fsdp", "context"), scatter_dimension=1, tiled=True),
        lax.psum_scatter(grad_gain_attn, ("fsdp", "context"), scatter_dimension=0, tiled=True),
        lax.psum_scatter(grad_gain_ffn, ("fsdp", "context"), scatter_dimension=0, tiled=True),
        lax.psum_scatter(grad_gain_query, ("fsdp", "context"), scatter_dimension=0, tiled=True),
        lax.psum_scatter(grad_gain_key, ("fsdp", "context"), scatter_dimension=0, tiled=True),
    )
    (
        shard_query,
        shard_key,
        shard_value,
        shard_out,
        shard_gate,
        shard_up,
        shard_down,
        shard_gain_attn,
        shard_gain_ffn,
        shard_gain_query,
        shard_gain_key,
    ) = all_shards
    return (
        out_rows.astype(jnp.bfloat16).reshape(1, tokens, width),
        grad_input.reshape(1, tokens, width),
        shard_query,
        shard_key,
        shard_value,
        shard_out,
        shard_gate,
        shard_up,
        shard_down,
        shard_gain_attn,
        shard_gain_ffn,
        shard_gain_query,
        shard_gain_key,
    )


def solution(mesh):
    return jax.shard_map(
        local,
        mesh=mesh,
        in_specs=(
            P("fsdp", "context", None),
            P("fsdp", "context"),
            P(("fsdp", "context"), "tensor"),
            P(("fsdp", "context"), "tensor"),
            P(("fsdp", "context"), "tensor"),
            P("tensor", ("fsdp", "context")),
            P(("fsdp", "context"), "tensor"),
            P(("fsdp", "context"), "tensor"),
            P("tensor", ("fsdp", "context")),
            P(("fsdp", "context")),
            P(("fsdp", "context")),
            P(("fsdp", "context")),
            P(("fsdp", "context")),
            P("fsdp", "context", None),
        ),
        out_specs=(
            P("fsdp", "context", None),
            P("fsdp", "context", None),
            P(("fsdp", "context"), "tensor"),
            P(("fsdp", "context"), "tensor"),
            P(("fsdp", "context"), "tensor"),
            P("tensor", ("fsdp", "context")),
            P(("fsdp", "context"), "tensor"),
            P(("fsdp", "context"), "tensor"),
            P("tensor", ("fsdp", "context")),
            P(("fsdp", "context")),
            P(("fsdp", "context")),
            P(("fsdp", "context")),
            P(("fsdp", "context")),
        ),
        check_vma=False,
    )
```

profile of v0, /device:TPU:0, one launch (start us, length us, event | category | flops | bytes accessed | tf_op | source)
XLA Modules:
  0.0 1409.3 jit_solution(14619079919306792789)
XLA Ops:
  10.0 1.3 fusion.75
  16.0 44.3 %all-reduce.9 = (bf16[1024]{0:T(1024)(128)(2,1)S(1)}, bf16[128]{0:T(256)(128)(2,1)S(1)}, bf16[128]{0:T(256)(128)(2,1)S(1)}, bf16[1024]{0:T(1024)(128)(2,1)S(1)}) all-reduce(bf16[1024]{0:T(1024)(128)(2,1)S(1)} %dynamic-update-slice, ...), channel_id=1, replica_groups=mesh['fsdp'=4,'context'=4,'tensor'=2] {'fsdp','context'}, use_global_device_ids=true, to_apply=%add | all-reduce | flops 2304 | bytes 9216
  60.4 6.2 all-gather
  66.6 1.1 fusion.38
  67.9 1.0 all-gather.9.cloned.1.call-done
  68.9 1.5 copy.99
  70.4 1.5 multiply_reduce_fusion.7
  72.2 10.9 all_gather.63
  83.3 42.3 %all-gather.13.cloned.1.call-done = bf16[1024,512]{1,0:T(8,128)(2,1)} async-done(((bf16[64,512]{1,0:T(8,128)(2,1)}), bf16[1024,512]{1,0:T(8,128)(2,1)}) %all-gather.13.cloned.1.call-update) | async-done | bytes 1048592 | tf_op jit(solution)/shard_map/all_gather | solution.py:68
  125.6 1.6 convolution_convert_fusion.2
  127.2 10.2 all_gather.67
  137.4 1.0 copy.104
  138.5 49.2 %all-gather.11.cloned.1.call-done = bf16[1024,1024]{1,0:T(8,128)(2,1)} async-done(((bf16[64,1024]{1,0:T(8,128)(2,1)}), bf16[1024,1024]{1,0:T(8,128)(2,1)}) %all-gather.11.cloned.1.call-update) | async-done | bytes 2097168 | tf_op jit(solution)/shard_map/all_gather | solution.py:66
  187.6 2.9 copy.101
  192.4 12.1 while.36
  195.0 1.8 conditional.4
  195.0 0.9 constant_dynamic-slice_fusion
  204.8 44.6 %all-gather.15.cloned.1.call-done = bf16[1024,1024]{0,1:T(8,128)(2,1)} async-done(((bf16[1024,64]{0,1:T(8,128)(2,1)}), bf16[1024,1024]{0,1:T(8,128)(2,1)}) %all-gather.15.cloned.1.call-update) | async-done | bytes 2097168 | tf_op jit(solution)/shard_map/all_gather | solution.py:69
  249.4 3.1 convolution_convert_fusion.1
  254.7 15.0 %all-reduce.16.cloned.1.call-done = bf16[128,1024]{1,0:T(8,128)(2,1)} async-done(((bf16[128,1024]{1,0:T(8,128)(2,1)}), bf16[128,1024]{1,0:T(8,128)(2,1)}) %all-reduce.16.cloned.1.call-update) | async-done | bytes 262160 | tf_op jit(solution)/shard_map/psum | solution.py:176
  269.8 1.1 multiply_reduce_fusion.3
  270.9 1.1 multiply_convert_fusion.4
  272.0 69.5 %all-gather.17.cloned.1.call-done = bf16[1024,1536]{1,0:T(8,128)(2,1)} async-done(((bf16[64,1536]{1,0:T(8,128)(2,1)}), bf16[1024,1536]{1,0:T(8,128)(2,1)}) %all-gather.17.cloned.1.call-update) | async-done | bytes 3145744 | tf_op jit(solution)/shard_map/all_gather | solution.py:70
  341.5 2.5 fusion.76
  344.0 66.7 %all-gather.19.cloned.1.call-done = bf16[1024,1536]{1,0:T(8,128)(2,1)} async-done(((bf16[64,1536]{1,0:T(8,128)(2,1)}), bf16[1024,1536]{1,0:T(8,128)(2,1)}) %all-gather.19.cloned.1.call-update) | async-done | bytes 3145744 | tf_op jit(solution)/shard_map/all_gather | solution.py:71
  410.7 2.5 fusion.77
  413.2 66.7 %all-gather.21.cloned.1.call-done = bf16[1536,1024]{0,1:T(8,128)(2,1)} async-done(((bf16[1536,64]{0,1:T(8,128)(2,1)}), bf16[1536,1024]{0,1:T(8,128)(2,1)}) %all-gather.21.cloned.1.call-update) | async-done | bytes 3145744 | tf_op jit(solution)/shard_map/all_gather | solution.py:72
  479.9 3.6 multiply_convert_fusion
  483.6 1.1 fusion.78
  484.7 1.0 copy-done.1
  485.7 1.8 fusion.16
  487.8 2.1 copy.108
  489.9 2.1 copy.109
  492.0 12.5 all-reduce.18.cloned.1.call-done
  504.5 1.3 fusion.34
  505.9 2.1 fusion.59
  508.1 21.2 %while.37 = (s32[]{:T(128)}, f32[128,4,2,128]{3,0,2,1:T(8,128)S(1)}, bf16[4,128,1024]{2,1,0:T(8,128)(2,1)}, s32[4]{0:T(128)S(1)}, s32[128]{0:T(128)S(1)}, /*inde...) while((s32[]{:T(128)}, ...), condition=%wide.region_17.0_spmd, body=%wide.region_14.17_spmd.sunk | while | flops 169525376 | bytes 7250243 | solution.py:402
  511.9 2.5 conditional.5
  511.9 1.0 constant_dynamic-slice_fusion.2
  529.5 3.8 convolution_convert_fusion
  535.1 1.7 fusion.79
  536.8 25.9 %reduce-scatter.9.cloned.1.call-done = bf16[128,1024]{1,0:T(8,128)(2,1)} async-done(((bf16[512,1024]{1,0:T(8,128)(2,1)}), bf16[128,1024]{1,0:T(8,128)(2,1)}) %reduce-scatter.9.cloned.1.call-update) | async-done | bytes 262160 | tf_op jit(solution)/shard_map/reduce_scatter | solution.py:412
  562.7 0.9 slice_convert_fusion
  564.5 1.0 multiply_subtract_fusion.1
  565.8 1.5 convolution_add_fusion.1
  567.4 1.2 fusion.17
  568.6 1.9 fusion.52
  570.6 1.8 fusion.61
  572.6 2.9 fusion.57
  576.4 2.8 fusion.54
  580.3 3.6 fusion.80
  584.0 0.9 copy-done.24
  584.9 3.6 fusion.81
  589.5 3.6 fusion.44
  594.5 2.5 all-reduce.10
  596.9 1.2 fusion.37
  598.2 76.0 %all-reduce.8 = (f32[1024]{0:T(1024)S(1)}, f32[1024]{0:T(1024)S(1)}, f32[128]{0:T(128)S(1)}, f32[128]{0:T(128)S(1)}) all-reduce(f32[1024]{0:T(1024)S(1)} %get-tuple-element.555, f32[1024]{0:T(1024)S(1)} %get-tuple-element.551, ...), channel_id=11, replica_groups=mesh['fsdp'=4,'context'=4,'tensor'=2] {'fsdp','context'}, use_global_device_ids=true, to_apply=%region_31.32.clone | all-reduce | flops 2304 | bytes 17920
  676.6 2.2 fusion.43
  678.8 75.3 %reduce-scatter.15.cloned.1.call-done = f32[64,512]{1,0:T(8,128)} async-done(((f32[1024,512]{1,0:T(8,128)}), f32[64,512]{1,0:T(8,128)}) %reduce-scatter.15.cloned.1.call-update) | async-done | bytes 131088 | tf_op jit(solution)/shard_map/reduce_scatter | solution.py:458
  754.1 94.5 %reduce-scatter.17.cloned.1.call-done = f32[1024,64]{0,1:T(8,128)} async-done(((f32[1024,1024]{0,1:T(8,128)}), f32[1024,64]{0,1:T(8,128)}) %reduce-scatter.17.cloned.1.call-update) | async-done | bytes 262160 | tf_op jit(solution)/shard_map/reduce_scatter | solution.py:459
  848.6 97.5 %reduce-scatter.11.cloned.1.call-done = f32[64,1024]{1,0:T(8,128)} async-done(((f32[1024,1024]{1,0:T(8,128)}), f32[64,1024]{1,0:T(8,128)}) %reduce-scatter.11.cloned.1.call-update) | async-done | bytes 262160 | tf_op jit(solution)/shard_map/reduce_scatter | solution.py:456
  946.1 152.8 %reduce-scatter.19.cloned.1.call-done = f32[64,1536]{1,0:T(8,128)} async-done(((f32[1024,1536]{1,0:T(8,128)}), f32[64,1536]{1,0:T(8,128)}) %reduce-scatter.19.cloned.1.call-update) | async-done | bytes 393232 | tf_op jit(solution)/shard_map/reduce_scatter | solution.py:460
  1098.9 151.8 %reduce-scatter.21.cloned.1.call-done = f32[64,1536]{1,0:T(8,128)} async-done(((f32[1024,1536]{1,0:T(8,128)}), f32[64,1536]{1,0:T(8,128)}) %reduce-scatter.21.cloned.1.call-update) | async-done | bytes 393232 | tf_op jit(solution)/shard_map/reduce_scatter | solution.py:461
  1250.6 151.8 %reduce-scatter.23.cloned.1.call-done = f32[1536,64]{0,1:T(8,128)} async-done(((f32[1536,1024]{0,1:T(8,128)}), f32[1536,64]{0,1:T(8,128)}) %reduce-scatter.23.cloned.1.call-update) | async-done | bytes 393232 | tf_op jit(solution)/shard_map/reduce_scatter | solution.py:462
  (208 shorter events, 38.1 us)
Async XLA Ops:
  7.2 61.7 %all-gather.9.cloned.1.call-start = ((), (), s32[]{:S(2)}) async-start(), calls=%async_computation.8 | async-start | bytes 1114112 | tf_op jit(solution)/shard_map/all_gather | solution.py:67
  7.9 117.7 %all-gather.13.cloned.1.call-start = ((), (), s32[]{:S(2)}) async-start(), calls=%async_computation.10 | async-start | bytes 1114112 | tf_op jit(solution)/shard_map/all_gather | solution.py:68
  8.7 179.0 %all-gather.11.cloned.1.call-start = ((), (), s32[]{:S(2)}) async-start(), calls=%async_computation.9 | async-start | bytes 2228224 | tf_op jit(solution)/shard_map/all_gather | solution.py:66
  9.4 240.0 %all-gather.15.cloned.1.call-start = ((), (), s32[]{:S(2)}) async-start(), calls=%async_computation.11 | async-start | bytes 2228224 | tf_op jit(solution)/shard_map/all_gather | solution.py:69
  10.0 259.8 %all-reduce.16.cloned.1.call-start = ((), (), s32[]{:S(2)}) async-start(), calls=%async_computation.12 | async-start | bytes 524288 | tf_op jit(solution)/shard_map/psum | solution.py:176
  68.9 56.7 %copy-start = (bf16[1,128,1024]{2,1,0:T(8,128)(2,1)S(1)}, bf16[1,128,1024]{2,1,0:T(8,128)(2,1)}, u32[]{:S(2)}) copy-start(bf16[1,128,1024]{2,1,0:T(8,128)(2,1)} %param.22) | copy-start | bytes 786436
  83.1 104.5 %copy-start.8 = (bf16[512,512]{1,0:T(8,128)(2,1)}, bf16[512,512]{1,0:T(8,128)(2,1)S(1)}, u32[]{:S(2)}) copy-start(bf16[512,512]{1,0:T(8,128)(2,1)S(1)} %all_gather.63) | copy-start | bytes 1572868
  137.4 50.2 %copy-start.9 = (bf16[512,512]{1,0:T(8,128)(2,1)}, bf16[512,512]{1,0:T(8,128)(2,1)S(1)}, u32[]{:S(2)}) copy-start(bf16[512,512]{1,0:T(8,128)(2,1)S(1)} %all_gather.67) | copy-start | bytes 1572868
  190.5 1.9 copy-start.29
  191.3 0.8 copy-start.5
  204.8 139.2 %copy-start.10 = (f32[128,4,2,128]{0,3,2,1:T(8,128)}, f32[128,4,2,128]{0,3,2,1:T(8,128)S(1)}, u32[]{:S(2)}) copy-start(f32[128,4,2,128]{0,3,2,1:T(8,128)S(1)} %copy.105) | copy-start | bytes 1572868
  204.8 136.7 %copy-start.21 = (bf16[128,4,2,128]{0,3,2,1:T(8,128)(2,1)}, bf16[128,4,2,128]{0,3,2,1:T(8,128)(2,1)S(1)}, u32[]{:S(2)}) copy-start(bf16[128,4,2,128]{0,3,2,1:T(8,128)(2,1)S(1)} %fusion.56) | copy-start | bytes 786436
  252.6 88.9 %all-gather.17.cloned.1.call-start = ((), (), s32[]{:S(2)}) async-start(), calls=%async_computation.13 | async-start | bytes 3342336 | tf_op jit(solution)/shard_map/all_gather | solution.py:70
  253.2 157.6 %all-gather.19.cloned.1.call-start = ((), (), s32[]{:S(2)}) async-start(), calls=%async_computation.14 | async-start | bytes 3342336 | tf_op jit(solution)/shard_map/all_gather | solution.py:71
  253.9 226.0 %all-gather.21.cloned.1.call-start = ((), (), s32[]{:S(2)}) async-start(), calls=%async_computation.15 | async-start | bytes 3342336 | tf_op jit(solution)/shard_map/all_gather | solution.py:72
  254.7 249.8 %all-reduce.18.cloned.1.call-start = ((), (), s32[]{:S(2)}) async-start(), calls=%async_computation.16 | async-start | bytes 524288 | tf_op jit(solution)/shard_map/psum | solution.py:317
  344.0 135.9 %copy-start.14 = (bf16[1,128,1024]{2,1,0:T(8,128)(2,1)S(1)}, bf16[1,128,1024]{2,1,0:T(8,128)(2,1)}, u32[]{:S(2)}) copy-start(bf16[1,128,1024]{2,1,0:T(8,128)(2,1)} %param.35) | copy-start | bytes 786436
  479.9 3.6 copy-start.2
  483.5 1.1 copy-start.25
  483.5 1.1 copy-start.23
  483.5 2.2 copy-start.1
  485.7 18.8 %copy-start.3 = (bf16[128,1024]{1,0:T(8,128)(2,1)S(1)}, bf16[128,1024]{1,0:T(8,128)(2,1)}, u32[]{:S(2)}) copy-start(bf16[128,1024]{1,0:T(8,128)(2,1)} %all-reduce.16.cloned.1.call-done) | copy-start | bytes 786436
  485.7 20.1 %copy-start.4 = (bf16[1024,1024]{0,1:T(8,128)(2,1)S(1)}, bf16[1024,1024]{0,1:T(8,128)(2,1)}, u32[]{:S(2)}) copy-start(bf16[1024,1024]{0,1:T(8,128)(2,1)} %all-gather.15.cloned.1.call-done) | copy-start | bytes 6291460
  487.6 75.1 %reduce-scatter.9.cloned.1.call-start = ((), (), s32[]{:S(2)}) async-start(), calls=%async_computation.17 | async-start | bytes 1310720 | tf_op jit(solution)/shard_map/reduce_scatter | solution.py:412
  504.5 3.4 copy-start.11
  508.1 21.3 %copy-start.17 = (bf16[128,1536]{1,0:T(8,128)(2,1)S(1)}, bf16[128,1536]{1,0:T(8,128)(2,1)}, u32[]{:S(2)}) copy-start(bf16[128,1536]{1,0:T(8,128)(2,1)} %get-tuple-element.623) | copy-start | bytes 1179652
  529.4 4.1 copy-start.6
  529.4 67.5 %all-reduce.20.cloned.1.call-start = ((), (), s32[]{:S(2)}) async-start(), calls=%async_computation.25 | async-start | bytes 1048576 | tf_op jit(solution)/shard_map/psum | solution.py:185
  533.4 1.7 copy-start.7
  533.7 32.1 %copy-start.12 = (bf16[1024,512]{1,0:T(8,128)(2,1)S(1)}, bf16[1024,512]{1,0:T(8,128)(2,1)}, u32[]{:S(2)}) copy-start(bf16[1024,512]{1,0:T(8,128)(2,1)} %all-gather.9.cloned.1.call-done) | copy-start | bytes 3145732
  533.9 0.7 copy-start.19
  536.8 30.6 %copy-start.13 = (bf16[1024,512]{1,0:T(8,128)(2,1)S(1)}, bf16[1024,512]{1,0:T(8,128)(2,1)}, u32[]{:S(2)}) copy-start(bf16[1024,512]{1,0:T(8,128)(2,1)} %all-gather.13.cloned.1.call-done) | copy-start | bytes 3145732
  564.5 2.9 copy-start.27
  567.4 3.2 copy-start.28
  568.6 110.2 %reduce-scatter.13.cloned.1.call-start = ((), (), s32[]{:S(2)}) async-start(), calls=%async_computation.19 | async-start | bytes 2228224 | tf_op jit(solution)/shard_map/reduce_scatter | solution.py:457
  570.5 2.0 copy-start.15
  570.5 2.0 copy-start.16
  570.5 2.0 copy-start.22
  570.6 183.5 %reduce-scatter.15.cloned.1.call-start = ((), (), s32[]{:S(2)}) async-start(), calls=%async_computation.20 | async-start | bytes 2228224 | tf_op jit(solution)/shard_map/reduce_scatter | solution.py:458
  572.5 276.1 %reduce-scatter.17.cloned.1.call-start = ((), (), s32[]{:S(2)}) async-start(), calls=%async_computation.21 | async-start | bytes 4456448 | tf_op jit(solution)/shard_map/reduce_scatter | solution.py:459
  575.5 1.0 copy-start.20
  575.5 370.6 %reduce-scatter.11.cloned.1.call-start = ((), (), s32[]{:S(2)}) async-start(), calls=%async_computation.18 | async-start | bytes 4456448 | tf_op jit(solution)/shard_map/reduce_scatter | solution.py:456
  579.3 1.0 copy-start.26
  579.3 519.6 %reduce-scatter.19.cloned.1.call-start = ((), (), s32[]{:S(2)}) async-start(), calls=%async_computation.22 | async-start | bytes 6684672 | tf_op jit(solution)/shard_map/reduce_scatter | solution.py:460
  583.9 1.0 copy-start.24
  583.9 666.7 %reduce-scatter.21.cloned.1.call-start = ((), (), s32[]{:S(2)}) async-start(), calls=%async_computation.23 | async-start | bytes 6684672 | tf_op jit(solution)/shard_map/reduce_scatter | solution.py:461
  588.5 1.0 copy-start.18
  588.5 813.9 %reduce-scatter.23.cloned.1.call-start = ((), (), s32[]{:S(2)}) async-start(), calls=%async_computation.24 | async-start | bytes 6684672 | tf_op jit(solution)/shard_map/reduce_scatter | solution.py:462
Sparse Core Ops, SparseCore 0:
  10.7 58.1 all-gather.8
  71.7 53.9 all-gather.12
  128.4 59.2 all-gather.10
  190.3 59.1 all-gather.14
  252.7 17.0 all-reduce.15
  272.4 69.0 all-gather.16
  344.3 66.3 all-gather.18
  413.5 66.3 all-gather.20
  487.7 16.7 all-reduce.17
  529.5 33.1 reduce-scatter.8
  568.7 18.6 all-reduce.19
  590.1 82.9 reduce-scatter.12
  675.9 78.1 reduce-scatter.14
  756.8 91.7 reduce-scatter.16
  851.3 94.7 reduce-scatter.10
  951.8 147.0 reduce-scatter.18
  1104.5 146.0 reduce-scatter.20
  1256.3 146.0 reduce-scatter.22
where the time goes:
time: 1410 us
  waiting for transfers between devices  1120 us (79%)
  blocking collectives  150 us (11%)
  matrix products  51 us (4%)
  local copies, waits for them, and re-layouts  42.6 us (3%)
  between operations  17.5 us (1%)
    reduce_scatter x1, waiting for transfers between devices, local(): lax.psum_scatter(grad_gate, ('fsdp', 'context'), scatter_dimension=0, til...  153 us
    reduce_scatter x1, waiting for transfers between devices, local(): lax.psum_scatter(grad_down, ('fsdp', 'context'), scatter_dimension=1, til...  152 us
    reduce_scatter x1, waiting for transfers between devices, local(): lax.psum_scatter(grad_up, ('fsdp', 'context'), scatter_dimension=0, tiled...  152 us
    unnamed x2, blocking collectives  120 us
    reduce_scatter x1, waiting for transfers between devices, local(): lax.psum_scatter(grad_wquery, ('fsdp', 'context'), scatter_dimension=0, t...  97.5 us
    reduce_scatter x1, waiting for transfers between devices, local(): lax.psum_scatter(grad_wout, ('fsdp', 'context'), scatter_dimension=1, til...  94.5 us
    reduce_scatter x1, waiting for transfers between devices, local(): lax.psum_scatter(grad_wvalue, ('fsdp', 'context'), scatter_dimension=0, t...  75.3 us
    all_gather x1, waiting for transfers between devices, gather_weights(): lax.all_gather(w_gate, ('fsdp', 'context'), axis=0, tiled=True)  69.5 us
  transfers between devices with their start and end apart: 18, of which 16 were waited for; matrix products, arithmetic and copies ran while one was open for 5% of the time, Pallas kernels for 0%

commit v1 on v0

v1 whole, which is shorter than its diff:
```python
import jax
import jax.numpy as jnp
from jax import lax
from jax.sharding import PartitionSpec as P

HEAD = 128
EPS = 1e-06
THETA = 1000000.0
BF = jnp.bfloat16
F32 = jnp.float32


def mm(a, b):
    return lax.dot_general(a, b, (((1,), (0,)), ((), ())), preferred_element_type=F32)


def mm_t(a, b):
    return lax.dot_general(a, b, (((1,), (1,)), ((), ())), preferred_element_type=F32)


def mt_m(a, b):
    return lax.dot_general(a, b, (((0,), (0,)), ((), ())), preferred_element_type=F32)


def norm_rows(v, g):
    r = lax.rsqrt(jnp.mean(v * v, axis=-1, keepdims=True) + EPS)
    return v * r * g, r


def norm_back(v, r, g, up):
    n = v * r
    w = up * g
    return r * (w - n * jnp.mean(w * n, axis=-1, keepdims=True)), up * n


def rope(v, cos, sin):
    a = v[..., : HEAD // 2]
    b = v[..., HEAD // 2 :]
    return jnp.concatenate([a * cos - b * sin, b * cos + a * sin], axis=-1)


def swap(x, axis, n, k):
    return lax.ppermute(x, axis, [(i, i ^ k) for i in range(n)])


def gather(x, axis, n):
    return [x] + [swap(x, axis, n, k) for k in range(1, n)]


def scatter(blocks, axis, n):
    return [blocks[0]] + [swap(blocks[k], axis, n, k) for k in range(1, n)]


def absolute(blocks, me, n):
    s = jnp.stack(blocks)
    return [lax.dynamic_index_in_dim(s, me ^ j, 0, keepdims=False) for j in range(n)]


def cols(w, start, width):
    return lax.dynamic_slice_in_dim(w, start, width, 1)


def lanes(v, width=128):
    return jnp.concatenate([v, jnp.zeros((width - v.shape[0],), v.dtype)])


def solution(mesh):
    F, C, T = mesh.shape["fsdp"], mesh.shape["context"], mesh.shape["tensor"]

    def local(
        hidden, segments, w_query, w_key, w_value, w_out, w_gate, w_up, w_down,
        gain_attn, gain_ffn, gain_query, gain_key, cotangent,
    ):
        f, c, t = lax.axis_index("fsdp"), lax.axis_index("context"), lax.axis_index("tensor")
        tokens, width = hidden.shape[1], hidden.shape[2]
        half = tokens // T
        rows = w_query.shape[0]
        grow = gain_query.shape[0]
        kv_local = w_key.shape[1] // HEAD
        qc = w_query.shape[1] // C
        kw = max(HEAD, w_key.shape[1] // C)
        hc = w_gate.shape[1] // F
        hp = -(-hc // 128) * 128
        qh, kh = qc // HEAD, kw // HEAD
        group = qh // kh
        aw = qc + 2 * kw
        R = T * C * half
        scale = HEAD ** (-0.5)

        def my_half(x):
            return lax.dynamic_slice_in_dim(x, t * half, half, 0)

        def swap_t(x):
            return swap(x, "tensor", T, 1)

        hid = hidden.reshape(tokens, width)
        x_half = my_half(hid)
        seg_half = my_half(segments.reshape(tokens)).astype(BF)
        seg_rows = jnp.zeros((8, width), BF).at[0, :half].set(seg_half)
        xs = jnp.stack(gather(jnp.concatenate([x_half, seg_rows], 0), "context", C))
        xs = jnp.stack([xs, swap_t(xs)])
        x_all = xs[:, :, :half].reshape(R, width).astype(F32)
        seg = xs[:, :, half, :half].reshape(R).astype(jnp.int32)

        gains = jnp.concatenate(
            [lanes(jnp.concatenate([gain_attn, gain_ffn])), lanes(gain_query), lanes(gain_key, aw - 256)]
        )
        gains = jnp.concatenate([gains[None], jnp.zeros((7, aw), BF)], 0)

        def attn_cols(d):
            ks = (d * kv_local // C) * HEAD
            return jnp.concatenate([cols(w_query, d * qc, qc), cols(w_key, ks, kw), cols(w_value, ks, kw)], 1)

        wq_parts = [jnp.concatenate([attn_cols(c ^ k), gains], 0) for k in range(C)]
        wq = jnp.stack(absolute(scatter(wq_parts, "context", C), c, C))
        wq = jnp.stack(absolute(gather(wq, "fsdp", F), f, F))
        g_rows = wq[:, :, rows].astype(F32)
        g_attn = g_rows[:, :, :rows].reshape(width)
        g_ffn = g_rows[:, :, rows : 2 * rows].reshape(width)
        g_q = g_rows[:, :, 128 : 128 + grow].reshape(HEAD)
        g_k = g_rows[:, :, 256 : 256 + grow].reshape(HEAD)
        w_qkv = wq[:, :, :rows].reshape(width, aw)
        wo_t = w_out.T
        wo = jnp.stack(absolute(scatter([cols(wo_t, (c ^ k) * qc, qc) for k in range(C)], "context", C), c, C))
        wo = jnp.stack(absolute(gather(wo, "fsdp", F), f, F)).reshape(width, qc)
        wd_t = w_down.T

        def ffn_cols(d):
            pad = jnp.zeros((rows, hp - hc), BF)
            return jnp.concatenate(sum([[cols(w, d * hc, hc), pad] for w in (w_gate, w_up, wd_t)], []), 1)

        wf = jnp.stack(absolute(scatter([ffn_cols(f ^ k) for k in range(F)], "fsdp", F), f, F))
        wf = jnp.stack(absolute(gather(wf, "context", C), c, C), 1).reshape(width, 3 * hp)
        wg, wu, wd = wf[:, :hp], wf[:, hp : 2 * hp], wf[:, 2 * hp :]

        idx = jnp.arange(R, dtype=jnp.int32)
        trel, k, i = idx // (C * half), (idx // half) % C, idx % half
        pos = (c ^ k) * tokens + (t ^ trel) * half + i
        freq = THETA ** (-(jnp.arange(HEAD // 2, dtype=F32) * 2.0 / HEAD))
        angle = pos.astype(F32)[:, None] * freq[None, :]
        cos, sin = jnp.cos(angle), jnp.sin(angle)
        allowed = (seg[:, None] == seg[None, :]) & (pos[:, None] >= pos[None, :])

        def head(x, j):
            return x[:, j * HEAD : (j + 1) * HEAD]

        def reduce(part, axis, n):
            own = part[: R // 2] + swap_t(part[R // 2 :].astype(BF)).astype(F32)
            own = own.reshape(n, half, width)
            got = scatter([own[0]] + [own[j].astype(BF) for j in range(1, n)], axis, n)
            return sum([b.astype(F32) for b in got])

        def spread(x, axis, n):
            s = jnp.stack(gather(x, axis, n))
            return jnp.stack([s, swap_t(s)]).reshape(R, width)

        def both_halves(x):
            y = swap_t(x)
            return jnp.where(t == 0, jnp.concatenate([x, y], 0), jnp.concatenate([y, x], 0))

        dy = spread(my_half(cotangent.reshape(tokens, width)), "fsdp", F)

        h, r1 = norm_rows(x_all, g_attn)
        h = h.astype(BF)
        raw = mm(h, w_qkv)
        q_raw = [head(raw, j) for j in range(qh)]
        k_raw = [head(raw, qh + j) for j in range(kh)]
        v = [head(raw, qh + kh + j).astype(BF) for j in range(kh)]
        qn = [norm_rows(a, g_q) for a in q_raw]
        kn = [norm_rows(a, g_k) for a in k_raw]
        q = [rope(a, cos, sin).astype(BF) for a, _ in qn]
        ky = [rope(a, cos, sin).astype(BF) for a, _ in kn]
        ex, tot, at = [], [], []
        for j in range(qh):
            s = mm_t(q[j], ky[j // group]) * scale
            e = jnp.where(allowed, jnp.exp(s), 0.0)
            total = jnp.sum(e, -1, keepdims=True)
            ex.append(e)
            tot.append(total)
            at.append(mm(e.astype(BF), v[j // group]) / total)
        o = jnp.concatenate([a.astype(BF) for a in at], 1)
        branch = reduce(mm_t(o, wo), "context", C)
        x_mid = x_half.astype(F32) + branch
        h2h, r2 = norm_rows(x_mid, g_ffn)
        h2 = spread(h2h.astype(BF), "fsdp", F)

        gate, up = mm(h2, wg), mm(h2, wu)
        sg = jax.nn.sigmoid(gate)
        u = (gate * sg * up).astype(BF)
        du = mm(dy, wd)
        d_gate = (du * up * sg * (1.0 + gate * (1.0 - sg))).astype(BF)
        d_up = (du * gate * sg).astype(BF)
        dh2 = reduce(mm_t(d_gate, wg) + mm_t(d_up, wu), "fsdp", F)
        out = (x_mid + reduce(mm_t(u, wd), "fsdp", F)).astype(BF)
        gf = jnp.concatenate([mt_m(h2, d_gate), mt_m(h2, d_up), mt_m(dy, u)], 1).astype(BF)
        gf = gf.reshape(F, C, rows, 3 * hp)
        gf = scatter([lax.dynamic_index_in_dim(gf, c ^ j, 1, keepdims=False) for j in range(C)], "context", C)
        gf = sum([b.astype(F32) for b in gf]).astype(BF)
        gf = scatter([lax.dynamic_index_in_dim(gf, f ^ j, 0, keepdims=False) for j in range(F)], "fsdp", F)
        gf = jnp.stack(absolute(gf, f, F), 1).astype(F32)
        ffn_grads = [gf[:, :, j * hp : j * hp + hc].reshape(rows, F * hc) for j in range(3)]

        inward, gn_rows = norm_back(x_mid, r2, g_ffn, dh2)
        dg_ffn = jnp.sum(gn_rows, 0)
        dx_mid = my_half(cotangent.reshape(tokens, width)).astype(F32) + inward
        dx = spread(dx_mid.astype(BF), "context", C)

        g_o = mt_m(dx, o).astype(BF)
        g_att = mm(dx, wo)
        dq, dk, dv = [], [0.0] * kh, [0.0] * kh
        for j in range(qh):
            g = head(g_att, j)
            gs = (g / tot[j]).astype(BF)
            dt = -jnp.sum(g * at[j], -1, keepdims=True) / tot[j]
            dv[j // group] += mt_m(ex[j].astype(BF), gs)
            ds = (ex[j] * (mm_t(gs, v[j // group]) + dt)).astype(BF)
            dq.append(mm(ds, ky[j // group]) * scale)
            dk[j // group] += mt_m(ds, q[j]) * scale
        dgq, dgk, draw = 0.0, 0.0, []
        for j in range(qh):
            a, b = norm_back(q_raw[j], qn[j][1], g_q, rope(dq[j], cos, -sin))
            draw.append(a.astype(BF))
            dgq += jnp.sum(b, 0)
        for j in range(kh):
            a, b = norm_back(k_raw[j], kn[j][1], g_k, rope(dk[j], cos, -sin))
            draw.append(a.astype(BF))
            dgk += jnp.sum(b, 0)
        draw = jnp.concatenate(draw + [a.astype(BF) for a in dv], 1)
        dh_part = mm_t(draw, w_qkv)
        dg_attn = jnp.sum(dh_part * (x_all * r1), 0)
        gq = mt_m(h, draw).reshape(F, C, rows, aw)
        extra = jnp.concatenate(
            [
                dg_attn.reshape(F, C, rows), dg_ffn.reshape(F, C, rows),
                jnp.zeros((F, C, 128 - 2 * rows), F32),
                dgq.reshape(F, C, grow), jnp.zeros((F, C, 128 - grow), F32),
                dgk.reshape(F, C, grow), jnp.zeros((F, C, aw - 256 - grow), F32),
            ],
            2,
        )[:, :, None]
        gq = jnp.concatenate([gq, extra, jnp.zeros((F, C, 7, aw), F32)], 2).astype(BF)

        def to_owner(g):
            g = scatter([lax.dynamic_index_in_dim(g, f ^ j, 0, keepdims=False) for j in range(F)], "fsdp", F)
            g = sum([b.astype(F32) for b in g]).astype(BF)
            g = scatter([lax.dynamic_index_in_dim(g, c ^ j, 0, keepdims=False) for j in range(C)], "context", C)
            return jnp.stack(absolute(g, c, C)).astype(F32)

        gq = to_owner(gq)
        go = to_owner(g_o.reshape(F, C, rows, qc))
        dh = reduce(dh_part, "context", C)
        inward, _ = norm_back(x_half.astype(F32), lax.rsqrt(jnp.mean(x_half.astype(F32) ** 2, -1, keepdims=True) + EPS), g_attn, dh)
        grad_hidden = (dx_mid + inward).astype(BF)

        ge = jnp.sum(gq[:, rows], 0)
        ge = ge + swap_t(ge)
        share = kw * C // w_key.shape[1]
        gq = jnp.swapaxes(gq[:, :rows], 0, 1)

        def kv_grad(g):
            return g.reshape(rows, C // share, share, kw).sum(2).reshape(rows, w_key.shape[1])

        return (
            both_halves(out).reshape(1, tokens, width),
            both_halves(grad_hidden).reshape(1, tokens, width),
            gq[:, :, :qc].reshape(rows, C * qc),
            kv_grad(gq[:, :, qc : qc + kw]),
            kv_grad(gq[:, :, qc + kw :]),
            jnp.swapaxes(go, 0, 1).reshape(rows, C * qc).T,
            ffn_grads[0], ffn_grads[1], ffn_grads[2].T,
            ge[:rows], ge[rows : 2 * rows], ge[128 : 128 + grow], ge[256 : 256 + grow],
        )

    both = ("fsdp", "context")
    seq, row, col, vec = P("fsdp", "context", None), P(both, "tensor"), P("tensor", both), P(both)
    return jax.shard_map(
        local,
        mesh=mesh,
        in_specs=(seq, P("fsdp", "context"), row, row, row, col, row, row, col, vec, vec, vec, vec, seq),
        out_specs=(seq, seq, row, row, row, col, row, row, col, vec, vec, vec, vec),
        check_vma=False,
    )
```

time: 1410 us -> 307 us (0.22)
  waiting for transfers between devices: 1120 us -> 119 us
  blocking collectives: 150 us -> 0 us
  starting transfers between devices: 0.9 us -> 87.8 us
  matrix products: 51 us -> 25.5 us
  other arithmetic: 11.7 us -> 37.1 us
  between operations: 17.5 us -> 2.24 us
    reduce_scatter x8 -> x0, waiting for transfers between devices: 750 us -> none  [the longest x1 153 us: local(): lax.psum_scatter(grad_gate, ('fsdp', 'context'), scatter_dimension=0, til...]
    all_gather x7 -> x0, waiting for transfers between devices: 340 us -> none  [the longest x1 69.5 us: gather_weights(): lax.all_gather(w_gate, ('fsdp', 'context'), axis=0, tiled=True)]
    unnamed x2 -> x0, blocking collectives: 120 us -> none
    ppermute x0 -> x71, waiting for transfers between devices: none -> 119 us  [swap(): return lax.ppermute(x, axis, [(i, i ^ k) for i in range(n)])]
    ppermute x0 -> x71, starting transfers between devices: none -> 87.8 us  [swap(): return lax.ppermute(x, axis, [(i, i ^ k) for i in range(n)])]
    psum x3 -> x0, waiting for transfers between devices: 27.6 us -> none  [the longest x1 15 us: forward_pass(): lax.psum(jnp.dot(attn_low, w_out, preferred_element_type=jnp.float32).ast...]
    all_gather x3 -> x0, blocking collectives: 27.3 us -> none  [the longest x1 10.9 us: forward_pass(): key_rows = lax.all_gather(key_low, 'context', axis=0, tiled=True)]
    dot_general x27, matrix products: 49 us -> 25.5 us  [the longest x9 11.7 us: mm_t(): lax.dot_general(a, b, (((1,), (1,)), ((), ())), preferred_element_type=F32)]
  transfers between devices with their start and end apart: 18 -> 71, of which waited for: 16 -> 33; matrix products, arithmetic and copies ran while one was open for 5% -> 19% of each run, Pallas kernels for 0% -> 0%
where the time goes in v1:
time: 307 us; the launch traced here: 306 us
  waiting for transfers between devices  119 us (39%)
  starting transfers between devices  87.8 us (29%)
  other arithmetic  37.1 us (12%)
  local copies, waits for them, and re-layouts  35.1 us (11%)
  matrix products  25.5 us (8%)
    ppermute x71, waiting for transfers between devices, swap(): return lax.ppermute(x, axis, [(i, i ^ k) for i in range(n)])  119 us
    ppermute x71, starting transfers between devices, swap(): return lax.ppermute(x, axis, [(i, i ^ k) for i in range(n)])  87.8 us
    dot_general x9, matrix products, mm_t(): lax.dot_general(a, b, (((1,), (1,)), ((), ())), preferred_element_type=F32)  11.7 us
    another operation x6, other arithmetic, spread(): return jnp.stack([s, swap_t(s)]).reshape(R, width)  7.24 us
    dot_general x9, matrix products, mt_m(): lax.dot_general(a, b, (((0,), (0,)), ((), ())), preferred_element_type=F32)  6.93 us
    dot_general x9, matrix products, mm(): lax.dot_general(a, b, (((1,), (0,)), ((), ())), preferred_element_type=F32)  6.87 us
  transfers between devices with their start and end apart: 71, of which 33 were waited for; matrix products, arithmetic and copies ran while one was open for 19% of the time, Pallas kernels for 0%

profile of v1, /device:TPU:0, one launch (start us, length us, event | category | flops | bytes accessed | tf_op | source)
XLA Modules:
  0.0 306.4 jit_solution(10052835584276371582)
XLA Ops:
  1.7 4.1 %collective-permute-start.36 = (bf16[64,1024]{1,0:T(8,128)(2,1)S(1)}, bf16[64,1024]{1,0:T(8,128)(2,1)S(1)}, u32[]{:S(2)}, u32[]{:S(2)}) collective-permute-start(bf16[64,1024]{1,0:T(8,128)(2,1)S(1)} %fusion.196), channel_id=1, source_target_pairs={{0,16},{8,24},{16,0},{24,8},{1,17},{9,25},{17,1},{25,9},{2,18},{10... | collective-permute-start | bytes 393224 | tf_op jit(solution)/shard_map/ppermute | solution.py:43
  5.8 1.6 collective-permute-start.35
  8.2 1.6 collective-permute-start.10
  9.8 1.5 collective-permute-start.12
  14.0 2.8 concatenate.139
  20.2 1.5 collective-permute-start.4
  21.7 1.5 collective-permute-start.5
  25.3 1.8 collective-permute-done.5
  29.1 2.5 collective-permute-start.26
  35.4 2.1 collective-permute-start.2
  37.5 4.2 %collective-permute-done.25 = bf16[64,1152]{1,0:T(8,128)(2,1)S(1)} collective-permute-done((bf16[64,1152]{1,0:T(8,128)(2,1)S(1)}, bf16[64,1152]{1,0:T(8,128)(2,1)S(1)}, u32[]{:S(2)}, u32[]{:S(2)}) %collective-permute-start.25) | collective-permute-done | bytes 147488 | tf_op jit(solution)/shard_map/ppermute | solution.py:43
  41.8 1.7 collective-permute-start.14
  43.5 3.4 %collective-permute-start.13 = (bf16[4,64,256]{2,1,0:T(8,128)(2,1)S(1)}, bf16[4,64,256]{2,1,0:T(8,128)(2,1)S(1)}, u32[]{:S(2)}, u32[]{:S(2)}) collective-permute-start(bf16[4,64,256]{2,1,0:T(8,128)(2,1)S(1)} %get-tuple-element.183), channel_id=1, source_target_pairs={{0,8},{8,0},{16,24},{24,16},{1,9},{9,1},{17,25},{25,17},{2,10},{10... | collective-permute-start | bytes 393224 | tf_op jit(solution)/shard_map/ppermute | solution.py:43
  46.9 1.5 collective-permute-start.15
  49.3 2.9 collective-permute-start.7
  53.2 1.5 collective-permute-start.9
  56.5 18.6 %collective-permute-done.8 = bf16[4,72,512]{2,1,0:T(8,128)(2,1)S(1)} collective-permute-done((bf16[4,72,512]{2,1,0:T(8,128)(2,1)S(1)}, bf16[4,72,512]{2,1,0:T(8,128)(2,1)S(1)}, u32[]{:S(2)}, u32[]{:S(2)}) %collective-permute-start.8) | collective-permute-done | bytes 294944 | tf_op jit(solution)/shard_map/ppermute | solution.py:43
  88.0 1.9 collective-permute-start.28
  91.7 2.3 pad_maximum_fusion.8
  94.0 2.3 copy.55
  96.3 1.6 fusion.155
  98.0 2.1 collective-permute-start.17
  101.3 2.9 collective-permute-done.28
  104.2 1.7 collective-permute-start.18
  106.4 12.4 %collective-permute-done.29 = bf16[4,64,1152]{2,1,0:T(8,128)(2,1)} collective-permute-done((bf16[4,64,1152]{2,1,0:T(8,128)(2,1)}, bf16[4,64,1152]{2,1,0:T(8,128)(2,1)}, u32[]{:S(2)}, u32[]{:S(2)}) %collective-permute-start.29) | collective-permute-done | bytes 589856 | tf_op jit(solution)/shard_map/ppermute | solution.py:43
  118.8 1.8 pad_maximum_fusion
  121.8 2.1 collective-permute-done.19
  124.2 5.7 %collective-permute-start.21 = (bf16[64,1024]{1,0:T(8,128)(2,1)S(1)}, bf16[64,1024]{1,0:T(8,128)(2,1)S(1)}, u32[]{:S(2)}, u32[]{:S(2)}) collective-permute-start(bf16[64,1024]{1,0:T(8,128)(2,1)S(1)} %multiply_convert_fusion.8), channel_id=1, source_target_pairs={{0,16},{8,24},{16,0},{24,8},{1,17},{9,25},{17,1},{25,9},{2,18},{10... | collective-permute-start | bytes 393224 | tf_op jit(solution)/shard_map/ppermute | solution.py:43
  130.0 2.3 collective-permute-start.22
  132.4 3.4 %collective-permute-done.21 = bf16[64,1024]{1,0:T(8,128)(2,1)S(1)} collective-permute-done((bf16[64,1024]{1,0:T(8,128)(2,1)S(1)}, bf16[64,1024]{1,0:T(8,128)(2,1)S(1)}, u32[]{:S(2)}, u32[]{:S(2)}) %collective-permute-start.21) | collective-permute-done | bytes 131104 | tf_op jit(solution)/shard_map/ppermute | solution.py:43
  136.4 4.3 %collective-permute-done.22 = bf16[64,1024]{1,0:T(8,128)(2,1)S(1)} collective-permute-done((bf16[64,1024]{1,0:T(8,128)(2,1)S(1)}, bf16[64,1024]{1,0:T(8,128)(2,1)S(1)}, u32[]{:S(2)}, u32[]{:S(2)}) %collective-permute-start.22) | collective-permute-done | bytes 131104 | tf_op jit(solution)/shard_map/ppermute | solution.py:43
  141.9 1.4 dynamic-slice_bitcast_fusion.6
  144.0 2.0 pad_maximum_fusion.1
  146.0 1.5 pad_maximum_fusion.7
  149.1 1.9 multiply_convert_fusion.2
  151.0 2.1 fusion.16
  153.1 1.6 convolution_convert_fusion.1
  154.7 2.3 copy.54
  157.0 2.1 fusion.21
  160.6 2.0 convolution_add_fusion
  164.8 2.1 collective-permute-start.66
  169.3 2.5 collective-permute-start.42
  173.7 6.8 %collective-permute-done.64 = bf16[4,64,1152]{2,1,0:T(8,128)(2,1)S(1)} collective-permute-done((bf16[4,64,1152]{2,1,0:T(8,128)(2,1)S(1)}, bf16[4,64,1152]{2,1,0:T(8,128)(2,1)S(1)}, u32[]{:S(2)}, u32[]{:S(2)}) %collective-permute-start.64) | collective-permute-done | bytes 589856 | tf_op jit(solution)/shard_map/ppermute | solution.py:43
  180.6 2.1 collective-permute-start.41
  182.7 10.7 %collective-permute-done.66 = bf16[4,64,1152]{2,1,0:T(8,128)(2,1)S(1)} collective-permute-done((bf16[4,64,1152]{2,1,0:T(8,128)(2,1)S(1)}, bf16[4,64,1152]{2,1,0:T(8,128)(2,1)S(1)}, u32[]{:S(2)}, u32[]{:S(2)}) %collective-permute-start.66) | collective-permute-done | bytes 589856 | tf_op jit(solution)/shard_map/ppermute | solution.py:43
  198.2 2.0 collective-permute-start.67
  203.4 1.5 collective-permute-start.44
  207.4 3.6 %collective-permute-done.68 = bf16[64,1152]{1,0:T(8,128)(2,1)} collective-permute-done((bf16[64,1152]{1,0:T(8,128)(2,1)}, bf16[64,1152]{1,0:T(8,128)(2,1)}, u32[]{:S(2)}, u32[]{:S(2)}) %collective-permute-start.68) | collective-permute-done | bytes 147488 | tf_op jit(solution)/shard_map/ppermute | solution.py:43
  225.1 1.9 dynamic-slice_bitcast_fusion.19
  227.0 2.8 collective-permute-start.58
  229.8 1.5 collective-permute-start.60
  232.3 3.2 %multiply_convert_fusion = (bf16[512,1024]{1,0:T(8,128)(2,1)S(1)}, bf16[1024]{0:T(1024)(128)(2,1)S(1)}, f32[512,1024]{1,0:T(8,128)}) fusion(bf16[2,4,64,1024]{3,2,1,0:T(8,128)(2,1)S(1)} %copy-done.7, f32[1024]{0:T(1024)S(1)} %mul.531, f32[512]{0:T(512)} %rsqrt.58, bf16[1024,512]{1,0:T(8,128)(2,1)S(1)} %bitcast.274, bf16[512,128]{0,1:T(8,128)(2,1)} %fusion.12, ...), kind=kOutput, calls=%fused_computation.5 | convolution fusion | flops 542112768 | bytes 5775360 | tf_op jit(solution)/shard_map/dot_general | solution.py:18
  238.9 4.6 %collective-permute-done.59 = bf16[4,64,256]{2,1,0:T(8,128)(2,1)} collective-permute-done((bf16[4,64,256]{2,1,0:T(8,128)(2,1)}, bf16[4,64,256]{2,1,0:T(8,128)(2,1)}, u32[]{:S(2)}, u32[]{:S(2)}) %collective-permute-start.59) | collective-permute-done | bytes 131104 | tf_op jit(solution)/shard_map/ppermute | solution.py:43
  245.7 1.8 collective-permute-start.54
  247.5 1.7 collective-permute-start.53
  249.2 1.5 collective-permute-start.62
  255.5 1.7 collective-permute-start.33
  257.2 3.3 %collective-permute-done.52 = bf16[4,72,512]{2,1,0:T(8,128)(2,1)S(1)} collective-permute-done((bf16[4,72,512]{2,1,0:T(8,128)(2,1)S(1)}, bf16[4,72,512]{2,1,0:T(8,128)(2,1)S(1)}, u32[]{:S(2)}, u32[]{:S(2)}) %collective-permute-start.52) | collective-permute-done | bytes 294944 | tf_op jit(solution)/shard_map/ppermute | solution.py:43
  261.7 16.5 %collective-permute-done.53 = bf16[4,72,512]{2,1,0:T(8,128)(2,1)S(1)} collective-permute-done((bf16[4,72,512]{2,1,0:T(8,128)(2,1)S(1)}, bf16[4,72,512]{2,1,0:T(8,128)(2,1)S(1)}, u32[]{:S(2)}, u32[]{:S(2)}) %collective-permute-start.53) | collective-permute-done | bytes 294944 | tf_op jit(solution)/shard_map/ppermute | solution.py:43
  278.4 2.2 collective-permute-start.57
  289.1 2.1 collective-permute-start.50
  292.7 2.3 collective-permute-done.48
  295.0 3.0 collective-permute-done.50
  299.6 2.6 collective-permute-done.32
  (420 shorter events, 101.5 us)
Async XLA Ops:
  1.7 27.4 %collective-permute-start.36 = (bf16[64,1024]{1,0:T(8,128)(2,1)S(1)}, bf16[64,1024]{1,0:T(8,128)(2,1)S(1)}, u32[]{:S(2)}, u32[]{:S(2)}) collective-permute-start(bf16[64,1024]{1,0:T(8,128)(2,1)S(1)} %fusion.196), channel_id=1, source_target_pairs={{0,16},{8,24},{16,0},{24,8},{1,17},{9,25},{17,1},{25,9},{2,18},{10... | collective-permute-start | bytes 393224 | tf_op jit(solution)/shard_map/ppermute | solution.py:43
  5.8 25.8 %collective-permute-start.35 = (bf16[64,1024]{1,0:T(8,128)(2,1)S(1)}, bf16[64,1024]{1,0:T(8,128)(2,1)S(1)}, u32[]{:S(2)}, u32[]{:S(2)}) collective-permute-start(bf16[64,1024]{1,0:T(8,128)(2,1)S(1)} %fusion.196), channel_id=1, source_target_pairs={{0,8},{8,0},{16,24},{24,16},{1,9},{9,1},{17,25},{25,17},{2,10},{10... | collective-permute-start | bytes 393224 | tf_op jit(solution)/shard_map/ppermute | solution.py:43
  8.2 12.0 %collective-permute-start.10 = (bf16[64,256]{1,0:T(8,128)(2,1)S(1)}, bf16[64,256]{1,0:T(8,128)(2,1)S(1)}, u32[]{:S(2)}, u32[]{:S(2)}) collective-permute-start(bf16[64,256]{1,0:T(8,128)(2,1)S(1)} %get-tuple-element.189), channel_id=1, source_target_pairs={{0,2},{2,0},{4,6},{6,4},{1,3},{3,1},{5,7},{7,5},{8,10},{10,8},{12,... | collective-permute-start | bytes 98312 | tf_op jit(solution)/shard_map/ppermute | solution.py:43
  9.8 12.0 %collective-permute-start.12 = (bf16[64,256]{1,0:T(8,128)(2,1)S(1)}, bf16[64,256]{1,0:T(8,128)(2,1)S(1)}, u32[]{:S(2)}, u32[]{:S(2)}) collective-permute-start(bf16[64,256]{1,0:T(8,128)(2,1)S(1)} %get-tuple-element.190), channel_id=1, source_target_pairs={{0,6},{2,4},{4,2},{6,0},{1,7},{3,5},{5,3},{7,1},{8,14},{10,12},{12... | collective-permute-start | bytes 98312 | tf_op jit(solution)/shard_map/ppermute | solution.py:43
  11.3 12.0 %collective-permute-start.11 = (bf16[64,256]{1,0:T(8,128)(2,1)S(1)}, bf16[64,256]{1,0:T(8,128)(2,1)S(1)}, u32[]{:S(2)}, u32[]{:S(2)}) collective-permute-start(bf16[64,256]{1,0:T(8,128)(2,1)S(1)} %get-tuple-element.191), channel_id=1, source_target_pairs={{0,4},{2,6},{4,0},{6,2},{1,5},{3,7},{5,1},{7,3},{8,12},{10,14},{12... | collective-permute-start | bytes 98312 | tf_op jit(solution)/shard_map/ppermute | solution.py:43
  20.2 5.0 %collective-permute-start.4 = (bf16[72,512]{1,0:T(8,128)(2,1)S(1)}, bf16[72,512]{1,0:T(8,128)(2,1)S(1)}, u32[]{:S(2)}, u32[]{:S(2)}) collective-permute-start(bf16[72,512]{1,0:T(8,128)(2,1)S(1)} %get-tuple-element.213), channel_id=1, source_target_pairs={{0,2},{2,0},{4,6},{6,4},{1,3},{3,1},{5,7},{7,5},{8,10},{10,8},{12,... | collective-permute-start | bytes 221192 | tf_op jit(solution)/shard_map/ppermute | solution.py:43
  21.7 5.3 %collective-permute-start.5 = (bf16[72,512]{1,0:T(8,128)(2,1)S(1)}, bf16[72,512]{1,0:T(8,128)(2,1)S(1)}, u32[]{:S(2)}, u32[]{:S(2)}) collective-permute-start(bf16[72,512]{1,0:T(8,128)(2,1)S(1)} %get-tuple-element.214), channel_id=1, source_target_pairs={{0,4},{2,6},{4,0},{6,2},{1,5},{3,7},{5,1},{7,3},{8,12},{10,14},{12... | collective-permute-start | bytes 221192 | tf_op jit(solution)/shard_map/ppermute | solution.py:43
  23.3 5.4 %collective-permute-start.6 = (bf16[72,512]{1,0:T(8,128)(2,1)S(1)}, bf16[72,512]{1,0:T(8,128)(2,1)S(1)}, u32[]{:S(2)}, u32[]{:S(2)}) collective-permute-start(bf16[72,512]{1,0:T(8,128)(2,1)S(1)} %get-tuple-element.215), channel_id=1, source_target_pairs={{0,6},{2,4},{4,2},{6,0},{1,7},{3,5},{5,3},{7,1},{8,14},{10,12},{12... | collective-permute-start | bytes 221192 | tf_op jit(solution)/shard_map/ppermute | solution.py:43
  25.3 8.3 %collective-permute-start.37 = (bf16[64,1024]{1,0:T(8,128)(2,1)S(1)}, bf16[64,1024]{1,0:T(8,128)(2,1)S(1)}, u32[]{:S(2)}, u32[]{:S(2)}) collective-permute-start(bf16[64,1024]{1,0:T(8,128)(2,1)S(1)} %fusion.196), channel_id=1, source_target_pairs={{0,24},{8,16},{16,8},{24,0},{1,25},{9,17},{17,9},{25,1},{2,26},{10... | collective-permute-start | bytes 393224 | tf_op jit(solution)/shard_map/ppermute | solution.py:43
  27.1 8.3 %collective-permute-start.1 = (bf16[72,1024]{1,0:T(8,128)(2,1)S(1)}, bf16[72,1024]{1,0:T(8,128)(2,1)S(1)}, u32[]{:S(2)}, u32[]{:S(2)}) collective-permute-start(bf16[72,1024]{1,0:T(8,128)(2,1)S(1)} %get-tuple-element.169), channel_id=1, source_target_pairs={{0,4},{2,6},{4,0},{6,2},{1,5},{3,7},{5,1},{7,3},{8,12},{10,14},{12... | collective-permute-start | bytes 442376 | tf_op jit(solution)/shard_map/ppermute | solution.py:43
  28.6 13.2 %collective-permute-start.25 = (bf16[64,1152]{1,0:T(8,128)(2,1)S(1)}, bf16[64,1152]{1,0:T(8,128)(2,1)S(1)}, u32[]{:S(2)}, u32[]{:S(2)}) collective-permute-start(bf16[64,1152]{1,0:T(8,128)(2,1)S(1)} %pad_maximum_fusion.34), channel_id=1, source_target_pairs={{0,16},{8,24},{16,0},{24,8},{1,17},{9,25},{17,1},{25,9},{2,18},{10... | collective-permute-start | bytes 442376 | tf_op jit(solution)/shard_map/ppermute | solution.py:43
  29.1 14.5 %collective-permute-start.26 = (bf16[64,1152]{1,0:T(8,128)(2,1)S(1)}, bf16[64,1152]{1,0:T(8,128)(2,1)S(1)}, u32[]{:S(2)}, u32[]{:S(2)}) collective-permute-start(bf16[64,1152]{1,0:T(8,128)(2,1)S(1)} %pad_maximum_fusion.35), channel_id=1, source_target_pairs={{0,24},{8,16},{16,8},{24,0},{1,25},{9,17},{17,9},{25,1},{2,26},{10... | collective-permute-start | bytes 442376 | tf_op jit(solution)/shard_map/ppermute | solution.py:43
  31.6 15.3 %collective-permute-start.24 = (bf16[64,1152]{1,0:T(8,128)(2,1)S(1)}, bf16[64,1152]{1,0:T(8,128)(2,1)S(1)}, u32[]{:S(2)}, u32[]{:S(2)}) collective-permute-start(bf16[64,1152]{1,0:T(8,128)(2,1)S(1)} %pad_maximum_fusion.33), channel_id=1, source_target_pairs={{0,8},{8,0},{16,24},{24,16},{1,9},{9,1},{17,25},{25,17},{2,10},{10... | collective-permute-start | bytes 442376 | tf_op jit(solution)/shard_map/ppermute | solution.py:43
  33.6 15.7 %collective-permute-start = (bf16[72,1024]{1,0:T(8,128)(2,1)S(1)}, bf16[72,1024]{1,0:T(8,128)(2,1)S(1)}, u32[]{:S(2)}, u32[]{:S(2)}) collective-permute-start(bf16[72,1024]{1,0:T(8,128)(2,1)S(1)} %get-tuple-element.169), channel_id=1, source_target_pairs={{0,2},{2,0},{4,6},{6,4},{1,3},{3,1},{5,7},{7,5},{8,10},{10,8},{12,... | collective-permute-start | bytes 442376 | tf_op jit(solution)/shard_map/ppermute | solution.py:43
  35.4 14.0 %collective-permute-start.2 = (bf16[72,1024]{1,0:T(8,128)(2,1)S(1)}, bf16[72,1024]{1,0:T(8,128)(2,1)S(1)}, u32[]{:S(2)}, u32[]{:S(2)}) collective-permute-start(bf16[72,1024]{1,0:T(8,128)(2,1)S(1)} %get-tuple-element.169), channel_id=1, source_target_pairs={{0,6},{2,4},{4,2},{6,0},{1,7},{3,5},{5,3},{7,1},{8,14},{10,12},{12... | collective-permute-start | bytes 442376 | tf_op jit(solution)/shard_map/ppermute | solution.py:43
  41.8 11.4 %collective-permute-start.14 = (bf16[4,64,256]{2,1,0:T(8,128)(2,1)S(1)}, bf16[4,64,256]{2,1,0:T(8,128)(2,1)S(1)}, u32[]{:S(2)}, u32[]{:S(2)}) collective-permute-start(bf16[4,64,256]{2,1,0:T(8,128)(2,1)S(1)} %get-tuple-element.183), channel_id=1, source_target_pairs={{0,16},{8,24},{16,0},{24,8},{1,17},{9,25},{17,1},{25,9},{2,18},{10... | collective-permute-start | bytes 393224 | tf_op jit(solution)/shard_map/ppermute | solution.py:43
  43.5 11.2 %collective-permute-start.13 = (bf16[4,64,256]{2,1,0:T(8,128)(2,1)S(1)}, bf16[4,64,256]{2,1,0:T(8,128)(2,1)S(1)}, u32[]{:S(2)}, u32[]{:S(2)}) collective-permute-start(bf16[4,64,256]{2,1,0:T(8,128)(2,1)S(1)} %get-tuple-element.183), channel_id=1, source_target_pairs={{0,8},{8,0},{16,24},{24,16},{1,9},{9,1},{17,25},{25,17},{2,10},{10... | collective-permute-start | bytes 393224 | tf_op jit(solution)/shard_map/ppermute | solution.py:43
  46.9 8.6 %collective-permute-start.15 = (bf16[4,64,256]{2,1,0:T(8,128)(2,1)S(1)}, bf16[4,64,256]{2,1,0:T(8,128)(2,1)S(1)}, u32[]{:S(2)}, u32[]{:S(2)}) collective-permute-start(bf16[4,64,256]{2,1,0:T(8,128)(2,1)S(1)} %get-tuple-element.183), channel_id=1, source_target_pairs={{0,24},{8,16},{16,8},{24,0},{1,25},{9,17},{17,9},{25,1},{2,26},{10... | collective-permute-start | bytes 393224 | tf_op jit(solution)/shard_map/ppermute | solution.py:43
  49.3 25.8 %collective-permute-start.8 = (bf16[4,72,512]{2,1,0:T(8,128)(2,1)S(1)}, bf16[4,72,512]{2,1,0:T(8,128)(2,1)S(1)}, u32[]{:S(2)}, u32[]{:S(2)}) collective-permute-start(bf16[4,72,512]{2,1,0:T(8,128)(2,1)S(1)} %get-tuple-element.137), channel_id=1, source_target_pairs={{0,16},{8,24},{16,0},{24,8},{1,17},{9,25},{17,1},{25,9},{2,18},{10... | collective-permute-start | bytes 884744 | tf_op jit(solution)/shard_map/ppermute | solution.py:43
  49.3 25.8 %collective-permute-start.7 = (bf16[4,72,512]{2,1,0:T(8,128)(2,1)S(1)}, bf16[4,72,512]{2,1,0:T(8,128)(2,1)S(1)}, u32[]{:S(2)}, u32[]{:S(2)}) collective-permute-start(bf16[4,72,512]{2,1,0:T(8,128)(2,1)S(1)} %get-tuple-element.137), channel_id=1, source_target_pairs={{0,8},{8,0},{16,24},{24,16},{1,9},{9,1},{17,25},{25,17},{2,10},{10... | collective-permute-start | bytes 884744 | tf_op jit(solution)/shard_map/ppermute | solution.py:43
  53.2 21.9 %collective-permute-start.9 = (bf16[4,72,512]{2,1,0:T(8,128)(2,1)S(1)}, bf16[4,72,512]{2,1,0:T(8,128)(2,1)S(1)}, u32[]{:S(2)}, u32[]{:S(2)}) collective-permute-start(bf16[4,72,512]{2,1,0:T(8,128)(2,1)S(1)} %get-tuple-element.137), channel_id=1, source_target_pairs={{0,24},{8,16},{16,8},{24,0},{1,25},{9,17},{17,9},{25,1},{2,26},{10... | collective-permute-start | bytes 884744 | tf_op jit(solution)/shard_map/ppermute | solution.py:43
  54.7 37.0 %collective-permute-start.38 = (bf16[4,64,1024]{2,1,0:T(8,128)(2,1)}, bf16[4,64,1024]{2,1,0:T(8,128)(2,1)}, u32[]{:S(2)}, u32[]{:S(2)}) collective-permute-start(bf16[4,64,1024]{2,1,0:T(8,128)(2,1)} %get-tuple-element.115), channel_id=1, source_target_pairs={{0,1},{1,0},{2,3},{3,2},{4,5},{5,4},{6,7},{7,6},{8,9},{9,8},{10,11... | collective-permute-start | bytes 1572872 | tf_op jit(solution)/shard_map/ppermute | solution.py:43
  55.5 22.0 %collective-permute-start.3 = (bf16[4,72,1024]{2,1,0:T(8,128)(2,1)}, bf16[4,72,1024]{2,1,0:T(8,128)(2,1)S(1)}, u32[]{:S(2)}, u32[]{:S(2)}) collective-permute-start(bf16[4,72,1024]{2,1,0:T(8,128)(2,1)} %get-tuple-element.100), channel_id=1, source_target_pairs={{0,1},{1,0},{2,3},{3,2},{4,5},{5,4},{6,7},{7,6},{8,9},{9,8},{10,11... | collective-permute-start | bytes 1769480 | tf_op jit(solution)/shard_map/ppermute | solution.py:43
  86.8 9.5 %collective-permute-start.16 = (bf16[256,1024]{1,0:T(8,128)(2,1)}, bf16[256,1024]{1,0:T(8,128)(2,1)}, u32[]{:S(2)}, u32[]{:S(2)}) collective-permute-start(bf16[256,1024]{1,0:T(8,128)(2,1)} %slice.498), channel_id=1, source_target_pairs={{0,1},{1,0},{2,3},{3,2},{4,5},{5,4},{6,7},{7,6},{8,9},{9,8},{10,11... | collective-permute-start | bytes 1572872 | tf_op jit(solution)/shard_map/ppermute | solution.py:43
  88.0 16.2 %collective-permute-start.28 = (bf16[4,64,1152]{2,1,0:T(8,128)(2,1)}, bf16[4,64,1152]{2,1,0:T(8,128)(2,1)}, u32[]{:S(2)}, u32[]{:S(2)}) collective-permute-start(bf16[4,64,1152]{2,1,0:T(8,128)(2,1)} %get-tuple-element.94), channel_id=1, source_target_pairs={{0,4},{2,6},{4,0},{6,2},{1,5},{3,7},{5,1},{7,3},{8,12},{10,14},{12... | collective-permute-start | bytes 1769480 | tf_op jit(solution)/shard_map/ppermute | solution.py:43
  89.9 16.5 %collective-permute-start.27 = (bf16[4,64,1152]{2,1,0:T(8,128)(2,1)}, bf16[4,64,1152]{2,1,0:T(8,128)(2,1)}, u32[]{:S(2)}, u32[]{:S(2)}) collective-permute-start(bf16[4,64,1152]{2,1,0:T(8,128)(2,1)} %get-tuple-element.94), channel_id=1, source_target_pairs={{0,2},{2,0},{4,6},{6,4},{1,3},{3,1},{5,7},{7,5},{8,10},{10,8},{12,... | collective-permute-start | bytes 1769480 | tf_op jit(solution)/shard_map/ppermute | solution.py:43
  90.8 28.0 %collective-permute-start.29 = (bf16[4,64,1152]{2,1,0:T(8,128)(2,1)}, bf16[4,64,1152]{2,1,0:T(8,128)(2,1)}, u32[]{:S(2)}, u32[]{:S(2)}) collective-permute-start(bf16[4,64,1152]{2,1,0:T(8,128)(2,1)} %get-tuple-element.94), channel_id=1, source_target_pairs={{0,6},{2,4},{4,2},{6,0},{1,7},{3,5},{5,3},{7,1},{8,14},{10,12},{12... | collective-permute-start | bytes 1769480 | tf_op jit(solution)/shard_map/ppermute | solution.py:43
  98.0 23.8 %collective-permute-start.17 = (bf16[64,1024]{1,0:T(8,128)(2,1)S(1)}, bf16[64,1024]{1,0:T(8,128)(2,1)S(1)}, u32[]{:S(2)}, u32[]{:S(2)}) collective-permute-start(bf16[64,1024]{1,0:T(8,128)(2,1)S(1)} %get-tuple-element.121), channel_id=1, source_target_pairs={{0,2},{2,0},{4,6},{6,4},{1,3},{3,1},{5,7},{7,5},{8,10},{10,8},{12,... | collective-permute-start | bytes 393224 | tf_op jit(solution)/shard_map/ppermute | solution.py:43
  100.1 23.8 %collective-permute-start.19 = (bf16[64,1024]{1,0:T(8,128)(2,1)S(1)}, bf16[64,1024]{1,0:T(8,128)(2,1)S(1)}, u32[]{:S(2)}, u32[]{:S(2)}) collective-permute-start(bf16[64,1024]{1,0:T(8,128)(2,1)S(1)} %get-tuple-element.122), channel_id=1, source_target_pairs={{0,6},{2,4},{4,2},{6,0},{1,7},{3,5},{5,3},{7,1},{8,14},{10,12},{12... | collective-permute-start | bytes 393224 | tf_op jit(solution)/shard_map/ppermute | solution.py:43
  104.2 19.7 %collective-permute-start.18 = (bf16[64,1024]{1,0:T(8,128)(2,1)S(1)}, bf16[64,1024]{1,0:T(8,128)(2,1)S(1)}, u32[]{:S(2)}, u32[]{:S(2)}) collective-permute-start(bf16[64,1024]{1,0:T(8,128)(2,1)S(1)} %get-tuple-element.123), channel_id=1, source_target_pairs={{0,4},{2,6},{4,0},{6,2},{1,5},{3,7},{5,1},{7,3},{8,12},{10,14},{12... | collective-permute-start | bytes 393224 | tf_op jit(solution)/shard_map/ppermute | solution.py:43
  124.2 11.6 %collective-permute-start.21 = (bf16[64,1024]{1,0:T(8,128)(2,1)S(1)}, bf16[64,1024]{1,0:T(8,128)(2,1)S(1)}, u32[]{:S(2)}, u32[]{:S(2)}) collective-permute-start(bf16[64,1024]{1,0:T(8,128)(2,1)S(1)} %multiply_convert_fusion.8), channel_id=1, source_target_pairs={{0,16},{8,24},{16,0},{24,8},{1,17},{9,25},{17,1},{25,9},{2,18},{10... | collective-permute-start | bytes 393224 | tf_op jit(solution)/shard_map/ppermute | solution.py:43
  129.9 6.5 %collective-permute-start.20 = (bf16[64,1024]{1,0:T(8,128)(2,1)S(1)}, bf16[64,1024]{1,0:T(8,128)(2,1)S(1)}, u32[]{:S(2)}, u32[]{:S(2)}) collective-permute-start(bf16[64,1024]{1,0:T(8,128)(2,1)S(1)} %multiply_convert_fusion.8), channel_id=1, source_target_pairs={{0,8},{8,0},{16,24},{24,16},{1,9},{9,1},{17,25},{25,17},{2,10},{10... | collective-permute-start | bytes 393224 | tf_op jit(solution)/shard_map/ppermute | solution.py:43
  130.0 10.7 %collective-permute-start.22 = (bf16[64,1024]{1,0:T(8,128)(2,1)S(1)}, bf16[64,1024]{1,0:T(8,128)(2,1)S(1)}, u32[]{:S(2)}, u32[]{:S(2)}) collective-permute-start(bf16[64,1024]{1,0:T(8,128)(2,1)S(1)} %multiply_convert_fusion.8), channel_id=1, source_target_pairs={{0,24},{8,16},{16,8},{24,0},{1,25},{9,17},{17,9},{25,1},{2,26},{10... | collective-permute-start | bytes 393224 | tf_op jit(solution)/shard_map/ppermute | solution.py:43
  162.8 5.0 %collective-permute-start.39 = (bf16[256,1024]{1,0:T(8,128)(2,1)S(1)}, bf16[256,1024]{1,0:T(8,128)(2,1)S(1)}, u32[]{:S(2)}, u32[]{:S(2)}) collective-permute-start(bf16[256,1024]{1,0:T(8,128)(2,1)S(1)} %slice.496), channel_id=1, source_target_pairs={{0,1},{1,0},{2,3},{3,2},{4,5},{5,4},{6,7},{7,6},{8,9},{9,8},{10,11... | collective-permute-start | bytes 1572872 | tf_op jit(solution)/shard_map/ppermute | solution.py:43
  163.4 5.9 %collective-permute-start.30 = (bf16[256,1024]{1,0:T(8,128)(2,1)S(1)}, bf16[256,1024]{1,0:T(8,128)(2,1)S(1)}, u32[]{:S(2)}, u32[]{:S(2)}) collective-permute-start(bf16[256,1024]{1,0:T(8,128)(2,1)S(1)} %slice.497), channel_id=1, source_target_pairs={{0,1},{1,0},{2,3},{3,2},{4,5},{5,4},{6,7},{7,6},{8,9},{9,8},{10,11... | collective-permute-start | bytes 1572872 | tf_op jit(solution)/shard_map/ppermute | solution.py:43
  164.3 16.3 %collective-permute-start.64 = (bf16[4,64,1152]{2,1,0:T(8,128)(2,1)S(1)}, bf16[4,64,1152]{2,1,0:T(8,128)(2,1)S(1)}, u32[]{:S(2)}, u32[]{:S(2)}) collective-permute-start(bf16[4,64,1152]{2,1,0:T(8,128)(2,1)S(1)} %get-tuple-element.55), channel_id=1, source_target_pairs={{0,2},{2,0},{4,6},{6,4},{1,3},{3,1},{5,7},{7,5},{8,10},{10,8},{12,... | collective-permute-start | bytes 1769480 | tf_op jit(solution)/shard_map/ppermute | solution.py:43
  164.8 28.5 %collective-permute-start.66 = (bf16[4,64,1152]{2,1,0:T(8,128)(2,1)S(1)}, bf16[4,64,1152]{2,1,0:T(8,128)(2,1)S(1)}, u32[]{:S(2)}, u32[]{:S(2)}) collective-permute-start(bf16[4,64,1152]{2,1,0:T(8,128)(2,1)S(1)} %get-tuple-element.56), channel_id=1, source_target_pairs={{0,6},{2,4},{4,2},{6,0},{1,7},{3,5},{5,3},{7,1},{8,14},{10,12},{12... | collective-permute-start | bytes 1769480 | tf_op jit(solution)/shard_map/ppermute | solution.py:43
  166.9 27.8 %collective-permute-start.65 = (bf16[4,64,1152]{2,1,0:T(8,128)(2,1)S(1)}, bf16[4,64,1152]{2,1,0:T(8,128)(2,1)S(1)}, u32[]{:S(2)}, u32[]{:S(2)}) collective-permute-start(bf16[4,64,1152]{2,1,0:T(8,128)(2,1)S(1)} %get-tuple-element.57), channel_id=1, source_target_pairs={{0,4},{2,6},{4,0},{6,2},{1,5},{3,7},{5,1},{7,3},{8,12},{10,14},{12... | collective-permute-start | bytes 1769480 | tf_op jit(solution)/shard_map/ppermute | solution.py:43
  168.1 30.2 %collective-permute-start.40 = (bf16[64,1024]{1,0:T(8,128)(2,1)S(1)}, bf16[64,1024]{1,0:T(8,128)(2,1)S(1)}, u32[]{:S(2)}, u32[]{:S(2)}) collective-permute-start(bf16[64,1024]{1,0:T(8,128)(2,1)S(1)} %get-tuple-element.111), channel_id=1, source_target_pairs={{0,8},{8,0},{16,24},{24,16},{1,9},{9,1},{17,25},{25,17},{2,10},{10... | collective-permute-start | bytes 393224 | tf_op jit(solution)/shard_map/ppermute | solution.py:43
  169.3 31.0 %collective-permute-start.42 = (bf16[64,1024]{1,0:T(8,128)(2,1)S(1)}, bf16[64,1024]{1,0:T(8,128)(2,1)S(1)}, u32[]{:S(2)}, u32[]{:S(2)}) collective-permute-start(bf16[64,1024]{1,0:T(8,128)(2,1)S(1)} %get-tuple-element.112), channel_id=1, source_target_pairs={{0,24},{8,16},{16,8},{24,0},{1,25},{9,17},{17,9},{25,1},{2,26},{10... | collective-permute-start | bytes 393224 | tf_op jit(solution)/shard_map/ppermute | solution.py:43
  180.6 19.7 %collective-permute-start.41 = (bf16[64,1024]{1,0:T(8,128)(2,1)S(1)}, bf16[64,1024]{1,0:T(8,128)(2,1)S(1)}, u32[]{:S(2)}, u32[]{:S(2)}) collective-permute-start(bf16[64,1024]{1,0:T(8,128)(2,1)S(1)} %get-tuple-element.113), channel_id=1, source_target_pairs={{0,16},{8,24},{16,0},{24,8},{1,17},{9,25},{17,1},{25,9},{2,18},{10... | collective-permute-start | bytes 393224 | tf_op jit(solution)/shard_map/ppermute | solution.py:43
  195.9 10.3 %collective-permute-start.69 = (bf16[64,1152]{1,0:T(8,128)(2,1)}, bf16[64,1152]{1,0:T(8,128)(2,1)}, u32[]{:S(2)}, u32[]{:S(2)}) collective-permute-start(bf16[64,1152]{1,0:T(8,128)(2,1)} %get-tuple-element.90), channel_id=1, source_target_pairs={{0,24},{8,16},{16,8},{24,0},{1,25},{9,17},{17,9},{25,1},{2,26},{10... | collective-permute-start | bytes 442376 | tf_op jit(solution)/shard_map/ppermute | solution.py:43
  197.1 13.9 %collective-permute-start.68 = (bf16[64,1152]{1,0:T(8,128)(2,1)}, bf16[64,1152]{1,0:T(8,128)(2,1)}, u32[]{:S(2)}, u32[]{:S(2)}) collective-permute-start(bf16[64,1152]{1,0:T(8,128)(2,1)} %get-tuple-element.91), channel_id=1, source_target_pairs={{0,16},{8,24},{16,0},{24,8},{1,17},{9,25},{17,1},{25,9},{2,18},{10... | collective-permute-start | bytes 442376 | tf_op jit(solution)/shard_map/ppermute | solution.py:43
  198.2 12.7 %collective-permute-start.67 = (bf16[64,1152]{1,0:T(8,128)(2,1)}, bf16[64,1152]{1,0:T(8,128)(2,1)}, u32[]{:S(2)}, u32[]{:S(2)}) collective-permute-start(bf16[64,1152]{1,0:T(8,128)(2,1)} %get-tuple-element.92), channel_id=1, source_target_pairs={{0,8},{8,0},{16,24},{24,16},{1,9},{9,1},{17,25},{25,17},{2,10},{10... | collective-permute-start | bytes 442376 | tf_op jit(solution)/shard_map/ppermute | solution.py:43
  202.5 9.6 %collective-permute-start.45 = (bf16[64,1024]{1,0:T(8,128)(2,1)}, bf16[64,1024]{1,0:T(8,128)(2,1)}, u32[]{:S(2)}, u32[]{:S(2)}) collective-permute-start(bf16[64,1024]{1,0:T(8,128)(2,1)} %fusion.144), channel_id=1, source_target_pairs={{0,6},{2,4},{4,2},{6,0},{1,7},{3,5},{5,3},{7,1},{8,14},{10,12},{12... | collective-permute-start | bytes 393224 | tf_op jit(solution)/shard_map/ppermute | solution.py:43
  203.4 8.8 %collective-permute-start.44 = (bf16[64,1024]{1,0:T(8,128)(2,1)}, bf16[64,1024]{1,0:T(8,128)(2,1)}, u32[]{:S(2)}, u32[]{:S(2)}) collective-permute-start(bf16[64,1024]{1,0:T(8,128)(2,1)} %fusion.144), channel_id=1, source_target_pairs={{0,4},{2,6},{4,0},{6,2},{1,5},{3,7},{5,1},{7,3},{8,12},{10,14},{12... | collective-permute-start | bytes 393224 | tf_op jit(solution)/shard_map/ppermute | solution.py:43
  206.2 6.0 %collective-permute-start.43 = (bf16[64,1024]{1,0:T(8,128)(2,1)}, bf16[64,1024]{1,0:T(8,128)(2,1)S(1)}, u32[]{:S(2)}, u32[]{:S(2)}) collective-permute-start(bf16[64,1024]{1,0:T(8,128)(2,1)} %fusion.144), channel_id=1, source_target_pairs={{0,2},{2,0},{4,6},{6,4},{1,3},{3,1},{5,7},{7,5},{8,10},{10,8},{12,... | collective-permute-start | bytes 393224 | tf_op jit(solution)/shard_map/ppermute | solution.py:43
  227.0 10.9 %collective-permute-start.58 = (bf16[4,64,256]{2,1,0:T(8,128)(2,1)}, bf16[4,64,256]{2,1,0:T(8,128)(2,1)}, u32[]{:S(2)}, u32[]{:S(2)}) collective-permute-start(bf16[4,64,256]{2,1,0:T(8,128)(2,1)} %get-tuple-element.101), channel_id=1, source_target_pairs={{0,8},{8,0},{16,24},{24,16},{1,9},{9,1},{17,25},{25,17},{2,10},{10... | collective-permute-start | bytes 393224 | tf_op jit(solution)/shard_map/ppermute | solution.py:43
  229.8 9.1 %collective-permute-start.60 = (bf16[4,64,256]{2,1,0:T(8,128)(2,1)}, bf16[4,64,256]{2,1,0:T(8,128)(2,1)}, u32[]{:S(2)}, u32[]{:S(2)}) collective-permute-start(bf16[4,64,256]{2,1,0:T(8,128)(2,1)} %get-tuple-element.102), channel_id=1, source_target_pairs={{0,24},{8,16},{16,8},{24,0},{1,25},{9,17},{17,9},{25,1},{2,26},{10... | collective-permute-start | bytes 393224 | tf_op jit(solution)/shard_map/ppermute | solution.py:43
  231.3 12.2 %collective-permute-start.59 = (bf16[4,64,256]{2,1,0:T(8,128)(2,1)}, bf16[4,64,256]{2,1,0:T(8,128)(2,1)}, u32[]{:S(2)}, u32[]{:S(2)}) collective-permute-start(bf16[4,64,256]{2,1,0:T(8,128)(2,1)} %get-tuple-element.103), channel_id=1, source_target_pairs={{0,16},{8,24},{16,0},{24,8},{1,17},{9,25},{17,1},{25,9},{2,18},{10... | collective-permute-start | bytes 393224 | tf_op jit(solution)/shard_map/ppermute | solution.py:43
  244.7 6.0 %collective-permute-start.63 = (bf16[64,256]{1,0:T(8,128)(2,1)S(1)}, bf16[64,256]{1,0:T(8,128)(2,1)S(1)}, u32[]{:S(2)}, u32[]{:S(2)}) collective-permute-start(bf16[64,256]{1,0:T(8,128)(2,1)S(1)} %get-tuple-element.175), channel_id=1, source_target_pairs={{0,6},{2,4},{4,2},{6,0},{1,7},{3,5},{5,3},{7,1},{8,14},{10,12},{12... | collective-permute-start | bytes 98312 | tf_op jit(solution)/shard_map/ppermute | solution.py:43
  245.7 14.9 %collective-permute-start.52 = (bf16[4,72,512]{2,1,0:T(8,128)(2,1)S(1)}, bf16[4,72,512]{2,1,0:T(8,128)(2,1)S(1)}, u32[]{:S(2)}, u32[]{:S(2)}) collective-permute-start(bf16[4,72,512]{2,1,0:T(8,128)(2,1)S(1)} %get-tuple-element.68), channel_id=1, source_target_pairs={{0,8},{8,0},{16,24},{24,16},{1,9},{9,1},{17,25},{25,17},{2,10},{10... | collective-permute-start | bytes 884744 | tf_op jit(solution)/shard_map/ppermute | solution.py:43
  245.7 16.0 %collective-permute-start.54 = (bf16[4,72,512]{2,1,0:T(8,128)(2,1)S(1)}, bf16[4,72,512]{2,1,0:T(8,128)(2,1)S(1)}, u32[]{:S(2)}, u32[]{:S(2)}) collective-permute-start(bf16[4,72,512]{2,1,0:T(8,128)(2,1)S(1)} %get-tuple-element.69), channel_id=1, source_target_pairs={{0,24},{8,16},{16,8},{24,0},{1,25},{9,17},{17,9},{25,1},{2,26},{10... | collective-permute-start | bytes 884744 | tf_op jit(solution)/shard_map/ppermute | solution.py:43
  247.5 30.7 %collective-permute-start.53 = (bf16[4,72,512]{2,1,0:T(8,128)(2,1)S(1)}, bf16[4,72,512]{2,1,0:T(8,128)(2,1)S(1)}, u32[]{:S(2)}, u32[]{:S(2)}) collective-permute-start(bf16[4,72,512]{2,1,0:T(8,128)(2,1)S(1)} %get-tuple-element.70), channel_id=1, source_target_pairs={{0,16},{8,24},{16,0},{24,8},{1,17},{9,25},{17,1},{25,9},{2,18},{10... | collective-permute-start | bytes 884744 | tf_op jit(solution)/shard_map/ppermute | solution.py:43
  249.2 5.2 %collective-permute-start.62 = (bf16[64,256]{1,0:T(8,128)(2,1)S(1)}, bf16[64,256]{1,0:T(8,128)(2,1)S(1)}, u32[]{:S(2)}, u32[]{:S(2)}) collective-permute-start(bf16[64,256]{1,0:T(8,128)(2,1)S(1)} %get-tuple-element.176), channel_id=1, source_target_pairs={{0,4},{2,6},{4,0},{6,2},{1,5},{3,7},{5,1},{7,3},{8,12},{10,14},{12... | collective-permute-start | bytes 98312 | tf_op jit(solution)/shard_map/ppermute | solution.py:43
  250.7 4.8 %collective-permute-start.61 = (bf16[64,256]{1,0:T(8,128)(2,1)S(1)}, bf16[64,256]{1,0:T(8,128)(2,1)S(1)}, u32[]{:S(2)}, u32[]{:S(2)}) collective-permute-start(bf16[64,256]{1,0:T(8,128)(2,1)S(1)} %get-tuple-element.177), channel_id=1, source_target_pairs={{0,2},{2,0},{4,6},{6,4},{1,3},{3,1},{5,7},{7,5},{8,10},{10,8},{12,... | collective-permute-start | bytes 98312 | tf_op jit(solution)/shard_map/ppermute | solution.py:43
  254.4 45.2 %collective-permute-start.31 = (bf16[64,1024]{1,0:T(8,128)(2,1)S(1)}, bf16[64,1024]{1,0:T(8,128)(2,1)S(1)}, u32[]{:S(2)}, u32[]{:S(2)}) collective-permute-start(bf16[64,1024]{1,0:T(8,128)(2,1)S(1)} %copy-done.50), channel_id=1, source_target_pairs={{0,8},{8,0},{16,24},{24,16},{1,9},{9,1},{17,25},{25,17},{2,10},{10... | collective-permute-start | bytes 393224 | tf_op jit(solution)/shard_map/ppermute | solution.py:43
  255.5 44.1 %collective-permute-start.33 = (bf16[64,1024]{1,0:T(8,128)(2,1)S(1)}, bf16[64,1024]{1,0:T(8,128)(2,1)S(1)}, u32[]{:S(2)}, u32[]{:S(2)}) collective-permute-start(bf16[64,1024]{1,0:T(8,128)(2,1)S(1)} %copy-done.49), channel_id=1, source_target_pairs={{0,24},{8,16},{16,8},{24,0},{1,25},{9,17},{17,9},{25,1},{2,26},{10... | collective-permute-start | bytes 393224 | tf_op jit(solution)/shard_map/ppermute | solution.py:43
  278.4 5.3 %collective-permute-start.57 = (bf16[72,512]{1,0:T(8,128)(2,1)S(1)}, bf16[72,512]{1,0:T(8,128)(2,1)S(1)}, u32[]{:S(2)}, u32[]{:S(2)}) collective-permute-start(bf16[72,512]{1,0:T(8,128)(2,1)S(1)} %get-tuple-element.133), channel_id=1, source_target_pairs={{0,6},{2,4},{4,2},{6,0},{1,7},{3,5},{5,3},{7,1},{8,14},{10,12},{12... | collective-permute-start | bytes 221192 | tf_op jit(solution)/shard_map/ppermute | solution.py:43
  283.8 4.5 %collective-permute-start.47 = (bf16[256,1024]{1,0:T(8,128)(2,1)S(1)}, bf16[256,1024]{1,0:T(8,128)(2,1)S(1)}, u32[]{:S(2)}, u32[]{:S(2)}) collective-permute-start(bf16[256,1024]{1,0:T(8,128)(2,1)S(1)} %slice.495), channel_id=1, source_target_pairs={{0,1},{1,0},{2,3},{3,2},{4,5},{5,4},{6,7},{7,6},{8,9},{9,8},{10,11... | collective-permute-start | bytes 1572872 | tf_op jit(solution)/shard_map/ppermute | solution.py:43
  288.5 6.4 %collective-permute-start.48 = (bf16[64,1024]{1,0:T(8,128)(2,1)S(1)}, bf16[64,1024]{1,0:T(8,128)(2,1)S(1)}, u32[]{:S(2)}, u32[]{:S(2)}) collective-permute-start(bf16[64,1024]{1,0:T(8,128)(2,1)S(1)} %get-tuple-element.106), channel_id=1, source_target_pairs={{0,2},{2,0},{4,6},{6,4},{1,3},{3,1},{5,7},{7,5},{8,10},{10,8},{12,... | collective-permute-start | bytes 393224 | tf_op jit(solution)/shard_map/ppermute | solution.py:43
  289.1 8.9 %collective-permute-start.50 = (bf16[64,1024]{1,0:T(8,128)(2,1)S(1)}, bf16[64,1024]{1,0:T(8,128)(2,1)S(1)}, u32[]{:S(2)}, u32[]{:S(2)}) collective-permute-start(bf16[64,1024]{1,0:T(8,128)(2,1)S(1)} %get-tuple-element.107), channel_id=1, source_target_pairs={{0,6},{2,4},{4,2},{6,0},{1,7},{3,5},{5,3},{7,1},{8,14},{10,12},{12... | collective-permute-start | bytes 393224 | tf_op jit(solution)/shard_map/ppermute | solution.py:43
  291.2 8.1 %collective-permute-start.49 = (bf16[64,1024]{1,0:T(8,128)(2,1)S(1)}, bf16[64,1024]{1,0:T(8,128)(2,1)S(1)}, u32[]{:S(2)}, u32[]{:S(2)}) collective-permute-start(bf16[64,1024]{1,0:T(8,128)(2,1)S(1)} %get-tuple-element.108), channel_id=1, source_target_pairs={{0,4},{2,6},{4,0},{6,2},{1,5},{3,7},{5,1},{7,3},{8,12},{10,14},{12... | collective-permute-start | bytes 393224 | tf_op jit(solution)/shard_map/ppermute | solution.py:43
  295.0 7.2 %collective-permute-start.32 = (bf16[64,1024]{1,0:T(8,128)(2,1)S(1)}, bf16[64,1024]{1,0:T(8,128)(2,1)S(1)}, u32[]{:S(2)}, u32[]{:S(2)}) collective-permute-start(bf16[64,1024]{1,0:T(8,128)(2,1)S(1)} %copy-done.48), channel_id=1, source_target_pairs={{0,16},{8,24},{16,0},{24,8},{1,17},{9,25},{17,1},{25,9},{2,18},{10... | collective-permute-start | bytes 393224 | tf_op jit(solution)/shard_map/ppermute | solution.py:43
  (90 other events, 418.7 us)

commit v2 on v1

v2 whole, which is shorter than its diff:
```python
import jax
import jax.numpy as jnp
from jax import lax
from jax.experimental import pallas as pl
from jax.experimental.pallas import tpu as pltpu
from jax.sharding import PartitionSpec as P

HEAD = 128
EPS = 1e-06
THETA = 1000000.0
BF = jnp.bfloat16
F32 = jnp.float32


def mm(a, b):
    return lax.dot_general(a, b, (((1,), (0,)), ((), ())), preferred_element_type=F32)


def mm_t(a, b):
    return lax.dot_general(a, b, (((1,), (1,)), ((), ())), preferred_element_type=F32)


def mt_m(a, b):
    return lax.dot_general(a, b, (((0,), (0,)), ((), ())), preferred_element_type=F32)


def inv_rms(v):
    return lax.rsqrt(jnp.mean(v * v, axis=-1, keepdims=True) + EPS)


def norm_back(v, r, g, up):
    n = v * r
    w = up * g
    return r * (w - n * jnp.mean(w * n, axis=-1, keepdims=True)), up * n


def swap(x, axis, n, k):
    return lax.ppermute(x, axis, [(i, i ^ k) for i in range(n)])


def bits(n):
    return n.bit_length() - 1


def turned(j, n):
    return sum(((j >> i) & 1) << (bits(n) - 1 - i) for i in range(bits(n)))


def mask_of(j, n, t):
    return j + t * (turned(j, n) - j)


def hop(x, axis, n, i):
    steps = [1 << i, 1 << (bits(n) - 1 - i)]
    return lax.ppermute(x, (axis, "tensor"), [(2 * d + t, 2 * (d ^ steps[t]) + t) for d in range(n) for t in range(2)])


def scatter(blocks, axis, n):
    got = {k: swap(blocks[k], axis, n, k) for k in range(n - 1, 0, -1)}
    return [blocks[0]] + [got[k] for k in range(1, n)]


def join(a, b):
    def body(a_ref, b_ref, o_ref):
        o_ref[: a.shape[0]] = a_ref[...]
        o_ref[a.shape[0] :] = b_ref[...]

    return call(body, [shape(2 * a.shape[0], *a.shape[1:])], [a, b], vmem_mb=8)[0]


def gather(x, axis, n):
    x = x[None]
    for i in range(bits(n)):
        got = hop(x, axis, n, i)
        if i < bits(n) - 1:
            x = join(x, got)
    return [x, got]


def reduce_blocks(low, high, axis, n, gate=None, first=None):
    for i in range(bits(n) - 1, -1, -1):
        got = hop(high, axis, n, i)
        if first is not None and i == bits(n) - 1:
            first.append(got)
        if gate is not None and i:
            got = after(got, gate)
        low = low.astype(F32) + got.astype(F32)
        if i:
            keep = low.shape[0] // 2
            low, high = low[:keep], low[keep:].astype(BF)
    return low[0]


def after(x, *deps):
    return lax.optimization_barrier((x, deps))[0]


def at(offset, size, unit):
    return pl.ds(pl.multiple_of(offset, unit), size)


def call(body, outs, args, scratch=(), flops=0, vmem_mb=20, hbm=0, hbm_outs=0):
    vmem = pl.BlockSpec(memory_space=pltpu.VMEM)
    far = pl.BlockSpec(memory_space=pltpu.MemorySpace.HBM)
    moved = sum(a.size * a.dtype.itemsize for a in list(args) + list(outs))
    return pl.pallas_call(
        body,
        out_shape=list(outs),
        in_specs=[far] * hbm + [vmem] * (len(args) - hbm),
        out_specs=[far] * hbm_outs + [vmem] * (len(outs) - hbm_outs),
        scratch_shapes=list(scratch),
        cost_estimate=pl.CostEstimate(flops=flops, bytes_accessed=moved, transcendentals=0),
        compiler_params=pltpu.CompilerParams(vmem_limit_bytes=vmem_mb * 1024 * 1024),
    )(*args)


def shape(*s, dtype=BF):
    return jax.ShapeDtypeStruct(s, dtype)


def solution(mesh):
    F, C, T = mesh.shape["fsdp"], mesh.shape["context"], mesh.shape["tensor"]

    def local(
        hidden, segments, w_query, w_key, w_value, w_out, w_gate, w_up, w_down,
        gain_attn, gain_ffn, gain_query, gain_key, cotangent,
    ):
        f, c, t = lax.axis_index("fsdp"), lax.axis_index("context"), lax.axis_index("tensor")
        tokens, width = hidden.shape[1], hidden.shape[2]
        half = tokens // T
        rows = w_query.shape[0]
        grow = gain_query.shape[0]
        kv_local = w_key.shape[1] // HEAD
        qc = w_query.shape[1] // C
        kw = max(HEAD, w_key.shape[1] // C)
        hc = w_gate.shape[1] // F
        hp = -(-hc // 128) * 128
        qh, kh = qc // HEAD, kw // HEAD
        group = qh // kh
        aw = qc + 2 * kw
        CR = C * rows
        R = T * C * half
        H = R // 2
        scale = HEAD ** (-0.5)
        share = kw * C // w_key.shape[1]
        wide = aw + qc + width
        CH, FH = C // 2, F // 2

        lane = (f * C + c) * rows % 128
        goff = (f * C + c) * grow

        hid = hidden.reshape(tokens, width)
        tall = max(rows, half)

        def me():
            return lax.axis_index("fsdp"), lax.axis_index("context")

        def ffn_pack(wg_ref, wu_ref, wd_ref, *refs):
            outs, sem = refs[:F], refs[F]
            mf, _ = me()
            copies = []
            for k in range(F):
                for j, w in enumerate((wg_ref, wu_ref, wd_ref)):
                    copies.append(pltpu.make_async_copy(w.at[:, at((mf ^ k) * hp, hp, 128)], outs[k].at[:, j * hp : (j + 1) * hp], sem.at[k, j]))
            for cp in copies:
                cp.start()
            for cp in copies:
                cp.wait()

        w_down = w_down.T
        if hp > hc:
            fill = [((0, 0), (0, 0), (0, hp - hc))]
            w_gate, w_up, w_down = [jnp.pad(w.reshape(rows, F, hc), *fill).reshape(rows, F * hp) for w in (w_gate, w_up, w_down)]
        wf = call(
            ffn_pack,
            [shape(rows, 3 * hp)] * F,
            [w_gate, w_up, w_down],
            [pltpu.SemaphoreType.DMA((F, 3))],
            hbm=3,
            vmem_mb=60,
        )
        def attn_pack(wq_ref, wk_ref, wv_ref, wo_ref, x_ref, ga_ref, gf_ref, gq_ref, gk_ref, s_ref, *refs):
            outs, sem = refs[:C], refs[C]
            mt = lax.axis_index("tensor")
            mf, mc = me()
            copies = []
            for k in range(C):
                d = mc ^ k
                ks = at(d * kv_local // C * HEAD, kw, 128)
                qs = at(d * qc, qc, 128)
                parts = [(wq_ref, qs, 0, qc), (wk_ref, ks, qc, kw), (wv_ref, ks, qc + kw, kw), (wo_ref, qs, aw, qc)]
                copies.append(pltpu.make_async_copy(x_ref.at[at(mt * half, half, half), :], outs[k].at[0:half, aw + qc :], sem.at[k, 4]))
                for m, (w, src, start, size) in enumerate(parts):
                    copies.append(pltpu.make_async_copy(w.at[:, src], outs[k].at[0:rows, start : start + size], sem.at[k, m]))
            for cp in copies:
                cp.start()
            dest = mf * C + mc
            lanes = lax.broadcasted_iota(jnp.int32, (8, 128), 1)
            docs = jnp.broadcast_to(s_ref[...].astype(F32), (8, 128))
            docs = jnp.where((lanes < half) == (mt == 0), docs, pltpu.roll(docs, half, 1))

            def placed(ref, want):
                size = ref.shape[1]
                r = lax.broadcasted_iota(jnp.int32, (size, 128), 0)
                pick = (lax.broadcasted_iota(jnp.int32, (size, 128), 1) == r + want).astype(F32).astype(BF)
                return mm(jnp.broadcast_to(ref[...].astype(F32), (8, size)).astype(BF), pick)[0:1]

            ln, hd = dest * rows % 128, dest * grow
            blank = jnp.zeros((1, aw - 384), F32) if aw > 384 else None
            first = [placed(ga_ref, ln), placed(gf_ref, ln), placed(gq_ref, hd)]
            first = jnp.concatenate(first + ([blank] if aw > 384 else []), 1)
            second = jnp.concatenate([placed(gk_ref, hd), jnp.zeros((1, aw - 128), F32)], 1)
            ext = jnp.concatenate([first, second, jnp.zeros((6, aw), F32)], 0).astype(BF)
            for k in range(C):
                outs[k][tall:, :aw] = ext
                outs[k][tall:, aw : aw + qc] = jnp.zeros((8, qc), BF)
                outs[k][tall:, aw + qc : aw + qc + 128] = docs.astype(BF)
                outs[k][tall:, aw + qc + 128 :] = jnp.zeros((8, width - 128), BF)
            for cp in copies:
                cp.wait()

        wa = call(
            attn_pack,
            [shape(tall + 8, wide)] * C,
            list(after((w_query, w_key, w_value, w_out.T, hid), wf[0]))
            + [v.reshape(1, -1) for v in (gain_attn, gain_ffn, gain_query, gain_key)]
            + [segments.reshape(1, tokens)],
            [pltpu.SemaphoreType.DMA((C, 5))],
            hbm=5,
            vmem_mb=60,
        )
        wa_got = scatter(wa, "context", C)

        wf = scatter(wf, "fsdp", F)

        def ffn_join(*refs):
            for k in range(F):
                refs[F][k] = refs[k][...]

        wf_got = wf
        wf = call(ffn_join, [shape(F, rows, 3 * hp)], [after(wf[0], wa_got[1])] + wf[1:], vmem_mb=8)[0]
        wf_first = hop(wf[None], "context", C, 0)
        wf_here = wf[None]

        def attn_join(*refs):
            b, qkv, o, x, docs = refs[:C], refs[C], refs[C + 1], refs[C + 2], refs[C + 3]
            mt = lax.axis_index("tensor")
            docs[...] = jnp.zeros_like(docs)
            for k in range(C):
                j = mask_of(k, C, mt)
                qkv[k * rows : (k + 1) * rows, :] = b[k][0:rows, :aw]
                o[k * rows : (k + 1) * rows, :] = b[k][0:rows, aw : aw + qc]
                x[at(j * half, half, half), :] = b[k][0:half, aw + qc :]
                docs[pl.ds(j, 1), :] = b[k][tall:, aw + qc : aw + qc + 128].astype(F32)[0:1]
            x[C * half :, :128] = docs[...].astype(BF)
            x[C * half :, 128:] = jnp.zeros((8, width - 128), BF)
            qkv[CR:, :] = jnp.concatenate([b[k][tall:, :aw].astype(F32)[0:2] for k in range(C)], 0).astype(BF)

        wq, wo, x_own = call(
            attn_join,
            [shape(CR + 2 * C, aw), shape(CR, qc), shape(C * half + 8, width)],
            [after(wa_got[0], wf_got)] + wa_got[1:],
            [pltpu.VMEM((8, 128), F32)],
        )
        wq = gather(wq, "fsdp", F)
        wo = gather(after(wo, wq[0]), "fsdp", F)

        def my_half(x):
            return lax.dynamic_slice_in_dim(x, t * half, half, 0)

        def other_half(x):
            return lax.dynamic_slice_in_dim(x, (1 - t) * half, half, 0)

        def swap_t(x):
            return swap(x, "tensor", T, 1)

        x_half = my_half(hid)
        xs = [x_own, swap_t(x_own)]

        idx = jnp.arange(R, dtype=jnp.int32)
        trel, k, i = idx // (C * half), (idx // half) % C, idx % half
        pos = (c ^ mask_of(k, C, t ^ trel)) * tokens + (t ^ trel) * half + i
        freq = THETA ** (-(jnp.arange(HEAD // 2, dtype=F32) * 2.0 / HEAD))
        angle = pos.astype(F32)[:, None] * freq[None, :]
        cos, sin = jnp.cos(angle), jnp.sin(angle)
        cos, sin = jnp.concatenate([cos, cos], 1), jnp.concatenate([-sin, sin], 1)
        pos_row = jnp.broadcast_to(pos[None], (8, R))
        pos_col = jnp.broadcast_to(pos[:, None], (R, 128))

        def find_allowed(a_ref, b_ref, pr_ref, pc_ref, out):
            copies = CH * (2 * half // 128)
            row = []
            for ref in (a_ref, b_ref):
                d = ref[C * half :, :128].astype(F32)
                d = jnp.concatenate([d] * (C * half // 128), 1)
                keep = lax.broadcasted_iota(jnp.int32, d.shape, 1) // half == lax.broadcasted_iota(jnp.int32, d.shape, 0)
                row.append(jnp.sum(jnp.where(keep, d, 0.0), 0, keepdims=True))
            row = jnp.broadcast_to(jnp.concatenate(row, 1), (8, R))
            first = (lax.broadcasted_iota(jnp.int32, (8, 128), 0) == 0).astype(F32).astype(BF)
            col = mt_m(row.astype(BF), first)
            pc = pc_ref[...]
            for m in range(R // 128):
                sl = slice(m * 128, (m + 1) * 128)
                ok = (col == row[0:1, sl]) & (pc >= pr_ref[0:1, sl])
                out[:, sl] = jnp.where(ok, 1.0, 0.0).astype(BF)

        allowed = call(find_allowed, [shape(R, R)], xs + [pos_row, pos_col])[0]

        def reduce(own, low, high, axis, n, gate=None, enter=None, first=None):
            keep = H // 2
            if high is None:
                low = swap_t(low)
                low, high = low[:keep], low[keep:]
            else:
                low, high = swap_t(low), swap_t(high)
            high = (own[keep:] + high.astype(F32)).astype(BF)
            low = own[:keep] + low.astype(F32)
            if enter is not None:
                high = after(high, enter)
            shaped = (n // 2, half, width)
            return reduce_blocks(low.reshape(shaped), high.reshape(shaped), axis, n, gate, first), high

        def spread(x, axis, n):
            b = [x]
            for i in range(bits(n)):
                b = b + [hop(a, axis, n, i) for a in b]
            return b + [swap_t(a) for a in b]

        def both_halves(x):
            y = swap_t(x)
            return jnp.where(t == 0, jnp.concatenate([x, y], 0), jnp.concatenate([y, x], 0))

        cot = cotangent.reshape(tokens, width)
        dys = gather(after(my_half(cot), wo[0]), "fsdp", F)
        dys = dys + [swap_t(b) for b in dys]

        def rotate(v, cs, sn):
            return v * cs + pltpu.roll(v, HEAD // 2, 1) * sn

        def split_rows(p, own, low, high):
            own[...] = p[:H]
            low[...] = p[H : H + H // 2].astype(BF)
            high[...] = p[H + H // 2 :].astype(BF)

        def split_whole(p, own, send):
            own[...] = p[:H]
            send[...] = p[H:].astype(BF)

        whole = [shape(H, width, dtype=F32), shape(H, width)]
        halves = [shape(H, width, dtype=F32), shape(H // 2, width), shape(H // 2, width)]

        got = wf_first
        for i in range(1, bits(C)):
            wf_here = join(wf_here, got)
            got = hop(wf_here, "context", C, i)
        wf = [wf_here, got]

        def attn_fwd(*refs):
            xb, wb, refs = refs[:2], refs[2:4], refs[4:]
            cs_ref, sn_ref, ok_ref = refs[:3]
            outs, o, gv, gqk = refs[3:9], refs[9], refs[10], refs[11]
            h, raw, q, ky, v, w = refs[12:18]
            sem = refs[18]
            mf, mc = me()
            mt = lax.axis_index("tensor")
            sent = [pltpu.make_async_copy(a, b, sem.at[m]) for m, (a, b) in enumerate(zip((h, raw, q, ky, v, w), outs))]
            gv[...] = jnp.zeros_like(gv)
            acc = jnp.zeros((2, 128), F32)
            for a in range(F):
                wa_ref = wb[a // FH]
                e = wa_ref[a % FH, CR:, :].astype(F32)
                for b in range(C):
                    dest = (mf ^ mask_of(a, F, mt)) * C + (mc ^ b)
                    w[at(dest * rows, rows, rows), :] = wa_ref[a % FH, b * rows : (b + 1) * rows, :]
                    blk = at(dest * rows // 128 * 128, 128, 128)
                    gv[0:1, blk] += e[2 * b : 2 * b + 1, 0:128]
                    gv[1:2, blk] += e[2 * b : 2 * b + 1, 128:256]
                    acc += jnp.concatenate([e[2 * b : 2 * b + 1, 256:384], e[2 * b + 1 : 2 * b + 2, 0:128]], 0)
            gqk[0:2, :] = acc
            g = gv[0:1, :]
            for b in range(2 * C):
                x = xb[b // C][b % C * half : (b % C + 1) * half, :].astype(F32)
                h[b * half : (b + 1) * half, :] = (x * inv_rms(x) * g).astype(BF)
            sent[0].start()
            sent[5].start()
            p = mm(h[...], w[...])
            raw[...] = p[:, : qc + kw]
            v[...] = p[:, qc + kw :].astype(BF)
            sent[1].start()
            sent[4].start()
            cs, sn = cs_ref[...], sn_ref[...]
            for j in range(qh + kh):
                a = p[:, j * HEAD : (j + 1) * HEAD]
                gg = gqk[0:1, :] if j < qh else gqk[1:2, :]
                rot = rotate(a * inv_rms(a) * gg, cs, sn).astype(BF)
                if j < qh:
                    q[:, j * HEAD : (j + 1) * HEAD] = rot
                else:
                    ky[:, (j - qh) * HEAD : (j - qh + 1) * HEAD] = rot
            sent[2].start()
            sent[3].start()
            ok = ok_ref[...].astype(F32) > 0.5
            for j in range(qh):
                qs = slice(j * HEAD, (j + 1) * HEAD)
                ks = slice(j // group * HEAD, (j // group + 1) * HEAD)
                e = jnp.where(ok, jnp.exp(mm_t(q[:, qs], ky[:, ks]) * scale), 0.0)
                o[:, qs] = (mm(e.astype(BF), v[:, ks]) / jnp.sum(e, -1, keepdims=True)).astype(BF)
            for cp in sent:
                cp.wait()

        kept = [shape(R, width), shape(R, qc + kw, dtype=F32), shape(R, qc), shape(R, kw), shape(R, kw), shape(width, aw)]
        h, raw, q, ky, v, w_qkv, o, gv, gqk = call(
            attn_fwd,
            kept + [shape(R, qc), shape(8, width, dtype=F32), shape(8, 128, dtype=F32)],
            xs + wq + [cos, sin, after(allowed, wf_first)],
            [pltpu.VMEM(a.shape, a.dtype) for a in kept] + [pltpu.SemaphoreType.DMA((6,))],
            flops=2 * R * width * aw + 4 * R * R * qc,
            hbm_outs=6,
        )

        def out_proj(o_ref, *refs):
            wb, own, low, high, w = refs[:2], *refs[2:]
            mf, mc = me()
            mt = lax.axis_index("tensor")
            for a in range(F):
                for b in range(C):
                    dest = (mf ^ mask_of(a, F, mt)) * C + (mc ^ b)
                    w[at(dest * rows, rows, rows), :] = wb[a // FH][a % FH, b * rows : (b + 1) * rows, :]
            split_rows(mm_t(o_ref[...], w[...]), own, low, high)

        res = call(
            out_proj,
            halves + [shape(width, qc)],
            [after(o, wf[1])] + wo,
            flops=2 * R * width * qc,
        )
        w_o = res[3]
        x_mid = x_half.astype(F32) + reduce(*res[:3], "context", C)[0]
        r2 = inv_rms(x_mid)
        g_ffn = gv[1:2]
        h2s = spread((x_mid * r2 * g_ffn).astype(BF), "fsdp", F)

        def ffn_pre(*refs):
            wb, db, w, dy, du = refs[:2], refs[2:6], *refs[6:]
            mf, mc = me()
            mt = lax.axis_index("tensor")
            for a in range(C):
                for b in range(F):
                    dest = (mf ^ b) * C + (mc ^ mask_of(a, C, mt))
                    w[at(dest * rows, rows, rows), :] = wb[a // CH][a % CH, b]
            for b in range(2 * F):
                dy[b * half : (b + 1) * half, :] = db[b // FH][b % FH]
            du[...] = mm(dy[...], w[:, 2 * hp :])

        w_f, dy, du = call(
            ffn_pre,
            [shape(width, 3 * hp), shape(R, width), shape(R, hp, dtype=F32)],
            wf + dys,
            flops=2 * R * width * hp,
        )

        def ffn_main(*refs):
            hb, w, du_ref, own, low, high, h2, act = refs[: 2 * F], *refs[2 * F :]
            for b in range(2 * F):
                h2[b * half : (b + 1) * half, :] = hb[b][...]
            p = mm(h2[...], w[:, : 2 * hp])
            gate, up = p[:, :hp], p[:, hp:]
            sg = 1.0 / (1.0 + jnp.exp(-gate))
            d = du_ref[...]
            sl = gate * sg
            act[:, :hp] = (d * up * sg * (1.0 + gate * (1.0 - sg))).astype(BF)
            act[:, hp : 2 * hp] = (d * sl).astype(BF)
            act[:, 2 * hp :] = (sl * up).astype(BF)
            split_rows(mm_t(act[:, : 2 * hp], w[:, : 2 * hp]), own, low, high)

        res = call(
            ffn_main,
            halves + [shape(R, width), shape(R, 3 * hp)],
            h2s + [w_f, du],
            flops=8 * R * width * hp,
        )
        h2, act = res[3:]
        dh2, dh2_sent = reduce(*res[:3], "fsdp", F)
        act = after(act, dh2_sent)

        def ffn_post(h2_ref, dy_ref, act_ref, w, *refs):
            own, send, gd, gu, g = refs[0], refs[1], refs[2:4], refs[4:6], refs[6]
            mf, mc = me()
            mt = lax.axis_index("tensor")
            g[:, : 2 * hp] = mt_m(h2_ref[...], act_ref[:, : 2 * hp]).astype(BF)
            g[:, 2 * hp :] = mt_m(dy_ref[...], act_ref[:, 2 * hp :]).astype(BF)
            for a in range(C):
                for b in range(F):
                    dest = (mf ^ b) * C + (mc ^ mask_of(a, C, mt))
                    src = at(dest * rows, rows, rows)
                    gu[a // CH][a % CH, b] = g[src, : 2 * hp]
                    gd[a // CH][a % CH, b] = g[src, 2 * hp :]
            split_whole(mm_t(act_ref[:, 2 * hp :], w[:, 2 * hp :]), own, send)

        res = call(
            ffn_post,
            whole + [shape(CH, F, rows, hp)] * 2 + [shape(CH, F, rows, 2 * hp)] * 2,
            [h2, dy, act, w_f],
            [pltpu.VMEM((width, 3 * hp), BF)],
            flops=8 * R * width * hp,
        )
        out_parts, down_parts, units_parts = list(res[:2]) + [None], res[2:4], res[4:6]

        inward, gn_rows = norm_back(x_mid, r2, g_ffn, dh2)
        dg_ffn = jnp.sum(gn_rows, 0, keepdims=True)
        dx_mid = my_half(cot).astype(F32) + inward
        dx_low = dx_mid.astype(BF)
        dxs = spread(dx_low, "context", C)
        units_first, out_first = [], []
        g_units = reduce_blocks(*after(units_parts, dxs[1:C]), "context", C, first=units_first)
        out = (x_mid + reduce(*out_parts, "fsdp", F, enter=dx_low, first=out_first)[0]).astype(BF)

        def out_back(*refs):
            db, o_ref, w, dx, ga, gb, g = refs[: 2 * C], *refs[2 * C : 2 * C + 4], refs[2 * C + 4 : -1], refs[-1]
            mf, mc = me()
            mt = lax.axis_index("tensor")
            for b in range(2 * C):
                dx[b * half : (b + 1) * half, :] = db[b][...]
            g[...] = mt_m(dx[...], o_ref[...]).astype(BF)
            for a in range(F):
                for b in range(C):
                    dest = (mf ^ mask_of(a, F, mt)) * C + (mc ^ b)
                    gb[a // FH][a % FH, b * rows : (b + 1) * rows, :] = g[at(dest * rows, rows, rows), :]
            ga[...] = mm(dx[...], w[...])

        res = call(
            out_back,
            [shape(R, width), shape(R, qc, dtype=F32)] + [shape(FH, CR, qc)] * 2,
            dxs + [o, w_o],
            [pltpu.VMEM((width, qc), BF)],
            flops=4 * R * width * qc,
        )
        o_first = []
        g_att, go = after(res[1], out_first[0]), reduce_blocks(*res[2:], "fsdp", F, first=o_first)
        g_down = reduce_blocks(*down_parts, "context", C, gate=res[1])

        def attn_back(*refs):
            xb, refs = refs[:2], refs[2:]
            ga, h_ref, raw, q, ky, v, w, gv_ref, gqk_ref, cs_ref, sn_ref, ok_ref, dgf, own, send = refs[:15]
            gb, draw, gs_ref, ex, gn = refs[15:17], *refs[17:]
            mf, mc = me()
            mt = lax.axis_index("tensor")
            cs, sn = cs_ref[...], sn_ref[...]
            ok = ok_ref[...].astype(F32) > 0.5
            dk, dv = [0.0] * kh, [0.0] * kh
            dgq, dgk = jnp.zeros((1, HEAD), F32), jnp.zeros((1, HEAD), F32)
            for j in range(qh):
                qs = slice(j * HEAD, (j + 1) * HEAD)
                ks = slice(j // group * HEAD, (j // group + 1) * HEAD)
                qj, kj, vj, g = q[:, qs], ky[:, ks], v[:, ks], ga[:, qs]
                e = jnp.where(ok, jnp.exp(mm_t(qj, kj) * scale), 0.0)
                inv = 1.0 / jnp.sum(e, -1, keepdims=True)
                eb = e.astype(BF)
                attn = mm(eb, vj) * inv
                gsc = (g * inv).astype(BF)
                dt = -jnp.sum(g * attn, -1, keepdims=True) * inv
                dv[j // group] += mt_m(eb, gsc)
                ds = (e * (mm_t(gsc, vj) + dt)).astype(BF)
                dk[j // group] += mt_m(ds, qj) * scale
                a = raw[:, qs]
                back, dg = norm_back(a, inv_rms(a), gqk_ref[0:1, :], rotate(mm(ds, kj) * scale, cs, -sn))
                draw[:, qs] = back.astype(BF)
                dgq += jnp.sum(dg, 0, keepdims=True)
            for j in range(kh):
                ks = slice(qc + j * HEAD, qc + (j + 1) * HEAD)
                a = raw[:, ks]
                back, dg = norm_back(a, inv_rms(a), gqk_ref[1:2, :], rotate(dk[j], cs, -sn))
                draw[:, ks] = back.astype(BF)
                dgk += jnp.sum(dg, 0, keepdims=True)
                draw[:, qc + kw + j * HEAD : qc + kw + (j + 1) * HEAD] = dv[j].astype(BF)
            gs_ref[...] = mt_m(h_ref[...], draw[...]).astype(BF)
            dh = mm_t(draw[...], w[...])
            split_whole(dh, own, send)
            total = jnp.zeros((1, width), F32)
            for b in range(2 * C):
                x = xb[b // C][b % C * half : (b % C + 1) * half, :].astype(F32)
                total += jnp.sum(dh[b * half : (b + 1) * half] * (x * inv_rms(x)), 0, keepdims=True)
            gn[0:1, :] = total
            gn[1:2, :] = dgf[...]
            ex[...] = jnp.zeros_like(ex)
            for a in range(F):
                for b in range(C):
                    dest = (mf ^ mask_of(a, F, mt)) * C + (mc ^ b)
                    gb[a // FH][a % FH, b * rows : (b + 1) * rows, :] = gs_ref[at(dest * rows, rows, rows), :]
                    blk = at(dest * rows // 128 * 128, 128, 128)
                    ex[2 * b : 2 * b + 1, 0:128] = gn[0:1, blk]
                    ex[2 * b : 2 * b + 1, 128:256] = gn[1:2, blk]
                    ex[2 * b : 2 * b + 1, 256:384] = dgq
                    ex[2 * b + 1 : 2 * b + 2, 0:128] = dgk
                gb[a // FH][a % FH, CR:, :] = ex[...].astype(BF)

        res = call(
            attn_back,
            whole + [shape(FH, CR + 2 * C, aw)] * 2,
            xs + [g_att, h, raw, q, ky, v, w_qkv, gv, gqk, cos, sin, allowed, dg_ffn],
            [pltpu.VMEM((R, aw), BF), pltpu.VMEM((width, aw), BF), pltpu.VMEM((2 * C, aw), F32), pltpu.VMEM((8, width), F32)],
            flops=4 * R * width * aw + 12 * R * R * qc,
        )
        gq = reduce_blocks(res[2], after(res[3], o_first[0]), "fsdp", F, gate=units_first[0]).astype(BF)
        gf = jnp.concatenate([g_units.astype(BF), g_down.astype(BF)], -1)
        gf = scatter([gf[0]] + [gf[k] for k in range(1, F)], "fsdp", F)

        def ffn_owner(*refs):
            b, outs = refs[:F], refs[F:]
            mf, _ = me()
            for k in range(F):
                d = at((mf ^ k) * hp, hp, 128)
                for m in range(3):
                    outs[m][:, d] = b[k][:, m * hp : (m + 1) * hp].astype(F32)

        ffn_grads = call(ffn_owner, [shape(rows, F * hp, dtype=F32)] * 3, gf)
        if hp > hc:
            ffn_grads = [g.reshape(rows, F, hp)[:, :, :hc].reshape(rows, F * hc) for g in ffn_grads]
        go = go.astype(BF)
        ga = []
        for j in range(C):
            both_grads = jnp.concatenate([gq[j * rows : (j + 1) * rows], go[j * rows : (j + 1) * rows]], 1)
            gains = jnp.pad(gq[CR + 2 * j : CR + 2 * j + 2], ((0, 6), (0, qc)))
            ga.append(jnp.concatenate([both_grads, gains], 0))
        ga = scatter([ga[0]] + list(after(ga[1:], g_units)), "context", C)
        dh = reduce(res[0], res[1], None, "context", C, enter=units_first[0])[0]
        x32 = x_half.astype(F32)
        inward, _ = norm_back(x32, inv_rms(x32), gv[0:1], dh)
        grad_hidden = (dx_mid + inward).astype(BF)

        def attn_owner(*refs):
            b, gwq, gwk, gwv, gwo, ge = refs[:C], *refs[C:]
            _, mc = me()
            if share > 1:
                gwk[...] = jnp.zeros_like(gwk)
                gwv[...] = jnp.zeros_like(gwv)
            e = jnp.zeros((8, aw), F32)
            for j in range(C):
                d = mc ^ j
                gwq[:, at(d * qc, qc, 128)] = b[j][0:rows, :qc].astype(F32)
                gwo[:, at(d * qc, qc, 128)] = b[j][0:rows, aw:].astype(F32)
                ks = at(d * kv_local // C * HEAD, kw, 128)
                gk = b[j][0:rows, qc : qc + kw].astype(F32)
                gw = b[j][0:rows, qc + kw : aw].astype(F32)
                if share > 1:
                    gwk[:, ks] += gk
                    gwv[:, ks] += gw
                else:
                    gwk[:, ks] = gk
                    gwv[:, ks] = gw
                e += b[j][rows:, :aw].astype(F32)
            ge[...] = e

        gwq, gwk, gwv, gwo, ge = call(
            attn_owner,
            [
                shape(rows, C * qc, dtype=F32), shape(rows, kv_local * HEAD, dtype=F32),
                shape(rows, kv_local * HEAD, dtype=F32), shape(rows, C * qc, dtype=F32), shape(8, aw, dtype=F32),
            ],
            ga,
        )
        ge = ge + swap_t(ge)

        def piece(row, start, off, size):
            return lax.dynamic_slice(ge, (row, start + off), (1, size)).reshape(size)

        return (
            both_halves(out).reshape(1, tokens, width),
            both_halves(grad_hidden).reshape(1, tokens, width),
            gwq, gwk, gwv, gwo.T,
            ffn_grads[0], ffn_grads[1], ffn_grads[2].T,
            piece(0, 0, lane, rows), piece(0, 128, lane, rows), piece(0, 256, goff, grow), piece(1, 0, goff, grow),
        )

    both = ("fsdp", "context")
    seq, row, col, vec = P("fsdp", "context", None), P(both, "tensor"), P("tensor", both), P(both)
    return jax.shard_map(
        local,
        mesh=mesh,
        in_specs=(seq, P("fsdp", "context"), row, row, row, col, row, row, col, vec, vec, vec, vec, seq),
        out_specs=(seq, seq, row, row, row, col, row, row, col, vec, vec, vec, vec),
        check_vma=False,
    )
```

time: 307 us -> 225 us (0.73)
  Pallas kernels: 0 us -> 26.8 us
  other arithmetic: 37.1 us -> 10.3 us
  local copies, waits for them, and re-layouts: 35.1 us -> 8.96 us
  matrix products: 25.5 us -> 0 us
  starting transfers between devices: 87.8 us -> 64.7 us
  waiting for transfers between devices: 119 us -> 112 us
    ppermute x71 -> x32, waiting for transfers between devices: 119 us -> 24.4 us  [swap(): return lax.ppermute(x, axis, [(i, i ^ k) for i in range(n)])]
    ppermute x0 -> x30, waiting for transfers between devices: none -> 87.7 us  [hop(): lax.ppermute(x, (axis, 'tensor'), [(2 * d + t, 2 * (d ^ steps[t]) + t) fo...]
    ppermute x71 -> x32, starting transfers between devices: 87.8 us -> 31 us  [swap(): return lax.ppermute(x, axis, [(i, i ^ k) for i in range(n)])]
    ppermute x0 -> x30, starting transfers between devices: none -> 33.7 us  [hop(): lax.ppermute(x, (axis, 'tensor'), [(2 * d + t, 2 * (d ^ steps[t]) + t) fo...]
    pallas_call x0 -> x18, Pallas kernels: none -> 26.8 us  [call(): pl.pallas_call(body, out_shape=list(outs), in_specs=[far] * hbm + [vmem]...]
    dot_general x27 -> x0, matrix products: 25.5 us -> none  [the longest x9 11.7 us: mm_t(): lax.dot_general(a, b, (((1,), (1,)), ((), ())), preferred_element_type=F32)]
    another operation x32 -> x0, other arithmetic: 20.7 us -> none  [the longest x6 7.24 us: spread(): return jnp.stack([s, swap_t(s)]).reshape(R, width)]
    dot_general x3 -> x0, local copies, waits for them, and re-layouts: 5.4 us -> none  [mt_m(): lax.dot_general(a, b, (((0,), (0,)), ((), ())), preferred_element_type=F32)]
  transfers between devices with their start and end apart: 71 -> 62, of which waited for: 33 -> 29; matrix products, arithmetic and copies ran while one was open for 19% -> 5% of each run, Pallas kernels for 0% -> 8%
where the time goes in v2:
time: 225 us; the launch traced here: 224 us
  waiting for transfers between devices  112 us (50%)
  starting transfers between devices  64.7 us (29%)
  Pallas kernels  26.8 us (12%)
  other arithmetic  10.3 us (5%)
  local copies, waits for them, and re-layouts  8.96 us (4%)
    ppermute x30, waiting for transfers between devices, hop(): lax.ppermute(x, (axis, 'tensor'), [(2 * d + t, 2 * (d ^ steps[t]) + t) fo...  87.7 us
    ppermute x30, starting transfers between devices, hop(): lax.ppermute(x, (axis, 'tensor'), [(2 * d + t, 2 * (d ^ steps[t]) + t) fo...  33.7 us
    ppermute x32, starting transfers between devices, swap(): return lax.ppermute(x, axis, [(i, i ^ k) for i in range(n)])  31 us
    pallas_call x18, Pallas kernels, call(): pl.pallas_call(body, out_shape=list(outs), in_specs=[far] * hbm + [vmem]...  26.8 us
    ppermute x32, waiting for transfers between devices, swap(): return lax.ppermute(x, axis, [(i, i ^ k) for i in range(n)])  24.4 us
    unnamed x74, local copies, waits for them, and re-layouts  6.47 us
  transfers between devices with their start and end apart: 62, of which 29 were waited for; matrix products, arithmetic and copies ran while one was open for 5% of the time, Pallas kernels for 8%

profile of v2, /device:TPU:0, one launch (start us, length us, event | category | flops | bytes accessed | tf_op | source)
XLA Modules:
  0.0 224.4 jit_solution(7005539786904565645)
XLA Ops:
  0.6 2.0 shard_map.237
  2.6 3.1 %shard_map.238 = (bf16[72,1792]{1,0:T(8,128)(2,1)}, bf16[72,1792]{1,0:T(8,128)(2,1)}, bf16[72,1792]{1,0:T(8,128)(2,1)}, bf16[72,1792]{1,0:T(8,128)(2,1)}) custom-call(bf16[64,1024]{1,0:T(8,128)(2,1)} %wq_ref, bf16[64,512]{1,0:T(8,128)(2,1)} %wk_ref, bf16[64,512]{1,0:T(8,128)(2,1)} %wv_ref, bf16[64,1024]{1,0:T(8,128)(2,1)} %bitcast.141, ...), custom_call_target="tpu_custom_call" | custom-call | bytes 1688352 | tf_op jit(solution)/shard_map/pallas_call | solution.py:106
  5.8 3.0 %collective-permute-start.3 = (bf16[72,1792]{1,0:T(8,128)(2,1)}, bf16[72,1792]{1,0:T(8,128)(2,1)S(1)}, u32[]{:S(2)}, u32[]{:S(2)}) collective-permute-start(bf16[72,1792]{1,0:T(8,128)(2,1)} %get-tuple-element.100), channel_id=1, source_target_pairs={{0,2},{2,0},{4,6},{6,4},{1,3},{3,1},{5,7},{7,5},{8,10},{10,8},{12,... | collective-permute-start | bytes 774152 | tf_op jit(solution)/shard_map/ppermute | solution.py:38
  8.8 1.6 collective-permute-start
  10.4 2.6 %collective-permute-start.1 = (bf16[64,1152]{1,0:T(8,128)(2,1)}, bf16[64,1152]{1,0:T(8,128)(2,1)S(1)}, u32[]{:S(2)}, u32[]{:S(2)}) collective-permute-start(bf16[64,1152]{1,0:T(8,128)(2,1)} %get-tuple-element.97), channel_id=1, source_target_pairs={{0,16},{8,24},{16,0},{24,8},{1,17},{9,25},{17,1},{25,9},{2,18},{10... | collective-permute-start | bytes 442376 | tf_op jit(solution)/shard_map/ppermute | solution.py:38
  13.2 2.0 collective-permute-done.3.refs_1_
  16.2 8.3 %collective-permute-done.1.refs_2_ = bf16[64,1152]{1,0:T(8,128)(2,1)S(1)} collective-permute-done((bf16[64,1152]{1,0:T(8,128)(2,1)}, bf16[64,1152]{1,0:T(8,128)(2,1)S(1)}, u32[]{:S(2)}, u32[]{:S(2)}) %collective-permute-start.1) | collective-permute-done | bytes 147488 | tf_op jit(solution)/shard_map/ppermute | solution.py:38
  26.4 1.5 collective-permute-start.4
  27.9 1.1 collective-permute-start.5
  29.0 7.6 %collective-permute-done.9.b_ref = bf16[1,4,64,1152]{3,2,1,0:T(8,128)(2,1)S(1)} collective-permute-done((bf16[1,4,64,1152]{3,2,1,0:T(8,128)(2,1)S(1)}, bf16[1,4,64,1152]{3,2,1,0:T(8,128)(2,1)S(1)}, u32[]{:S(2)}, u32[]{:S(2)}) %collective-permute-start.9) | collective-permute-done | bytes 589856 | tf_op jit(solution)/shard_map/ppermute | solution.py:55
  36.7 1.2 collective-permute-start.10
  37.9 2.1 collective-permute-done.5.refs_3_
  40.1 3.4 %collective-permute-start.7 = (bf16[1,264,512]{2,1,0:T(8,128)(2,1)S(1)}, bf16[1,264,512]{2,1,0:T(8,128)(2,1)S(1)}, u32[]{:S(2)}, u32[]{:S(2)}) collective-permute-start(bf16[1,264,512]{2,1,0:T(8,128)(2,1)S(1)} %bitcast.126), channel_id=1, source_target_pairs={{0,8},{1,17},{8,0},{9,25},{16,24},{17,1},{24,16},{25,9},{2,10},{3,... | collective-permute-start | bytes 811016 | tf_op jit(solution)/shard_map/ppermute | solution.py:55
  43.6 6.4 %collective-permute-start.6 = (bf16[264,1024]{1,0:T(8,128)(2,1)S(1)}, bf16[264,1024]{1,0:T(8,128)(2,1)S(1)}, u32[]{:S(2)}, u32[]{:S(2)}) collective-permute-start(bf16[264,1024]{1,0:T(8,128)(2,1)S(1)} %get-tuple-element.103.a_ref.refs_0_), channel_id=1, source_target_pairs={{0,1},{1,0},{2,3},{3,2},{4,5},{5,4},{6,7},{7,6},{8,9},{9,8},{10,11... | collective-permute-start | bytes 1622024 | tf_op jit(solution)/shard_map/ppermute | solution.py:38
  50.1 1.6 collective-permute-start.8
  52.7 7.8 %collective-permute-done.11.b_ref = bf16[1,256,256]{2,1,0:T(8,128)(2,1)S(1)} collective-permute-done((bf16[1,256,256]{2,1,0:T(8,128)(2,1)S(1)}, bf16[1,256,256]{2,1,0:T(8,128)(2,1)S(1)}, u32[]{:S(2)}, u32[]{:S(2)}) %collective-permute-start.11) | collective-permute-done | bytes 131104 | tf_op jit(solution)/shard_map/ppermute | solution.py:55
  60.5 1.6 collective-permute-start.12
  62.8 8.3 %collective-permute-done.8.refs_3_ = bf16[2,264,512]{2,1,0:T(8,128)(2,1)S(1)} collective-permute-done((bf16[2,264,512]{2,1,0:T(8,128)(2,1)S(1)}, bf16[2,264,512]{2,1,0:T(8,128)(2,1)S(1)}, u32[]{:S(2)}, u32[]{:S(2)}) %collective-permute-start.8) | collective-permute-done | bytes 540704 | tf_op jit(solution)/shard_map/ppermute | solution.py:55
  71.1 3.9 %shard_map.243 = (bf16[512,1024]{1,0:T(8,128)(2,1)S(1)}, f32[512,384]{1,0:T(8,128)S(1)}, bf16[512,256]{1,0:T(8,128)(2,1)S(1)}, bf16[512,128]{1,0:T(8,128)(2,1)S(...) custom-call(bf16[264,1024]{1,0:T(8,128)(2,1)S(1)} %get-tuple-element, ...), custom_call_target="tpu_custom_call" | custom-call | flops 805306368 | bytes 6918144 | tf_op jit(solution)/shard_map/pallas_call | solution.py:106
  77.6 1.2 copy-done.18
  78.8 7.8 %collective-permute-start.14 = (bf16[128,1024]{1,0:T(8,128)(2,1)S(1)}, bf16[128,1024]{1,0:T(8,128)(2,1)S(1)}, u32[]{:S(2)}, u32[]{:S(2)}) collective-permute-start(bf16[128,1024]{1,0:T(8,128)(2,1)S(1)} %get-tuple-element.113), channel_id=1, source_target_pairs={{0,1},{1,0},{2,3},{3,2},{4,5},{5,4},{6,7},{7,6},{8,9},{9,8},{10,11... | collective-permute-start | bytes 786440 | tf_op jit(solution)/shard_map/ppermute | solution.py:38
  86.6 1.2 collective-permute-done.14
  89.1 1.5 collective-permute-start.15
  91.7 5.9 %collective-permute-done.24.b_ref = bf16[1,64,1024]{2,1,0:T(8,128)(2,1)S(1)} collective-permute-done((bf16[1,64,1024]{2,1,0:T(8,128)(2,1)S(1)}, bf16[1,64,1024]{2,1,0:T(8,128)(2,1)S(1)}, u32[]{:S(2)}, u32[]{:S(2)}) %collective-permute-start.24) | collective-permute-done | bytes 131104 | tf_op jit(solution)/shard_map/ppermute | solution.py:55
  97.8 1.2 convert_add_fusion.10
  99.0 1.1 collective-permute-start.16
  100.1 4.0 %collective-permute-done.16 = bf16[1,64,1024]{2,1,0:T(8,128)(2,1)S(1)} collective-permute-done((bf16[1,64,1024]{2,1,0:T(8,128)(2,1)S(1)}, bf16[1,64,1024]{2,1,0:T(8,128)(2,1)S(1)}, u32[]{:S(2)}, u32[]{:S(2)}) %collective-permute-start.16) | collective-permute-done | bytes 131104 | tf_op jit(solution)/shard_map/ppermute | solution.py:55
  105.2 1.8 collective-permute-done.25.refs_3_
  107.4 4.0 %collective-permute-done.17.refs_1_ = bf16[64,1024]{1,0:T(8,128)(2,1)S(1)} collective-permute-done((bf16[64,1024]{1,0:T(8,128)(2,1)S(1)}, bf16[64,1024]{1,0:T(8,128)(2,1)S(1)}, u32[]{:S(2)}, u32[]{:S(2)}) %collective-permute-start.17) | collective-permute-done | bytes 131104 | tf_op jit(solution)/shard_map/ppermute | solution.py:55
  111.4 2.1 collective-permute-start.19
  114.0 4.0 %collective-permute-done.19.refs_3_ = bf16[64,1024]{1,0:T(8,128)(2,1)S(1)} collective-permute-done((bf16[64,1024]{1,0:T(8,128)(2,1)S(1)}, bf16[64,1024]{1,0:T(8,128)(2,1)S(1)}, u32[]{:S(2)}, u32[]{:S(2)}) %collective-permute-start.19) | collective-permute-done | bytes 131104 | tf_op jit(solution)/shard_map/ppermute | solution.py:55
  118.0 2.2 shard_map.248
  120.2 2.6 %shard_map.249 = (f32[256,1024]{1,0:T(8,128)S(1)}, bf16[128,1024]{1,0:T(8,128)(2,1)S(1)}, bf16[128,1024]{1,0:T(8,128)(2,1)S(1)}, bf16[512,1024]{1,0:T(8,128)(2,1)S(1)}, bf16[512,1152]{1,0:T(8,128)(2,1)S(1)}) custom-call(bf16[64,1024]{1,0:T(8,128)(2,1)S(1)} %multiply_convert_fusion.refs_0_, bf16[64,1024]{1,0:T(8,128)(2,1)S(1)} %collective-permute-done.17.refs_1_, ...), custom_call_target="tpu_custom_call" | custom-call | flops 1610612736 | bytes 7995392 | tf_op jit(solution)/shard_map/pallas_call | solution.py:106
  123.5 1.1 collective-permute-done.30
  125.1 1.4 collective-permute-start.31
  126.5 8.4 %collective-permute-done.31 = bf16[2,64,1024]{2,1,0:T(8,128)(2,1)S(1)} collective-permute-done((bf16[2,64,1024]{2,1,0:T(8,128)(2,1)S(1)}, bf16[2,64,1024]{2,1,0:T(8,128)(2,1)S(1)}, u32[]{:S(2)}, u32[]{:S(2)}) %collective-permute-start.31) | collective-permute-done | bytes 262176 | tf_op jit(solution)/shard_map/ppermute | solution.py:55
  135.4 2.3 %shard_map.250 = (f32[256,1024]{1,0:T(8,128)S(1)}, bf16[256,1024]{1,0:T(8,128)(2,1)S(1)}, bf16[2,4,64,384]{3,2,1,0:T(8,128)(2,1)S(1)}, bf16[2,4,64,384]{3,2,1,0:...) custom-call(bf16[512,1024]{1,0:T(8,128)(2,1)S(1)} %get-tuple-element.118.h2_ref, ...), custom_call_target="tpu_custom_call" | custom-call | flops 1610612736 | bytes 9568256 | tf_op jit(solution)/shard_map/pallas_call | solution.py:106
  137.7 2.3 %collective-permute-done.32 = bf16[1,64,1024]{2,1,0:T(8,128)(2,1)S(1)} collective-permute-done((bf16[1,64,1024]{2,1,0:T(8,128)(2,1)S(1)}, bf16[1,64,1024]{2,1,0:T(8,128)(2,1)S(1)}, u32[]{:S(2)}, u32[]{:S(2)}) %collective-permute-start.32) | collective-permute-done | bytes 131104 | tf_op jit(solution)/shard_map/ppermute | solution.py:55
  141.2 1.4 collective-permute-start.36
  143.7 1.5 collective-permute-start.37
  145.2 1.7 collective-permute-done.36.refs_1_
  146.9 1.9 collective-permute-start.38
  149.5 2.6 %collective-permute-done.38.refs_3_ = bf16[64,1024]{1,0:T(8,128)(2,1)S(1)} collective-permute-done((bf16[64,1024]{1,0:T(8,128)(2,1)}, bf16[64,1024]{1,0:T(8,128)(2,1)S(1)}, u32[]{:S(2)}, u32[]{:S(2)}) %collective-permute-start.38) | collective-permute-done | bytes 131104 | tf_op jit(solution)/shard_map/ppermute | solution.py:55
  152.1 1.3 collective-permute-done.33
  153.4 1.3 convert_add_fusion.6
  154.8 1.2 collective-permute-start.44
  157.0 2.3 %shard_map.251 = (bf16[512,1024]{1,0:T(8,128)(2,1)}, f32[512,256]{1,0:T(8,128)S(1)}, bf16[2,256,256]{2,1,0:T(8,128)(2,1)S(1)}, bf16[2,256,256]{2,1,0:T(8,128)(2,1)S(1)}) custom-call(bf16[64,1024]{1,0:T(8,128)(2,1)S(1)} %get-tuple-element.167.refs_0_, bf16[64,1024]{1,0:T(8,128)(2,1)} %collective-permute-done.36.refs_1_, ...), custom_call_target="tpu_custom_call" | custom-call | flops 536870912 | bytes 3932160 | tf_op jit(solution)/shard_map/pallas_call | solution.py:106
  160.3 5.2 %shard_map.252 = (f32[256,1024]{1,0:T(8,128)S(1)}, bf16[256,1024]{1,0:T(8,128)(2,1)S(1)}, bf16[2,264,512]{2,1,0:T(8,128)(2,1)S(1)}, bf16[2,264,512]{2,1,0:T(8,128)(2,1)S(1)}) custom-call(bf16[264,1024]{1,0:T(8,128)(2,1)S(1)} %get-tuple-element.103.a_ref.refs_0_, bf16[264,1024]{1,0:T(8,128)(2,1)S(1)} %collective-permute-done.6.b_ref.refs_1_, ...), custom_call_target="tpu_custom_call" | custom-call | flops 1879048192 | bytes 8757248 | tf_op jit(solution)/shard_map/pallas_call | solution.py:106
  166.0 2.6 %collective-permute-start.48 = (bf16[2,256,256]{2,1,0:T(8,128)(2,1)S(1)}, bf16[2,256,256]{2,1,0:T(8,128)(2,1)S(1)}, u32[]{:S(2)}, u32[]{:S(2)}) collective-permute-start(bf16[2,256,256]{2,1,0:T(8,128)(2,1)S(1)} %get-tuple-element.146), channel_id=1, source_target_pairs={{0,16},{1,9},{8,24},{9,1},{16,0},{17,25},{24,8},{25,17},{2,18},{3,... | collective-permute-start | bytes 786440 | tf_op jit(solution)/shard_map/ppermute | solution.py:55
  168.7 1.2 collective-permute-start.57
  170.0 5.0 %collective-permute-done.48 = bf16[2,256,256]{2,1,0:T(8,128)(2,1)S(1)} collective-permute-done((bf16[2,256,256]{2,1,0:T(8,128)(2,1)S(1)}, bf16[2,256,256]{2,1,0:T(8,128)(2,1)S(1)}, u32[]{:S(2)}, u32[]{:S(2)}) %collective-permute-start.48) | collective-permute-done | bytes 262176 | tf_op jit(solution)/shard_map/ppermute | solution.py:55
  175.1 2.3 %collective-permute-start.51 = (bf16[1,256,256]{2,1,0:T(8,128)(2,1)S(1)}, bf16[1,256,256]{2,1,0:T(8,128)(2,1)S(1)}, u32[]{:S(2)}, u32[]{:S(2)}) collective-permute-start(bf16[1,256,256]{2,1,0:T(8,128)(2,1)S(1)} %slice.379), channel_id=1, source_target_pairs={{0,8},{1,17},{8,0},{9,25},{16,24},{17,1},{24,16},{25,9},{2,10},{3,... | collective-permute-start | bytes 393224 | tf_op jit(solution)/shard_map/ppermute | solution.py:55
  177.6 6.5 %collective-permute-done.51 = bf16[1,256,256]{2,1,0:T(8,128)(2,1)S(1)} collective-permute-done((bf16[1,256,256]{2,1,0:T(8,128)(2,1)S(1)}, bf16[1,256,256]{2,1,0:T(8,128)(2,1)S(1)}, u32[]{:S(2)}, u32[]{:S(2)}) %collective-permute-start.51) | collective-permute-done | bytes 131104 | tf_op jit(solution)/shard_map/ppermute | solution.py:55
  184.3 2.4 %collective-permute-start.45 = (bf16[2,64,1024]{2,1,0:T(8,128)(2,1)S(1)}, bf16[2,64,1024]{2,1,0:T(8,128)(2,1)S(1)}, u32[]{:S(2)}, u32[]{:S(2)}) collective-permute-start(bf16[2,64,1024]{2,1,0:T(8,128)(2,1)S(1)} %bitcast.136), channel_id=1, source_target_pairs={{0,4},{1,3},{2,6},{3,1},{4,0},{5,7},{6,2},{7,5},{8,12},{9,11},{10,... | collective-permute-start | bytes 786440 | tf_op jit(solution)/shard_map/ppermute | solution.py:55
  186.9 1.4 collective-permute-start.52
  188.4 5.2 %collective-permute-done.49 = bf16[2,264,512]{2,1,0:T(8,128)(2,1)S(1)} collective-permute-done((bf16[2,264,512]{2,1,0:T(8,128)(2,1)S(1)}, bf16[2,264,512]{2,1,0:T(8,128)(2,1)S(1)}, u32[]{:S(2)}, u32[]{:S(2)}) %collective-permute-start.49) | collective-permute-done | bytes 540704 | tf_op jit(solution)/shard_map/ppermute | solution.py:55
  193.7 1.2 collective-permute-start.46
  195.1 3.6 %collective-permute-done.46 = bf16[1,64,1024]{2,1,0:T(8,128)(2,1)S(1)} collective-permute-done((bf16[1,64,1024]{2,1,0:T(8,128)(2,1)S(1)}, bf16[1,64,1024]{2,1,0:T(8,128)(2,1)S(1)}, u32[]{:S(2)}, u32[]{:S(2)}) %collective-permute-start.46) | collective-permute-done | bytes 131104 | tf_op jit(solution)/shard_map/ppermute | solution.py:55
  199.5 1.5 collective-permute-start.59
  201.3 7.7 %collective-permute-done.50 = bf16[1,264,512]{2,1,0:T(8,128)(2,1)S(1)} collective-permute-done((bf16[1,264,512]{2,1,0:T(8,128)(2,1)S(1)}, bf16[1,264,512]{2,1,0:T(8,128)(2,1)S(1)}, u32[]{:S(2)}, u32[]{:S(2)}) %collective-permute-start.50) | collective-permute-done | bytes 270368 | tf_op jit(solution)/shard_map/ppermute | solution.py:55
  210.8 3.1 %collective-permute-done.53.refs_1_ = bf16[72,768]{1,0:T(8,128)(2,1)S(1)} collective-permute-done((bf16[72,768]{1,0:T(8,128)(2,1)S(1)}, bf16[72,768]{1,0:T(8,128)(2,1)S(1)}, u32[]{:S(2)}, u32[]{:S(2)}) %collective-permute-start.53) | collective-permute-done | bytes 110624 | tf_op jit(solution)/shard_map/ppermute | solution.py:38
  214.8 1.7 collective-permute-start.55
  216.5 3.9 %collective-permute-done.55.refs_3_ = bf16[72,768]{1,0:T(8,128)(2,1)S(1)} collective-permute-done((bf16[72,768]{1,0:T(8,128)(2,1)S(1)}, bf16[72,768]{1,0:T(8,128)(2,1)S(1)}, u32[]{:S(2)}, u32[]{:S(2)}) %collective-permute-start.55) | collective-permute-done | bytes 110624 | tf_op jit(solution)/shard_map/ppermute | solution.py:38
  222.2 1.1 shard_map.254
  (210 shorter events, 26.8 us)
Async XLA Ops:
  5.8 9.5 %collective-permute-start.3 = (bf16[72,1792]{1,0:T(8,128)(2,1)}, bf16[72,1792]{1,0:T(8,128)(2,1)S(1)}, u32[]{:S(2)}, u32[]{:S(2)}) collective-permute-start(bf16[72,1792]{1,0:T(8,128)(2,1)} %get-tuple-element.100), channel_id=1, source_target_pairs={{0,2},{2,0},{4,6},{6,4},{1,3},{3,1},{5,7},{7,5},{8,10},{10,8},{12,... | collective-permute-start | bytes 774152 | tf_op jit(solution)/shard_map/ppermute | solution.py:38
  8.8 7.4 %collective-permute-start = (bf16[64,1152]{1,0:T(8,128)(2,1)}, bf16[64,1152]{1,0:T(8,128)(2,1)S(1)}, u32[]{:S(2)}, u32[]{:S(2)}) collective-permute-start(bf16[64,1152]{1,0:T(8,128)(2,1)} %get-tuple-element.96), channel_id=1, source_target_pairs={{0,8},{8,0},{16,24},{24,16},{1,9},{9,1},{17,25},{25,17},{2,10},{10... | collective-permute-start | bytes 442376 | tf_op jit(solution)/shard_map/ppermute | solution.py:38
  10.4 14.1 %collective-permute-start.1 = (bf16[64,1152]{1,0:T(8,128)(2,1)}, bf16[64,1152]{1,0:T(8,128)(2,1)S(1)}, u32[]{:S(2)}, u32[]{:S(2)}) collective-permute-start(bf16[64,1152]{1,0:T(8,128)(2,1)} %get-tuple-element.97), channel_id=1, source_target_pairs={{0,16},{8,24},{16,0},{24,8},{1,17},{9,25},{17,1},{25,9},{2,18},{10... | collective-permute-start | bytes 442376 | tf_op jit(solution)/shard_map/ppermute | solution.py:38
  13.0 11.5 %collective-permute-start.2 = (bf16[64,1152]{1,0:T(8,128)(2,1)}, bf16[64,1152]{1,0:T(8,128)(2,1)S(1)}, u32[]{:S(2)}, u32[]{:S(2)}) collective-permute-start(bf16[64,1152]{1,0:T(8,128)(2,1)} %get-tuple-element.98), channel_id=1, source_target_pairs={{0,24},{8,16},{16,8},{24,0},{1,25},{9,17},{17,9},{25,1},{2,26},{10... | collective-permute-start | bytes 442376 | tf_op jit(solution)/shard_map/ppermute | solution.py:38
  25.5 11.2 %collective-permute-start.9 = (bf16[1,4,64,1152]{3,2,1,0:T(8,128)(2,1)S(1)}, bf16[1,4,64,1152]{3,2,1,0:T(8,128)(2,1)S(1)}, u32[]{:S(2)}, u32[]{:S(2)}) collective-permute-start(bf16[1,4,64,1152]{3,2,1,0:T(8,128)(2,1)S(1)} %bitcast.122), channel_id=1, source_target_pairs={{0,2},{1,5},{2,0},{3,7},{4,6},{5,1},{6,4},{7,3},{8,10},{9,13},{10,... | collective-permute-start | bytes 1769480 | tf_op jit(solution)/shard_map/ppermute | solution.py:55
  26.4 11.5 %collective-permute-start.4 = (bf16[72,1792]{1,0:T(8,128)(2,1)S(1)}, bf16[72,1792]{1,0:T(8,128)(2,1)S(1)}, u32[]{:S(2)}, u32[]{:S(2)}) collective-permute-start(bf16[72,1792]{1,0:T(8,128)(2,1)S(1)} %copy-done.36), channel_id=1, source_target_pairs={{0,4},{2,6},{4,0},{6,2},{1,5},{3,7},{5,1},{7,3},{8,12},{10,14},{12... | collective-permute-start | bytes 774152 | tf_op jit(solution)/shard_map/ppermute | solution.py:38
  27.9 12.2 %collective-permute-start.5 = (bf16[72,1792]{1,0:T(8,128)(2,1)S(1)}, bf16[72,1792]{1,0:T(8,128)(2,1)S(1)}, u32[]{:S(2)}, u32[]{:S(2)}) collective-permute-start(bf16[72,1792]{1,0:T(8,128)(2,1)S(1)} %copy-done.35), channel_id=1, source_target_pairs={{0,6},{2,4},{4,2},{6,0},{1,7},{3,5},{5,3},{7,1},{8,14},{10,12},{12... | collective-permute-start | bytes 774152 | tf_op jit(solution)/shard_map/ppermute | solution.py:38
  36.7 40.3 %collective-permute-start.10 = (bf16[2,4,64,1152]{3,2,1,0:T(8,128)(2,1)S(1)}, bf16[2,4,64,1152]{3,2,1,0:T(8,128)(2,1)}, u32[]{:S(2)}, u32[]{:S(2)}) collective-permute-start(bf16[2,4,64,1152]{3,2,1,0:T(8,128)(2,1)S(1)} %shard_map.244.refs_0_), channel_id=1, source_target_pairs={{0,4},{1,3},{2,6},{3,1},{4,0},{5,7},{6,2},{7,5},{8,12},{9,11},{10,... | collective-permute-start | bytes 3538952 | tf_op jit(solution)/shard_map/ppermute | solution.py:55
  40.1 9.9 %collective-permute-start.7 = (bf16[1,264,512]{2,1,0:T(8,128)(2,1)S(1)}, bf16[1,264,512]{2,1,0:T(8,128)(2,1)S(1)}, u32[]{:S(2)}, u32[]{:S(2)}) collective-permute-start(bf16[1,264,512]{2,1,0:T(8,128)(2,1)S(1)} %bitcast.126), channel_id=1, source_target_pairs={{0,8},{1,17},{8,0},{9,25},{16,24},{17,1},{24,16},{25,9},{2,10},{3,... | collective-permute-start | bytes 811016 | tf_op jit(solution)/shard_map/ppermute | solution.py:55
  43.6 18.8 %collective-permute-start.6 = (bf16[264,1024]{1,0:T(8,128)(2,1)S(1)}, bf16[264,1024]{1,0:T(8,128)(2,1)S(1)}, u32[]{:S(2)}, u32[]{:S(2)}) collective-permute-start(bf16[264,1024]{1,0:T(8,128)(2,1)S(1)} %get-tuple-element.103.a_ref.refs_0_), channel_id=1, source_target_pairs={{0,1},{1,0},{2,3},{3,2},{4,5},{5,4},{6,7},{7,6},{8,9},{9,8},{10,11... | collective-permute-start | bytes 1622024 | tf_op jit(solution)/shard_map/ppermute | solution.py:38
  50.1 21.0 %collective-permute-start.8 = (bf16[2,264,512]{2,1,0:T(8,128)(2,1)S(1)}, bf16[2,264,512]{2,1,0:T(8,128)(2,1)S(1)}, u32[]{:S(2)}, u32[]{:S(2)}) collective-permute-start(bf16[2,264,512]{2,1,0:T(8,128)(2,1)S(1)} %shard_map.240.refs_2_), channel_id=1, source_target_pairs={{0,16},{1,9},{8,24},{9,1},{16,0},{17,25},{24,8},{25,17},{2,18},{3,... | collective-permute-start | bytes 1622024 | tf_op jit(solution)/shard_map/ppermute | solution.py:55
  51.7 8.8 %collective-permute-start.11 = (bf16[1,256,256]{2,1,0:T(8,128)(2,1)S(1)}, bf16[1,256,256]{2,1,0:T(8,128)(2,1)S(1)}, u32[]{:S(2)}, u32[]{:S(2)}) collective-permute-start(bf16[1,256,256]{2,1,0:T(8,128)(2,1)S(1)} %bitcast.128), channel_id=1, source_target_pairs={{0,8},{1,17},{8,0},{9,25},{16,24},{17,1},{24,16},{25,9},{2,10},{3,... | collective-permute-start | bytes 393224 | tf_op jit(solution)/shard_map/ppermute | solution.py:55
  60.5 16.5 %collective-permute-start.12 = (bf16[2,256,256]{2,1,0:T(8,128)(2,1)S(1)}, bf16[2,256,256]{2,1,0:T(8,128)(2,1)S(1)}, u32[]{:S(2)}, u32[]{:S(2)}) collective-permute-start(bf16[2,256,256]{2,1,0:T(8,128)(2,1)S(1)} %shard_map.245.refs_0_), channel_id=1, source_target_pairs={{0,16},{1,9},{8,24},{9,1},{16,0},{17,25},{24,8},{25,17},{2,18},{3,... | collective-permute-start | bytes 786440 | tf_op jit(solution)/shard_map/ppermute | solution.py:55
  78.8 9.0 %collective-permute-start.14 = (bf16[128,1024]{1,0:T(8,128)(2,1)S(1)}, bf16[128,1024]{1,0:T(8,128)(2,1)S(1)}, u32[]{:S(2)}, u32[]{:S(2)}) collective-permute-start(bf16[128,1024]{1,0:T(8,128)(2,1)S(1)} %get-tuple-element.113), channel_id=1, source_target_pairs={{0,1},{1,0},{2,3},{3,2},{4,5},{5,4},{6,7},{7,6},{8,9},{9,8},{10,11... | collective-permute-start | bytes 786440 | tf_op jit(solution)/shard_map/ppermute | solution.py:38
  86.6 1.5 collective-permute-start.13
  89.1 8.7 %collective-permute-start.15 = (bf16[2,64,1024]{2,1,0:T(8,128)(2,1)}, bf16[2,64,1024]{2,1,0:T(8,128)(2,1)}, u32[]{:S(2)}, u32[]{:S(2)}) collective-permute-start(bf16[2,64,1024]{2,1,0:T(8,128)(2,1)} %bitcast.11), channel_id=1, source_target_pairs={{0,4},{1,3},{2,6},{3,1},{4,0},{5,7},{6,2},{7,5},{8,12},{9,11},{10,... | collective-permute-start | bytes 786440 | tf_op jit(solution)/shard_map/ppermute | solution.py:55
  91.7 6.0 %collective-permute-start.24 = (bf16[1,64,1024]{2,1,0:T(8,128)(2,1)S(1)}, bf16[1,64,1024]{2,1,0:T(8,128)(2,1)S(1)}, u32[]{:S(2)}, u32[]{:S(2)}) collective-permute-start(bf16[1,64,1024]{2,1,0:T(8,128)(2,1)S(1)} %bitcast.124), channel_id=1, source_target_pairs={{0,8},{1,17},{8,0},{9,25},{16,24},{17,1},{24,16},{25,9},{2,10},{3,... | collective-permute-start | bytes 393224 | tf_op jit(solution)/shard_map/ppermute | solution.py:55
  97.7 9.4 %collective-permute-start.25 = (bf16[2,64,1024]{2,1,0:T(8,128)(2,1)S(1)}, bf16[2,64,1024]{2,1,0:T(8,128)(2,1)S(1)}, u32[]{:S(2)}, u32[]{:S(2)}) collective-permute-start(bf16[2,64,1024]{2,1,0:T(8,128)(2,1)S(1)} %shard_map.247.refs_2_), channel_id=1, source_target_pairs={{0,16},{1,9},{8,24},{9,1},{16,0},{17,25},{24,8},{25,17},{2,18},{3,... | collective-permute-start | bytes 786440 | tf_op jit(solution)/shard_map/ppermute | solution.py:55
  97.7 15.7 %collective-permute-start.26 = (bf16[2,64,1024]{2,1,0:T(8,128)(2,1)S(1)}, bf16[2,64,1024]{2,1,0:T(8,128)(2,1)S(1)}, u32[]{:S(2)}, u32[]{:S(2)}) collective-permute-start(bf16[2,64,1024]{2,1,0:T(8,128)(2,1)S(1)} %shard_map.247.refs_2_), channel_id=1, source_target_pairs={{0,1},{1,0},{2,3},{3,2},{4,5},{5,4},{6,7},{7,6},{8,9},{9,8},{10,11... | collective-permute-start | bytes 786440 | tf_op jit(solution)/shard_map/ppermute | solution.py:38
  99.0 19.0 %copy-start.24 = (f32[2,64,1024]{2,1,0:T(8,128)}, f32[2,64,1024]{2,1,0:T(8,128)S(1)}, u32[]{:S(2)}) copy-start(f32[2,64,1024]{2,1,0:T(8,128)S(1)} %convert_add_fusion.10) | copy-start | bytes 1572868
  99.0 5.0 %collective-permute-start.16 = (bf16[1,64,1024]{2,1,0:T(8,128)(2,1)S(1)}, bf16[1,64,1024]{2,1,0:T(8,128)(2,1)S(1)}, u32[]{:S(2)}, u32[]{:S(2)}) collective-permute-start(bf16[1,64,1024]{2,1,0:T(8,128)(2,1)S(1)} %slice.383), channel_id=1, source_target_pairs={{0,2},{1,5},{2,0},{3,7},{4,6},{5,1},{6,4},{7,3},{8,10},{9,13},{10,... | collective-permute-start | bytes 393224 | tf_op jit(solution)/shard_map/ppermute | solution.py:55
  104.2 36.1 %copy-start.20 = (f32[64,1024]{1,0:T(8,128)}, f32[64,1024]{1,0:T(8,128)S(1)}, u32[]{:S(2)}) copy-start(f32[64,1024]{1,0:T(8,128)S(1)} %get-tuple-element.170) | copy-start | bytes 786436
  104.4 7.0 %collective-permute-start.17 = (bf16[64,1024]{1,0:T(8,128)(2,1)S(1)}, bf16[64,1024]{1,0:T(8,128)(2,1)S(1)}, u32[]{:S(2)}, u32[]{:S(2)}) collective-permute-start(bf16[64,1024]{1,0:T(8,128)(2,1)S(1)} %multiply_convert_fusion.refs_0_), channel_id=1, source_target_pairs={{0,8},{1,17},{8,0},{9,25},{16,24},{17,1},{24,16},{25,9},{2,10},{3,... | collective-permute-start | bytes 393224 | tf_op jit(solution)/shard_map/ppermute | solution.py:55
  107.0 11.0 %collective-permute-start.27 = (bf16[2,64,1024]{2,1,0:T(8,128)(2,1)S(1)}, bf16[2,64,1024]{2,1,0:T(8,128)(2,1)S(1)}, u32[]{:S(2)}, u32[]{:S(2)}) collective-permute-start(bf16[2,64,1024]{2,1,0:T(8,128)(2,1)S(1)} %collective-permute-done.25.refs_3_), channel_id=1, source_target_pairs={{0,1},{1,0},{2,3},{3,2},{4,5},{5,4},{6,7},{7,6},{8,9},{9,8},{10,11... | collective-permute-start | bytes 786440 | tf_op jit(solution)/shard_map/ppermute | solution.py:38
  107.0 7.0 %collective-permute-start.18 = (bf16[64,1024]{1,0:T(8,128)(2,1)S(1)}, bf16[64,1024]{1,0:T(8,128)(2,1)S(1)}, u32[]{:S(2)}, u32[]{:S(2)}) collective-permute-start(bf16[64,1024]{1,0:T(8,128)(2,1)S(1)} %multiply_convert_fusion.refs_0_), channel_id=1, source_target_pairs={{0,16},{1,9},{8,24},{9,1},{16,0},{17,25},{24,8},{25,17},{2,18},{3,... | collective-permute-start | bytes 393224 | tf_op jit(solution)/shard_map/ppermute | solution.py:55
  111.4 6.6 %collective-permute-start.19 = (bf16[64,1024]{1,0:T(8,128)(2,1)S(1)}, bf16[64,1024]{1,0:T(8,128)(2,1)S(1)}, u32[]{:S(2)}, u32[]{:S(2)}) collective-permute-start(bf16[64,1024]{1,0:T(8,128)(2,1)S(1)} %collective-permute-done.17.refs_1_), channel_id=1, source_target_pairs={{0,16},{1,9},{8,24},{9,1},{16,0},{17,25},{24,8},{25,17},{2,18},{3,... | collective-permute-start | bytes 393224 | tf_op jit(solution)/shard_map/ppermute | solution.py:55
  113.5 6.8 %collective-permute-start.20 = (bf16[64,1024]{1,0:T(8,128)(2,1)S(1)}, bf16[64,1024]{1,0:T(8,128)(2,1)S(1)}, u32[]{:S(2)}, u32[]{:S(2)}) collective-permute-start(bf16[64,1024]{1,0:T(8,128)(2,1)S(1)} %multiply_convert_fusion.refs_0_), channel_id=1, source_target_pairs={{0,1},{1,0},{2,3},{3,2},{4,5},{5,4},{6,7},{7,6},{8,9},{9,8},{10,11... | collective-permute-start | bytes 393224 | tf_op jit(solution)/shard_map/ppermute | solution.py:38
  113.5 6.8 %collective-permute-start.21 = (bf16[64,1024]{1,0:T(8,128)(2,1)S(1)}, bf16[64,1024]{1,0:T(8,128)(2,1)S(1)}, u32[]{:S(2)}, u32[]{:S(2)}) collective-permute-start(bf16[64,1024]{1,0:T(8,128)(2,1)S(1)} %collective-permute-done.17.refs_1_), channel_id=1, source_target_pairs={{0,1},{1,0},{2,3},{3,2},{4,5},{5,4},{6,7},{7,6},{8,9},{9,8},{10,11... | collective-permute-start | bytes 393224 | tf_op jit(solution)/shard_map/ppermute | solution.py:38
  114.0 6.3 %collective-permute-start.22 = (bf16[64,1024]{1,0:T(8,128)(2,1)S(1)}, bf16[64,1024]{1,0:T(8,128)(2,1)S(1)}, u32[]{:S(2)}, u32[]{:S(2)}) collective-permute-start(bf16[64,1024]{1,0:T(8,128)(2,1)S(1)} %collective-permute-done.18.refs_2_), channel_id=1, source_target_pairs={{0,1},{1,0},{2,3},{3,2},{4,5},{5,4},{6,7},{7,6},{8,9},{9,8},{10,11... | collective-permute-start | bytes 393224 | tf_op jit(solution)/shard_map/ppermute | solution.py:38
  118.0 2.2 collective-permute-start.23
  122.9 1.7 collective-permute-start.30
  123.5 1.5 collective-permute-start.28
  125.1 9.8 %collective-permute-start.31 = (bf16[2,64,1024]{2,1,0:T(8,128)(2,1)S(1)}, bf16[2,64,1024]{2,1,0:T(8,128)(2,1)S(1)}, u32[]{:S(2)}, u32[]{:S(2)}) collective-permute-start(bf16[2,64,1024]{2,1,0:T(8,128)(2,1)S(1)} %bitcast.137), channel_id=1, source_target_pairs={{0,16},{1,9},{8,24},{9,1},{16,0},{17,25},{24,8},{25,17},{2,18},{3,... | collective-permute-start | bytes 786440 | tf_op jit(solution)/shard_map/ppermute | solution.py:55
  135.0 5.0 %collective-permute-start.32 = (bf16[1,64,1024]{2,1,0:T(8,128)(2,1)S(1)}, bf16[1,64,1024]{2,1,0:T(8,128)(2,1)S(1)}, u32[]{:S(2)}, u32[]{:S(2)}) collective-permute-start(bf16[1,64,1024]{2,1,0:T(8,128)(2,1)S(1)} %slice.382), channel_id=1, source_target_pairs={{0,8},{1,17},{8,0},{9,25},{16,24},{17,1},{24,16},{25,9},{2,10},{3,... | collective-permute-start | bytes 393224 | tf_op jit(solution)/shard_map/ppermute | solution.py:55
  137.7 4.9 %collective-permute-start.29 = (bf16[256,1024]{1,0:T(8,128)(2,1)S(1)}, bf16[256,1024]{1,0:T(8,128)(2,1)S(1)}, u32[]{:S(2)}, u32[]{:S(2)}) collective-permute-start(bf16[256,1024]{1,0:T(8,128)(2,1)S(1)} %get-tuple-element.125), channel_id=1, source_target_pairs={{0,1},{1,0},{2,3},{3,2},{4,5},{5,4},{6,7},{7,6},{8,9},{9,8},{10,11... | collective-permute-start | bytes 1572872 | tf_op jit(solution)/shard_map/ppermute | solution.py:38
  141.2 5.7 %collective-permute-start.36 = (bf16[64,1024]{1,0:T(8,128)(2,1)S(1)}, bf16[64,1024]{1,0:T(8,128)(2,1)}, u32[]{:S(2)}, u32[]{:S(2)}) collective-permute-start(bf16[64,1024]{1,0:T(8,128)(2,1)S(1)} %get-tuple-element.167.refs_0_), channel_id=1, source_target_pairs={{0,2},{1,5},{2,0},{3,7},{4,6},{5,1},{6,4},{7,3},{8,10},{9,13},{10,... | collective-permute-start | bytes 393224 | tf_op jit(solution)/shard_map/ppermute | solution.py:55
  143.6 9.9 %collective-permute-start.33 = (bf16[2,64,1024]{2,1,0:T(8,128)(2,1)}, bf16[2,64,1024]{2,1,0:T(8,128)(2,1)}, u32[]{:S(2)}, u32[]{:S(2)}) collective-permute-start(bf16[2,64,1024]{2,1,0:T(8,128)(2,1)} %bitcast.21), channel_id=1, source_target_pairs={{0,16},{1,9},{8,24},{9,1},{16,0},{17,25},{24,8},{25,17},{2,18},{3,... | collective-permute-start | bytes 786440 | tf_op jit(solution)/shard_map/ppermute | solution.py:55
  143.7 5.2 %collective-permute-start.37 = (bf16[64,1024]{1,0:T(8,128)(2,1)S(1)}, bf16[64,1024]{1,0:T(8,128)(2,1)S(1)}, u32[]{:S(2)}, u32[]{:S(2)}) collective-permute-start(bf16[64,1024]{1,0:T(8,128)(2,1)S(1)} %get-tuple-element.167.refs_0_), channel_id=1, source_target_pairs={{0,4},{1,3},{2,6},{3,1},{4,0},{5,7},{6,2},{7,5},{8,12},{9,11},{10,... | collective-permute-start | bytes 393224 | tf_op jit(solution)/shard_map/ppermute | solution.py:55
  146.9 5.2 %collective-permute-start.38 = (bf16[64,1024]{1,0:T(8,128)(2,1)}, bf16[64,1024]{1,0:T(8,128)(2,1)S(1)}, u32[]{:S(2)}, u32[]{:S(2)}) collective-permute-start(bf16[64,1024]{1,0:T(8,128)(2,1)} %collective-permute-done.36.refs_1_), channel_id=1, source_target_pairs={{0,4},{1,3},{2,6},{3,1},{4,0},{5,7},{6,2},{7,5},{8,12},{9,11},{10,... | collective-permute-start | bytes 393224 | tf_op jit(solution)/shard_map/ppermute | solution.py:55
  148.8 19.8 %collective-permute-start.56 = (bf16[2,4,64,384]{3,2,1,0:T(8,128)(2,1)}, bf16[2,4,64,384]{3,2,1,0:T(8,128)(2,1)S(1)}, u32[]{:S(2)}, u32[]{:S(2)}) collective-permute-start(bf16[2,4,64,384]{3,2,1,0:T(8,128)(2,1)} %copy-done.9), channel_id=1, source_target_pairs={{0,4},{1,3},{2,6},{3,1},{4,0},{5,7},{6,2},{7,5},{8,12},{9,11},{10,... | collective-permute-start | bytes 1179656 | tf_op jit(solution)/shard_map/ppermute | solution.py:55
  148.9 5.8 %collective-permute-start.39 = (bf16[64,1024]{1,0:T(8,128)(2,1)S(1)}, bf16[64,1024]{1,0:T(8,128)(2,1)S(1)}, u32[]{:S(2)}, u32[]{:S(2)}) collective-permute-start(bf16[64,1024]{1,0:T(8,128)(2,1)S(1)} %get-tuple-element.167.refs_0_), channel_id=1, source_target_pairs={{0,1},{1,0},{2,3},{3,2},{4,5},{5,4},{6,7},{7,6},{8,9},{9,8},{10,11... | collective-permute-start | bytes 393224 | tf_op jit(solution)/shard_map/ppermute | solution.py:38
  149.0 7.0 %collective-permute-start.40 = (bf16[64,1024]{1,0:T(8,128)(2,1)}, bf16[64,1024]{1,0:T(8,128)(2,1)S(1)}, u32[]{:S(2)}, u32[]{:S(2)}) collective-permute-start(bf16[64,1024]{1,0:T(8,128)(2,1)} %collective-permute-done.36.refs_1_), channel_id=1, source_target_pairs={{0,1},{1,0},{2,3},{3,2},{4,5},{5,4},{6,7},{7,6},{8,9},{9,8},{10,11... | collective-permute-start | bytes 393224 | tf_op jit(solution)/shard_map/ppermute | solution.py:38
  152.1 3.9 %collective-permute-start.41 = (bf16[64,1024]{1,0:T(8,128)(2,1)S(1)}, bf16[64,1024]{1,0:T(8,128)(2,1)S(1)}, u32[]{:S(2)}, u32[]{:S(2)}) collective-permute-start(bf16[64,1024]{1,0:T(8,128)(2,1)S(1)} %collective-permute-done.37.refs_2_), channel_id=1, source_target_pairs={{0,1},{1,0},{2,3},{3,2},{4,5},{5,4},{6,7},{7,6},{8,9},{9,8},{10,11... | collective-permute-start | bytes 393224 | tf_op jit(solution)/shard_map/ppermute | solution.py:38
  153.4 2.5 %collective-permute-start.42 = (bf16[64,1024]{1,0:T(8,128)(2,1)S(1)}, bf16[64,1024]{1,0:T(8,128)(2,1)S(1)}, u32[]{:S(2)}, u32[]{:S(2)}) collective-permute-start(bf16[64,1024]{1,0:T(8,128)(2,1)S(1)} %collective-permute-done.38.refs_3_), channel_id=1, source_target_pairs={{0,1},{1,0},{2,3},{3,2},{4,5},{5,4},{6,7},{7,6},{8,9},{9,8},{10,11... | collective-permute-start | bytes 393224 | tf_op jit(solution)/shard_map/ppermute | solution.py:38
  154.8 29.5 %collective-permute-start.44 = (bf16[2,4,64,768]{3,2,1,0:T(8,128)(2,1)}, bf16[2,4,64,768]{3,2,1,0:T(8,128)(2,1)S(1)}, u32[]{:S(2)}, u32[]{:S(2)}) collective-permute-start(bf16[2,4,64,768]{3,2,1,0:T(8,128)(2,1)} %copy-done.8), channel_id=1, source_target_pairs={{0,4},{1,3},{2,6},{3,1},{4,0},{5,7},{6,2},{7,5},{8,12},{9,11},{10,... | collective-permute-start | bytes 2359304 | tf_op jit(solution)/shard_map/ppermute | solution.py:55
  155.9 14.0 %collective-permute-start.34 = (bf16[1,64,1024]{2,1,0:T(8,128)(2,1)S(1)}, bf16[1,64,1024]{2,1,0:T(8,128)(2,1)S(1)}, u32[]{:S(2)}, u32[]{:S(2)}) collective-permute-start(bf16[1,64,1024]{2,1,0:T(8,128)(2,1)S(1)} %slice.381), channel_id=1, source_target_pairs={{0,8},{1,17},{8,0},{9,25},{16,24},{17,1},{24,16},{25,9},{2,10},{3,... | collective-permute-start | bytes 393224 | tf_op jit(solution)/shard_map/ppermute | solution.py:55
  165.5 18.6 %collective-permute-start.43 = (bf16[256,1024]{1,0:T(8,128)(2,1)S(1)}, bf16[256,1024]{1,0:T(8,128)(2,1)S(1)}, u32[]{:S(2)}, u32[]{:S(2)}) collective-permute-start(bf16[256,1024]{1,0:T(8,128)(2,1)S(1)} %get-tuple-element.139), channel_id=1, source_target_pairs={{0,1},{1,0},{2,3},{3,2},{4,5},{5,4},{6,7},{7,6},{8,9},{9,8},{10,11... | collective-permute-start | bytes 1572872 | tf_op jit(solution)/shard_map/ppermute | solution.py:38
  166.0 9.0 %collective-permute-start.48 = (bf16[2,256,256]{2,1,0:T(8,128)(2,1)S(1)}, bf16[2,256,256]{2,1,0:T(8,128)(2,1)S(1)}, u32[]{:S(2)}, u32[]{:S(2)}) collective-permute-start(bf16[2,256,256]{2,1,0:T(8,128)(2,1)S(1)} %get-tuple-element.146), channel_id=1, source_target_pairs={{0,16},{1,9},{8,24},{9,1},{16,0},{17,25},{24,8},{25,17},{2,18},{3,... | collective-permute-start | bytes 786440 | tf_op jit(solution)/shard_map/ppermute | solution.py:55
  168.7 8.7 %collective-permute-start.57 = (bf16[1,4,64,384]{3,2,1,0:T(8,128)(2,1)S(1)}, bf16[1,4,64,384]{3,2,1,0:T(8,128)(2,1)S(1)}, u32[]{:S(2)}, u32[]{:S(2)}) collective-permute-start(bf16[1,4,64,384]{3,2,1,0:T(8,128)(2,1)S(1)} %slice.378), channel_id=1, source_target_pairs={{0,2},{1,5},{2,0},{3,7},{4,6},{5,1},{6,4},{7,3},{8,10},{9,13},{10,... | collective-permute-start | bytes 589832 | tf_op jit(solution)/shard_map/ppermute | solution.py:55
  169.9 40.1 %collective-permute-start.35 = (bf16[64,1024]{1,0:T(8,128)(2,1)S(1)}, bf16[64,1024]{1,0:T(8,128)(2,1)S(1)}, u32[]{:S(2)}, u32[]{:S(2)}) collective-permute-start(bf16[64,1024]{1,0:T(8,128)(2,1)S(1)} %fusion.20), channel_id=1, source_target_pairs={{0,1},{1,0},{2,3},{3,2},{4,5},{5,4},{6,7},{7,6},{8,9},{9,8},{10,11... | collective-permute-start | bytes 393224 | tf_op jit(solution)/shard_map/ppermute | solution.py:38
  175.1 9.0 %collective-permute-start.51 = (bf16[1,256,256]{2,1,0:T(8,128)(2,1)S(1)}, bf16[1,256,256]{2,1,0:T(8,128)(2,1)S(1)}, u32[]{:S(2)}, u32[]{:S(2)}) collective-permute-start(bf16[1,256,256]{2,1,0:T(8,128)(2,1)S(1)} %slice.379), channel_id=1, source_target_pairs={{0,8},{1,17},{8,0},{9,25},{16,24},{17,1},{24,16},{25,9},{2,10},{3,... | collective-permute-start | bytes 393224 | tf_op jit(solution)/shard_map/ppermute | solution.py:55
  177.5 16.2 %collective-permute-start.49 = (bf16[2,264,512]{2,1,0:T(8,128)(2,1)S(1)}, bf16[2,264,512]{2,1,0:T(8,128)(2,1)S(1)}, u32[]{:S(2)}, u32[]{:S(2)}) collective-permute-start(bf16[2,264,512]{2,1,0:T(8,128)(2,1)S(1)} %get-tuple-element.147), channel_id=1, source_target_pairs={{0,16},{1,9},{8,24},{9,1},{16,0},{17,25},{24,8},{25,17},{2,18},{3,... | collective-permute-start | bytes 1622024 | tf_op jit(solution)/shard_map/ppermute | solution.py:55
  184.3 9.3 %collective-permute-start.45 = (bf16[2,64,1024]{2,1,0:T(8,128)(2,1)S(1)}, bf16[2,64,1024]{2,1,0:T(8,128)(2,1)S(1)}, u32[]{:S(2)}, u32[]{:S(2)}) collective-permute-start(bf16[2,64,1024]{2,1,0:T(8,128)(2,1)S(1)} %bitcast.136), channel_id=1, source_target_pairs={{0,4},{1,3},{2,6},{3,1},{4,0},{5,7},{6,2},{7,5},{8,12},{9,11},{10,... | collective-permute-start | bytes 786440 | tf_op jit(solution)/shard_map/ppermute | solution.py:55
  186.9 12.3 %collective-permute-start.52 = (bf16[1,4,64,768]{3,2,1,0:T(8,128)(2,1)S(1)}, bf16[1,4,64,768]{3,2,1,0:T(8,128)(2,1)S(1)}, u32[]{:S(2)}, u32[]{:S(2)}) collective-permute-start(bf16[1,4,64,768]{3,2,1,0:T(8,128)(2,1)S(1)} %slice.376), channel_id=1, source_target_pairs={{0,2},{1,5},{2,0},{3,7},{4,6},{5,1},{6,4},{7,3},{8,10},{9,13},{10,... | collective-permute-start | bytes 1179656 | tf_op jit(solution)/shard_map/ppermute | solution.py:55
  193.7 5.0 %collective-permute-start.46 = (bf16[1,64,1024]{2,1,0:T(8,128)(2,1)S(1)}, bf16[1,64,1024]{2,1,0:T(8,128)(2,1)S(1)}, u32[]{:S(2)}, u32[]{:S(2)}) collective-permute-start(bf16[1,64,1024]{2,1,0:T(8,128)(2,1)S(1)} %slice.380), channel_id=1, source_target_pairs={{0,2},{1,5},{2,0},{3,7},{4,6},{5,1},{6,4},{7,3},{8,10},{9,13},{10,... | collective-permute-start | bytes 393224 | tf_op jit(solution)/shard_map/ppermute | solution.py:55
  195.1 13.9 %collective-permute-start.50 = (bf16[1,264,512]{2,1,0:T(8,128)(2,1)S(1)}, bf16[1,264,512]{2,1,0:T(8,128)(2,1)S(1)}, u32[]{:S(2)}, u32[]{:S(2)}) collective-permute-start(bf16[1,264,512]{2,1,0:T(8,128)(2,1)S(1)} %slice.377), channel_id=1, source_target_pairs={{0,8},{1,17},{8,0},{9,25},{16,24},{17,1},{24,16},{25,9},{2,10},{3,... | collective-permute-start | bytes 811016 | tf_op jit(solution)/shard_map/ppermute | solution.py:55
  199.2 22.2 %collective-permute-start.47 = (bf16[64,1024]{1,0:T(8,128)(2,1)S(1)}, bf16[64,1024]{1,0:T(8,128)(2,1)S(1)}, u32[]{:S(2)}, u32[]{:S(2)}) collective-permute-start(bf16[64,1024]{1,0:T(8,128)(2,1)S(1)} %fusion.12), channel_id=1, source_target_pairs={{0,1},{1,0},{2,3},{3,2},{4,5},{5,4},{6,7},{7,6},{8,9},{9,8},{10,11... | collective-permute-start | bytes 393224 | tf_op jit(solution)/shard_map/ppermute | solution.py:38
  199.4 22.8 %collective-permute-start.58 = (bf16[64,1152]{1,0:T(8,128)(2,1)S(1)}, bf16[64,1152]{1,0:T(8,128)(2,1)S(1)}, u32[]{:S(2)}, u32[]{:S(2)}) collective-permute-start(bf16[64,1152]{1,0:T(8,128)(2,1)S(1)} %get-tuple-element.183), channel_id=1, source_target_pairs={{0,8},{8,0},{16,24},{24,16},{1,9},{9,1},{17,25},{25,17},{2,10},{10... | collective-permute-start | bytes 442376 | tf_op jit(solution)/shard_map/ppermute | solution.py:38
  199.5 22.7 %collective-permute-start.59 = (bf16[64,1152]{1,0:T(8,128)(2,1)S(1)}, bf16[64,1152]{1,0:T(8,128)(2,1)S(1)}, u32[]{:S(2)}, u32[]{:S(2)}) collective-permute-start(bf16[64,1152]{1,0:T(8,128)(2,1)S(1)} %get-tuple-element.184), channel_id=1, source_target_pairs={{0,16},{8,24},{16,0},{24,8},{1,17},{9,25},{17,1},{25,9},{2,18},{10... | collective-permute-start | bytes 442376 | tf_op jit(solution)/shard_map/ppermute | solution.py:38
  209.1 4.8 %collective-permute-start.53 = (bf16[72,768]{1,0:T(8,128)(2,1)S(1)}, bf16[72,768]{1,0:T(8,128)(2,1)S(1)}, u32[]{:S(2)}, u32[]{:S(2)}) collective-permute-start(bf16[72,768]{1,0:T(8,128)(2,1)S(1)} %fusion.35), channel_id=1, source_target_pairs={{0,2},{2,0},{4,6},{6,4},{1,3},{3,1},{5,7},{7,5},{8,10},{10,8},{12,... | collective-permute-start | bytes 331784 | tf_op jit(solution)/shard_map/ppermute | solution.py:38
  210.0 4.7 %collective-permute-start.54 = (bf16[72,768]{1,0:T(8,128)(2,1)S(1)}, bf16[72,768]{1,0:T(8,128)(2,1)S(1)}, u32[]{:S(2)}, u32[]{:S(2)}) collective-permute-start(bf16[72,768]{1,0:T(8,128)(2,1)S(1)} %fusion.36), channel_id=1, source_target_pairs={{0,4},{2,6},{4,0},{6,2},{1,5},{3,7},{5,1},{7,3},{8,12},{10,14},{12... | collective-permute-start | bytes 331784 | tf_op jit(solution)/shard_map/ppermute | solution.py:38
  213.9 8.2 %collective-permute-start.60 = (bf16[64,1152]{1,0:T(8,128)(2,1)S(1)}, bf16[64,1152]{1,0:T(8,128)(2,1)S(1)}, u32[]{:S(2)}, u32[]{:S(2)}) collective-permute-start(bf16[64,1152]{1,0:T(8,128)(2,1)S(1)} %get-tuple-element.181), channel_id=1, source_target_pairs={{0,24},{8,16},{16,8},{24,0},{1,25},{9,17},{17,9},{25,1},{2,26},{10... | collective-permute-start | bytes 442376 | tf_op jit(solution)/shard_map/ppermute | solution.py:38
  214.8 5.6 %collective-permute-start.55 = (bf16[72,768]{1,0:T(8,128)(2,1)S(1)}, bf16[72,768]{1,0:T(8,128)(2,1)S(1)}, u32[]{:S(2)}, u32[]{:S(2)}) collective-permute-start(bf16[72,768]{1,0:T(8,128)(2,1)S(1)} %fusion.37), channel_id=1, source_target_pairs={{0,6},{2,4},{4,2},{6,0},{1,7},{3,5},{5,3},{7,1},{8,14},{10,12},{12... | collective-permute-start | bytes 331784 | tf_op jit(solution)/shard_map/ppermute | solution.py:38
  221.4 1.9 collective-permute-start.61
  (35 other events, 182.6 us)

commit v3 on v2

--- a/solution.py
+++ b/solution.py
@@ -68,22 +68,26 @@
     return call(body, [shape(2 * a.shape[0], *a.shape[1:])], [a, b], vmem_mb=8)[0]
 
 
-def gather(x, axis, n):
+def gather(x, axis, n, gate=None, first=None):
     x = x[None]
     for i in range(bits(n)):
         got = hop(x, axis, n, i)
+        if first is not None and i == 0:
+            first.append(got)
         if i < bits(n) - 1:
-            x = join(x, got)
+            x = join(x, got if gate is None else after(got, gate))
     return [x, got]
 
 
-def reduce_blocks(low, high, axis, n, gate=None, first=None):
+def reduce_blocks(low, high, axis, n, gate=None, first=None, last=None):
     for i in range(bits(n) - 1, -1, -1):
         got = hop(high, axis, n, i)
         if first is not None and i == bits(n) - 1:
             first.append(got)
         if gate is not None and i:
             got = after(got, gate)
+        if last is not None and not i:
+            got = after(got, last)
         low = low.astype(F32) + got.astype(F32)
         if i:
             keep = low.shape[0] // 2
@@ -171,14 +175,6 @@
         if hp > hc:
             fill = [((0, 0), (0, 0), (0, hp - hc))]
             w_gate, w_up, w_down = [jnp.pad(w.reshape(rows, F, hc), *fill).reshape(rows, F * hp) for w in (w_gate, w_up, w_down)]
-        wf = call(
-            ffn_pack,
-            [shape(rows, 3 * hp)] * F,
-            [w_gate, w_up, w_down],
-            [pltpu.SemaphoreType.DMA((F, 3))],
-            hbm=3,
-            vmem_mb=60,
-        )
         def attn_pack(wq_ref, wk_ref, wv_ref, wo_ref, x_ref, ga_ref, gf_ref, gq_ref, gk_ref, s_ref, *refs):
             outs, sem = refs[:C], refs[C]
             mt = lax.axis_index("tensor")
@@ -222,25 +218,25 @@
         wa = call(
             attn_pack,
             [shape(tall + 8, wide)] * C,
-            list(after((w_query, w_key, w_value, w_out.T, hid), wf[0]))
+            [w_query, w_key, w_value, w_out.T, hid]
             + [v.reshape(1, -1) for v in (gain_attn, gain_ffn, gain_query, gain_key)]
             + [segments.reshape(1, tokens)],
             [pltpu.SemaphoreType.DMA((C, 5))],
             hbm=5,
             vmem_mb=60,
         )
+
+        wf = call(
+            ffn_pack,
+            [shape(rows, 3 * hp)] * F,
+            list(after((w_gate, w_up, w_down), wa[0])),
+            [pltpu.SemaphoreType.DMA((F, 3))],
+            hbm=3,
+            vmem_mb=60,
+        )
         wa_got = scatter(wa, "context", C)
 
         wf = scatter(wf, "fsdp", F)
-
-        def ffn_join(*refs):
-            for k in range(F):
-                refs[F][k] = refs[k][...]
-
-        wf_got = wf
-        wf = call(ffn_join, [shape(F, rows, 3 * hp)], [after(wf[0], wa_got[1])] + wf[1:], vmem_mb=8)[0]
-        wf_first = hop(wf[None], "context", C, 0)
-        wf_here = wf[None]
 
         def attn_join(*refs):
             b, qkv, o, x, docs = refs[:C], refs[C], refs[C + 1], refs[C + 2], refs[C + 3]
@@ -259,10 +255,20 @@
         wq, wo, x_own = call(
             attn_join,
             [shape(CR + 2 * C, aw), shape(CR, qc), shape(C * half + 8, width)],
-            [after(wa_got[0], wf_got)] + wa_got[1:],
+            [after(wa_got[0], wf[1])] + wa_got[1:],
             [pltpu.VMEM((8, 128), F32)],
         )
-        wq = gather(wq, "fsdp", F)
+        def ffn_join(*refs):
+            for k in range(F):
+                refs[F][k] = refs[k][...]
+
+        wf_got = wf
+        wf = call(ffn_join, [shape(F, rows, 3 * hp)], [after(wf[0], wq)] + wf[1:], vmem_mb=8)[0]
+        wf_first = hop(wf[None], "context", C, 0)
+        wf_here = wf[None]
+
+        q_here = []
+        wq = gather(wq, "fsdp", F, gate=wf, first=q_here)
         wo = gather(after(wo, wq[0]), "fsdp", F)
 
         def my_half(x):
@@ -306,7 +312,7 @@
 
         allowed = call(find_allowed, [shape(R, R)], xs + [pos_row, pos_col])[0]
 
-        def reduce(own, low, high, axis, n, gate=None, enter=None, first=None):
+        def reduce(own, low, high, axis, n, enter=None, first=None, last=None):
             keep = H // 2
             if high is None:
                 low = swap_t(low)
@@ -318,7 +324,7 @@
             if enter is not None:
                 high = after(high, enter)
             shaped = (n // 2, half, width)
-            return reduce_blocks(low.reshape(shaped), high.reshape(shaped), axis, n, gate, first), high
+            return reduce_blocks(low.reshape(shaped), high.reshape(shaped), axis, n, None, first, last), high
 
         def spread(x, axis, n):
             b = [x]
@@ -331,9 +337,6 @@
             return jnp.where(t == 0, jnp.concatenate([x, y], 0), jnp.concatenate([y, x], 0))
 
         cot = cotangent.reshape(tokens, width)
-        dys = gather(after(my_half(cot), wo[0]), "fsdp", F)
-        dys = dys + [swap_t(b) for b in dys]
-
         def rotate(v, cs, sn):
             return v * cs + pltpu.roll(v, HEAD // 2, 1) * sn
 
@@ -349,7 +352,7 @@
         whole = [shape(H, width, dtype=F32), shape(H, width)]
         halves = [shape(H, width, dtype=F32), shape(H // 2, width), shape(H // 2, width)]
 
-        got = wf_first
+        got = after(wf_first, q_here[0])
         for i in range(1, bits(C)):
             wf_here = join(wf_here, got)
             got = hop(wf_here, "context", C, i)
@@ -412,33 +415,14 @@
         h, raw, q, ky, v, w_qkv, o, gv, gqk = call(
             attn_fwd,
             kept + [shape(R, qc), shape(8, width, dtype=F32), shape(8, 128, dtype=F32)],
-            xs + wq + [cos, sin, after(allowed, wf_first)],
+            xs + wq + [cos, sin, after(allowed, wf_first, wo[0])],
             [pltpu.VMEM(a.shape, a.dtype) for a in kept] + [pltpu.SemaphoreType.DMA((6,))],
             flops=2 * R * width * aw + 4 * R * R * qc,
             hbm_outs=6,
         )
 
-        def out_proj(o_ref, *refs):
-            wb, own, low, high, w = refs[:2], *refs[2:]
-            mf, mc = me()
-            mt = lax.axis_index("tensor")
-            for a in range(F):
-                for b in range(C):
-                    dest = (mf ^ mask_of(a, F, mt)) * C + (mc ^ b)
-                    w[at(dest * rows, rows, rows), :] = wb[a // FH][a % FH, b * rows : (b + 1) * rows, :]
-            split_rows(mm_t(o_ref[...], w[...]), own, low, high)
-
-        res = call(
-            out_proj,
-            halves + [shape(width, qc)],
-            [after(o, wf[1])] + wo,
-            flops=2 * R * width * qc,
-        )
-        w_o = res[3]
-        x_mid = x_half.astype(F32) + reduce(*res[:3], "context", C)[0]
-        r2 = inv_rms(x_mid)
-        g_ffn = gv[1:2]
-        h2s = spread((x_mid * r2 * g_ffn).astype(BF), "fsdp", F)
+        dys = gather(after(my_half(cot), gv), "fsdp", F)
+        dys = dys + [swap_t(b) for b in dys]
 
         def ffn_pre(*refs):
             wb, db, w, dy, du = refs[:2], refs[2:6], *refs[6:]
@@ -458,6 +442,28 @@
             wf + dys,
             flops=2 * R * width * hp,
         )
+
+        def out_proj(o_ref, *refs):
+            wb, own, low, high, w = refs[:2], *refs[2:]
+            mf, mc = me()
+            mt = lax.axis_index("tensor")
+            for a in range(F):
+                for b in range(C):
+                    dest = (mf ^ mask_of(a, F, mt)) * C + (mc ^ b)
+                    w[at(dest * rows, rows, rows), :] = wb[a // FH][a % FH, b * rows : (b + 1) * rows, :]
+            split_rows(mm_t(o_ref[...], w[...]), own, low, high)
+
+        res = call(
+            out_proj,
+            halves + [shape(width, qc)],
+            [after(o, wf[1])] + wo,
+            flops=2 * R * width * qc,
+        )
+        w_o = res[3]
+        x_mid = x_half.astype(F32) + reduce(*res[:3], "context", C, last=du)[0]
+        r2 = inv_rms(x_mid)
+        g_ffn = gv[1:2]
+        h2s = spread((x_mid * r2 * g_ffn).astype(BF), "fsdp", F)
 
         def ffn_main(*refs):
             hb, w, du_ref, own, low, high, h2, act = refs[: 2 * F], *refs[2 * F :]
@@ -515,34 +521,24 @@
         g_units = reduce_blocks(*after(units_parts, dxs[1:C]), "context", C, first=units_first)
         out = (x_mid + reduce(*out_parts, "fsdp", F, enter=dx_low, first=out_first)[0]).astype(BF)
 
-        def out_back(*refs):
-            db, o_ref, w, dx, ga, gb, g = refs[: 2 * C], *refs[2 * C : 2 * C + 4], refs[2 * C + 4 : -1], refs[-1]
-            mf, mc = me()
-            mt = lax.axis_index("tensor")
+        far = [after(w_o, out_first[0]), q, ky, v, raw, h, w_qkv]
+
+        def attn_back(*refs):
+            far, refs = refs[:7], refs[7:]
+            xb, db, refs = refs[:2], refs[2 : 2 + 2 * C], refs[2 + 2 * C :]
+            gv_ref, gqk_ref, cs_ref, sn_ref, ok_ref, dgf, own, send = refs[:8]
+            gb, dx, draw, gs_ref, ex, gn, ga = refs[8:10], *refs[10:16]
+            wo_ref, q, ky, v, raw, h_ref, w = refs[16:23]
+            sem = refs[23]
+            loads = [pltpu.make_async_copy(a, b, sem.at[m]) for m, (a, b) in enumerate(zip(far, refs[16:23]))]
+            for cp in loads:
+                cp.start()
             for b in range(2 * C):
                 dx[b * half : (b + 1) * half, :] = db[b][...]
-            g[...] = mt_m(dx[...], o_ref[...]).astype(BF)
-            for a in range(F):
-                for b in range(C):
-                    dest = (mf ^ mask_of(a, F, mt)) * C + (mc ^ b)
-                    gb[a // FH][a % FH, b * rows : (b + 1) * rows, :] = g[at(dest * rows, rows, rows), :]
-            ga[...] = mm(dx[...], w[...])
-
-        res = call(
-            out_back,
-            [shape(R, width), shape(R, qc, dtype=F32)] + [shape(FH, CR, qc)] * 2,
-            dxs + [o, w_o],
-            [pltpu.VMEM((width, qc), BF)],
-            flops=4 * R * width * qc,
-        )
-        o_first = []
-        g_att, go = after(res[1], out_first[0]), reduce_blocks(*res[2:], "fsdp", F, first=o_first)
-        g_down = reduce_blocks(*down_parts, "context", C, gate=res[1])
-
-        def attn_back(*refs):
-            xb, refs = refs[:2], refs[2:]
-            ga, h_ref, raw, q, ky, v, w, gv_ref, gqk_ref, cs_ref, sn_ref, ok_ref, dgf, own, send = refs[:15]
-            gb, draw, gs_ref, ex, gn = refs[15:17], *refs[17:]
+            loads[0].wait()
+            ga[...] = mm(dx[...], wo_ref[...])
+            for cp in loads[1:5]:
+                cp.wait()
             mf, mc = me()
             mt = lax.axis_index("tensor")
             cs, sn = cs_ref[...], sn_ref[...]
@@ -573,6 +569,8 @@
                 draw[:, ks] = back.astype(BF)
                 dgk += jnp.sum(dg, 0, keepdims=True)
                 draw[:, qc + kw + j * HEAD : qc + kw + (j + 1) * HEAD] = dv[j].astype(BF)
+            for cp in loads[5:]:
+                cp.wait()
             gs_ref[...] = mt_m(h_ref[...], draw[...]).astype(BF)
             dh = mm_t(draw[...], w[...])
             split_whole(dh, own, send)
@@ -596,14 +594,40 @@
 
         res = call(
             attn_back,
-            whole + [shape(FH, CR + 2 * C, aw)] * 2,
-            xs + [g_att, h, raw, q, ky, v, w_qkv, gv, gqk, cos, sin, allowed, dg_ffn],
-            [pltpu.VMEM((R, aw), BF), pltpu.VMEM((width, aw), BF), pltpu.VMEM((2 * C, aw), F32), pltpu.VMEM((8, width), F32)],
-            flops=4 * R * width * aw + 12 * R * R * qc,
-        )
-        gq = reduce_blocks(res[2], after(res[3], o_first[0]), "fsdp", F, gate=units_first[0]).astype(BF)
+            whole + [shape(FH, CR + 2 * C, aw)] * 2 + [shape(R, width)],
+            far + xs + dxs + [gv, gqk, cos, sin, allowed, dg_ffn],
+            [pltpu.VMEM((R, aw), BF), pltpu.VMEM((width, aw), BF), pltpu.VMEM((2 * C, aw), F32), pltpu.VMEM((8, width), F32), pltpu.VMEM((R, qc), F32)]
+            + [pltpu.VMEM(a.shape, a.dtype) for a in far]
+            + [pltpu.SemaphoreType.DMA((7,))],
+            hbm=7,
+            flops=2 * R * width * qc + 4 * R * width * aw + 12 * R * R * qc,
+            vmem_mb=24,
+        )
+        g_down = reduce_blocks(*down_parts, "context", C, gate=res[0])
+        def out_grad(dx, o_ref, ga, gb, g):
+            refs = (ga, gb)
+            mf, mc = me()
+            mt = lax.axis_index("tensor")
+            g[...] = mt_m(dx[...], o_ref[...]).astype(BF)
+            for a in range(F):
+                for b in range(C):
+                    dest = (mf ^ mask_of(a, F, mt)) * C + (mc ^ b)
+                    refs[a // FH][a % FH, b * rows : (b + 1) * rows, :] = g[at(dest * rows, rows, rows), :]
+
+        go = call(
+            out_grad,
+            [shape(FH, CR, qc)] * 2,
+            [after(res[4], units_first[0]), o],
+            [pltpu.VMEM((width, qc), BF)],
+            flops=2 * R * width * qc,
+        )
+        dh, dh_sent = reduce(res[0], res[1], None, "context", C, enter=units_first[0])
+        q_first = []
+        gq = reduce_blocks(res[2], res[3], "fsdp", F, gate=(g_units, g_down, go[1], dh_sent), first=q_first).astype(BF)
+        o_first = []
+        go = reduce_blocks(go[0], go[1], "fsdp", F, first=o_first)
         gf = jnp.concatenate([g_units.astype(BF), g_down.astype(BF)], -1)
-        gf = scatter([gf[0]] + [gf[k] for k in range(1, F)], "fsdp", F)
+        gf = scatter([gf[0]] + list(after([gf[k] for k in range(1, F)], q_first[0], o_first[0])), "fsdp", F)
 
         def ffn_owner(*refs):
             b, outs = refs[:F], refs[F:]
@@ -622,11 +646,12 @@
             both_grads = jnp.concatenate([gq[j * rows : (j + 1) * rows], go[j * rows : (j + 1) * rows]], 1)
             gains = jnp.pad(gq[CR + 2 * j : CR + 2 * j + 2], ((0, 6), (0, qc)))
             ga.append(jnp.concatenate([both_grads, gains], 0))
-        ga = scatter([ga[0]] + list(after(ga[1:], g_units)), "context", C)
-        dh = reduce(res[0], res[1], None, "context", C, enter=units_first[0])[0]
+        ga = scatter(ga, "context", C)
         x32 = x_half.astype(F32)
         inward, _ = norm_back(x32, inv_rms(x32), gv[0:1], dh)
         grad_hidden = (dx_mid + inward).astype(BF)
+
+        rows_out = [both_halves(out).reshape(1, tokens, width), both_halves(grad_hidden).reshape(1, tokens, width)]
 
         def attn_owner(*refs):
             b, gwq, gwk, gwv, gwo, ge = refs[:C], *refs[C:]
@@ -657,7 +682,7 @@
                 shape(rows, C * qc, dtype=F32), shape(rows, kv_local * HEAD, dtype=F32),
                 shape(rows, kv_local * HEAD, dtype=F32), shape(rows, C * qc, dtype=F32), shape(8, aw, dtype=F32),
             ],
-            ga,
+            [after(ga[0], rows_out)] + ga[1:],
         )
         ge = ge + swap_t(ge)
 
@@ -665,8 +690,7 @@
             return lax.dynamic_slice(ge, (row, start + off), (1, size)).reshape(size)
 
         return (
-            both_halves(out).reshape(1, tokens, width),
-            both_halves(grad_hidden).reshape(1, tokens, width),
+            *rows_out,
             gwq, gwk, gwv, gwo.T,
             ffn_grads[0], ffn_grads[1], ffn_grads[2].T,
             piece(0, 0, lane, rows), piece(0, 128, lane, rows), piece(0, 256, goff, grow), piece(1, 0, goff, grow),

time: 225 us -> 208 us (0.924)
  waiting for transfers between devices: 112 us -> 98.8 us
  starting transfers between devices: 64.7 us -> 56.6 us
  local copies, waits for them, and re-layouts: 8.96 us -> 12.5 us
    ppermute x32, starting transfers between devices: 31 us -> 22.7 us  [swap(): return lax.ppermute(x, axis, [(i, i ^ k) for i in range(n)])]
    ppermute x32, waiting for transfers between devices: 24.4 us -> 16.7 us  [swap(): return lax.ppermute(x, axis, [(i, i ^ k) for i in range(n)])]
    ppermute x30, waiting for transfers between devices: 87.7 us -> 82.1 us  [hop(): lax.ppermute(x, (axis, 'tensor'), [(2 * d + t, 2 * (d ^ steps[t]) + t) fo...]
    unnamed x74 -> x72, local copies, waits for them, and re-layouts: 6.47 us -> 10 us
  transfers between devices with their start and end apart: 62 -> 62, of which waited for: 29 -> 28; matrix products, arithmetic and copies ran while one was open for 5% -> 5% of each run, Pallas kernels for 8% -> 9%
where the time goes in v3:
time: 208 us
  waiting for transfers between devices  98.8 us (48%)
  starting transfers between devices  56.6 us (27%)
  Pallas kernels  28.8 us (14%)
  local copies, waits for them, and re-layouts  12.5 us (6%)
  other arithmetic  9.61 us (5%)
    ppermute x30, waiting for transfers between devices, hop(): lax.ppermute(x, (axis, 'tensor'), [(2 * d + t, 2 * (d ^ steps[t]) + t) fo...  82.1 us
    ppermute x30, starting transfers between devices, hop(): lax.ppermute(x, (axis, 'tensor'), [(2 * d + t, 2 * (d ^ steps[t]) + t) fo...  33.9 us
    pallas_call x18, Pallas kernels, call(): pl.pallas_call(body, out_shape=list(outs), in_specs=[far] * hbm + [vmem]...  28.8 us
    ppermute x32, starting transfers between devices, swap(): return lax.ppermute(x, axis, [(i, i ^ k) for i in range(n)])  22.7 us
    ppermute x32, waiting for transfers between devices, swap(): return lax.ppermute(x, axis, [(i, i ^ k) for i in range(n)])  16.7 us
    unnamed x72, local copies, waits for them, and re-layouts  10 us
  transfers between devices with their start and end apart: 62, of which 28 were waited for; matrix products, arithmetic and copies ran while one was open for 5% of the time, Pallas kernels for 9%

profile of v3, /device:TPU:0, one launch (start us, length us, event | category | flops | bytes accessed | tf_op | source)
XLA Modules:
  0.0 207.8 jit_solution(10308455740660765225)
XLA Ops:
  0.7 3.1 %shard_map.237 = (bf16[72,1792]{1,0:T(8,128)(2,1)}, bf16[72,1792]{1,0:T(8,128)(2,1)}, bf16[72,1792]{1,0:T(8,128)(2,1)}, bf16[72,1792]{1,0:T(8,128)(2,1)}) custom-call(bf16[64,1024]{1,0:T(8,128)(2,1)} %wq_ref.1, bf16[64,512]{1,0:T(8,128)(2,1)} %wk_ref.1, bf16[64,512]{1,0:T(8,128)(2,1)} %wv_ref.1, bf16[64,1024]{1,0:T(8,128)(2,1)} %bitcast.142, ...), custom_call_target="tpu_custom_call" | custom-call | bytes 1688352 | tf_op jit(solution)/shard_map/pallas_call | solution.py:110
  3.8 2.0 shard_map.238
  5.8 3.1 %collective-permute-start = (bf16[64,1152]{1,0:T(8,128)(2,1)}, bf16[64,1152]{1,0:T(8,128)(2,1)S(1)}, u32[]{:S(2)}, u32[]{:S(2)}) collective-permute-start(bf16[64,1152]{1,0:T(8,128)(2,1)} %get-tuple-element.95), channel_id=1, source_target_pairs={{0,8},{8,0},{16,24},{24,16},{1,9},{9,1},{17,25},{25,17},{2,10},{10... | collective-permute-start | bytes 442376 | tf_op jit(solution)/shard_map/ppermute | solution.py:38
  8.9 1.5 collective-permute-start.1
  10.4 1.5 collective-permute-start.2
  12.4 2.6 %collective-permute-start.6 = (bf16[64,1152]{1,0:T(8,128)(2,1)}, bf16[64,1152]{1,0:T(8,128)(2,1)S(1)}, u32[]{:S(2)}, u32[]{:S(2)}) collective-permute-start(bf16[64,1152]{1,0:T(8,128)(2,1)} %get-tuple-element.104), channel_id=1, source_target_pairs={{0,16},{8,24},{16,0},{24,8},{1,17},{9,25},{17,1},{25,9},{2,18},{10... | collective-permute-start | bytes 442376 | tf_op jit(solution)/shard_map/ppermute | solution.py:38
  15.0 1.7 collective-permute-start.7
  16.7 1.5 collective-permute-done.1.refs_1_
  18.2 5.3 %collective-permute-done.2.refs_2_ = bf16[72,1792]{1,0:T(8,128)(2,1)S(1)} collective-permute-done((bf16[72,1792]{1,0:T(8,128)(2,1)}, bf16[72,1792]{1,0:T(8,128)(2,1)S(1)}, u32[]{:S(2)}, u32[]{:S(2)}) %collective-permute-start.2) | collective-permute-done | bytes 258080 | tf_op jit(solution)/shard_map/ppermute | solution.py:38
  25.7 1.7 collective-permute-start.9
  27.4 3.1 %collective-permute-start.5 = (bf16[1,264,512]{2,1,0:T(8,128)(2,1)S(1)}, bf16[1,264,512]{2,1,0:T(8,128)(2,1)S(1)}, u32[]{:S(2)}, u32[]{:S(2)}) collective-permute-start(bf16[1,264,512]{2,1,0:T(8,128)(2,1)S(1)} %bitcast.126), channel_id=1, source_target_pairs={{0,8},{1,17},{8,0},{9,25},{16,24},{17,1},{24,16},{25,9},{2,10},{3,... | collective-permute-start | bytes 811016 | tf_op jit(solution)/shard_map/ppermute | solution.py:55
  30.5 6.2 %collective-permute-done.5.b_ref = bf16[1,264,512]{2,1,0:T(8,128)(2,1)S(1)} collective-permute-done((bf16[1,264,512]{2,1,0:T(8,128)(2,1)S(1)}, bf16[1,264,512]{2,1,0:T(8,128)(2,1)S(1)}, u32[]{:S(2)}, u32[]{:S(2)}) %collective-permute-start.5) | collective-permute-done | bytes 270368 | tf_op jit(solution)/shard_map/ppermute | solution.py:55
  36.7 1.1 collective-permute-start.11
  37.9 3.9 %collective-permute-start.8 = (bf16[2,264,512]{2,1,0:T(8,128)(2,1)S(1)}, bf16[2,264,512]{2,1,0:T(8,128)(2,1)S(1)}, u32[]{:S(2)}, u32[]{:S(2)}) collective-permute-start(bf16[2,264,512]{2,1,0:T(8,128)(2,1)S(1)} %shard_map.241.refs_2_), channel_id=1, source_target_pairs={{0,16},{1,9},{8,24},{9,1},{16,0},{17,25},{24,8},{25,17},{2,18},{3,... | collective-permute-start | bytes 1622024 | tf_op jit(solution)/shard_map/ppermute | solution.py:55
  41.8 1.0 fusion.37
  42.8 13.0 %collective-permute-done.10.b_ref = bf16[1,256,256]{2,1,0:T(8,128)(2,1)S(1)} collective-permute-done((bf16[1,256,256]{2,1,0:T(8,128)(2,1)S(1)}, bf16[1,256,256]{2,1,0:T(8,128)(2,1)S(1)}, u32[]{:S(2)}, u32[]{:S(2)}) %collective-permute-start.10) | collective-permute-done | bytes 131104 | tf_op jit(solution)/shard_map/ppermute | solution.py:55
  55.8 3.6 %collective-permute-start.12 = (bf16[2,256,256]{2,1,0:T(8,128)(2,1)S(1)}, bf16[2,256,256]{2,1,0:T(8,128)(2,1)S(1)}, u32[]{:S(2)}, u32[]{:S(2)}) collective-permute-start(bf16[2,256,256]{2,1,0:T(8,128)(2,1)S(1)} %shard_map.243.refs_0_), channel_id=1, source_target_pairs={{0,16},{1,9},{8,24},{9,1},{16,0},{17,25},{24,8},{25,17},{2,18},{3,... | collective-permute-start | bytes 786440 | tf_op jit(solution)/shard_map/ppermute | solution.py:55
  60.1 3.9 %shard_map.244 = (bf16[512,1024]{1,0:T(8,128)(2,1)S(1)}, f32[512,384]{1,0:T(8,128)S(1)}, bf16[512,256]{1,0:T(8,128)(2,1)S(1)}, bf16[512,128]{1,0:T(8,128)(2,1)S(...) custom-call(bf16[264,1024]{1,0:T(8,128)(2,1)S(1)} %get-tuple-element, ...), custom_call_target="tpu_custom_call" | custom-call | flops 805306368 | bytes 6918144 | tf_op jit(solution)/shard_map/pallas_call | solution.py:110
  66.9 1.3 shard_map.246
  68.2 1.0 copy-done
  71.5 6.4 %collective-permute-done.17.b_ref = bf16[1,64,1024]{2,1,0:T(8,128)(2,1)S(1)} collective-permute-done((bf16[1,64,1024]{2,1,0:T(8,128)(2,1)S(1)}, bf16[1,64,1024]{2,1,0:T(8,128)(2,1)S(1)}, u32[]{:S(2)}, u32[]{:S(2)}) %collective-permute-start.17) | collective-permute-done | bytes 131104 | tf_op jit(solution)/shard_map/ppermute | solution.py:55
  78.0 1.5 add_convert_fusion.3
  80.1 7.6 %collective-permute-done.18.refs_3_ = bf16[2,64,1024]{2,1,0:T(8,128)(2,1)S(1)} collective-permute-done((bf16[2,64,1024]{2,1,0:T(8,128)(2,1)S(1)}, bf16[2,64,1024]{2,1,0:T(8,128)(2,1)S(1)}, u32[]{:S(2)}, u32[]{:S(2)}) %collective-permute-start.18) | collective-permute-done | bytes 262176 | tf_op jit(solution)/shard_map/ppermute | solution.py:55
  87.8 1.6 collective-permute-start.16
  89.4 2.2 %shard_map.248 = (bf16[1024,1152]{1,0:T(8,128)(2,1)S(1)}, bf16[512,1024]{1,0:T(8,128)(2,1)S(1)}, f32[512,384]{1,0:T(8,128)S(1)}) custom-call(bf16[2,4,64,1152]{3,2,1,0:T(8,128)(2,1)S(1)} %shard_map.245.refs_0_, bf16[2,4,64,1152]{3,2,1,0:T(8,128)(2,1)} %collective-permute-done.11.refs_1_, bf16[2,64,1024]{2,1,0:T(8,128)(2,1)S(1)} %shard_map.247.refs_2_, ...), custom_call_target="tpu_custom_call" | custom-call | flops 402653184 | bytes 7602176 | tf_op jit(solution)/shard_map/pallas_call | solution.py:110
  91.6 1.2 collective-permute-done.16
  93.3 1.9 collective-permute-start.22
  95.3 6.0 %collective-permute-done.21.refs_1_ = bf16[64,1024]{1,0:T(8,128)(2,1)S(1)} collective-permute-done((bf16[64,1024]{1,0:T(8,128)(2,1)S(1)}, bf16[64,1024]{1,0:T(8,128)(2,1)S(1)}, u32[]{:S(2)}, u32[]{:S(2)}) %collective-permute-start.21) | collective-permute-done | bytes 131104 | tf_op jit(solution)/shard_map/ppermute | solution.py:55
  102.2 5.7 %collective-permute-done.23.refs_3_ = bf16[64,1024]{1,0:T(8,128)(2,1)S(1)} collective-permute-done((bf16[64,1024]{1,0:T(8,128)(2,1)S(1)}, bf16[64,1024]{1,0:T(8,128)(2,1)S(1)}, u32[]{:S(2)}, u32[]{:S(2)}) %collective-permute-start.23) | collective-permute-done | bytes 131104 | tf_op jit(solution)/shard_map/ppermute | solution.py:55
  108.0 1.3 collective-permute-done.27.refs_7_
  109.3 2.6 %shard_map.249 = (f32[256,1024]{1,0:T(8,128)S(1)}, bf16[128,1024]{1,0:T(8,128)(2,1)S(1)}, bf16[128,1024]{1,0:T(8,128)(2,1)S(1)}, bf16[512,1024]{1,0:T(8,128)(2,1)S(1)}, bf16[512,1152]{1,0:T(8,128)(2,1)S(1)}) custom-call(bf16[64,1024]{1,0:T(8,128)(2,1)S(1)} %multiply_convert_fusion.refs_0_, bf16[64,1024]{1,0:T(8,128)(2,1)S(1)} %collective-permute-done.21.refs_1_, ...), custom_call_target="tpu_custom_call" | custom-call | flops 1610612736 | bytes 7995392 | tf_op jit(solution)/shard_map/pallas_call | solution.py:110
  112.6 1.0 collective-permute-done.30
  114.2 9.6 %collective-permute-done.31 = bf16[2,64,1024]{2,1,0:T(8,128)(2,1)S(1)} collective-permute-done((bf16[2,64,1024]{2,1,0:T(8,128)(2,1)S(1)}, bf16[2,64,1024]{2,1,0:T(8,128)(2,1)S(1)}, u32[]{:S(2)}, u32[]{:S(2)}) %collective-permute-start.31) | collective-permute-done | bytes 262176 | tf_op jit(solution)/shard_map/ppermute | solution.py:55
  123.9 2.3 %shard_map.250 = (f32[256,1024]{1,0:T(8,128)S(1)}, bf16[256,1024]{1,0:T(8,128)(2,1)S(1)}, bf16[2,4,64,384]{3,2,1,0:T(8,128)(2,1)S(1)}, bf16[2,4,64,384]{3,2,1,0:...) custom-call(bf16[512,1024]{1,0:T(8,128)(2,1)S(1)} %get-tuple-element.121.h2_ref, ...), custom_call_target="tpu_custom_call" | custom-call | flops 1610612736 | bytes 9568256 | tf_op jit(solution)/shard_map/pallas_call | solution.py:110
  126.3 2.6 %collective-permute-done.32 = bf16[1,64,1024]{2,1,0:T(8,128)(2,1)S(1)} collective-permute-done((bf16[1,64,1024]{2,1,0:T(8,128)(2,1)S(1)}, bf16[1,64,1024]{2,1,0:T(8,128)(2,1)S(1)}, u32[]{:S(2)}, u32[]{:S(2)}) %collective-permute-start.32) | collective-permute-done | bytes 131104 | tf_op jit(solution)/shard_map/ppermute | solution.py:55
  129.9 1.5 collective-permute-start.36
  131.4 1.0 add_convert_fusion.1
  133.6 2.5 %collective-permute-done.36.refs_10_ = bf16[64,1024]{1,0:T(8,128)(2,1)} collective-permute-done((bf16[64,1024]{1,0:T(8,128)(2,1)S(1)}, bf16[64,1024]{1,0:T(8,128)(2,1)}, u32[]{:S(2)}, u32[]{:S(2)}) %collective-permute-start.36) | collective-permute-done | bytes 131104 | tf_op jit(solution)/shard_map/ppermute | solution.py:55
  136.1 2.0 collective-permute-start.50
  138.7 2.6 %collective-permute-done.38.refs_12_ = bf16[64,1024]{1,0:T(8,128)(2,1)S(1)} collective-permute-done((bf16[64,1024]{1,0:T(8,128)(2,1)}, bf16[64,1024]{1,0:T(8,128)(2,1)S(1)}, u32[]{:S(2)}, u32[]{:S(2)}) %collective-permute-start.38) | collective-permute-done | bytes 131104 | tf_op jit(solution)/shard_map/ppermute | solution.py:55
  141.3 1.3 collective-permute-done.33
  142.6 1.2 convert_add_fusion.6
  144.5 1.2 copy-done.8
  145.7 1.1 copy-done.10
  146.9 1.0 copy-done.20
  147.9 8.2 %shard_map.251 = (f32[256,1024]{1,0:T(8,128)S(1)}, bf16[256,1024]{1,0:T(8,128)(2,1)S(1)}, bf16[2,264,512]{2,1,0:T(8,128)(2,1)S(1)}, bf16[2,264,512]{2,1,0:T(8,128)(2,1)S(1)}, bf16[512,1024]{1,0:T(8,128)(2,1)S(1)}) custom-call(bf16[1024,256]{1,0:T(8,128)(2,1)S(1)} %copy-done.20, bf16[512,256]{1,0:T(8,128)(2,1)S(1)} %copy-done.14, ...), custom_call_target="tpu_custom_call" | custom-call | flops 2147483648 | bytes 10854400 | tf_op jit(solution)/shard_map/pallas_call | solution.py:110
  156.4 2.6 %collective-permute-start.48 = (bf16[2,264,512]{2,1,0:T(8,128)(2,1)S(1)}, bf16[2,264,512]{2,1,0:T(8,128)(2,1)S(1)}, u32[]{:S(2)}, u32[]{:S(2)}) collective-permute-start(bf16[2,264,512]{2,1,0:T(8,128)(2,1)S(1)} %get-tuple-element.147), channel_id=1, source_target_pairs={{0,16},{1,9},{8,24},{9,1},{16,0},{17,25},{24,8},{25,17},{2,18},{3,... | collective-permute-start | bytes 1622024 | tf_op jit(solution)/shard_map/ppermute | solution.py:55
  159.2 1.5 collective-permute-start.51
  160.8 4.1 %collective-permute-done.51 = bf16[1,4,64,384]{3,2,1,0:T(8,128)(2,1)S(1)} collective-permute-done((bf16[1,4,64,384]{3,2,1,0:T(8,128)(2,1)S(1)}, bf16[1,4,64,384]{3,2,1,0:T(8,128)(2,1)S(1)}, u32[]{:S(2)}, u32[]{:S(2)}) %collective-permute-start.51) | collective-permute-done | bytes 196640 | tf_op jit(solution)/shard_map/ppermute | solution.py:55
  165.1 1.2 collective-permute-start.45
  168.6 5.8 %collective-permute-done.45 = bf16[2,64,1024]{2,1,0:T(8,128)(2,1)S(1)} collective-permute-done((bf16[2,64,1024]{2,1,0:T(8,128)(2,1)S(1)}, bf16[2,64,1024]{2,1,0:T(8,128)(2,1)S(1)}, u32[]{:S(2)}, u32[]{:S(2)}) %collective-permute-start.45) | collective-permute-done | bytes 262176 | tf_op jit(solution)/shard_map/ppermute | solution.py:55
  174.4 1.5 collective-permute-start.46
  176.0 1.1 collective-permute-done.53
  177.1 1.9 collective-permute-start.54
  180.4 2.0 collective-permute-start.58
  183.3 1.5 collective-permute-start.59
  184.8 2.0 collective-permute-start.60
  188.3 5.5 %collective-permute-done.52 = bf16[1,264,512]{2,1,0:T(8,128)(2,1)S(1)} collective-permute-done((bf16[1,264,512]{2,1,0:T(8,128)(2,1)S(1)}, bf16[1,264,512]{2,1,0:T(8,128)(2,1)S(1)}, u32[]{:S(2)}, u32[]{:S(2)}) %collective-permute-start.52) | collective-permute-done | bytes 270368 | tf_op jit(solution)/shard_map/ppermute | solution.py:55
  194.0 1.6 collective-permute-start.55
  196.2 2.7 %collective-permute-done.55.refs_1_ = bf16[72,768]{1,0:T(8,128)(2,1)S(1)} collective-permute-done((bf16[72,768]{1,0:T(8,128)(2,1)S(1)}, bf16[72,768]{1,0:T(8,128)(2,1)S(1)}, u32[]{:S(2)}, u32[]{:S(2)}) %collective-permute-start.55) | collective-permute-done | bytes 110624 | tf_op jit(solution)/shard_map/ppermute | solution.py:38
  198.9 1.4 collective-permute-start.57
  200.3 1.1 collective-permute-done.56.refs_2_
  201.4 3.1 %collective-permute-done.57.refs_3_ = bf16[72,768]{1,0:T(8,128)(2,1)S(1)} collective-permute-done((bf16[72,768]{1,0:T(8,128)(2,1)S(1)}, bf16[72,768]{1,0:T(8,128)(2,1)S(1)}, u32[]{:S(2)}, u32[]{:S(2)}) %collective-permute-start.57) | collective-permute-done | bytes 110624 | tf_op jit(solution)/shard_map/ppermute | solution.py:38
  205.5 1.1 shard_map.254
  (208 shorter events, 25.2 us)
Async XLA Ops:
  5.8 9.2 %collective-permute-start = (bf16[64,1152]{1,0:T(8,128)(2,1)}, bf16[64,1152]{1,0:T(8,128)(2,1)S(1)}, u32[]{:S(2)}, u32[]{:S(2)}) collective-permute-start(bf16[64,1152]{1,0:T(8,128)(2,1)} %get-tuple-element.95), channel_id=1, source_target_pairs={{0,8},{8,0},{16,24},{24,16},{1,9},{9,1},{17,25},{25,17},{2,10},{10... | collective-permute-start | bytes 442376 | tf_op jit(solution)/shard_map/ppermute | solution.py:38
  8.9 9.3 %collective-permute-start.1 = (bf16[72,1792]{1,0:T(8,128)(2,1)}, bf16[72,1792]{1,0:T(8,128)(2,1)S(1)}, u32[]{:S(2)}, u32[]{:S(2)}) collective-permute-start(bf16[72,1792]{1,0:T(8,128)(2,1)} %get-tuple-element.97), channel_id=1, source_target_pairs={{0,2},{2,0},{4,6},{6,4},{1,3},{3,1},{5,7},{7,5},{8,10},{10,8},{12,... | collective-permute-start | bytes 774152 | tf_op jit(solution)/shard_map/ppermute | solution.py:38
  10.4 13.1 %collective-permute-start.2 = (bf16[72,1792]{1,0:T(8,128)(2,1)}, bf16[72,1792]{1,0:T(8,128)(2,1)S(1)}, u32[]{:S(2)}, u32[]{:S(2)}) collective-permute-start(bf16[72,1792]{1,0:T(8,128)(2,1)} %get-tuple-element.98), channel_id=1, source_target_pairs={{0,4},{2,6},{4,0},{6,2},{1,5},{3,7},{5,1},{7,3},{8,12},{10,14},{12... | collective-permute-start | bytes 774152 | tf_op jit(solution)/shard_map/ppermute | solution.py:38
  11.9 11.6 %collective-permute-start.3 = (bf16[72,1792]{1,0:T(8,128)(2,1)}, bf16[72,1792]{1,0:T(8,128)(2,1)S(1)}, u32[]{:S(2)}, u32[]{:S(2)}) collective-permute-start(bf16[72,1792]{1,0:T(8,128)(2,1)} %get-tuple-element.99), channel_id=1, source_target_pairs={{0,6},{2,4},{4,2},{6,0},{1,7},{3,5},{5,3},{7,1},{8,14},{10,12},{12... | collective-permute-start | bytes 774152 | tf_op jit(solution)/shard_map/ppermute | solution.py:38
  12.4 12.3 %collective-permute-start.6 = (bf16[64,1152]{1,0:T(8,128)(2,1)}, bf16[64,1152]{1,0:T(8,128)(2,1)S(1)}, u32[]{:S(2)}, u32[]{:S(2)}) collective-permute-start(bf16[64,1152]{1,0:T(8,128)(2,1)} %get-tuple-element.104), channel_id=1, source_target_pairs={{0,16},{8,24},{16,0},{24,8},{1,17},{9,25},{17,1},{25,9},{2,18},{10... | collective-permute-start | bytes 442376 | tf_op jit(solution)/shard_map/ppermute | solution.py:38
  15.0 9.7 %collective-permute-start.7 = (bf16[64,1152]{1,0:T(8,128)(2,1)}, bf16[64,1152]{1,0:T(8,128)(2,1)S(1)}, u32[]{:S(2)}, u32[]{:S(2)}) collective-permute-start(bf16[64,1152]{1,0:T(8,128)(2,1)} %get-tuple-element.105), channel_id=1, source_target_pairs={{0,24},{8,16},{16,8},{24,0},{1,25},{9,17},{17,9},{25,1},{2,26},{10... | collective-permute-start | bytes 442376 | tf_op jit(solution)/shard_map/ppermute | solution.py:38
  25.7 11.0 %collective-permute-start.9 = (bf16[1,4,64,1152]{3,2,1,0:T(8,128)(2,1)S(1)}, bf16[1,4,64,1152]{3,2,1,0:T(8,128)(2,1)S(1)}, u32[]{:S(2)}, u32[]{:S(2)}) collective-permute-start(bf16[1,4,64,1152]{3,2,1,0:T(8,128)(2,1)S(1)} %bitcast.122), channel_id=1, source_target_pairs={{0,2},{1,5},{2,0},{3,7},{4,6},{5,1},{6,4},{7,3},{8,10},{9,13},{10,... | collective-permute-start | bytes 1769480 | tf_op jit(solution)/shard_map/ppermute | solution.py:55
  27.4 9.3 %collective-permute-start.5 = (bf16[1,264,512]{2,1,0:T(8,128)(2,1)S(1)}, bf16[1,264,512]{2,1,0:T(8,128)(2,1)S(1)}, u32[]{:S(2)}, u32[]{:S(2)}) collective-permute-start(bf16[1,264,512]{2,1,0:T(8,128)(2,1)S(1)} %bitcast.126), channel_id=1, source_target_pairs={{0,8},{1,17},{8,0},{9,25},{16,24},{17,1},{24,16},{25,9},{2,10},{3,... | collective-permute-start | bytes 811016 | tf_op jit(solution)/shard_map/ppermute | solution.py:55
  36.7 30.2 %collective-permute-start.11 = (bf16[2,4,64,1152]{3,2,1,0:T(8,128)(2,1)S(1)}, bf16[2,4,64,1152]{3,2,1,0:T(8,128)(2,1)}, u32[]{:S(2)}, u32[]{:S(2)}) collective-permute-start(bf16[2,4,64,1152]{3,2,1,0:T(8,128)(2,1)S(1)} %shard_map.245.refs_0_), channel_id=1, source_target_pairs={{0,4},{1,3},{2,6},{3,1},{4,0},{5,7},{6,2},{7,5},{8,12},{9,11},{10,... | collective-permute-start | bytes 3538952 | tf_op jit(solution)/shard_map/ppermute | solution.py:55
  37.8 21.8 %collective-permute-start.4 = (bf16[264,1024]{1,0:T(8,128)(2,1)S(1)}, bf16[264,1024]{1,0:T(8,128)(2,1)S(1)}, u32[]{:S(2)}, u32[]{:S(2)}) collective-permute-start(bf16[264,1024]{1,0:T(8,128)(2,1)S(1)} %get-tuple-element.100.a_ref.refs_0_.refs_7_), channel_id=1, source_target_pairs={{0,1},{1,0},{2,3},{3,2},{4,5},{5,4},{6,7},{7,6},{8,9},{9,8},{10,11... | collective-permute-start | bytes 1622024 | tf_op jit(solution)/shard_map/ppermute | solution.py:38
  37.9 22.1 %collective-permute-start.8 = (bf16[2,264,512]{2,1,0:T(8,128)(2,1)S(1)}, bf16[2,264,512]{2,1,0:T(8,128)(2,1)S(1)}, u32[]{:S(2)}, u32[]{:S(2)}) collective-permute-start(bf16[2,264,512]{2,1,0:T(8,128)(2,1)S(1)} %shard_map.241.refs_2_), channel_id=1, source_target_pairs={{0,16},{1,9},{8,24},{9,1},{16,0},{17,25},{24,8},{25,17},{2,18},{3,... | collective-permute-start | bytes 1622024 | tf_op jit(solution)/shard_map/ppermute | solution.py:55
  41.8 14.0 %collective-permute-start.10 = (bf16[1,256,256]{2,1,0:T(8,128)(2,1)S(1)}, bf16[1,256,256]{2,1,0:T(8,128)(2,1)S(1)}, u32[]{:S(2)}, u32[]{:S(2)}) collective-permute-start(bf16[1,256,256]{2,1,0:T(8,128)(2,1)S(1)} %bitcast.128), channel_id=1, source_target_pairs={{0,8},{1,17},{8,0},{9,25},{16,24},{17,1},{24,16},{25,9},{2,10},{3,... | collective-permute-start | bytes 393224 | tf_op jit(solution)/shard_map/ppermute | solution.py:55
  55.8 11.1 %collective-permute-start.12 = (bf16[2,256,256]{2,1,0:T(8,128)(2,1)S(1)}, bf16[2,256,256]{2,1,0:T(8,128)(2,1)S(1)}, u32[]{:S(2)}, u32[]{:S(2)}) collective-permute-start(bf16[2,256,256]{2,1,0:T(8,128)(2,1)S(1)} %shard_map.243.refs_0_), channel_id=1, source_target_pairs={{0,16},{1,9},{8,24},{9,1},{16,0},{17,25},{24,8},{25,17},{2,18},{3,... | collective-permute-start | bytes 786440 | tf_op jit(solution)/shard_map/ppermute | solution.py:55
  70.0 8.0 %collective-permute-start.14 = (bf16[128,1024]{1,0:T(8,128)(2,1)}, bf16[128,1024]{1,0:T(8,128)(2,1)}, u32[]{:S(2)}, u32[]{:S(2)}) collective-permute-start(bf16[128,1024]{1,0:T(8,128)(2,1)} %get-tuple-element.115), channel_id=1, source_target_pairs={{0,1},{1,0},{2,3},{3,2},{4,5},{5,4},{6,7},{7,6},{8,9},{9,8},{10,11... | collective-permute-start | bytes 786440 | tf_op jit(solution)/shard_map/ppermute | solution.py:38
  70.0 8.0 %collective-permute-start.13 = (bf16[128,1024]{1,0:T(8,128)(2,1)}, bf16[128,1024]{1,0:T(8,128)(2,1)}, u32[]{:S(2)}, u32[]{:S(2)}) collective-permute-start(bf16[128,1024]{1,0:T(8,128)(2,1)} %get-tuple-element.114), channel_id=1, source_target_pairs={{0,1},{1,0},{2,3},{3,2},{4,5},{5,4},{6,7},{7,6},{8,9},{9,8},{10,11... | collective-permute-start | bytes 786440 | tf_op jit(solution)/shard_map/ppermute | solution.py:38
  71.5 6.4 %collective-permute-start.17 = (bf16[1,64,1024]{2,1,0:T(8,128)(2,1)S(1)}, bf16[1,64,1024]{2,1,0:T(8,128)(2,1)S(1)}, u32[]{:S(2)}, u32[]{:S(2)}) collective-permute-start(bf16[1,64,1024]{2,1,0:T(8,128)(2,1)S(1)} %bitcast.124), channel_id=1, source_target_pairs={{0,8},{1,17},{8,0},{9,25},{16,24},{17,1},{24,16},{25,9},{2,10},{3,... | collective-permute-start | bytes 393224 | tf_op jit(solution)/shard_map/ppermute | solution.py:55
  77.9 9.8 %collective-permute-start.18 = (bf16[2,64,1024]{2,1,0:T(8,128)(2,1)S(1)}, bf16[2,64,1024]{2,1,0:T(8,128)(2,1)S(1)}, u32[]{:S(2)}, u32[]{:S(2)}) collective-permute-start(bf16[2,64,1024]{2,1,0:T(8,128)(2,1)S(1)} %shard_map.247.refs_2_), channel_id=1, source_target_pairs={{0,16},{1,9},{8,24},{9,1},{16,0},{17,25},{24,8},{25,17},{2,18},{3,... | collective-permute-start | bytes 786440 | tf_op jit(solution)/shard_map/ppermute | solution.py:55
  79.5 8.2 %collective-permute-start.15 = (bf16[2,64,1024]{2,1,0:T(8,128)(2,1)S(1)}, bf16[2,64,1024]{2,1,0:T(8,128)(2,1)S(1)}, u32[]{:S(2)}, u32[]{:S(2)}) collective-permute-start(bf16[2,64,1024]{2,1,0:T(8,128)(2,1)S(1)} %bitcast.137), channel_id=1, source_target_pairs={{0,4},{1,3},{2,6},{3,1},{4,0},{5,7},{6,2},{7,5},{8,12},{9,11},{10,... | collective-permute-start | bytes 786440 | tf_op jit(solution)/shard_map/ppermute | solution.py:55
  80.1 9.3 %collective-permute-start.19 = (bf16[2,64,1024]{2,1,0:T(8,128)(2,1)S(1)}, bf16[2,64,1024]{2,1,0:T(8,128)(2,1)S(1)}, u32[]{:S(2)}, u32[]{:S(2)}) collective-permute-start(bf16[2,64,1024]{2,1,0:T(8,128)(2,1)S(1)} %shard_map.247.refs_2_), channel_id=1, source_target_pairs={{0,1},{1,0},{2,3},{3,2},{4,5},{5,4},{6,7},{7,6},{8,9},{9,8},{10,11... | collective-permute-start | bytes 786440 | tf_op jit(solution)/shard_map/ppermute | solution.py:38
  87.7 1.7 collective-permute-start.20
  87.8 5.0 %collective-permute-start.16 = (bf16[1,64,1024]{2,1,0:T(8,128)(2,1)S(1)}, bf16[1,64,1024]{2,1,0:T(8,128)(2,1)S(1)}, u32[]{:S(2)}, u32[]{:S(2)}) collective-permute-start(bf16[1,64,1024]{2,1,0:T(8,128)(2,1)S(1)} %slice.381), channel_id=1, source_target_pairs={{0,2},{1,5},{2,0},{3,7},{4,6},{5,1},{6,4},{7,3},{8,10},{9,13},{10,... | collective-permute-start | bytes 393224 | tf_op jit(solution)/shard_map/ppermute | solution.py:55
  93.0 36.1 %copy-start.21 = (f32[64,1024]{1,0:T(8,128)}, f32[64,1024]{1,0:T(8,128)S(1)}, u32[]{:S(2)}) copy-start(f32[64,1024]{1,0:T(8,128)S(1)} %get-tuple-element.174) | copy-start | bytes 786436
  93.2 8.1 %collective-permute-start.21 = (bf16[64,1024]{1,0:T(8,128)(2,1)S(1)}, bf16[64,1024]{1,0:T(8,128)(2,1)S(1)}, u32[]{:S(2)}, u32[]{:S(2)}) collective-permute-start(bf16[64,1024]{1,0:T(8,128)(2,1)S(1)} %multiply_convert_fusion.refs_0_), channel_id=1, source_target_pairs={{0,8},{1,17},{8,0},{9,25},{16,24},{17,1},{24,16},{25,9},{2,10},{3,... | collective-permute-start | bytes 393224 | tf_op jit(solution)/shard_map/ppermute | solution.py:55
  93.3 8.9 %collective-permute-start.22 = (bf16[64,1024]{1,0:T(8,128)(2,1)S(1)}, bf16[64,1024]{1,0:T(8,128)(2,1)S(1)}, u32[]{:S(2)}, u32[]{:S(2)}) collective-permute-start(bf16[64,1024]{1,0:T(8,128)(2,1)S(1)} %multiply_convert_fusion.refs_0_), channel_id=1, source_target_pairs={{0,16},{1,9},{8,24},{9,1},{16,0},{17,25},{24,8},{25,17},{2,18},{3,... | collective-permute-start | bytes 393224 | tf_op jit(solution)/shard_map/ppermute | solution.py:55
  101.3 6.7 %collective-permute-start.23 = (bf16[64,1024]{1,0:T(8,128)(2,1)S(1)}, bf16[64,1024]{1,0:T(8,128)(2,1)S(1)}, u32[]{:S(2)}, u32[]{:S(2)}) collective-permute-start(bf16[64,1024]{1,0:T(8,128)(2,1)S(1)} %collective-permute-done.21.refs_1_), channel_id=1, source_target_pairs={{0,16},{1,9},{8,24},{9,1},{16,0},{17,25},{24,8},{25,17},{2,18},{3,... | collective-permute-start | bytes 393224 | tf_op jit(solution)/shard_map/ppermute | solution.py:55
  101.7 6.3 %collective-permute-start.24 = (bf16[64,1024]{1,0:T(8,128)(2,1)S(1)}, bf16[64,1024]{1,0:T(8,128)(2,1)S(1)}, u32[]{:S(2)}, u32[]{:S(2)}) collective-permute-start(bf16[64,1024]{1,0:T(8,128)(2,1)S(1)} %multiply_convert_fusion.refs_0_), channel_id=1, source_target_pairs={{0,1},{1,0},{2,3},{3,2},{4,5},{5,4},{6,7},{7,6},{8,9},{9,8},{10,11... | collective-permute-start | bytes 393224 | tf_op jit(solution)/shard_map/ppermute | solution.py:38
  101.7 6.3 %collective-permute-start.25 = (bf16[64,1024]{1,0:T(8,128)(2,1)S(1)}, bf16[64,1024]{1,0:T(8,128)(2,1)S(1)}, u32[]{:S(2)}, u32[]{:S(2)}) collective-permute-start(bf16[64,1024]{1,0:T(8,128)(2,1)S(1)} %collective-permute-done.21.refs_1_), channel_id=1, source_target_pairs={{0,1},{1,0},{2,3},{3,2},{4,5},{5,4},{6,7},{7,6},{8,9},{9,8},{10,11... | collective-permute-start | bytes 393224 | tf_op jit(solution)/shard_map/ppermute | solution.py:38
  102.2 5.8 %collective-permute-start.26 = (bf16[64,1024]{1,0:T(8,128)(2,1)S(1)}, bf16[64,1024]{1,0:T(8,128)(2,1)S(1)}, u32[]{:S(2)}, u32[]{:S(2)}) collective-permute-start(bf16[64,1024]{1,0:T(8,128)(2,1)S(1)} %collective-permute-done.22.refs_2_), channel_id=1, source_target_pairs={{0,1},{1,0},{2,3},{3,2},{4,5},{5,4},{6,7},{7,6},{8,9},{9,8},{10,11... | collective-permute-start | bytes 393224 | tf_op jit(solution)/shard_map/ppermute | solution.py:38
  108.0 1.3 collective-permute-start.27
  112.0 1.6 collective-permute-start.30
  112.2 1.8 collective-permute-start.28
  114.1 9.6 %collective-permute-start.31 = (bf16[2,64,1024]{2,1,0:T(8,128)(2,1)S(1)}, bf16[2,64,1024]{2,1,0:T(8,128)(2,1)S(1)}, u32[]{:S(2)}, u32[]{:S(2)}) collective-permute-start(bf16[2,64,1024]{2,1,0:T(8,128)(2,1)S(1)} %bitcast.138), channel_id=1, source_target_pairs={{0,16},{1,9},{8,24},{9,1},{16,0},{17,25},{24,8},{25,17},{2,18},{3,... | collective-permute-start | bytes 786440 | tf_op jit(solution)/shard_map/ppermute | solution.py:55
  123.8 5.0 %collective-permute-start.32 = (bf16[1,64,1024]{2,1,0:T(8,128)(2,1)S(1)}, bf16[1,64,1024]{2,1,0:T(8,128)(2,1)S(1)}, u32[]{:S(2)}, u32[]{:S(2)}) collective-permute-start(bf16[1,64,1024]{2,1,0:T(8,128)(2,1)S(1)} %slice.380), channel_id=1, source_target_pairs={{0,8},{1,17},{8,0},{9,25},{16,24},{17,1},{24,16},{25,9},{2,10},{3,... | collective-permute-start | bytes 393224 | tf_op jit(solution)/shard_map/ppermute | solution.py:55
  126.2 5.2 %collective-permute-start.29 = (bf16[256,1024]{1,0:T(8,128)(2,1)S(1)}, bf16[256,1024]{1,0:T(8,128)(2,1)S(1)}, u32[]{:S(2)}, u32[]{:S(2)}) collective-permute-start(bf16[256,1024]{1,0:T(8,128)(2,1)S(1)} %get-tuple-element.128), channel_id=1, source_target_pairs={{0,1},{1,0},{2,3},{3,2},{4,5},{5,4},{6,7},{7,6},{8,9},{9,8},{10,11... | collective-permute-start | bytes 1572872 | tf_op jit(solution)/shard_map/ppermute | solution.py:38
  129.9 6.2 %collective-permute-start.36 = (bf16[64,1024]{1,0:T(8,128)(2,1)S(1)}, bf16[64,1024]{1,0:T(8,128)(2,1)}, u32[]{:S(2)}, u32[]{:S(2)}) collective-permute-start(bf16[64,1024]{1,0:T(8,128)(2,1)S(1)} %get-tuple-element.171.refs_9_), channel_id=1, source_target_pairs={{0,2},{1,5},{2,0},{3,7},{4,6},{5,1},{6,4},{7,3},{8,10},{9,13},{10,... | collective-permute-start | bytes 393224 | tf_op jit(solution)/shard_map/ppermute | solution.py:55
  132.5 10.2 %collective-permute-start.33 = (bf16[2,64,1024]{2,1,0:T(8,128)(2,1)}, bf16[2,64,1024]{2,1,0:T(8,128)(2,1)}, u32[]{:S(2)}, u32[]{:S(2)}) collective-permute-start(bf16[2,64,1024]{2,1,0:T(8,128)(2,1)} %bitcast.21), channel_id=1, source_target_pairs={{0,16},{1,9},{8,24},{9,1},{16,0},{17,25},{24,8},{25,17},{2,18},{3,... | collective-permute-start | bytes 786440 | tf_op jit(solution)/shard_map/ppermute | solution.py:55
  133.0 11.5 %copy-start.18 = (bf16[512,128]{1,0:T(8,128)(2,1)S(1)}, bf16[512,128]{1,0:T(8,128)(2,1)}, u32[]{:S(2)}) copy-start(bf16[512,128]{1,0:T(8,128)(2,1)} %copy-done.17) | copy-start | bytes 393220
  133.0 5.2 %collective-permute-start.37 = (bf16[64,1024]{1,0:T(8,128)(2,1)S(1)}, bf16[64,1024]{1,0:T(8,128)(2,1)S(1)}, u32[]{:S(2)}, u32[]{:S(2)}) collective-permute-start(bf16[64,1024]{1,0:T(8,128)(2,1)S(1)} %get-tuple-element.171.refs_9_), channel_id=1, source_target_pairs={{0,4},{1,3},{2,6},{3,1},{4,0},{5,7},{6,2},{7,5},{8,12},{9,11},{10,... | collective-permute-start | bytes 393224 | tf_op jit(solution)/shard_map/ppermute | solution.py:55
  136.1 5.2 %collective-permute-start.38 = (bf16[64,1024]{1,0:T(8,128)(2,1)}, bf16[64,1024]{1,0:T(8,128)(2,1)S(1)}, u32[]{:S(2)}, u32[]{:S(2)}) collective-permute-start(bf16[64,1024]{1,0:T(8,128)(2,1)} %collective-permute-done.36.refs_10_), channel_id=1, source_target_pairs={{0,4},{1,3},{2,6},{3,1},{4,0},{5,7},{6,2},{7,5},{8,12},{9,11},{10,... | collective-permute-start | bytes 393224 | tf_op jit(solution)/shard_map/ppermute | solution.py:55
  136.1 22.9 %collective-permute-start.50 = (bf16[2,4,64,384]{3,2,1,0:T(8,128)(2,1)}, bf16[2,4,64,384]{3,2,1,0:T(8,128)(2,1)S(1)}, u32[]{:S(2)}, u32[]{:S(2)}) collective-permute-start(bf16[2,4,64,384]{3,2,1,0:T(8,128)(2,1)} %copy-done.12), channel_id=1, source_target_pairs={{0,4},{1,3},{2,6},{3,1},{4,0},{5,7},{6,2},{7,5},{8,12},{9,11},{10,... | collective-permute-start | bytes 1179656 | tf_op jit(solution)/shard_map/ppermute | solution.py:55
  138.2 5.7 %collective-permute-start.39 = (bf16[64,1024]{1,0:T(8,128)(2,1)S(1)}, bf16[64,1024]{1,0:T(8,128)(2,1)S(1)}, u32[]{:S(2)}, u32[]{:S(2)}) collective-permute-start(bf16[64,1024]{1,0:T(8,128)(2,1)S(1)} %get-tuple-element.171.refs_9_), channel_id=1, source_target_pairs={{0,1},{1,0},{2,3},{3,2},{4,5},{5,4},{6,7},{7,6},{8,9},{9,8},{10,11... | collective-permute-start | bytes 393224 | tf_op jit(solution)/shard_map/ppermute | solution.py:38
  138.2 6.3 %collective-permute-start.40 = (bf16[64,1024]{1,0:T(8,128)(2,1)}, bf16[64,1024]{1,0:T(8,128)(2,1)S(1)}, u32[]{:S(2)}, u32[]{:S(2)}) collective-permute-start(bf16[64,1024]{1,0:T(8,128)(2,1)} %collective-permute-done.36.refs_10_), channel_id=1, source_target_pairs={{0,1},{1,0},{2,3},{3,2},{4,5},{5,4},{6,7},{7,6},{8,9},{9,8},{10,11... | collective-permute-start | bytes 393224 | tf_op jit(solution)/shard_map/ppermute | solution.py:38
  141.3 3.1 %collective-permute-start.41 = (bf16[64,1024]{1,0:T(8,128)(2,1)S(1)}, bf16[64,1024]{1,0:T(8,128)(2,1)S(1)}, u32[]{:S(2)}, u32[]{:S(2)}) collective-permute-start(bf16[64,1024]{1,0:T(8,128)(2,1)S(1)} %collective-permute-done.37.refs_11_), channel_id=1, source_target_pairs={{0,1},{1,0},{2,3},{3,2},{4,5},{5,4},{6,7},{7,6},{8,9},{9,8},{10,11... | collective-permute-start | bytes 393224 | tf_op jit(solution)/shard_map/ppermute | solution.py:38
  142.6 1.8 collective-permute-start.42
  143.9 21.2 %collective-permute-start.44 = (bf16[2,4,64,768]{3,2,1,0:T(8,128)(2,1)}, bf16[2,4,64,768]{3,2,1,0:T(8,128)(2,1)S(1)}, u32[]{:S(2)}, u32[]{:S(2)}) collective-permute-start(bf16[2,4,64,768]{3,2,1,0:T(8,128)(2,1)} %copy-done.11), channel_id=1, source_target_pairs={{0,4},{1,3},{2,6},{3,1},{4,0},{5,7},{6,2},{7,5},{8,12},{9,11},{10,... | collective-permute-start | bytes 2359304 | tf_op jit(solution)/shard_map/ppermute | solution.py:55
  144.4 16.3 %collective-permute-start.34 = (bf16[1,64,1024]{2,1,0:T(8,128)(2,1)S(1)}, bf16[1,64,1024]{2,1,0:T(8,128)(2,1)S(1)}, u32[]{:S(2)}, u32[]{:S(2)}) collective-permute-start(bf16[1,64,1024]{2,1,0:T(8,128)(2,1)S(1)} %slice.379), channel_id=1, source_target_pairs={{0,8},{1,17},{8,0},{9,25},{16,24},{17,1},{24,16},{25,9},{2,10},{3,... | collective-permute-start | bytes 393224 | tf_op jit(solution)/shard_map/ppermute | solution.py:55
  156.1 8.9 %collective-permute-start.43 = (bf16[256,1024]{1,0:T(8,128)(2,1)S(1)}, bf16[256,1024]{1,0:T(8,128)(2,1)S(1)}, u32[]{:S(2)}, u32[]{:S(2)}) collective-permute-start(bf16[256,1024]{1,0:T(8,128)(2,1)S(1)} %get-tuple-element.141), channel_id=1, source_target_pairs={{0,1},{1,0},{2,3},{3,2},{4,5},{5,4},{6,7},{7,6},{8,9},{9,8},{10,11... | collective-permute-start | bytes 1572872 | tf_op jit(solution)/shard_map/ppermute | solution.py:38
  156.4 23.7 %collective-permute-start.48 = (bf16[2,264,512]{2,1,0:T(8,128)(2,1)S(1)}, bf16[2,264,512]{2,1,0:T(8,128)(2,1)S(1)}, u32[]{:S(2)}, u32[]{:S(2)}) collective-permute-start(bf16[2,264,512]{2,1,0:T(8,128)(2,1)S(1)} %get-tuple-element.147), channel_id=1, source_target_pairs={{0,16},{1,9},{8,24},{9,1},{16,0},{17,25},{24,8},{25,17},{2,18},{3,... | collective-permute-start | bytes 1622024 | tf_op jit(solution)/shard_map/ppermute | solution.py:55
  159.2 5.7 %collective-permute-start.51 = (bf16[1,4,64,384]{3,2,1,0:T(8,128)(2,1)S(1)}, bf16[1,4,64,384]{3,2,1,0:T(8,128)(2,1)S(1)}, u32[]{:S(2)}, u32[]{:S(2)}) collective-permute-start(bf16[1,4,64,384]{3,2,1,0:T(8,128)(2,1)S(1)} %slice.376), channel_id=1, source_target_pairs={{0,2},{1,5},{2,0},{3,7},{4,6},{5,1},{6,4},{7,3},{8,10},{9,13},{10,... | collective-permute-start | bytes 589832 | tf_op jit(solution)/shard_map/ppermute | solution.py:55
  160.7 24.0 %collective-permute-start.35 = (bf16[64,1024]{1,0:T(8,128)(2,1)S(1)}, bf16[64,1024]{1,0:T(8,128)(2,1)S(1)}, u32[]{:S(2)}, u32[]{:S(2)}) collective-permute-start(bf16[64,1024]{1,0:T(8,128)(2,1)S(1)} %fusion.20), channel_id=1, source_target_pairs={{0,1},{1,0},{2,3},{3,2},{4,5},{5,4},{6,7},{7,6},{8,9},{9,8},{10,11... | collective-permute-start | bytes 393224 | tf_op jit(solution)/shard_map/ppermute | solution.py:38
  165.1 9.2 %collective-permute-start.45 = (bf16[2,64,1024]{2,1,0:T(8,128)(2,1)S(1)}, bf16[2,64,1024]{2,1,0:T(8,128)(2,1)S(1)}, u32[]{:S(2)}, u32[]{:S(2)}) collective-permute-start(bf16[2,64,1024]{2,1,0:T(8,128)(2,1)S(1)} %bitcast.136), channel_id=1, source_target_pairs={{0,4},{1,3},{2,6},{3,1},{4,0},{5,7},{6,2},{7,5},{8,12},{9,11},{10,... | collective-permute-start | bytes 786440 | tf_op jit(solution)/shard_map/ppermute | solution.py:55
  166.9 10.1 %collective-permute-start.53 = (bf16[2,256,256]{2,1,0:T(8,128)(2,1)S(1)}, bf16[2,256,256]{2,1,0:T(8,128)(2,1)S(1)}, u32[]{:S(2)}, u32[]{:S(2)}) collective-permute-start(bf16[2,256,256]{2,1,0:T(8,128)(2,1)S(1)} %get-tuple-element.154), channel_id=1, source_target_pairs={{0,16},{1,9},{8,24},{9,1},{16,0},{17,25},{24,8},{25,17},{2,18},{3,... | collective-permute-start | bytes 786440 | tf_op jit(solution)/shard_map/ppermute | solution.py:55
  167.7 12.3 %collective-permute-start.49 = (bf16[1,4,64,768]{3,2,1,0:T(8,128)(2,1)S(1)}, bf16[1,4,64,768]{3,2,1,0:T(8,128)(2,1)S(1)}, u32[]{:S(2)}, u32[]{:S(2)}) collective-permute-start(bf16[1,4,64,768]{3,2,1,0:T(8,128)(2,1)S(1)} %slice.374), channel_id=1, source_target_pairs={{0,2},{1,5},{2,0},{3,7},{4,6},{5,1},{6,4},{7,3},{8,10},{9,13},{10,... | collective-permute-start | bytes 1179656 | tf_op jit(solution)/shard_map/ppermute | solution.py:55
  174.4 5.0 %collective-permute-start.46 = (bf16[1,64,1024]{2,1,0:T(8,128)(2,1)S(1)}, bf16[1,64,1024]{2,1,0:T(8,128)(2,1)S(1)}, u32[]{:S(2)}, u32[]{:S(2)}) collective-permute-start(bf16[1,64,1024]{2,1,0:T(8,128)(2,1)S(1)} %slice.378), channel_id=1, source_target_pairs={{0,2},{1,5},{2,0},{3,7},{4,6},{5,1},{6,4},{7,3},{8,10},{9,13},{10,... | collective-permute-start | bytes 393224 | tf_op jit(solution)/shard_map/ppermute | solution.py:55
  177.1 6.2 %collective-permute-start.54 = (bf16[1,256,256]{2,1,0:T(8,128)(2,1)S(1)}, bf16[1,256,256]{2,1,0:T(8,128)(2,1)S(1)}, u32[]{:S(2)}, u32[]{:S(2)}) collective-permute-start(bf16[1,256,256]{2,1,0:T(8,128)(2,1)S(1)} %slice.377), channel_id=1, source_target_pairs={{0,8},{1,17},{8,0},{9,25},{16,24},{17,1},{24,16},{25,9},{2,10},{3,... | collective-permute-start | bytes 393224 | tf_op jit(solution)/shard_map/ppermute | solution.py:55
  179.9 7.7 %collective-permute-start.47 = (bf16[64,1024]{1,0:T(8,128)(2,1)S(1)}, bf16[64,1024]{1,0:T(8,128)(2,1)S(1)}, u32[]{:S(2)}, u32[]{:S(2)}) collective-permute-start(bf16[64,1024]{1,0:T(8,128)(2,1)S(1)} %fusion.12), channel_id=1, source_target_pairs={{0,1},{1,0},{2,3},{3,2},{4,5},{5,4},{6,7},{7,6},{8,9},{9,8},{10,11... | collective-permute-start | bytes 393224 | tf_op jit(solution)/shard_map/ppermute | solution.py:38
  180.4 13.5 %collective-permute-start.52 = (bf16[1,264,512]{2,1,0:T(8,128)(2,1)S(1)}, bf16[1,264,512]{2,1,0:T(8,128)(2,1)S(1)}, u32[]{:S(2)}, u32[]{:S(2)}) collective-permute-start(bf16[1,264,512]{2,1,0:T(8,128)(2,1)S(1)} %slice.375), channel_id=1, source_target_pairs={{0,8},{1,17},{8,0},{9,25},{16,24},{17,1},{24,16},{25,9},{2,10},{3,... | collective-permute-start | bytes 811016 | tf_op jit(solution)/shard_map/ppermute | solution.py:55
  180.4 25.0 %collective-permute-start.58 = (bf16[64,1152]{1,0:T(8,128)(2,1)S(1)}, bf16[64,1152]{1,0:T(8,128)(2,1)S(1)}, u32[]{:S(2)}, u32[]{:S(2)}) collective-permute-start(bf16[64,1152]{1,0:T(8,128)(2,1)S(1)} %get-tuple-element.162), channel_id=1, source_target_pairs={{0,8},{8,0},{16,24},{24,16},{1,9},{9,1},{17,25},{25,17},{2,10},{10... | collective-permute-start | bytes 442376 | tf_op jit(solution)/shard_map/ppermute | solution.py:38
  183.3 22.2 %collective-permute-start.59 = (bf16[64,1152]{1,0:T(8,128)(2,1)S(1)}, bf16[64,1152]{1,0:T(8,128)(2,1)S(1)}, u32[]{:S(2)}, u32[]{:S(2)}) collective-permute-start(bf16[64,1152]{1,0:T(8,128)(2,1)S(1)} %get-tuple-element.163), channel_id=1, source_target_pairs={{0,16},{8,24},{16,0},{24,8},{1,17},{9,25},{17,1},{25,9},{2,18},{10... | collective-permute-start | bytes 442376 | tf_op jit(solution)/shard_map/ppermute | solution.py:38
  184.8 20.7 %collective-permute-start.60 = (bf16[64,1152]{1,0:T(8,128)(2,1)S(1)}, bf16[64,1152]{1,0:T(8,128)(2,1)S(1)}, u32[]{:S(2)}, u32[]{:S(2)}) collective-permute-start(bf16[64,1152]{1,0:T(8,128)(2,1)S(1)} %get-tuple-element.164), channel_id=1, source_target_pairs={{0,24},{8,16},{16,8},{24,0},{1,25},{9,17},{17,9},{25,1},{2,26},{10... | collective-permute-start | bytes 442376 | tf_op jit(solution)/shard_map/ppermute | solution.py:38
  194.0 4.9 %collective-permute-start.55 = (bf16[72,768]{1,0:T(8,128)(2,1)S(1)}, bf16[72,768]{1,0:T(8,128)(2,1)S(1)}, u32[]{:S(2)}, u32[]{:S(2)}) collective-permute-start(bf16[72,768]{1,0:T(8,128)(2,1)S(1)} %fusion.34), channel_id=1, source_target_pairs={{0,2},{2,0},{4,6},{6,4},{1,3},{3,1},{5,7},{7,5},{8,10},{10,8},{12,... | collective-permute-start | bytes 331784 | tf_op jit(solution)/shard_map/ppermute | solution.py:38
  195.6 5.8 %collective-permute-start.56 = (bf16[72,768]{1,0:T(8,128)(2,1)S(1)}, bf16[72,768]{1,0:T(8,128)(2,1)S(1)}, u32[]{:S(2)}, u32[]{:S(2)}) collective-permute-start(bf16[72,768]{1,0:T(8,128)(2,1)S(1)} %fusion.35), channel_id=1, source_target_pairs={{0,4},{2,6},{4,0},{6,2},{1,5},{3,7},{5,1},{7,3},{8,12},{10,14},{12... | collective-permute-start | bytes 331784 | tf_op jit(solution)/shard_map/ppermute | solution.py:38
  198.9 5.6 %collective-permute-start.57 = (bf16[72,768]{1,0:T(8,128)(2,1)S(1)}, bf16[72,768]{1,0:T(8,128)(2,1)S(1)}, u32[]{:S(2)}, u32[]{:S(2)}) collective-permute-start(bf16[72,768]{1,0:T(8,128)(2,1)S(1)} %fusion.36), channel_id=1, source_target_pairs={{0,6},{2,4},{4,2},{6,0},{1,7},{3,5},{5,3},{7,1},{8,14},{10,12},{12... | collective-permute-start | bytes 331784 | tf_op jit(solution)/shard_map/ppermute | solution.py:38
  205.5 1.2 collective-permute-start.61
  (34 other events, 126.9 us)

commit v4 on v3

--- a/solution.py
+++ b/solution.py
@@ -107,6 +107,8 @@
     vmem = pl.BlockSpec(memory_space=pltpu.VMEM)
     far = pl.BlockSpec(memory_space=pltpu.MemorySpace.HBM)
     moved = sum(a.size * a.dtype.itemsize for a in list(args) + list(outs))
+    outs = [pltpu.HBM(a.shape, a.dtype) for a in outs[:hbm_outs]] + list(outs[hbm_outs:])
+    args = [pltpu.with_memory_space_constraint(a, pltpu.HBM) for a in args[:hbm]] + list(args[hbm:])
     return pl.pallas_call(
         body,
         out_shape=list(outs),
@@ -176,9 +178,14 @@
             fill = [((0, 0), (0, 0), (0, hp - hc))]
             w_gate, w_up, w_down = [jnp.pad(w.reshape(rows, F, hc), *fill).reshape(rows, F * hp) for w in (w_gate, w_up, w_down)]
         def attn_pack(wq_ref, wk_ref, wv_ref, wo_ref, x_ref, ga_ref, gf_ref, gq_ref, gk_ref, s_ref, *refs):
-            outs, sem = refs[:C], refs[C]
+            outs, sem, small = refs[:C], refs[C], refs[C + 1 : C + 6]
             mt = lax.axis_index("tensor")
             mf, mc = me()
+            given = (ga_ref, gf_ref, gq_ref, gk_ref, s_ref)
+            early = [pltpu.make_async_copy(a, b, sem.at[0, 5 + m]) for m, (a, b) in enumerate(zip(given, small))]
+            for cp in early:
+                cp.start()
+            ga_ref, gf_ref, gq_ref, gk_ref, s_ref = small
             copies = []
             for k in range(C):
                 d = mc ^ k
@@ -190,6 +197,8 @@
                     copies.append(pltpu.make_async_copy(w.at[:, src], outs[k].at[0:rows, start : start + size], sem.at[k, m]))
             for cp in copies:
                 cp.start()
+            for cp in early:
+                cp.wait()
             dest = mf * C + mc
             lanes = lax.broadcasted_iota(jnp.int32, (8, 128), 1)
             docs = jnp.broadcast_to(s_ref[...].astype(F32), (8, 128))
@@ -221,9 +230,11 @@
             [w_query, w_key, w_value, w_out.T, hid]
             + [v.reshape(1, -1) for v in (gain_attn, gain_ffn, gain_query, gain_key)]
             + [segments.reshape(1, tokens)],
-            [pltpu.SemaphoreType.DMA((C, 5))],
-            hbm=5,
-            vmem_mb=60,
+            [pltpu.SemaphoreType.DMA((C, 10))]
+            + [pltpu.VMEM((1, v.shape[0]), BF) for v in (gain_attn, gain_ffn, gain_query, gain_key)]
+            + [pltpu.VMEM((1, tokens), jnp.int32)],
+            hbm=10,
+            vmem_mb=16,
         )
 
         wf = call(
@@ -232,7 +243,7 @@
             list(after((w_gate, w_up, w_down), wa[0])),
             [pltpu.SemaphoreType.DMA((F, 3))],
             hbm=3,
-            vmem_mb=60,
+            vmem_mb=16,
         )
         wa_got = scatter(wa, "context", C)
 
@@ -255,21 +266,21 @@
         wq, wo, x_own = call(
             attn_join,
             [shape(CR + 2 * C, aw), shape(CR, qc), shape(C * half + 8, width)],
-            [after(wa_got[0], wf[1])] + wa_got[1:],
+            [after(wa_got[0], wf[1], wf[F - 1])] + wa_got[1:],
             [pltpu.VMEM((8, 128), F32)],
         )
+        q_here = []
+        wq = gather(wq, "fsdp", F, first=q_here)
+        wo = gather(after(wo, wq[0]), "fsdp", F)
+
         def ffn_join(*refs):
             for k in range(F):
                 refs[F][k] = refs[k][...]
 
         wf_got = wf
-        wf = call(ffn_join, [shape(F, rows, 3 * hp)], [after(wf[0], wq)] + wf[1:], vmem_mb=8)[0]
+        wf = call(ffn_join, [shape(F, rows, 3 * hp)], [after(wf[0], q_here[0])] + wf[1:], vmem_mb=8)[0]
         wf_first = hop(wf[None], "context", C, 0)
         wf_here = wf[None]
-
-        q_here = []
-        wq = gather(wq, "fsdp", F, gate=wf, first=q_here)
-        wo = gather(after(wo, wq[0]), "fsdp", F)
 
         def my_half(x):
             return lax.dynamic_slice_in_dim(x, t * half, half, 0)
@@ -312,7 +323,7 @@
 
         allowed = call(find_allowed, [shape(R, R)], xs + [pos_row, pos_col])[0]
 
-        def reduce(own, low, high, axis, n, enter=None, first=None, last=None):
+        def pair_sum(own, low, high, enter=None):
             keep = H // 2
             if high is None:
                 low = swap_t(low)
@@ -323,14 +334,21 @@
             low = own[:keep] + low.astype(F32)
             if enter is not None:
                 high = after(high, enter)
+            return low, high
+
+        def finish(low, high, axis, n, first=None, last=None):
             shaped = (n // 2, half, width)
-            return reduce_blocks(low.reshape(shaped), high.reshape(shaped), axis, n, None, first, last), high
-
-        def spread(x, axis, n):
-            b = [x]
-            for i in range(bits(n)):
+            return reduce_blocks(low.reshape(shaped), high.reshape(shaped), axis, n, None, first, last)
+
+        def reduce(own, low, high, axis, n, enter=None, first=None, last=None):
+            low, high = pair_sum(own, low, high, enter)
+            return finish(low, high, axis, n, first, last), high
+
+        def spread(b, axis, n, start=0, late=None):
+            for i in range(start, bits(n)):
                 b = b + [hop(a, axis, n, i) for a in b]
-            return b + [swap_t(a) for a in b]
+            last = b[-1] if late is None else after(b[-1], late)
+            return b + [swap_t(a) for a in b[:-1] + [last]]
 
         def both_halves(x):
             y = swap_t(x)
@@ -352,7 +370,7 @@
         whole = [shape(H, width, dtype=F32), shape(H, width)]
         halves = [shape(H, width, dtype=F32), shape(H // 2, width), shape(H // 2, width)]
 
-        got = after(wf_first, q_here[0])
+        got = after(wf_first, wo[0])
         for i in range(1, bits(C)):
             wf_here = join(wf_here, got)
             got = hop(wf_here, "context", C, i)
@@ -421,8 +439,39 @@
             hbm_outs=6,
         )
 
-        dys = gather(after(my_half(cot), gv), "fsdp", F)
-        dys = dys + [swap_t(b) for b in dys]
+        def out_proj(o_ref, *refs):
+            wb, w_far, o_far, own, low, high, w, sem = refs[:2], *refs[2:]
+            mf, mc = me()
+            mt = lax.axis_index("tensor")
+            kept = [pltpu.make_async_copy(o_ref, o_far, sem.at[0]), pltpu.make_async_copy(w, w_far, sem.at[1])]
+            kept[0].start()
+            for a in range(F):
+                for b in range(C):
+                    dest = (mf ^ mask_of(a, F, mt)) * C + (mc ^ b)
+                    w[at(dest * rows, rows, rows), :] = wb[a // FH][a % FH, b * rows : (b + 1) * rows, :]
+            kept[1].start()
+            split_rows(mm_t(o_ref[...], w[...]), own, low, high)
+            for cp in kept:
+                cp.wait()
+
+        res = call(
+            out_proj,
+            [shape(width, qc), shape(R, qc)] + halves,
+            [o] + wo,
+            [pltpu.VMEM((width, qc), BF), pltpu.SemaphoreType.DMA((2,))],
+            hbm_outs=2,
+            flops=2 * R * width * qc,
+        )
+        w_o, o = res[:2]
+        low, high = pair_sum(*res[2:])
+        branch_first = []
+        x_mid = x_half.astype(F32) + finish(low, high, "context", C, first=branch_first)
+        dys = gather(after(my_half(cot), gv), "fsdp", F, gate=branch_first[0])
+        r2 = inv_rms(x_mid)
+        g_ffn = gv[1:2]
+        h2s = [(x_mid * r2 * g_ffn).astype(BF)]
+        h2s = h2s + [hop(h2s[0], "fsdp", F, 0)]
+        dys = dys + [swap_t(dys[0]), swap_t(after(dys[1], h2s[1]))]
 
         def ffn_pre(*refs):
             wb, db, w, dy, du = refs[:2], refs[2:6], *refs[6:]
@@ -443,27 +492,7 @@
             flops=2 * R * width * hp,
         )
 
-        def out_proj(o_ref, *refs):
-            wb, own, low, high, w = refs[:2], *refs[2:]
-            mf, mc = me()
-            mt = lax.axis_index("tensor")
-            for a in range(F):
-                for b in range(C):
-                    dest = (mf ^ mask_of(a, F, mt)) * C + (mc ^ b)
-                    w[at(dest * rows, rows, rows), :] = wb[a // FH][a % FH, b * rows : (b + 1) * rows, :]
-            split_rows(mm_t(o_ref[...], w[...]), own, low, high)
-
-        res = call(
-            out_proj,
-            halves + [shape(width, qc)],
-            [after(o, wf[1])] + wo,
-            flops=2 * R * width * qc,
-        )
-        w_o = res[3]
-        x_mid = x_half.astype(F32) + reduce(*res[:3], "context", C, last=du)[0]
-        r2 = inv_rms(x_mid)
-        g_ffn = gv[1:2]
-        h2s = spread((x_mid * r2 * g_ffn).astype(BF), "fsdp", F)
+        h2s = spread(h2s, "fsdp", F, 1, late=du)
 
         def ffn_main(*refs):
             hb, w, du_ref, own, low, high, h2, act = refs[: 2 * F], *refs[2 * F :]
@@ -516,12 +545,12 @@
         dg_ffn = jnp.sum(gn_rows, 0, keepdims=True)
         dx_mid = my_half(cot).astype(F32) + inward
         dx_low = dx_mid.astype(BF)
-        dxs = spread(dx_low, "context", C)
+        dxs = spread([dx_low], "context", C)
         units_first, out_first = [], []
         g_units = reduce_blocks(*after(units_parts, dxs[1:C]), "context", C, first=units_first)
         out = (x_mid + reduce(*out_parts, "fsdp", F, enter=dx_low, first=out_first)[0]).astype(BF)
 
-        far = [after(w_o, out_first[0]), q, ky, v, raw, h, w_qkv]
+        far = [w_o, q, ky, v, raw, h, w_qkv]
 
         def attn_back(*refs):
             far, refs = refs[:7], refs[7:]
@@ -603,7 +632,7 @@
             flops=2 * R * width * qc + 4 * R * width * aw + 12 * R * R * qc,
             vmem_mb=24,
         )
-        g_down = reduce_blocks(*down_parts, "context", C, gate=res[0])
+        g_down = reduce_blocks(*after(down_parts, dxs[1:C]), "context", C, gate=res[0])
         def out_grad(dx, o_ref, ga, gb, g):
             refs = (ga, gb)
             mf, mc = me()
@@ -646,7 +675,7 @@
             both_grads = jnp.concatenate([gq[j * rows : (j + 1) * rows], go[j * rows : (j + 1) * rows]], 1)
             gains = jnp.pad(gq[CR + 2 * j : CR + 2 * j + 2], ((0, 6), (0, qc)))
             ga.append(jnp.concatenate([both_grads, gains], 0))
-        ga = scatter(ga, "context", C)
+        ga = scatter([ga[0]] + list(after(ga[1:], gf[1])), "context", C)
         x32 = x_half.astype(F32)
         inward, _ = norm_back(x32, inv_rms(x32), gv[0:1], dh)
         grad_hidden = (dx_mid + inward).astype(BF)

time: 208 us -> 190 us (0.913)
  waiting for transfers between devices: 98.8 us -> 73.6 us
  starting transfers between devices: 56.6 us -> 76.4 us
  local copies, waits for them, and re-layouts: 12.5 us -> 3.16 us
  Pallas kernels: 28.8 us -> 24.5 us
    ppermute x30, waiting for transfers between devices: 82.1 us -> 54.4 us  [hop(): lax.ppermute(x, (axis, 'tensor'), [(2 * d + t, 2 * (d ^ steps[t]) + t) fo...]
    ppermute x30, starting transfers between devices: 33.9 us -> 50.9 us  [hop(): lax.ppermute(x, (axis, 'tensor'), [(2 * d + t, 2 * (d ^ steps[t]) + t) fo...]
    unnamed x72 -> x40, local copies, waits for them, and re-layouts: 10 us -> 0.72 us
    pallas_call x18, Pallas kernels: 28.8 us -> 24.5 us  [call(): pl.pallas_call(body, out_shape=list(outs), in_specs=[far] * hbm + [vmem]...]
    ppermute x32, starting transfers between devices: 22.7 us -> 25.5 us  [swap(): return lax.ppermute(x, axis, [(i, i ^ k) for i in range(n)])]
    ppermute x32, waiting for transfers between devices: 16.7 us -> 19.2 us  [swap(): return lax.ppermute(x, axis, [(i, i ^ k) for i in range(n)])]
  transfers between devices with their start and end apart: 62 -> 62, of which waited for: 28 -> 32; matrix products, arithmetic and copies ran while one was open for 5% -> 5% of each run, Pallas kernels for 9% -> 10%
where the time goes in v4:
time: 190 us; the launch traced here: 189 us
  starting transfers between devices  76.4 us (40%)
  waiting for transfers between devices  73.6 us (39%)
  Pallas kernels  24.5 us (13%)
  other arithmetic  10.1 us (5%)
  local copies, waits for them, and re-layouts  3.16 us (2%)
    ppermute x30, waiting for transfers between devices, hop(): lax.ppermute(x, (axis, 'tensor'), [(2 * d + t, 2 * (d ^ steps[t]) + t) fo...  54.4 us
    ppermute x30, starting transfers between devices, hop(): lax.ppermute(x, (axis, 'tensor'), [(2 * d + t, 2 * (d ^ steps[t]) + t) fo...  50.9 us
    ppermute x32, starting transfers between devices, swap(): return lax.ppermute(x, axis, [(i, i ^ k) for i in range(n)])  25.5 us
    pallas_call x18, Pallas kernels, call(): pl.pallas_call(body, out_shape=list(outs), in_specs=[far] * hbm + [vmem]...  24.5 us
    ppermute x32, waiting for transfers between devices, swap(): return lax.ppermute(x, axis, [(i, i ^ k) for i in range(n)])  19.2 us
  transfers between devices with their start and end apart: 62, of which 32 were waited for; matrix products, arithmetic and copies ran while one was open for 5% of the time, Pallas kernels for 10%

profile of v4, /device:TPU:0, one launch (start us, length us, event | category | flops | bytes accessed | tf_op | source)
XLA Modules:
  0.0 189.2 jit_solution(3934416889372159637)
XLA Ops:
  0.6 1.7 shard_map.237
  2.3 3.0 %collective-permute-start.2 = (bf16[72,1792]{1,0:T(8,128)(2,1)S(1)}, bf16[72,1792]{1,0:T(8,128)(2,1)S(1)}, u32[]{:S(2)}, u32[]{:S(2)}) collective-permute-start(bf16[72,1792]{1,0:T(8,128)(2,1)S(1)} %get-tuple-element.103), channel_id=1, source_target_pairs={{0,2},{2,0},{4,6},{6,4},{1,3},{3,1},{5,7},{7,5},{8,10},{10,8},{12,... | collective-permute-start | bytes 774152 | tf_op jit(solution)/shard_map/ppermute | solution.py:38
  5.4 1.5 collective-permute-start.3
  6.9 1.2 shard_map.238
  8.1 2.1 %collective-permute-start = (bf16[64,1152]{1,0:T(8,128)(2,1)S(1)}, bf16[64,1152]{1,0:T(8,128)(2,1)S(1)}, u32[]{:S(2)}, u32[]{:S(2)}) collective-permute-start(bf16[64,1152]{1,0:T(8,128)(2,1)S(1)} %get-tuple-element.100), channel_id=1, source_target_pairs={{0,8},{8,0},{16,24},{24,16},{1,9},{9,1},{17,25},{25,17},{2,10},{10... | collective-permute-start | bytes 442376 | tf_op jit(solution)/shard_map/ppermute | solution.py:38
  10.2 2.5 %collective-permute-start.1 = (bf16[64,1152]{1,0:T(8,128)(2,1)S(1)}, bf16[64,1152]{1,0:T(8,128)(2,1)S(1)}, u32[]{:S(2)}, u32[]{:S(2)}) collective-permute-start(bf16[64,1152]{1,0:T(8,128)(2,1)S(1)} %get-tuple-element.101), channel_id=1, source_target_pairs={{0,24},{8,16},{16,8},{24,0},{1,25},{9,17},{17,9},{25,1},{2,26},{10... | collective-permute-start | bytes 442376 | tf_op jit(solution)/shard_map/ppermute | solution.py:38
  12.7 1.5 collective-permute-done.refs_1_
  14.2 4.3 %collective-permute-done.1.refs_3_ = bf16[64,1152]{1,0:T(8,128)(2,1)S(1)} collective-permute-done((bf16[64,1152]{1,0:T(8,128)(2,1)S(1)}, bf16[64,1152]{1,0:T(8,128)(2,1)S(1)}, u32[]{:S(2)}, u32[]{:S(2)}) %collective-permute-start.1) | collective-permute-done | bytes 147488 | tf_op jit(solution)/shard_map/ppermute | solution.py:38
  18.7 1.6 collective-permute-start.6
  20.3 2.6 %collective-permute-start.8 = (bf16[64,1152]{1,0:T(8,128)(2,1)S(1)}, bf16[64,1152]{1,0:T(8,128)(2,1)S(1)}, u32[]{:S(2)}, u32[]{:S(2)}) collective-permute-start(bf16[64,1152]{1,0:T(8,128)(2,1)S(1)} %get-tuple-element.110), channel_id=1, source_target_pairs={{0,16},{8,24},{16,0},{24,8},{1,17},{9,25},{17,1},{25,9},{2,18},{10... | collective-permute-start | bytes 442376 | tf_op jit(solution)/shard_map/ppermute | solution.py:38
  23.0 4.2 %collective-permute-done.6.b_ref = bf16[1,264,512]{2,1,0:T(8,128)(2,1)S(1)} collective-permute-done((bf16[1,264,512]{2,1,0:T(8,128)(2,1)S(1)}, bf16[1,264,512]{2,1,0:T(8,128)(2,1)S(1)}, u32[]{:S(2)}, u32[]{:S(2)}) %collective-permute-start.6) | collective-permute-done | bytes 270368 | tf_op jit(solution)/shard_map/ppermute | solution.py:55
  27.2 2.9 %collective-permute-start.7 = (bf16[2,264,512]{2,1,0:T(8,128)(2,1)S(1)}, bf16[2,264,512]{2,1,0:T(8,128)(2,1)S(1)}, u32[]{:S(2)}, u32[]{:S(2)}) collective-permute-start(bf16[2,264,512]{2,1,0:T(8,128)(2,1)S(1)} %shard_map.240.refs_2_), channel_id=1, source_target_pairs={{0,16},{1,9},{8,24},{9,1},{16,0},{17,25},{24,8},{25,17},{2,18},{3,... | collective-permute-start | bytes 1622024 | tf_op jit(solution)/shard_map/ppermute | solution.py:55
  30.1 1.4 collective-permute-done.8.refs_2_
  31.5 1.5 collective-permute-start.9
  34.6 9.7 %collective-permute-done.10.b_ref = bf16[1,256,256]{2,1,0:T(8,128)(2,1)S(1)} collective-permute-done((bf16[1,256,256]{2,1,0:T(8,128)(2,1)S(1)}, bf16[1,256,256]{2,1,0:T(8,128)(2,1)S(1)}, u32[]{:S(2)}, u32[]{:S(2)}) %collective-permute-start.10) | collective-permute-done | bytes 131104 | tf_op jit(solution)/shard_map/ppermute | solution.py:55
  44.3 2.4 %collective-permute-start.11 = (bf16[2,256,256]{2,1,0:T(8,128)(2,1)S(1)}, bf16[2,256,256]{2,1,0:T(8,128)(2,1)S(1)}, u32[]{:S(2)}, u32[]{:S(2)}) collective-permute-start(bf16[2,256,256]{2,1,0:T(8,128)(2,1)S(1)} %shard_map.243.refs_0_), channel_id=1, source_target_pairs={{0,16},{1,9},{8,24},{9,1},{16,0},{17,25},{24,8},{25,17},{2,18},{3,... | collective-permute-start | bytes 786440 | tf_op jit(solution)/shard_map/ppermute | solution.py:55
  47.4 3.3 %shard_map.244 = (bf16[512,1024]{1,0:T(8,128)(2,1)}, f32[512,384]{1,0:T(8,128)}, bf16[512,256]{1,0:T(8,128)(2,1)}, bf16[512,128]{1,0:T(8,128)(2,1)}, bf16[512,12...) custom-call(bf16[264,1024]{1,0:T(8,128)(2,1)S(1)} %get-tuple-element, ...), custom_call_target="tpu_custom_call" | custom-call | flops 805306368 | bytes 6918144 | tf_op jit(solution)/shard_map/pallas_call | solution.py:112
  50.7 2.1 %collective-permute-done.11.refs_1_ = bf16[2,256,256]{2,1,0:T(8,128)(2,1)S(1)} collective-permute-done((bf16[2,256,256]{2,1,0:T(8,128)(2,1)S(1)}, bf16[2,256,256]{2,1,0:T(8,128)(2,1)S(1)}, u32[]{:S(2)}, u32[]{:S(2)}) %collective-permute-start.11) | collective-permute-done | bytes 262176 | tf_op jit(solution)/shard_map/ppermute | solution.py:55
  53.7 1.5 collective-permute-start.13
  55.4 1.1 collective-permute-done.13
  57.9 1.8 collective-permute-start.14
  61.0 2.8 %collective-permute-start.23 = (bf16[1,64,1024]{2,1,0:T(8,128)(2,1)S(1)}, bf16[1,64,1024]{2,1,0:T(8,128)(2,1)S(1)}, u32[]{:S(2)}, u32[]{:S(2)}) collective-permute-start(bf16[1,64,1024]{2,1,0:T(8,128)(2,1)S(1)} %bitcast.124), channel_id=1, source_target_pairs={{0,8},{1,17},{8,0},{9,25},{16,24},{17,1},{24,16},{25,9},{2,10},{3,... | collective-permute-start | bytes 393224 | tf_op jit(solution)/shard_map/ppermute | solution.py:55
  65.6 1.5 collective-permute-start.15
  67.1 2.6 %collective-permute-start.24 = (bf16[2,64,1024]{2,1,0:T(8,128)(2,1)S(1)}, bf16[2,64,1024]{2,1,0:T(8,128)(2,1)S(1)}, u32[]{:S(2)}, u32[]{:S(2)}) collective-permute-start(bf16[2,64,1024]{2,1,0:T(8,128)(2,1)S(1)} %shard_map.247.refs_2_), channel_id=1, source_target_pairs={{0,16},{1,9},{8,24},{9,1},{16,0},{17,25},{24,8},{25,17},{2,18},{3,... | collective-permute-start | bytes 786440 | tf_op jit(solution)/shard_map/ppermute | solution.py:55
  69.7 2.3 %collective-permute-done.15 = bf16[1,64,1024]{2,1,0:T(8,128)(2,1)S(1)} collective-permute-done((bf16[1,64,1024]{2,1,0:T(8,128)(2,1)S(1)}, bf16[1,64,1024]{2,1,0:T(8,128)(2,1)S(1)}, u32[]{:S(2)}, u32[]{:S(2)}) %collective-permute-start.15) | collective-permute-done | bytes 131104 | tf_op jit(solution)/shard_map/ppermute | solution.py:55
  72.8 2.8 %collective-permute-start.16 = (bf16[64,1024]{1,0:T(8,128)(2,1)S(1)}, bf16[64,1024]{1,0:T(8,128)(2,1)S(1)}, u32[]{:S(2)}, u32[]{:S(2)}) collective-permute-start(bf16[64,1024]{1,0:T(8,128)(2,1)S(1)} %multiply_convert_fusion.refs_0_), channel_id=1, source_target_pairs={{0,8},{1,17},{8,0},{9,25},{16,24},{17,1},{24,16},{25,9},{2,10},{3,... | collective-permute-start | bytes 393224 | tf_op jit(solution)/shard_map/ppermute | solution.py:55
  75.6 3.4 %collective-permute-done.24.refs_3_ = bf16[2,64,1024]{2,1,0:T(8,128)(2,1)S(1)} collective-permute-done((bf16[2,64,1024]{2,1,0:T(8,128)(2,1)S(1)}, bf16[2,64,1024]{2,1,0:T(8,128)(2,1)S(1)}, u32[]{:S(2)}, u32[]{:S(2)}) %collective-permute-start.24) | collective-permute-done | bytes 262176 | tf_op jit(solution)/shard_map/ppermute | solution.py:55
  80.0 2.5 %collective-permute-start.17 = (bf16[64,1024]{1,0:T(8,128)(2,1)S(1)}, bf16[64,1024]{1,0:T(8,128)(2,1)S(1)}, u32[]{:S(2)}, u32[]{:S(2)}) collective-permute-start(bf16[64,1024]{1,0:T(8,128)(2,1)S(1)} %multiply_convert_fusion.refs_0_), channel_id=1, source_target_pairs={{0,16},{1,9},{8,24},{9,1},{16,0},{17,25},{24,8},{25,17},{2,18},{3,... | collective-permute-start | bytes 393224 | tf_op jit(solution)/shard_map/ppermute | solution.py:55
  82.9 3.0 %collective-permute-done.17.refs_2_ = bf16[64,1024]{1,0:T(8,128)(2,1)S(1)} collective-permute-done((bf16[64,1024]{1,0:T(8,128)(2,1)S(1)}, bf16[64,1024]{1,0:T(8,128)(2,1)S(1)}, u32[]{:S(2)}, u32[]{:S(2)}) %collective-permute-start.17) | collective-permute-done | bytes 131104 | tf_op jit(solution)/shard_map/ppermute | solution.py:55
  87.4 2.3 %collective-permute-done.18.refs_3_ = bf16[64,1024]{1,0:T(8,128)(2,1)S(1)} collective-permute-done((bf16[64,1024]{1,0:T(8,128)(2,1)S(1)}, bf16[64,1024]{1,0:T(8,128)(2,1)S(1)}, u32[]{:S(2)}, u32[]{:S(2)}) %collective-permute-start.18) | collective-permute-done | bytes 131104 | tf_op jit(solution)/shard_map/ppermute | solution.py:55
  89.7 1.3 collective-permute-done.27.refs_7_
  91.0 2.6 %shard_map.249 = (f32[256,1024]{1,0:T(8,128)S(1)}, bf16[128,1024]{1,0:T(8,128)(2,1)S(1)}, bf16[128,1024]{1,0:T(8,128)(2,1)S(1)}, bf16[512,1024]{1,0:T(8,128)(2,1)S(1)}, bf16[512,1152]{1,0:T(8,128)(2,1)S(1)}) custom-call(bf16[64,1024]{1,0:T(8,128)(2,1)S(1)} %multiply_convert_fusion.refs_0_, bf16[64,1024]{1,0:T(8,128)(2,1)S(1)} %collective-permute-done.16.refs_1_, ...), custom_call_target="tpu_custom_call" | custom-call | flops 1610612736 | bytes 7995392 | tf_op jit(solution)/shard_map/pallas_call | solution.py:112
  94.2 1.0 collective-permute-done.30
  95.8 1.5 collective-permute-start.31
  97.3 7.0 %collective-permute-done.31 = bf16[2,64,1024]{2,1,0:T(8,128)(2,1)S(1)} collective-permute-done((bf16[2,64,1024]{2,1,0:T(8,128)(2,1)S(1)}, bf16[2,64,1024]{2,1,0:T(8,128)(2,1)S(1)}, u32[]{:S(2)}, u32[]{:S(2)}) %collective-permute-start.31) | collective-permute-done | bytes 262176 | tf_op jit(solution)/shard_map/ppermute | solution.py:55
  104.4 3.2 %collective-permute-start.32 = (bf16[1,64,1024]{2,1,0:T(8,128)(2,1)S(1)}, bf16[1,64,1024]{2,1,0:T(8,128)(2,1)S(1)}, u32[]{:S(2)}, u32[]{:S(2)}) collective-permute-start(bf16[1,64,1024]{2,1,0:T(8,128)(2,1)S(1)} %slice.380), channel_id=1, source_target_pairs={{0,8},{1,17},{8,0},{9,25},{16,24},{17,1},{24,16},{25,9},{2,10},{3,... | collective-permute-start | bytes 393224 | tf_op jit(solution)/shard_map/ppermute | solution.py:55
  107.6 2.5 %shard_map.250 = (f32[256,1024]{1,0:T(8,128)S(1)}, bf16[256,1024]{1,0:T(8,128)(2,1)S(1)}, bf16[2,4,64,384]{3,2,1,0:T(8,128)(2,1)S(1)}, bf16[2,4,64,384]{3,2,1,0:...) custom-call(bf16[512,1024]{1,0:T(8,128)(2,1)S(1)} %get-tuple-element.126.h2_ref, ...), custom_call_target="tpu_custom_call" | custom-call | flops 1610612736 | bytes 9568256 | tf_op jit(solution)/shard_map/pallas_call | solution.py:112
  112.1 1.6 collective-permute-start.36
  114.8 2.1 %collective-permute-start.33 = (bf16[2,64,1024]{2,1,0:T(8,128)(2,1)}, bf16[2,64,1024]{2,1,0:T(8,128)(2,1)}, u32[]{:S(2)}, u32[]{:S(2)}) collective-permute-start(bf16[2,64,1024]{2,1,0:T(8,128)(2,1)} %bitcast.21), channel_id=1, source_target_pairs={{0,16},{1,9},{8,24},{9,1},{16,0},{17,25},{24,8},{25,17},{2,18},{3,... | collective-permute-start | bytes 786440 | tf_op jit(solution)/shard_map/ppermute | solution.py:55
  117.3 2.7 %collective-permute-start.38 = (bf16[64,1024]{1,0:T(8,128)(2,1)}, bf16[64,1024]{1,0:T(8,128)(2,1)S(1)}, u32[]{:S(2)}, u32[]{:S(2)}) collective-permute-start(bf16[64,1024]{1,0:T(8,128)(2,1)} %collective-permute-done.36.refs_10_), channel_id=1, source_target_pairs={{0,4},{1,3},{2,6},{3,1},{4,0},{5,7},{6,2},{7,5},{8,12},{9,11},{10,... | collective-permute-start | bytes 393224 | tf_op jit(solution)/shard_map/ppermute | solution.py:55
  120.5 1.3 collective-permute-done.37.refs_11_
  121.8 1.4 collective-permute-done.38.refs_12_
  123.2 1.9 %collective-permute-start.50 = (bf16[2,4,64,384]{3,2,1,0:T(8,128)(2,1)}, bf16[2,4,64,384]{3,2,1,0:T(8,128)(2,1)S(1)}, u32[]{:S(2)}, u32[]{:S(2)}) collective-permute-start(bf16[2,4,64,384]{3,2,1,0:T(8,128)(2,1)} %copy-done.3), channel_id=1, source_target_pairs={{0,4},{1,3},{2,6},{3,1},{4,0},{5,7},{6,2},{7,5},{8,12},{9,11},{10,... | collective-permute-start | bytes 1179656 | tf_op jit(solution)/shard_map/ppermute | solution.py:55
  125.2 1.2 convert_add_fusion.6
  127.0 2.0 %collective-permute-start.34 = (bf16[1,64,1024]{2,1,0:T(8,128)(2,1)S(1)}, bf16[1,64,1024]{2,1,0:T(8,128)(2,1)S(1)}, u32[]{:S(2)}, u32[]{:S(2)}) collective-permute-start(bf16[1,64,1024]{2,1,0:T(8,128)(2,1)S(1)} %slice.379), channel_id=1, source_target_pairs={{0,8},{1,17},{8,0},{9,25},{16,24},{17,1},{24,16},{25,9},{2,10},{3,... | collective-permute-start | bytes 393224 | tf_op jit(solution)/shard_map/ppermute | solution.py:55
  128.9 8.3 %shard_map.251 = (f32[256,1024]{1,0:T(8,128)S(1)}, bf16[256,1024]{1,0:T(8,128)(2,1)S(1)}, bf16[2,264,512]{2,1,0:T(8,128)(2,1)S(1)}, bf16[2,264,512]{2,1,0:T(8,128)(2,1)S(1)}, bf16[512,1024]{1,0:T(8,128)(2,1)S(1)}) custom-call(bf16[1024,256]{1,0:T(8,128)(2,1)} %get-tuple-element.136.refs_0_, bf16[512,256]{1,0:T(8,128)(2,1)} %get-tuple-element.137.refs_1_, ...), custom_call_target="tpu_custom_call" | custom-call | flops 2147483648 | bytes 10854400 | tf_op jit(solution)/shard_map/pallas_call | solution.py:112
  137.3 2.6 %collective-permute-start.48 = (bf16[2,264,512]{2,1,0:T(8,128)(2,1)S(1)}, bf16[2,264,512]{2,1,0:T(8,128)(2,1)S(1)}, u32[]{:S(2)}, u32[]{:S(2)}) collective-permute-start(bf16[2,264,512]{2,1,0:T(8,128)(2,1)S(1)} %get-tuple-element.151), channel_id=1, source_target_pairs={{0,16},{1,9},{8,24},{9,1},{16,0},{17,25},{24,8},{25,17},{2,18},{3,... | collective-permute-start | bytes 1622024 | tf_op jit(solution)/shard_map/ppermute | solution.py:55
  140.0 1.7 collective-permute-start.51
  141.9 3.9 %collective-permute-done.51 = bf16[1,4,64,384]{3,2,1,0:T(8,128)(2,1)S(1)} collective-permute-done((bf16[1,4,64,384]{3,2,1,0:T(8,128)(2,1)S(1)}, bf16[1,4,64,384]{3,2,1,0:T(8,128)(2,1)S(1)}, u32[]{:S(2)}, u32[]{:S(2)}) %collective-permute-start.51) | collective-permute-done | bytes 196640 | tf_op jit(solution)/shard_map/ppermute | solution.py:55
  148.1 1.2 collective-permute-start.49
  149.4 5.9 %collective-permute-done.45 = bf16[2,64,1024]{2,1,0:T(8,128)(2,1)S(1)} collective-permute-done((bf16[2,64,1024]{2,1,0:T(8,128)(2,1)S(1)}, bf16[2,64,1024]{2,1,0:T(8,128)(2,1)S(1)}, u32[]{:S(2)}, u32[]{:S(2)}) %collective-permute-start.45) | collective-permute-done | bytes 262176 | tf_op jit(solution)/shard_map/ppermute | solution.py:55
  155.3 1.7 collective-permute-start.46
  157.7 2.6 %collective-permute-start.54 = (bf16[1,256,256]{2,1,0:T(8,128)(2,1)S(1)}, bf16[1,256,256]{2,1,0:T(8,128)(2,1)S(1)}, u32[]{:S(2)}, u32[]{:S(2)}) collective-permute-start(bf16[1,256,256]{2,1,0:T(8,128)(2,1)S(1)} %slice.377), channel_id=1, source_target_pairs={{0,8},{1,17},{8,0},{9,25},{16,24},{17,1},{24,16},{25,9},{2,10},{3,... | collective-permute-start | bytes 393224 | tf_op jit(solution)/shard_map/ppermute | solution.py:55
  161.5 1.8 collective-permute-start.55
  164.6 1.0 collective-permute-start.59
  165.7 2.8 %collective-permute-start.60 = (bf16[64,1152]{1,0:T(8,128)(2,1)S(1)}, bf16[64,1152]{1,0:T(8,128)(2,1)S(1)}, u32[]{:S(2)}, u32[]{:S(2)}) collective-permute-start(bf16[64,1152]{1,0:T(8,128)(2,1)S(1)} %get-tuple-element.174), channel_id=1, source_target_pairs={{0,24},{8,16},{16,8},{24,0},{1,25},{9,17},{17,9},{25,1},{2,26},{10... | collective-permute-start | bytes 442376 | tf_op jit(solution)/shard_map/ppermute | solution.py:38
  170.0 4.4 %collective-permute-done.52 = bf16[1,264,512]{2,1,0:T(8,128)(2,1)S(1)} collective-permute-done((bf16[1,264,512]{2,1,0:T(8,128)(2,1)S(1)}, bf16[1,264,512]{2,1,0:T(8,128)(2,1)S(1)}, u32[]{:S(2)}, u32[]{:S(2)}) %collective-permute-start.52) | collective-permute-done | bytes 270368 | tf_op jit(solution)/shard_map/ppermute | solution.py:55
  174.7 2.0 %collective-permute-done.55.refs_1_ = bf16[64,1152]{1,0:T(8,128)(2,1)S(1)} collective-permute-done((bf16[64,1152]{1,0:T(8,128)(2,1)S(1)}, bf16[64,1152]{1,0:T(8,128)(2,1)S(1)}, u32[]{:S(2)}, u32[]{:S(2)}) %collective-permute-start.55) | collective-permute-done | bytes 147488 | tf_op jit(solution)/shard_map/ppermute | solution.py:38
  176.7 1.9 %collective-permute-start.56 = (bf16[72,768]{1,0:T(8,128)(2,1)S(1)}, bf16[72,768]{1,0:T(8,128)(2,1)S(1)}, u32[]{:S(2)}, u32[]{:S(2)}) collective-permute-start(bf16[72,768]{1,0:T(8,128)(2,1)S(1)} %fusion.34), channel_id=1, source_target_pairs={{0,2},{2,0},{4,6},{6,4},{1,3},{3,1},{5,7},{7,5},{8,10},{10,8},{12,... | collective-permute-start | bytes 331784 | tf_op jit(solution)/shard_map/ppermute | solution.py:38
  178.6 1.6 collective-permute-start.57
  180.2 1.3 collective-permute-done.56.refs_1_
  181.5 1.8 collective-permute-done.57.refs_2_
  183.3 2.5 %collective-permute-done.58.refs_3_ = bf16[72,768]{1,0:T(8,128)(2,1)S(1)} collective-permute-done((bf16[72,768]{1,0:T(8,128)(2,1)S(1)}, bf16[72,768]{1,0:T(8,128)(2,1)S(1)}, u32[]{:S(2)}, u32[]{:S(2)}) %collective-permute-start.58) | collective-permute-done | bytes 110624 | tf_op jit(solution)/shard_map/ppermute | solution.py:38
  186.8 1.1 shard_map.254
  (176 shorter events, 26.9 us)
Async XLA Ops:
  2.3 16.2 %collective-permute-start.2 = (bf16[72,1792]{1,0:T(8,128)(2,1)S(1)}, bf16[72,1792]{1,0:T(8,128)(2,1)S(1)}, u32[]{:S(2)}, u32[]{:S(2)}) collective-permute-start(bf16[72,1792]{1,0:T(8,128)(2,1)S(1)} %get-tuple-element.103), channel_id=1, source_target_pairs={{0,2},{2,0},{4,6},{6,4},{1,3},{3,1},{5,7},{7,5},{8,10},{10,8},{12,... | collective-permute-start | bytes 774152 | tf_op jit(solution)/shard_map/ppermute | solution.py:38
  5.4 13.2 %collective-permute-start.3 = (bf16[72,1792]{1,0:T(8,128)(2,1)S(1)}, bf16[72,1792]{1,0:T(8,128)(2,1)S(1)}, u32[]{:S(2)}, u32[]{:S(2)}) collective-permute-start(bf16[72,1792]{1,0:T(8,128)(2,1)S(1)} %get-tuple-element.104), channel_id=1, source_target_pairs={{0,4},{2,6},{4,0},{6,2},{1,5},{3,7},{5,1},{7,3},{8,12},{10,14},{12... | collective-permute-start | bytes 774152 | tf_op jit(solution)/shard_map/ppermute | solution.py:38
  6.9 11.7 %collective-permute-start.4 = (bf16[72,1792]{1,0:T(8,128)(2,1)S(1)}, bf16[72,1792]{1,0:T(8,128)(2,1)S(1)}, u32[]{:S(2)}, u32[]{:S(2)}) collective-permute-start(bf16[72,1792]{1,0:T(8,128)(2,1)S(1)} %get-tuple-element.105), channel_id=1, source_target_pairs={{0,6},{2,4},{4,2},{6,0},{1,7},{3,5},{5,3},{7,1},{8,14},{10,12},{12... | collective-permute-start | bytes 774152 | tf_op jit(solution)/shard_map/ppermute | solution.py:38
  8.1 6.1 %collective-permute-start = (bf16[64,1152]{1,0:T(8,128)(2,1)S(1)}, bf16[64,1152]{1,0:T(8,128)(2,1)S(1)}, u32[]{:S(2)}, u32[]{:S(2)}) collective-permute-start(bf16[64,1152]{1,0:T(8,128)(2,1)S(1)} %get-tuple-element.100), channel_id=1, source_target_pairs={{0,8},{8,0},{16,24},{24,16},{1,9},{9,1},{17,25},{25,17},{2,10},{10... | collective-permute-start | bytes 442376 | tf_op jit(solution)/shard_map/ppermute | solution.py:38
  10.2 8.4 %collective-permute-start.1 = (bf16[64,1152]{1,0:T(8,128)(2,1)S(1)}, bf16[64,1152]{1,0:T(8,128)(2,1)S(1)}, u32[]{:S(2)}, u32[]{:S(2)}) collective-permute-start(bf16[64,1152]{1,0:T(8,128)(2,1)S(1)} %get-tuple-element.101), channel_id=1, source_target_pairs={{0,24},{8,16},{16,8},{24,0},{1,25},{9,17},{17,9},{25,1},{2,26},{10... | collective-permute-start | bytes 442376 | tf_op jit(solution)/shard_map/ppermute | solution.py:38
  18.7 8.5 %collective-permute-start.6 = (bf16[1,264,512]{2,1,0:T(8,128)(2,1)S(1)}, bf16[1,264,512]{2,1,0:T(8,128)(2,1)S(1)}, u32[]{:S(2)}, u32[]{:S(2)}) collective-permute-start(bf16[1,264,512]{2,1,0:T(8,128)(2,1)S(1)} %bitcast.126), channel_id=1, source_target_pairs={{0,8},{1,17},{8,0},{9,25},{16,24},{17,1},{24,16},{25,9},{2,10},{3,... | collective-permute-start | bytes 811016 | tf_op jit(solution)/shard_map/ppermute | solution.py:55
  20.3 11.2 %collective-permute-start.8 = (bf16[64,1152]{1,0:T(8,128)(2,1)S(1)}, bf16[64,1152]{1,0:T(8,128)(2,1)S(1)}, u32[]{:S(2)}, u32[]{:S(2)}) collective-permute-start(bf16[64,1152]{1,0:T(8,128)(2,1)S(1)} %get-tuple-element.110), channel_id=1, source_target_pairs={{0,16},{8,24},{16,0},{24,8},{1,17},{9,25},{17,1},{25,9},{2,18},{10... | collective-permute-start | bytes 442376 | tf_op jit(solution)/shard_map/ppermute | solution.py:38
  22.9 24.0 %collective-permute-start.5 = (bf16[264,1024]{1,0:T(8,128)(2,1)S(1)}, bf16[264,1024]{1,0:T(8,128)(2,1)S(1)}, u32[]{:S(2)}, u32[]{:S(2)}) collective-permute-start(bf16[264,1024]{1,0:T(8,128)(2,1)S(1)} %get-tuple-element.106.a_ref.refs_0_.refs_7_), channel_id=1, source_target_pairs={{0,1},{1,0},{2,3},{3,2},{4,5},{5,4},{6,7},{7,6},{8,9},{9,8},{10,11... | collective-permute-start | bytes 1622024 | tf_op jit(solution)/shard_map/ppermute | solution.py:38
  27.2 20.2 %collective-permute-start.7 = (bf16[2,264,512]{2,1,0:T(8,128)(2,1)S(1)}, bf16[2,264,512]{2,1,0:T(8,128)(2,1)S(1)}, u32[]{:S(2)}, u32[]{:S(2)}) collective-permute-start(bf16[2,264,512]{2,1,0:T(8,128)(2,1)S(1)} %shard_map.240.refs_2_), channel_id=1, source_target_pairs={{0,16},{1,9},{8,24},{9,1},{16,0},{17,25},{24,8},{25,17},{2,18},{3,... | collective-permute-start | bytes 1622024 | tf_op jit(solution)/shard_map/ppermute | solution.py:55
  31.5 15.9 %collective-permute-start.9 = (bf16[1,4,64,1152]{3,2,1,0:T(8,128)(2,1)S(1)}, bf16[1,4,64,1152]{3,2,1,0:T(8,128)(2,1)S(1)}, u32[]{:S(2)}, u32[]{:S(2)}) collective-permute-start(bf16[1,4,64,1152]{3,2,1,0:T(8,128)(2,1)S(1)} %bitcast.122), channel_id=1, source_target_pairs={{0,2},{1,5},{2,0},{3,7},{4,6},{5,1},{6,4},{7,3},{8,10},{9,13},{10,... | collective-permute-start | bytes 1769480 | tf_op jit(solution)/shard_map/ppermute | solution.py:55
  33.0 11.2 %collective-permute-start.10 = (bf16[1,256,256]{2,1,0:T(8,128)(2,1)S(1)}, bf16[1,256,256]{2,1,0:T(8,128)(2,1)S(1)}, u32[]{:S(2)}, u32[]{:S(2)}) collective-permute-start(bf16[1,256,256]{2,1,0:T(8,128)(2,1)S(1)} %bitcast.128), channel_id=1, source_target_pairs={{0,8},{1,17},{8,0},{9,25},{16,24},{17,1},{24,16},{25,9},{2,10},{3,... | collective-permute-start | bytes 393224 | tf_op jit(solution)/shard_map/ppermute | solution.py:55
  44.3 8.5 %collective-permute-start.11 = (bf16[2,256,256]{2,1,0:T(8,128)(2,1)S(1)}, bf16[2,256,256]{2,1,0:T(8,128)(2,1)S(1)}, u32[]{:S(2)}, u32[]{:S(2)}) collective-permute-start(bf16[2,256,256]{2,1,0:T(8,128)(2,1)S(1)} %shard_map.243.refs_0_), channel_id=1, source_target_pairs={{0,16},{1,9},{8,24},{9,1},{16,0},{17,25},{24,8},{25,17},{2,18},{3,... | collective-permute-start | bytes 786440 | tf_op jit(solution)/shard_map/ppermute | solution.py:55
  53.7 2.7 %collective-permute-start.13 = (bf16[128,1024]{1,0:T(8,128)(2,1)S(1)}, bf16[128,1024]{1,0:T(8,128)(2,1)S(1)}, u32[]{:S(2)}, u32[]{:S(2)}) collective-permute-start(bf16[128,1024]{1,0:T(8,128)(2,1)S(1)} %get-tuple-element.117), channel_id=1, source_target_pairs={{0,1},{1,0},{2,3},{3,2},{4,5},{5,4},{6,7},{7,6},{8,9},{9,8},{10,11... | collective-permute-start | bytes 786440 | tf_op jit(solution)/shard_map/ppermute | solution.py:38
  55.3 1.5 collective-permute-start.12
  57.9 6.7 %collective-permute-start.14 = (bf16[2,64,1024]{2,1,0:T(8,128)(2,1)}, bf16[2,64,1024]{2,1,0:T(8,128)(2,1)}, u32[]{:S(2)}, u32[]{:S(2)}) collective-permute-start(bf16[2,64,1024]{2,1,0:T(8,128)(2,1)} %bitcast.11), channel_id=1, source_target_pairs={{0,4},{1,3},{2,6},{3,1},{4,0},{5,7},{6,2},{7,5},{8,12},{9,11},{10,... | collective-permute-start | bytes 786440 | tf_op jit(solution)/shard_map/ppermute | solution.py:55
  60.6 11.4 %copy-start.10 = (bf16[1,128,1024]{2,1,0:T(8,128)(2,1)S(1)}, bf16[1,128,1024]{2,1,0:T(8,128)(2,1)}, u32[]{:S(2)}) copy-start(bf16[1,128,1024]{2,1,0:T(8,128)(2,1)} %param.14) | copy-start | bytes 786436
  60.6 25.8 %collective-permute-start.22 = (bf16[2,4,64,1152]{3,2,1,0:T(8,128)(2,1)S(1)}, bf16[2,4,64,1152]{3,2,1,0:T(8,128)(2,1)S(1)}, u32[]{:S(2)}, u32[]{:S(2)}) collective-permute-start(bf16[2,4,64,1152]{3,2,1,0:T(8,128)(2,1)S(1)} %shard_map.246.refs_0_), channel_id=1, source_target_pairs={{0,4},{1,3},{2,6},{3,1},{4,0},{5,7},{6,2},{7,5},{8,12},{9,11},{10,... | collective-permute-start | bytes 3538952 | tf_op jit(solution)/shard_map/ppermute | solution.py:55
  61.0 6.1 %collective-permute-start.23 = (bf16[1,64,1024]{2,1,0:T(8,128)(2,1)S(1)}, bf16[1,64,1024]{2,1,0:T(8,128)(2,1)S(1)}, u32[]{:S(2)}, u32[]{:S(2)}) collective-permute-start(bf16[1,64,1024]{2,1,0:T(8,128)(2,1)S(1)} %bitcast.124), channel_id=1, source_target_pairs={{0,8},{1,17},{8,0},{9,25},{16,24},{17,1},{24,16},{25,9},{2,10},{3,... | collective-permute-start | bytes 393224 | tf_op jit(solution)/shard_map/ppermute | solution.py:55
  65.6 6.4 %collective-permute-start.15 = (bf16[1,64,1024]{2,1,0:T(8,128)(2,1)S(1)}, bf16[1,64,1024]{2,1,0:T(8,128)(2,1)S(1)}, u32[]{:S(2)}, u32[]{:S(2)}) collective-permute-start(bf16[1,64,1024]{2,1,0:T(8,128)(2,1)S(1)} %slice.381), channel_id=1, source_target_pairs={{0,2},{1,5},{2,0},{3,7},{4,6},{5,1},{6,4},{7,3},{8,10},{9,13},{10,... | collective-permute-start | bytes 393224 | tf_op jit(solution)/shard_map/ppermute | solution.py:55
  67.1 11.9 %collective-permute-start.24 = (bf16[2,64,1024]{2,1,0:T(8,128)(2,1)S(1)}, bf16[2,64,1024]{2,1,0:T(8,128)(2,1)S(1)}, u32[]{:S(2)}, u32[]{:S(2)}) collective-permute-start(bf16[2,64,1024]{2,1,0:T(8,128)(2,1)S(1)} %shard_map.247.refs_2_), channel_id=1, source_target_pairs={{0,16},{1,9},{8,24},{9,1},{16,0},{17,25},{24,8},{25,17},{2,18},{3,... | collective-permute-start | bytes 786440 | tf_op jit(solution)/shard_map/ppermute | solution.py:55
  72.2 39.0 %copy-start.4 = (f32[64,1024]{1,0:T(8,128)}, f32[64,1024]{1,0:T(8,128)S(1)}, u32[]{:S(2)}) copy-start(f32[64,1024]{1,0:T(8,128)S(1)} %get-tuple-element.184) | copy-start | bytes 786436
  72.8 6.2 %collective-permute-start.16 = (bf16[64,1024]{1,0:T(8,128)(2,1)S(1)}, bf16[64,1024]{1,0:T(8,128)(2,1)S(1)}, u32[]{:S(2)}, u32[]{:S(2)}) collective-permute-start(bf16[64,1024]{1,0:T(8,128)(2,1)S(1)} %multiply_convert_fusion.refs_0_), channel_id=1, source_target_pairs={{0,8},{1,17},{8,0},{9,25},{16,24},{17,1},{24,16},{25,9},{2,10},{3,... | collective-permute-start | bytes 393224 | tf_op jit(solution)/shard_map/ppermute | solution.py:55
  75.6 7.3 %collective-permute-start.25 = (bf16[2,64,1024]{2,1,0:T(8,128)(2,1)S(1)}, bf16[2,64,1024]{2,1,0:T(8,128)(2,1)S(1)}, u32[]{:S(2)}, u32[]{:S(2)}) collective-permute-start(bf16[2,64,1024]{2,1,0:T(8,128)(2,1)S(1)} %shard_map.247.refs_2_), channel_id=1, source_target_pairs={{0,1},{1,0},{2,3},{3,2},{4,5},{5,4},{6,7},{7,6},{8,9},{9,8},{10,11... | collective-permute-start | bytes 786440 | tf_op jit(solution)/shard_map/ppermute | solution.py:38
  79.0 6.9 %collective-permute-start.26 = (bf16[2,64,1024]{2,1,0:T(8,128)(2,1)S(1)}, bf16[2,64,1024]{2,1,0:T(8,128)(2,1)S(1)}, u32[]{:S(2)}, u32[]{:S(2)}) collective-permute-start(bf16[2,64,1024]{2,1,0:T(8,128)(2,1)S(1)} %collective-permute-done.24.refs_3_), channel_id=1, source_target_pairs={{0,1},{1,0},{2,3},{3,2},{4,5},{5,4},{6,7},{7,6},{8,9},{9,8},{10,11... | collective-permute-start | bytes 786440 | tf_op jit(solution)/shard_map/ppermute | solution.py:38
  80.0 6.0 %collective-permute-start.17 = (bf16[64,1024]{1,0:T(8,128)(2,1)S(1)}, bf16[64,1024]{1,0:T(8,128)(2,1)S(1)}, u32[]{:S(2)}, u32[]{:S(2)}) collective-permute-start(bf16[64,1024]{1,0:T(8,128)(2,1)S(1)} %multiply_convert_fusion.refs_0_), channel_id=1, source_target_pairs={{0,16},{1,9},{8,24},{9,1},{16,0},{17,25},{24,8},{25,17},{2,18},{3,... | collective-permute-start | bytes 393224 | tf_op jit(solution)/shard_map/ppermute | solution.py:55
  82.5 7.2 %collective-permute-start.18 = (bf16[64,1024]{1,0:T(8,128)(2,1)S(1)}, bf16[64,1024]{1,0:T(8,128)(2,1)S(1)}, u32[]{:S(2)}, u32[]{:S(2)}) collective-permute-start(bf16[64,1024]{1,0:T(8,128)(2,1)S(1)} %collective-permute-done.16.refs_1_), channel_id=1, source_target_pairs={{0,16},{1,9},{8,24},{9,1},{16,0},{17,25},{24,8},{25,17},{2,18},{3,... | collective-permute-start | bytes 393224 | tf_op jit(solution)/shard_map/ppermute | solution.py:55
  82.9 6.8 %collective-permute-start.19 = (bf16[64,1024]{1,0:T(8,128)(2,1)S(1)}, bf16[64,1024]{1,0:T(8,128)(2,1)S(1)}, u32[]{:S(2)}, u32[]{:S(2)}) collective-permute-start(bf16[64,1024]{1,0:T(8,128)(2,1)S(1)} %multiply_convert_fusion.refs_0_), channel_id=1, source_target_pairs={{0,1},{1,0},{2,3},{3,2},{4,5},{5,4},{6,7},{7,6},{8,9},{9,8},{10,11... | collective-permute-start | bytes 393224 | tf_op jit(solution)/shard_map/ppermute | solution.py:38
  85.9 3.7 %collective-permute-start.20 = (bf16[64,1024]{1,0:T(8,128)(2,1)S(1)}, bf16[64,1024]{1,0:T(8,128)(2,1)S(1)}, u32[]{:S(2)}, u32[]{:S(2)}) collective-permute-start(bf16[64,1024]{1,0:T(8,128)(2,1)S(1)} %collective-permute-done.16.refs_1_), channel_id=1, source_target_pairs={{0,1},{1,0},{2,3},{3,2},{4,5},{5,4},{6,7},{7,6},{8,9},{9,8},{10,11... | collective-permute-start | bytes 393224 | tf_op jit(solution)/shard_map/ppermute | solution.py:38
  85.9 3.7 %collective-permute-start.21 = (bf16[64,1024]{1,0:T(8,128)(2,1)S(1)}, bf16[64,1024]{1,0:T(8,128)(2,1)S(1)}, u32[]{:S(2)}, u32[]{:S(2)}) collective-permute-start(bf16[64,1024]{1,0:T(8,128)(2,1)S(1)} %collective-permute-done.17.refs_2_), channel_id=1, source_target_pairs={{0,1},{1,0},{2,3},{3,2},{4,5},{5,4},{6,7},{7,6},{8,9},{9,8},{10,11... | collective-permute-start | bytes 393224 | tf_op jit(solution)/shard_map/ppermute | solution.py:38
  89.7 1.3 collective-permute-start.27
  93.7 1.6 collective-permute-start.30
  93.9 1.8 collective-permute-start.28
  95.8 8.5 %collective-permute-start.31 = (bf16[2,64,1024]{2,1,0:T(8,128)(2,1)S(1)}, bf16[2,64,1024]{2,1,0:T(8,128)(2,1)S(1)}, u32[]{:S(2)}, u32[]{:S(2)}) collective-permute-start(bf16[2,64,1024]{2,1,0:T(8,128)(2,1)S(1)} %bitcast.137), channel_id=1, source_target_pairs={{0,16},{1,9},{8,24},{9,1},{16,0},{17,25},{24,8},{25,17},{2,18},{3,... | collective-permute-start | bytes 786440 | tf_op jit(solution)/shard_map/ppermute | solution.py:55
  104.4 6.6 %collective-permute-start.32 = (bf16[1,64,1024]{2,1,0:T(8,128)(2,1)S(1)}, bf16[1,64,1024]{2,1,0:T(8,128)(2,1)S(1)}, u32[]{:S(2)}, u32[]{:S(2)}) collective-permute-start(bf16[1,64,1024]{2,1,0:T(8,128)(2,1)S(1)} %slice.380), channel_id=1, source_target_pairs={{0,8},{1,17},{8,0},{9,25},{16,24},{17,1},{24,16},{25,9},{2,10},{3,... | collective-permute-start | bytes 393224 | tf_op jit(solution)/shard_map/ppermute | solution.py:55
  110.1 3.7 %collective-permute-start.29 = (bf16[256,1024]{1,0:T(8,128)(2,1)S(1)}, bf16[256,1024]{1,0:T(8,128)(2,1)S(1)}, u32[]{:S(2)}, u32[]{:S(2)}) collective-permute-start(bf16[256,1024]{1,0:T(8,128)(2,1)S(1)} %get-tuple-element.133), channel_id=1, source_target_pairs={{0,1},{1,0},{2,3},{3,2},{4,5},{5,4},{6,7},{7,6},{8,9},{9,8},{10,11... | collective-permute-start | bytes 1572872 | tf_op jit(solution)/shard_map/ppermute | solution.py:38
  112.1 5.2 %collective-permute-start.36 = (bf16[64,1024]{1,0:T(8,128)(2,1)S(1)}, bf16[64,1024]{1,0:T(8,128)(2,1)}, u32[]{:S(2)}, u32[]{:S(2)}) collective-permute-start(bf16[64,1024]{1,0:T(8,128)(2,1)S(1)} %get-tuple-element.181.refs_9_), channel_id=1, source_target_pairs={{0,2},{1,5},{2,0},{3,7},{4,6},{5,1},{6,4},{7,3},{8,10},{9,13},{10,... | collective-permute-start | bytes 393224 | tf_op jit(solution)/shard_map/ppermute | solution.py:55
  114.8 10.5 %collective-permute-start.33 = (bf16[2,64,1024]{2,1,0:T(8,128)(2,1)}, bf16[2,64,1024]{2,1,0:T(8,128)(2,1)}, u32[]{:S(2)}, u32[]{:S(2)}) collective-permute-start(bf16[2,64,1024]{2,1,0:T(8,128)(2,1)} %bitcast.21), channel_id=1, source_target_pairs={{0,16},{1,9},{8,24},{9,1},{16,0},{17,25},{24,8},{25,17},{2,18},{3,... | collective-permute-start | bytes 786440 | tf_op jit(solution)/shard_map/ppermute | solution.py:55
  116.9 5.0 %collective-permute-start.37 = (bf16[64,1024]{1,0:T(8,128)(2,1)S(1)}, bf16[64,1024]{1,0:T(8,128)(2,1)S(1)}, u32[]{:S(2)}, u32[]{:S(2)}) collective-permute-start(bf16[64,1024]{1,0:T(8,128)(2,1)S(1)} %get-tuple-element.181.refs_9_), channel_id=1, source_target_pairs={{0,4},{1,3},{2,6},{3,1},{4,0},{5,7},{6,2},{7,5},{8,12},{9,11},{10,... | collective-permute-start | bytes 393224 | tf_op jit(solution)/shard_map/ppermute | solution.py:55
  117.3 6.0 %collective-permute-start.38 = (bf16[64,1024]{1,0:T(8,128)(2,1)}, bf16[64,1024]{1,0:T(8,128)(2,1)S(1)}, u32[]{:S(2)}, u32[]{:S(2)}) collective-permute-start(bf16[64,1024]{1,0:T(8,128)(2,1)} %collective-permute-done.36.refs_10_), channel_id=1, source_target_pairs={{0,4},{1,3},{2,6},{3,1},{4,0},{5,7},{6,2},{7,5},{8,12},{9,11},{10,... | collective-permute-start | bytes 393224 | tf_op jit(solution)/shard_map/ppermute | solution.py:55
  120.0 6.5 %collective-permute-start.39 = (bf16[64,1024]{1,0:T(8,128)(2,1)S(1)}, bf16[64,1024]{1,0:T(8,128)(2,1)S(1)}, u32[]{:S(2)}, u32[]{:S(2)}) collective-permute-start(bf16[64,1024]{1,0:T(8,128)(2,1)S(1)} %get-tuple-element.181.refs_9_), channel_id=1, source_target_pairs={{0,1},{1,0},{2,3},{3,2},{4,5},{5,4},{6,7},{7,6},{8,9},{9,8},{10,11... | collective-permute-start | bytes 393224 | tf_op jit(solution)/shard_map/ppermute | solution.py:38
  120.0 7.0 %collective-permute-start.40 = (bf16[64,1024]{1,0:T(8,128)(2,1)}, bf16[64,1024]{1,0:T(8,128)(2,1)S(1)}, u32[]{:S(2)}, u32[]{:S(2)}) collective-permute-start(bf16[64,1024]{1,0:T(8,128)(2,1)} %collective-permute-done.36.refs_10_), channel_id=1, source_target_pairs={{0,1},{1,0},{2,3},{3,2},{4,5},{5,4},{6,7},{7,6},{8,9},{9,8},{10,11... | collective-permute-start | bytes 393224 | tf_op jit(solution)/shard_map/ppermute | solution.py:38
  121.8 7.1 %collective-permute-start.41 = (bf16[64,1024]{1,0:T(8,128)(2,1)S(1)}, bf16[64,1024]{1,0:T(8,128)(2,1)S(1)}, u32[]{:S(2)}, u32[]{:S(2)}) collective-permute-start(bf16[64,1024]{1,0:T(8,128)(2,1)S(1)} %collective-permute-done.37.refs_11_), channel_id=1, source_target_pairs={{0,1},{1,0},{2,3},{3,2},{4,5},{5,4},{6,7},{7,6},{8,9},{9,8},{10,11... | collective-permute-start | bytes 393224 | tf_op jit(solution)/shard_map/ppermute | solution.py:38
  123.2 16.7 %collective-permute-start.50 = (bf16[2,4,64,384]{3,2,1,0:T(8,128)(2,1)}, bf16[2,4,64,384]{3,2,1,0:T(8,128)(2,1)S(1)}, u32[]{:S(2)}, u32[]{:S(2)}) collective-permute-start(bf16[2,4,64,384]{3,2,1,0:T(8,128)(2,1)} %copy-done.3), channel_id=1, source_target_pairs={{0,4},{1,3},{2,6},{3,1},{4,0},{5,7},{6,2},{7,5},{8,12},{9,11},{10,... | collective-permute-start | bytes 1179656 | tf_op jit(solution)/shard_map/ppermute | solution.py:55
  125.2 3.7 %collective-permute-start.42 = (bf16[64,1024]{1,0:T(8,128)(2,1)S(1)}, bf16[64,1024]{1,0:T(8,128)(2,1)S(1)}, u32[]{:S(2)}, u32[]{:S(2)}) collective-permute-start(bf16[64,1024]{1,0:T(8,128)(2,1)S(1)} %collective-permute-done.38.refs_12_), channel_id=1, source_target_pairs={{0,1},{1,0},{2,3},{3,2},{4,5},{5,4},{6,7},{7,6},{8,9},{9,8},{10,11... | collective-permute-start | bytes 393224 | tf_op jit(solution)/shard_map/ppermute | solution.py:38
  126.5 19.5 %collective-permute-start.44 = (bf16[2,4,64,768]{3,2,1,0:T(8,128)(2,1)S(1)}, bf16[2,4,64,768]{3,2,1,0:T(8,128)(2,1)S(1)}, u32[]{:S(2)}, u32[]{:S(2)}) collective-permute-start(bf16[2,4,64,768]{3,2,1,0:T(8,128)(2,1)S(1)} %copy-done.2), channel_id=1, source_target_pairs={{0,4},{1,3},{2,6},{3,1},{4,0},{5,7},{6,2},{7,5},{8,12},{9,11},{10,... | collective-permute-start | bytes 2359304 | tf_op jit(solution)/shard_map/ppermute | solution.py:55
  127.0 14.8 %collective-permute-start.34 = (bf16[1,64,1024]{2,1,0:T(8,128)(2,1)S(1)}, bf16[1,64,1024]{2,1,0:T(8,128)(2,1)S(1)}, u32[]{:S(2)}, u32[]{:S(2)}) collective-permute-start(bf16[1,64,1024]{2,1,0:T(8,128)(2,1)S(1)} %slice.379), channel_id=1, source_target_pairs={{0,8},{1,17},{8,0},{9,25},{16,24},{17,1},{24,16},{25,9},{2,10},{3,... | collective-permute-start | bytes 393224 | tf_op jit(solution)/shard_map/ppermute | solution.py:55
  137.2 8.6 %collective-permute-start.43 = (bf16[256,1024]{1,0:T(8,128)(2,1)S(1)}, bf16[256,1024]{1,0:T(8,128)(2,1)S(1)}, u32[]{:S(2)}, u32[]{:S(2)}) collective-permute-start(bf16[256,1024]{1,0:T(8,128)(2,1)S(1)} %get-tuple-element.145), channel_id=1, source_target_pairs={{0,1},{1,0},{2,3},{3,2},{4,5},{5,4},{6,7},{7,6},{8,9},{9,8},{10,11... | collective-permute-start | bytes 1572872 | tf_op jit(solution)/shard_map/ppermute | solution.py:38
  137.3 23.7 %collective-permute-start.48 = (bf16[2,264,512]{2,1,0:T(8,128)(2,1)S(1)}, bf16[2,264,512]{2,1,0:T(8,128)(2,1)S(1)}, u32[]{:S(2)}, u32[]{:S(2)}) collective-permute-start(bf16[2,264,512]{2,1,0:T(8,128)(2,1)S(1)} %get-tuple-element.151), channel_id=1, source_target_pairs={{0,16},{1,9},{8,24},{9,1},{16,0},{17,25},{24,8},{25,17},{2,18},{3,... | collective-permute-start | bytes 1622024 | tf_op jit(solution)/shard_map/ppermute | solution.py:55
  140.0 5.7 %collective-permute-start.51 = (bf16[1,4,64,384]{3,2,1,0:T(8,128)(2,1)S(1)}, bf16[1,4,64,384]{3,2,1,0:T(8,128)(2,1)S(1)}, u32[]{:S(2)}, u32[]{:S(2)}) collective-permute-start(bf16[1,4,64,384]{3,2,1,0:T(8,128)(2,1)S(1)} %slice.376), channel_id=1, source_target_pairs={{0,2},{1,5},{2,0},{3,7},{4,6},{5,1},{6,4},{7,3},{8,10},{9,13},{10,... | collective-permute-start | bytes 589832 | tf_op jit(solution)/shard_map/ppermute | solution.py:55
  141.8 23.9 %collective-permute-start.35 = (bf16[64,1024]{1,0:T(8,128)(2,1)S(1)}, bf16[64,1024]{1,0:T(8,128)(2,1)S(1)}, u32[]{:S(2)}, u32[]{:S(2)}) collective-permute-start(bf16[64,1024]{1,0:T(8,128)(2,1)S(1)} %fusion.20), channel_id=1, source_target_pairs={{0,1},{1,0},{2,3},{3,2},{4,5},{5,4},{6,7},{7,6},{8,9},{9,8},{10,11... | collective-permute-start | bytes 393224 | tf_op jit(solution)/shard_map/ppermute | solution.py:38
  146.0 9.2 %collective-permute-start.45 = (bf16[2,64,1024]{2,1,0:T(8,128)(2,1)S(1)}, bf16[2,64,1024]{2,1,0:T(8,128)(2,1)S(1)}, u32[]{:S(2)}, u32[]{:S(2)}) collective-permute-start(bf16[2,64,1024]{2,1,0:T(8,128)(2,1)S(1)} %bitcast.136), channel_id=1, source_target_pairs={{0,4},{1,3},{2,6},{3,1},{4,0},{5,7},{6,2},{7,5},{8,12},{9,11},{10,... | collective-permute-start | bytes 786440 | tf_op jit(solution)/shard_map/ppermute | solution.py:55
  147.3 10.3 %collective-permute-start.53 = (bf16[2,256,256]{2,1,0:T(8,128)(2,1)S(1)}, bf16[2,256,256]{2,1,0:T(8,128)(2,1)S(1)}, u32[]{:S(2)}, u32[]{:S(2)}) collective-permute-start(bf16[2,256,256]{2,1,0:T(8,128)(2,1)S(1)} %get-tuple-element.161), channel_id=1, source_target_pairs={{0,16},{1,9},{8,24},{9,1},{16,0},{17,25},{24,8},{25,17},{2,18},{3,... | collective-permute-start | bytes 786440 | tf_op jit(solution)/shard_map/ppermute | solution.py:55
  148.1 12.7 %collective-permute-start.49 = (bf16[1,4,64,768]{3,2,1,0:T(8,128)(2,1)S(1)}, bf16[1,4,64,768]{3,2,1,0:T(8,128)(2,1)S(1)}, u32[]{:S(2)}, u32[]{:S(2)}) collective-permute-start(bf16[1,4,64,768]{3,2,1,0:T(8,128)(2,1)S(1)} %slice.374), channel_id=1, source_target_pairs={{0,2},{1,5},{2,0},{3,7},{4,6},{5,1},{6,4},{7,3},{8,10},{9,13},{10,... | collective-permute-start | bytes 1179656 | tf_op jit(solution)/shard_map/ppermute | solution.py:55
  155.3 5.0 %collective-permute-start.46 = (bf16[1,64,1024]{2,1,0:T(8,128)(2,1)S(1)}, bf16[1,64,1024]{2,1,0:T(8,128)(2,1)S(1)}, u32[]{:S(2)}, u32[]{:S(2)}) collective-permute-start(bf16[1,64,1024]{2,1,0:T(8,128)(2,1)S(1)} %slice.378), channel_id=1, source_target_pairs={{0,2},{1,5},{2,0},{3,7},{4,6},{5,1},{6,4},{7,3},{8,10},{9,13},{10,... | collective-permute-start | bytes 393224 | tf_op jit(solution)/shard_map/ppermute | solution.py:55
  157.7 6.9 %collective-permute-start.54 = (bf16[1,256,256]{2,1,0:T(8,128)(2,1)S(1)}, bf16[1,256,256]{2,1,0:T(8,128)(2,1)S(1)}, u32[]{:S(2)}, u32[]{:S(2)}) collective-permute-start(bf16[1,256,256]{2,1,0:T(8,128)(2,1)S(1)} %slice.377), channel_id=1, source_target_pairs={{0,8},{1,17},{8,0},{9,25},{16,24},{17,1},{24,16},{25,9},{2,10},{3,... | collective-permute-start | bytes 393224 | tf_op jit(solution)/shard_map/ppermute | solution.py:55
  160.8 8.5 %collective-permute-start.47 = (bf16[64,1024]{1,0:T(8,128)(2,1)S(1)}, bf16[64,1024]{1,0:T(8,128)(2,1)S(1)}, u32[]{:S(2)}, u32[]{:S(2)}) collective-permute-start(bf16[64,1024]{1,0:T(8,128)(2,1)S(1)} %fusion.12), channel_id=1, source_target_pairs={{0,1},{1,0},{2,3},{3,2},{4,5},{5,4},{6,7},{7,6},{8,9},{9,8},{10,11... | collective-permute-start | bytes 393224 | tf_op jit(solution)/shard_map/ppermute | solution.py:38
  161.3 13.2 %collective-permute-start.52 = (bf16[1,264,512]{2,1,0:T(8,128)(2,1)S(1)}, bf16[1,264,512]{2,1,0:T(8,128)(2,1)S(1)}, u32[]{:S(2)}, u32[]{:S(2)}) collective-permute-start(bf16[1,264,512]{2,1,0:T(8,128)(2,1)S(1)} %slice.375), channel_id=1, source_target_pairs={{0,8},{1,17},{8,0},{9,25},{16,24},{17,1},{24,16},{25,9},{2,10},{3,... | collective-permute-start | bytes 811016 | tf_op jit(solution)/shard_map/ppermute | solution.py:55
  161.5 15.1 %collective-permute-start.55 = (bf16[64,1152]{1,0:T(8,128)(2,1)S(1)}, bf16[64,1152]{1,0:T(8,128)(2,1)S(1)}, u32[]{:S(2)}, u32[]{:S(2)}) collective-permute-start(bf16[64,1152]{1,0:T(8,128)(2,1)S(1)} %get-tuple-element.165), channel_id=1, source_target_pairs={{0,8},{8,0},{16,24},{24,16},{1,9},{9,1},{17,25},{25,17},{2,10},{10... | collective-permute-start | bytes 442376 | tf_op jit(solution)/shard_map/ppermute | solution.py:38
  164.6 22.2 %collective-permute-start.59 = (bf16[64,1152]{1,0:T(8,128)(2,1)S(1)}, bf16[64,1152]{1,0:T(8,128)(2,1)S(1)}, u32[]{:S(2)}, u32[]{:S(2)}) collective-permute-start(bf16[64,1152]{1,0:T(8,128)(2,1)S(1)} %get-tuple-element.173), channel_id=1, source_target_pairs={{0,16},{8,24},{16,0},{24,8},{1,17},{9,25},{17,1},{25,9},{2,18},{10... | collective-permute-start | bytes 442376 | tf_op jit(solution)/shard_map/ppermute | solution.py:38
  165.7 21.1 %collective-permute-start.60 = (bf16[64,1152]{1,0:T(8,128)(2,1)S(1)}, bf16[64,1152]{1,0:T(8,128)(2,1)S(1)}, u32[]{:S(2)}, u32[]{:S(2)}) collective-permute-start(bf16[64,1152]{1,0:T(8,128)(2,1)S(1)} %get-tuple-element.174), channel_id=1, source_target_pairs={{0,24},{8,16},{16,8},{24,0},{1,25},{9,17},{17,9},{25,1},{2,26},{10... | collective-permute-start | bytes 442376 | tf_op jit(solution)/shard_map/ppermute | solution.py:38
  176.7 4.8 %collective-permute-start.56 = (bf16[72,768]{1,0:T(8,128)(2,1)S(1)}, bf16[72,768]{1,0:T(8,128)(2,1)S(1)}, u32[]{:S(2)}, u32[]{:S(2)}) collective-permute-start(bf16[72,768]{1,0:T(8,128)(2,1)S(1)} %fusion.34), channel_id=1, source_target_pairs={{0,2},{2,0},{4,6},{6,4},{1,3},{3,1},{5,7},{7,5},{8,10},{10,8},{12,... | collective-permute-start | bytes 331784 | tf_op jit(solution)/shard_map/ppermute | solution.py:38
  178.6 4.7 %collective-permute-start.57 = (bf16[72,768]{1,0:T(8,128)(2,1)S(1)}, bf16[72,768]{1,0:T(8,128)(2,1)S(1)}, u32[]{:S(2)}, u32[]{:S(2)}) collective-permute-start(bf16[72,768]{1,0:T(8,128)(2,1)S(1)} %fusion.35), channel_id=1, source_target_pairs={{0,4},{2,6},{4,0},{6,2},{1,5},{3,7},{5,1},{7,3},{8,12},{10,14},{12... | collective-permute-start | bytes 331784 | tf_op jit(solution)/shard_map/ppermute | solution.py:38
  180.2 5.6 %collective-permute-start.58 = (bf16[72,768]{1,0:T(8,128)(2,1)S(1)}, bf16[72,768]{1,0:T(8,128)(2,1)S(1)}, u32[]{:S(2)}, u32[]{:S(2)}) collective-permute-start(bf16[72,768]{1,0:T(8,128)(2,1)S(1)} %fusion.36), channel_id=1, source_target_pairs={{0,6},{2,4},{4,2},{6,0},{1,7},{3,5},{5,3},{7,1},{8,14},{10,12},{12... | collective-permute-start | bytes 331784 | tf_op jit(solution)/shard_map/ppermute | solution.py:38
  186.8 1.2 collective-permute-start.61
  (18 other events, 72.8 us)

commit v5 on v4

--- a/solution.py
+++ b/solution.py
@@ -682,13 +682,17 @@
 
         rows_out = [both_halves(out).reshape(1, tokens, width), both_halves(grad_hidden).reshape(1, tokens, width)]
 
+        def gain_sum(*refs):
+            refs[C][...] = sum([refs[j][rows:, :aw].astype(F32) for j in range(C)])
+
+        ge = call(gain_sum, [shape(8, aw, dtype=F32)], [after(ga[0], rows_out)] + ga[1:])[0]
+
         def attn_owner(*refs):
-            b, gwq, gwk, gwv, gwo, ge = refs[:C], *refs[C:]
+            b, gwq, gwk, gwv, gwo = refs[:C], *refs[C:]
             _, mc = me()
             if share > 1:
                 gwk[...] = jnp.zeros_like(gwk)
                 gwv[...] = jnp.zeros_like(gwv)
-            e = jnp.zeros((8, aw), F32)
             for j in range(C):
                 d = mc ^ j
                 gwq[:, at(d * qc, qc, 128)] = b[j][0:rows, :qc].astype(F32)
@@ -702,16 +706,14 @@
                 else:
                     gwk[:, ks] = gk
                     gwv[:, ks] = gw
-                e += b[j][rows:, :aw].astype(F32)
-            ge[...] = e
-
-        gwq, gwk, gwv, gwo, ge = call(
+
+        gwq, gwk, gwv, gwo = call(
             attn_owner,
             [
                 shape(rows, C * qc, dtype=F32), shape(rows, kv_local * HEAD, dtype=F32),
-                shape(rows, kv_local * HEAD, dtype=F32), shape(rows, C * qc, dtype=F32), shape(8, aw, dtype=F32),
+                shape(rows, kv_local * HEAD, dtype=F32), shape(rows, C * qc, dtype=F32),
             ],
-            [after(ga[0], rows_out)] + ga[1:],
+            [after(ga[0], rows_out, ge)] + ga[1:],
         )
         ge = ge + swap_t(ge)
 

time: 190 us -> 190 us (level)
    pallas_call x18 -> x19, Pallas kernels: 24.5 us -> 24.5 us  [call(): pl.pallas_call(body, out_shape=list(outs), in_specs=[far] * hbm + [vmem]...]
  transfers between devices with their start and end apart: 62 -> 62, of which waited for: 32 -> 31; matrix products, arithmetic and copies ran while one was open for 5% -> 5% of each run, Pallas kernels for 10% -> 10%
where the time goes in v5:
time: 190 us; the launch traced here: 189 us
  starting transfers between devices  76.4 us (40%)
  waiting for transfers between devices  73.5 us (39%)
  Pallas kernels  24.5 us (13%)
  other arithmetic  10.1 us (5%)
  local copies, waits for them, and re-layouts  3.17 us (2%)
    ppermute x30, waiting for transfers between devices, hop(): lax.ppermute(x, (axis, 'tensor'), [(2 * d + t, 2 * (d ^ steps[t]) + t) fo...  54.4 us
    ppermute x30, starting transfers between devices, hop(): lax.ppermute(x, (axis, 'tensor'), [(2 * d + t, 2 * (d ^ steps[t]) + t) fo...  50.9 us
    ppermute x32, starting transfers between devices, swap(): return lax.ppermute(x, axis, [(i, i ^ k) for i in range(n)])  25.6 us
    pallas_call x19, Pallas kernels, call(): pl.pallas_call(body, out_shape=list(outs), in_specs=[far] * hbm + [vmem]...  24.5 us
    ppermute x32, waiting for transfers between devices, swap(): return lax.ppermute(x, axis, [(i, i ^ k) for i in range(n)])  19.2 us
  transfers between devices with their start and end apart: 62, of which 31 were waited for; matrix products, arithmetic and copies ran while one was open for 5% of the time, Pallas kernels for 10%

profile of v5, /device:TPU:0, one launch (start us, length us, event | category | flops | bytes accessed | tf_op | source)
XLA Modules:
  0.0 189.2 jit_solution(2475069818358668808)
XLA Ops:
  0.6 1.7 shard_map.237
  2.3 3.0 %collective-permute-start.2 = (bf16[72,1792]{1,0:T(8,128)(2,1)S(1)}, bf16[72,1792]{1,0:T(8,128)(2,1)S(1)}, u32[]{:S(2)}, u32[]{:S(2)}) collective-permute-start(bf16[72,1792]{1,0:T(8,128)(2,1)S(1)} %get-tuple-element.103), channel_id=1, source_target_pairs={{0,2},{2,0},{4,6},{6,4},{1,3},{3,1},{5,7},{7,5},{8,10},{10,8},{12,... | collective-permute-start | bytes 774152 | tf_op jit(solution)/shard_map/ppermute | solution.py:38
  5.4 1.5 collective-permute-start.3
  6.9 1.2 shard_map.238
  8.1 2.1 %collective-permute-start = (bf16[64,1152]{1,0:T(8,128)(2,1)S(1)}, bf16[64,1152]{1,0:T(8,128)(2,1)S(1)}, u32[]{:S(2)}, u32[]{:S(2)}) collective-permute-start(bf16[64,1152]{1,0:T(8,128)(2,1)S(1)} %get-tuple-element.100), channel_id=1, source_target_pairs={{0,8},{8,0},{16,24},{24,16},{1,9},{9,1},{17,25},{25,17},{2,10},{10... | collective-permute-start | bytes 442376 | tf_op jit(solution)/shard_map/ppermute | solution.py:38
  10.2 2.5 %collective-permute-start.1 = (bf16[64,1152]{1,0:T(8,128)(2,1)S(1)}, bf16[64,1152]{1,0:T(8,128)(2,1)S(1)}, u32[]{:S(2)}, u32[]{:S(2)}) collective-permute-start(bf16[64,1152]{1,0:T(8,128)(2,1)S(1)} %get-tuple-element.101), channel_id=1, source_target_pairs={{0,24},{8,16},{16,8},{24,0},{1,25},{9,17},{17,9},{25,1},{2,26},{10... | collective-permute-start | bytes 442376 | tf_op jit(solution)/shard_map/ppermute | solution.py:38
  12.7 1.5 collective-permute-done.refs_1_
  14.2 4.3 %collective-permute-done.1.refs_3_ = bf16[64,1152]{1,0:T(8,128)(2,1)S(1)} collective-permute-done((bf16[64,1152]{1,0:T(8,128)(2,1)S(1)}, bf16[64,1152]{1,0:T(8,128)(2,1)S(1)}, u32[]{:S(2)}, u32[]{:S(2)}) %collective-permute-start.1) | collective-permute-done | bytes 147488 | tf_op jit(solution)/shard_map/ppermute | solution.py:38
  18.7 1.6 collective-permute-start.6
  20.3 2.6 %collective-permute-start.8 = (bf16[64,1152]{1,0:T(8,128)(2,1)S(1)}, bf16[64,1152]{1,0:T(8,128)(2,1)S(1)}, u32[]{:S(2)}, u32[]{:S(2)}) collective-permute-start(bf16[64,1152]{1,0:T(8,128)(2,1)S(1)} %get-tuple-element.110), channel_id=1, source_target_pairs={{0,16},{8,24},{16,0},{24,8},{1,17},{9,25},{17,1},{25,9},{2,18},{10... | collective-permute-start | bytes 442376 | tf_op jit(solution)/shard_map/ppermute | solution.py:38
  23.0 4.2 %collective-permute-done.6.b_ref = bf16[1,264,512]{2,1,0:T(8,128)(2,1)S(1)} collective-permute-done((bf16[1,264,512]{2,1,0:T(8,128)(2,1)S(1)}, bf16[1,264,512]{2,1,0:T(8,128)(2,1)S(1)}, u32[]{:S(2)}, u32[]{:S(2)}) %collective-permute-start.6) | collective-permute-done | bytes 270368 | tf_op jit(solution)/shard_map/ppermute | solution.py:55
  27.2 2.9 %collective-permute-start.7 = (bf16[2,264,512]{2,1,0:T(8,128)(2,1)S(1)}, bf16[2,264,512]{2,1,0:T(8,128)(2,1)S(1)}, u32[]{:S(2)}, u32[]{:S(2)}) collective-permute-start(bf16[2,264,512]{2,1,0:T(8,128)(2,1)S(1)} %shard_map.240.refs_2_), channel_id=1, source_target_pairs={{0,16},{1,9},{8,24},{9,1},{16,0},{17,25},{24,8},{25,17},{2,18},{3,... | collective-permute-start | bytes 1622024 | tf_op jit(solution)/shard_map/ppermute | solution.py:55
  30.1 1.4 collective-permute-done.8.refs_2_
  31.5 1.5 collective-permute-start.9
  34.6 9.7 %collective-permute-done.10.b_ref = bf16[1,256,256]{2,1,0:T(8,128)(2,1)S(1)} collective-permute-done((bf16[1,256,256]{2,1,0:T(8,128)(2,1)S(1)}, bf16[1,256,256]{2,1,0:T(8,128)(2,1)S(1)}, u32[]{:S(2)}, u32[]{:S(2)}) %collective-permute-start.10) | collective-permute-done | bytes 131104 | tf_op jit(solution)/shard_map/ppermute | solution.py:55
  44.3 2.4 %collective-permute-start.11 = (bf16[2,256,256]{2,1,0:T(8,128)(2,1)S(1)}, bf16[2,256,256]{2,1,0:T(8,128)(2,1)S(1)}, u32[]{:S(2)}, u32[]{:S(2)}) collective-permute-start(bf16[2,256,256]{2,1,0:T(8,128)(2,1)S(1)} %shard_map.243.refs_0_), channel_id=1, source_target_pairs={{0,16},{1,9},{8,24},{9,1},{16,0},{17,25},{24,8},{25,17},{2,18},{3,... | collective-permute-start | bytes 786440 | tf_op jit(solution)/shard_map/ppermute | solution.py:55
  47.4 3.3 %shard_map.244 = (bf16[512,1024]{1,0:T(8,128)(2,1)}, f32[512,384]{1,0:T(8,128)}, bf16[512,256]{1,0:T(8,128)(2,1)}, bf16[512,128]{1,0:T(8,128)(2,1)}, bf16[512,12...) custom-call(bf16[264,1024]{1,0:T(8,128)(2,1)S(1)} %get-tuple-element, ...), custom_call_target="tpu_custom_call" | custom-call | flops 805306368 | bytes 6918144 | tf_op jit(solution)/shard_map/pallas_call | solution.py:112
  50.7 2.1 %collective-permute-done.11.refs_1_ = bf16[2,256,256]{2,1,0:T(8,128)(2,1)S(1)} collective-permute-done((bf16[2,256,256]{2,1,0:T(8,128)(2,1)S(1)}, bf16[2,256,256]{2,1,0:T(8,128)(2,1)S(1)}, u32[]{:S(2)}, u32[]{:S(2)}) %collective-permute-start.11) | collective-permute-done | bytes 262176 | tf_op jit(solution)/shard_map/ppermute | solution.py:55
  53.7 1.5 collective-permute-start.13
  55.4 1.1 collective-permute-done.13
  57.9 1.8 collective-permute-start.14
  61.0 2.8 %collective-permute-start.23 = (bf16[1,64,1024]{2,1,0:T(8,128)(2,1)S(1)}, bf16[1,64,1024]{2,1,0:T(8,128)(2,1)S(1)}, u32[]{:S(2)}, u32[]{:S(2)}) collective-permute-start(bf16[1,64,1024]{2,1,0:T(8,128)(2,1)S(1)} %bitcast.124), channel_id=1, source_target_pairs={{0,8},{1,17},{8,0},{9,25},{16,24},{17,1},{24,16},{25,9},{2,10},{3,... | collective-permute-start | bytes 393224 | tf_op jit(solution)/shard_map/ppermute | solution.py:55
  65.6 1.5 collective-permute-start.15
  67.1 2.6 %collective-permute-start.24 = (bf16[2,64,1024]{2,1,0:T(8,128)(2,1)S(1)}, bf16[2,64,1024]{2,1,0:T(8,128)(2,1)S(1)}, u32[]{:S(2)}, u32[]{:S(2)}) collective-permute-start(bf16[2,64,1024]{2,1,0:T(8,128)(2,1)S(1)} %shard_map.247.refs_2_), channel_id=1, source_target_pairs={{0,16},{1,9},{8,24},{9,1},{16,0},{17,25},{24,8},{25,17},{2,18},{3,... | collective-permute-start | bytes 786440 | tf_op jit(solution)/shard_map/ppermute | solution.py:55
  69.7 2.3 %collective-permute-done.15 = bf16[1,64,1024]{2,1,0:T(8,128)(2,1)S(1)} collective-permute-done((bf16[1,64,1024]{2,1,0:T(8,128)(2,1)S(1)}, bf16[1,64,1024]{2,1,0:T(8,128)(2,1)S(1)}, u32[]{:S(2)}, u32[]{:S(2)}) %collective-permute-start.15) | collective-permute-done | bytes 131104 | tf_op jit(solution)/shard_map/ppermute | solution.py:55
  72.8 2.8 %collective-permute-start.16 = (bf16[64,1024]{1,0:T(8,128)(2,1)S(1)}, bf16[64,1024]{1,0:T(8,128)(2,1)S(1)}, u32[]{:S(2)}, u32[]{:S(2)}) collective-permute-start(bf16[64,1024]{1,0:T(8,128)(2,1)S(1)} %multiply_convert_fusion.refs_0_), channel_id=1, source_target_pairs={{0,8},{1,17},{8,0},{9,25},{16,24},{17,1},{24,16},{25,9},{2,10},{3,... | collective-permute-start | bytes 393224 | tf_op jit(solution)/shard_map/ppermute | solution.py:55
  75.6 3.4 %collective-permute-done.24.refs_3_ = bf16[2,64,1024]{2,1,0:T(8,128)(2,1)S(1)} collective-permute-done((bf16[2,64,1024]{2,1,0:T(8,128)(2,1)S(1)}, bf16[2,64,1024]{2,1,0:T(8,128)(2,1)S(1)}, u32[]{:S(2)}, u32[]{:S(2)}) %collective-permute-start.24) | collective-permute-done | bytes 262176 | tf_op jit(solution)/shard_map/ppermute | solution.py:55
  80.0 2.5 %collective-permute-start.17 = (bf16[64,1024]{1,0:T(8,128)(2,1)S(1)}, bf16[64,1024]{1,0:T(8,128)(2,1)S(1)}, u32[]{:S(2)}, u32[]{:S(2)}) collective-permute-start(bf16[64,1024]{1,0:T(8,128)(2,1)S(1)} %multiply_convert_fusion.refs_0_), channel_id=1, source_target_pairs={{0,16},{1,9},{8,24},{9,1},{16,0},{17,25},{24,8},{25,17},{2,18},{3,... | collective-permute-start | bytes 393224 | tf_op jit(solution)/shard_map/ppermute | solution.py:55
  82.9 3.0 %collective-permute-done.17.refs_2_ = bf16[64,1024]{1,0:T(8,128)(2,1)S(1)} collective-permute-done((bf16[64,1024]{1,0:T(8,128)(2,1)S(1)}, bf16[64,1024]{1,0:T(8,128)(2,1)S(1)}, u32[]{:S(2)}, u32[]{:S(2)}) %collective-permute-start.17) | collective-permute-done | bytes 131104 | tf_op jit(solution)/shard_map/ppermute | solution.py:55
  87.4 2.3 %collective-permute-done.18.refs_3_ = bf16[64,1024]{1,0:T(8,128)(2,1)S(1)} collective-permute-done((bf16[64,1024]{1,0:T(8,128)(2,1)S(1)}, bf16[64,1024]{1,0:T(8,128)(2,1)S(1)}, u32[]{:S(2)}, u32[]{:S(2)}) %collective-permute-start.18) | collective-permute-done | bytes 131104 | tf_op jit(solution)/shard_map/ppermute | solution.py:55
  89.7 1.3 collective-permute-done.27.refs_7_
  91.0 2.6 %shard_map.249 = (f32[256,1024]{1,0:T(8,128)S(1)}, bf16[128,1024]{1,0:T(8,128)(2,1)S(1)}, bf16[128,1024]{1,0:T(8,128)(2,1)S(1)}, bf16[512,1024]{1,0:T(8,128)(2,1)S(1)}, bf16[512,1152]{1,0:T(8,128)(2,1)S(1)}) custom-call(bf16[64,1024]{1,0:T(8,128)(2,1)S(1)} %multiply_convert_fusion.refs_0_, bf16[64,1024]{1,0:T(8,128)(2,1)S(1)} %collective-permute-done.16.refs_1_, ...), custom_call_target="tpu_custom_call" | custom-call | flops 1610612736 | bytes 7995392 | tf_op jit(solution)/shard_map/pallas_call | solution.py:112
  94.2 1.0 collective-permute-done.30
  95.8 1.5 collective-permute-start.31
  97.3 7.0 %collective-permute-done.31 = bf16[2,64,1024]{2,1,0:T(8,128)(2,1)S(1)} collective-permute-done((bf16[2,64,1024]{2,1,0:T(8,128)(2,1)S(1)}, bf16[2,64,1024]{2,1,0:T(8,128)(2,1)S(1)}, u32[]{:S(2)}, u32[]{:S(2)}) %collective-permute-start.31) | collective-permute-done | bytes 262176 | tf_op jit(solution)/shard_map/ppermute | solution.py:55
  104.4 3.2 %collective-permute-start.32 = (bf16[1,64,1024]{2,1,0:T(8,128)(2,1)S(1)}, bf16[1,64,1024]{2,1,0:T(8,128)(2,1)S(1)}, u32[]{:S(2)}, u32[]{:S(2)}) collective-permute-start(bf16[1,64,1024]{2,1,0:T(8,128)(2,1)S(1)} %slice.380), channel_id=1, source_target_pairs={{0,8},{1,17},{8,0},{9,25},{16,24},{17,1},{24,16},{25,9},{2,10},{3,... | collective-permute-start | bytes 393224 | tf_op jit(solution)/shard_map/ppermute | solution.py:55
  107.6 2.5 %shard_map.250 = (f32[256,1024]{1,0:T(8,128)S(1)}, bf16[256,1024]{1,0:T(8,128)(2,1)S(1)}, bf16[2,4,64,384]{3,2,1,0:T(8,128)(2,1)S(1)}, bf16[2,4,64,384]{3,2,1,0:...) custom-call(bf16[512,1024]{1,0:T(8,128)(2,1)S(1)} %get-tuple-element.126.h2_ref, ...), custom_call_target="tpu_custom_call" | custom-call | flops 1610612736 | bytes 9568256 | tf_op jit(solution)/shard_map/pallas_call | solution.py:112
  112.1 1.6 collective-permute-start.36
  114.8 2.1 %collective-permute-start.33 = (bf16[2,64,1024]{2,1,0:T(8,128)(2,1)}, bf16[2,64,1024]{2,1,0:T(8,128)(2,1)}, u32[]{:S(2)}, u32[]{:S(2)}) collective-permute-start(bf16[2,64,1024]{2,1,0:T(8,128)(2,1)} %bitcast.21), channel_id=1, source_target_pairs={{0,16},{1,9},{8,24},{9,1},{16,0},{17,25},{24,8},{25,17},{2,18},{3,... | collective-permute-start | bytes 786440 | tf_op jit(solution)/shard_map/ppermute | solution.py:55
  117.3 2.7 %collective-permute-start.38 = (bf16[64,1024]{1,0:T(8,128)(2,1)}, bf16[64,1024]{1,0:T(8,128)(2,1)S(1)}, u32[]{:S(2)}, u32[]{:S(2)}) collective-permute-start(bf16[64,1024]{1,0:T(8,128)(2,1)} %collective-permute-done.36.refs_10_), channel_id=1, source_target_pairs={{0,4},{1,3},{2,6},{3,1},{4,0},{5,7},{6,2},{7,5},{8,12},{9,11},{10,... | collective-permute-start | bytes 393224 | tf_op jit(solution)/shard_map/ppermute | solution.py:55
  120.5 1.3 collective-permute-done.37.refs_11_
  121.8 1.4 collective-permute-done.38.refs_12_
  123.2 1.9 %collective-permute-start.50 = (bf16[2,4,64,384]{3,2,1,0:T(8,128)(2,1)}, bf16[2,4,64,384]{3,2,1,0:T(8,128)(2,1)S(1)}, u32[]{:S(2)}, u32[]{:S(2)}) collective-permute-start(bf16[2,4,64,384]{3,2,1,0:T(8,128)(2,1)} %copy-done.3), channel_id=1, source_target_pairs={{0,4},{1,3},{2,6},{3,1},{4,0},{5,7},{6,2},{7,5},{8,12},{9,11},{10,... | collective-permute-start | bytes 1179656 | tf_op jit(solution)/shard_map/ppermute | solution.py:55
  125.2 1.2 convert_add_fusion.6
  127.0 2.0 %collective-permute-start.34 = (bf16[1,64,1024]{2,1,0:T(8,128)(2,1)S(1)}, bf16[1,64,1024]{2,1,0:T(8,128)(2,1)S(1)}, u32[]{:S(2)}, u32[]{:S(2)}) collective-permute-start(bf16[1,64,1024]{2,1,0:T(8,128)(2,1)S(1)} %slice.379), channel_id=1, source_target_pairs={{0,8},{1,17},{8,0},{9,25},{16,24},{17,1},{24,16},{25,9},{2,10},{3,... | collective-permute-start | bytes 393224 | tf_op jit(solution)/shard_map/ppermute | solution.py:55
  128.9 8.3 %shard_map.251 = (f32[256,1024]{1,0:T(8,128)S(1)}, bf16[256,1024]{1,0:T(8,128)(2,1)S(1)}, bf16[2,264,512]{2,1,0:T(8,128)(2,1)S(1)}, bf16[2,264,512]{2,1,0:T(8,128)(2,1)S(1)}, bf16[512,1024]{1,0:T(8,128)(2,1)S(1)}) custom-call(bf16[1024,256]{1,0:T(8,128)(2,1)} %get-tuple-element.136.refs_0_, bf16[512,256]{1,0:T(8,128)(2,1)} %get-tuple-element.137.refs_1_, ...), custom_call_target="tpu_custom_call" | custom-call | flops 2147483648 | bytes 10854400 | tf_op jit(solution)/shard_map/pallas_call | solution.py:112
  137.3 2.6 %collective-permute-start.48 = (bf16[2,264,512]{2,1,0:T(8,128)(2,1)S(1)}, bf16[2,264,512]{2,1,0:T(8,128)(2,1)S(1)}, u32[]{:S(2)}, u32[]{:S(2)}) collective-permute-start(bf16[2,264,512]{2,1,0:T(8,128)(2,1)S(1)} %get-tuple-element.151), channel_id=1, source_target_pairs={{0,16},{1,9},{8,24},{9,1},{16,0},{17,25},{24,8},{25,17},{2,18},{3,... | collective-permute-start | bytes 1622024 | tf_op jit(solution)/shard_map/ppermute | solution.py:55
  140.0 1.7 collective-permute-start.51
  141.9 3.9 %collective-permute-done.51 = bf16[1,4,64,384]{3,2,1,0:T(8,128)(2,1)S(1)} collective-permute-done((bf16[1,4,64,384]{3,2,1,0:T(8,128)(2,1)S(1)}, bf16[1,4,64,384]{3,2,1,0:T(8,128)(2,1)S(1)}, u32[]{:S(2)}, u32[]{:S(2)}) %collective-permute-start.51) | collective-permute-done | bytes 196640 | tf_op jit(solution)/shard_map/ppermute | solution.py:55
  148.1 1.2 collective-permute-start.49
  149.4 5.9 %collective-permute-done.45 = bf16[2,64,1024]{2,1,0:T(8,128)(2,1)S(1)} collective-permute-done((bf16[2,64,1024]{2,1,0:T(8,128)(2,1)S(1)}, bf16[2,64,1024]{2,1,0:T(8,128)(2,1)S(1)}, u32[]{:S(2)}, u32[]{:S(2)}) %collective-permute-start.45) | collective-permute-done | bytes 262176 | tf_op jit(solution)/shard_map/ppermute | solution.py:55
  155.3 1.7 collective-permute-start.46
  157.7 2.6 %collective-permute-start.54 = (bf16[1,256,256]{2,1,0:T(8,128)(2,1)S(1)}, bf16[1,256,256]{2,1,0:T(8,128)(2,1)S(1)}, u32[]{:S(2)}, u32[]{:S(2)}) collective-permute-start(bf16[1,256,256]{2,1,0:T(8,128)(2,1)S(1)} %slice.377), channel_id=1, source_target_pairs={{0,8},{1,17},{8,0},{9,25},{16,24},{17,1},{24,16},{25,9},{2,10},{3,... | collective-permute-start | bytes 393224 | tf_op jit(solution)/shard_map/ppermute | solution.py:55
  161.5 1.8 collective-permute-start.55
  164.6 1.0 collective-permute-start.59
  165.7 2.8 %collective-permute-start.60 = (bf16[64,1152]{1,0:T(8,128)(2,1)S(1)}, bf16[64,1152]{1,0:T(8,128)(2,1)S(1)}, u32[]{:S(2)}, u32[]{:S(2)}) collective-permute-start(bf16[64,1152]{1,0:T(8,128)(2,1)S(1)} %get-tuple-element.175), channel_id=1, source_target_pairs={{0,24},{8,16},{16,8},{24,0},{1,25},{9,17},{17,9},{25,1},{2,26},{10... | collective-permute-start | bytes 442376 | tf_op jit(solution)/shard_map/ppermute | solution.py:38
  170.0 4.4 %collective-permute-done.52 = bf16[1,264,512]{2,1,0:T(8,128)(2,1)S(1)} collective-permute-done((bf16[1,264,512]{2,1,0:T(8,128)(2,1)S(1)}, bf16[1,264,512]{2,1,0:T(8,128)(2,1)S(1)}, u32[]{:S(2)}, u32[]{:S(2)}) %collective-permute-start.52) | collective-permute-done | bytes 270368 | tf_op jit(solution)/shard_map/ppermute | solution.py:55
  174.7 2.0 %collective-permute-done.55.refs_1_ = bf16[64,1152]{1,0:T(8,128)(2,1)S(1)} collective-permute-done((bf16[64,1152]{1,0:T(8,128)(2,1)S(1)}, bf16[64,1152]{1,0:T(8,128)(2,1)S(1)}, u32[]{:S(2)}, u32[]{:S(2)}) %collective-permute-start.55) | collective-permute-done | bytes 147488 | tf_op jit(solution)/shard_map/ppermute | solution.py:38
  176.7 1.9 %collective-permute-start.56 = (bf16[72,768]{1,0:T(8,128)(2,1)S(1)}, bf16[72,768]{1,0:T(8,128)(2,1)S(1)}, u32[]{:S(2)}, u32[]{:S(2)}) collective-permute-start(bf16[72,768]{1,0:T(8,128)(2,1)S(1)} %fusion.34), channel_id=1, source_target_pairs={{0,2},{2,0},{4,6},{6,4},{1,3},{3,1},{5,7},{7,5},{8,10},{10,8},{12,... | collective-permute-start | bytes 331784 | tf_op jit(solution)/shard_map/ppermute | solution.py:38
  178.6 1.6 collective-permute-start.57
  180.2 1.3 collective-permute-done.56.refs_1_
  181.5 1.8 collective-permute-done.57.refs_2_
  183.3 2.5 %collective-permute-done.58.refs_3_ = bf16[72,768]{1,0:T(8,128)(2,1)S(1)} collective-permute-done((bf16[72,768]{1,0:T(8,128)(2,1)S(1)}, bf16[72,768]{1,0:T(8,128)(2,1)S(1)}, u32[]{:S(2)}, u32[]{:S(2)}) %collective-permute-start.58) | collective-permute-done | bytes 110624 | tf_op jit(solution)/shard_map/ppermute | solution.py:38
  186.0 1.1 shard_map.255
  (177 shorter events, 26.9 us)
Async XLA Ops:
  2.3 16.2 %collective-permute-start.2 = (bf16[72,1792]{1,0:T(8,128)(2,1)S(1)}, bf16[72,1792]{1,0:T(8,128)(2,1)S(1)}, u32[]{:S(2)}, u32[]{:S(2)}) collective-permute-start(bf16[72,1792]{1,0:T(8,128)(2,1)S(1)} %get-tuple-element.103), channel_id=1, source_target_pairs={{0,2},{2,0},{4,6},{6,4},{1,3},{3,1},{5,7},{7,5},{8,10},{10,8},{12,... | collective-permute-start | bytes 774152 | tf_op jit(solution)/shard_map/ppermute | solution.py:38
  5.4 13.2 %collective-permute-start.3 = (bf16[72,1792]{1,0:T(8,128)(2,1)S(1)}, bf16[72,1792]{1,0:T(8,128)(2,1)S(1)}, u32[]{:S(2)}, u32[]{:S(2)}) collective-permute-start(bf16[72,1792]{1,0:T(8,128)(2,1)S(1)} %get-tuple-element.104), channel_id=1, source_target_pairs={{0,4},{2,6},{4,0},{6,2},{1,5},{3,7},{5,1},{7,3},{8,12},{10,14},{12... | collective-permute-start | bytes 774152 | tf_op jit(solution)/shard_map/ppermute | solution.py:38
  6.9 11.7 %collective-permute-start.4 = (bf16[72,1792]{1,0:T(8,128)(2,1)S(1)}, bf16[72,1792]{1,0:T(8,128)(2,1)S(1)}, u32[]{:S(2)}, u32[]{:S(2)}) collective-permute-start(bf16[72,1792]{1,0:T(8,128)(2,1)S(1)} %get-tuple-element.105), channel_id=1, source_target_pairs={{0,6},{2,4},{4,2},{6,0},{1,7},{3,5},{5,3},{7,1},{8,14},{10,12},{12... | collective-permute-start | bytes 774152 | tf_op jit(solution)/shard_map/ppermute | solution.py:38
  8.1 6.1 %collective-permute-start = (bf16[64,1152]{1,0:T(8,128)(2,1)S(1)}, bf16[64,1152]{1,0:T(8,128)(2,1)S(1)}, u32[]{:S(2)}, u32[]{:S(2)}) collective-permute-start(bf16[64,1152]{1,0:T(8,128)(2,1)S(1)} %get-tuple-element.100), channel_id=1, source_target_pairs={{0,8},{8,0},{16,24},{24,16},{1,9},{9,1},{17,25},{25,17},{2,10},{10... | collective-permute-start | bytes 442376 | tf_op jit(solution)/shard_map/ppermute | solution.py:38
  10.2 8.4 %collective-permute-start.1 = (bf16[64,1152]{1,0:T(8,128)(2,1)S(1)}, bf16[64,1152]{1,0:T(8,128)(2,1)S(1)}, u32[]{:S(2)}, u32[]{:S(2)}) collective-permute-start(bf16[64,1152]{1,0:T(8,128)(2,1)S(1)} %get-tuple-element.101), channel_id=1, source_target_pairs={{0,24},{8,16},{16,8},{24,0},{1,25},{9,17},{17,9},{25,1},{2,26},{10... | collective-permute-start | bytes 442376 | tf_op jit(solution)/shard_map/ppermute | solution.py:38
  18.7 8.5 %collective-permute-start.6 = (bf16[1,264,512]{2,1,0:T(8,128)(2,1)S(1)}, bf16[1,264,512]{2,1,0:T(8,128)(2,1)S(1)}, u32[]{:S(2)}, u32[]{:S(2)}) collective-permute-start(bf16[1,264,512]{2,1,0:T(8,128)(2,1)S(1)} %bitcast.126), channel_id=1, source_target_pairs={{0,8},{1,17},{8,0},{9,25},{16,24},{17,1},{24,16},{25,9},{2,10},{3,... | collective-permute-start | bytes 811016 | tf_op jit(solution)/shard_map/ppermute | solution.py:55
  20.3 11.2 %collective-permute-start.8 = (bf16[64,1152]{1,0:T(8,128)(2,1)S(1)}, bf16[64,1152]{1,0:T(8,128)(2,1)S(1)}, u32[]{:S(2)}, u32[]{:S(2)}) collective-permute-start(bf16[64,1152]{1,0:T(8,128)(2,1)S(1)} %get-tuple-element.110), channel_id=1, source_target_pairs={{0,16},{8,24},{16,0},{24,8},{1,17},{9,25},{17,1},{25,9},{2,18},{10... | collective-permute-start | bytes 442376 | tf_op jit(solution)/shard_map/ppermute | solution.py:38
  22.9 24.0 %collective-permute-start.5 = (bf16[264,1024]{1,0:T(8,128)(2,1)S(1)}, bf16[264,1024]{1,0:T(8,128)(2,1)S(1)}, u32[]{:S(2)}, u32[]{:S(2)}) collective-permute-start(bf16[264,1024]{1,0:T(8,128)(2,1)S(1)} %get-tuple-element.106.a_ref.refs_0_.refs_7_), channel_id=1, source_target_pairs={{0,1},{1,0},{2,3},{3,2},{4,5},{5,4},{6,7},{7,6},{8,9},{9,8},{10,11... | collective-permute-start | bytes 1622024 | tf_op jit(solution)/shard_map/ppermute | solution.py:38
  27.2 20.2 %collective-permute-start.7 = (bf16[2,264,512]{2,1,0:T(8,128)(2,1)S(1)}, bf16[2,264,512]{2,1,0:T(8,128)(2,1)S(1)}, u32[]{:S(2)}, u32[]{:S(2)}) collective-permute-start(bf16[2,264,512]{2,1,0:T(8,128)(2,1)S(1)} %shard_map.240.refs_2_), channel_id=1, source_target_pairs={{0,16},{1,9},{8,24},{9,1},{16,0},{17,25},{24,8},{25,17},{2,18},{3,... | collective-permute-start | bytes 1622024 | tf_op jit(solution)/shard_map/ppermute | solution.py:55
  31.5 15.9 %collective-permute-start.9 = (bf16[1,4,64,1152]{3,2,1,0:T(8,128)(2,1)S(1)}, bf16[1,4,64,1152]{3,2,1,0:T(8,128)(2,1)S(1)}, u32[]{:S(2)}, u32[]{:S(2)}) collective-permute-start(bf16[1,4,64,1152]{3,2,1,0:T(8,128)(2,1)S(1)} %bitcast.122), channel_id=1, source_target_pairs={{0,2},{1,5},{2,0},{3,7},{4,6},{5,1},{6,4},{7,3},{8,10},{9,13},{10,... | collective-permute-start | bytes 1769480 | tf_op jit(solution)/shard_map/ppermute | solution.py:55
  33.0 11.2 %collective-permute-start.10 = (bf16[1,256,256]{2,1,0:T(8,128)(2,1)S(1)}, bf16[1,256,256]{2,1,0:T(8,128)(2,1)S(1)}, u32[]{:S(2)}, u32[]{:S(2)}) collective-permute-start(bf16[1,256,256]{2,1,0:T(8,128)(2,1)S(1)} %bitcast.128), channel_id=1, source_target_pairs={{0,8},{1,17},{8,0},{9,25},{16,24},{17,1},{24,16},{25,9},{2,10},{3,... | collective-permute-start | bytes 393224 | tf_op jit(solution)/shard_map/ppermute | solution.py:55
  44.3 8.5 %collective-permute-start.11 = (bf16[2,256,256]{2,1,0:T(8,128)(2,1)S(1)}, bf16[2,256,256]{2,1,0:T(8,128)(2,1)S(1)}, u32[]{:S(2)}, u32[]{:S(2)}) collective-permute-start(bf16[2,256,256]{2,1,0:T(8,128)(2,1)S(1)} %shard_map.243.refs_0_), channel_id=1, source_target_pairs={{0,16},{1,9},{8,24},{9,1},{16,0},{17,25},{24,8},{25,17},{2,18},{3,... | collective-permute-start | bytes 786440 | tf_op jit(solution)/shard_map/ppermute | solution.py:55
  53.7 2.7 %collective-permute-start.13 = (bf16[128,1024]{1,0:T(8,128)(2,1)S(1)}, bf16[128,1024]{1,0:T(8,128)(2,1)S(1)}, u32[]{:S(2)}, u32[]{:S(2)}) collective-permute-start(bf16[128,1024]{1,0:T(8,128)(2,1)S(1)} %get-tuple-element.117), channel_id=1, source_target_pairs={{0,1},{1,0},{2,3},{3,2},{4,5},{5,4},{6,7},{7,6},{8,9},{9,8},{10,11... | collective-permute-start | bytes 786440 | tf_op jit(solution)/shard_map/ppermute | solution.py:38
  55.3 1.5 collective-permute-start.12
  57.9 6.7 %collective-permute-start.14 = (bf16[2,64,1024]{2,1,0:T(8,128)(2,1)}, bf16[2,64,1024]{2,1,0:T(8,128)(2,1)}, u32[]{:S(2)}, u32[]{:S(2)}) collective-permute-start(bf16[2,64,1024]{2,1,0:T(8,128)(2,1)} %bitcast.11), channel_id=1, source_target_pairs={{0,4},{1,3},{2,6},{3,1},{4,0},{5,7},{6,2},{7,5},{8,12},{9,11},{10,... | collective-permute-start | bytes 786440 | tf_op jit(solution)/shard_map/ppermute | solution.py:55
  60.6 11.4 %copy-start.10 = (bf16[1,128,1024]{2,1,0:T(8,128)(2,1)S(1)}, bf16[1,128,1024]{2,1,0:T(8,128)(2,1)}, u32[]{:S(2)}) copy-start(bf16[1,128,1024]{2,1,0:T(8,128)(2,1)} %param.14) | copy-start | bytes 786436
  60.6 25.8 %collective-permute-start.22 = (bf16[2,4,64,1152]{3,2,1,0:T(8,128)(2,1)S(1)}, bf16[2,4,64,1152]{3,2,1,0:T(8,128)(2,1)S(1)}, u32[]{:S(2)}, u32[]{:S(2)}) collective-permute-start(bf16[2,4,64,1152]{3,2,1,0:T(8,128)(2,1)S(1)} %shard_map.246.refs_0_), channel_id=1, source_target_pairs={{0,4},{1,3},{2,6},{3,1},{4,0},{5,7},{6,2},{7,5},{8,12},{9,11},{10,... | collective-permute-start | bytes 3538952 | tf_op jit(solution)/shard_map/ppermute | solution.py:55
  61.0 6.1 %collective-permute-start.23 = (bf16[1,64,1024]{2,1,0:T(8,128)(2,1)S(1)}, bf16[1,64,1024]{2,1,0:T(8,128)(2,1)S(1)}, u32[]{:S(2)}, u32[]{:S(2)}) collective-permute-start(bf16[1,64,1024]{2,1,0:T(8,128)(2,1)S(1)} %bitcast.124), channel_id=1, source_target_pairs={{0,8},{1,17},{8,0},{9,25},{16,24},{17,1},{24,16},{25,9},{2,10},{3,... | collective-permute-start | bytes 393224 | tf_op jit(solution)/shard_map/ppermute | solution.py:55
  65.6 6.4 %collective-permute-start.15 = (bf16[1,64,1024]{2,1,0:T(8,128)(2,1)S(1)}, bf16[1,64,1024]{2,1,0:T(8,128)(2,1)S(1)}, u32[]{:S(2)}, u32[]{:S(2)}) collective-permute-start(bf16[1,64,1024]{2,1,0:T(8,128)(2,1)S(1)} %slice.381), channel_id=1, source_target_pairs={{0,2},{1,5},{2,0},{3,7},{4,6},{5,1},{6,4},{7,3},{8,10},{9,13},{10,... | collective-permute-start | bytes 393224 | tf_op jit(solution)/shard_map/ppermute | solution.py:55
  67.1 11.9 %collective-permute-start.24 = (bf16[2,64,1024]{2,1,0:T(8,128)(2,1)S(1)}, bf16[2,64,1024]{2,1,0:T(8,128)(2,1)S(1)}, u32[]{:S(2)}, u32[]{:S(2)}) collective-permute-start(bf16[2,64,1024]{2,1,0:T(8,128)(2,1)S(1)} %shard_map.247.refs_2_), channel_id=1, source_target_pairs={{0,16},{1,9},{8,24},{9,1},{16,0},{17,25},{24,8},{25,17},{2,18},{3,... | collective-permute-start | bytes 786440 | tf_op jit(solution)/shard_map/ppermute | solution.py:55
  72.2 39.0 %copy-start.4 = (f32[64,1024]{1,0:T(8,128)}, f32[64,1024]{1,0:T(8,128)S(1)}, u32[]{:S(2)}) copy-start(f32[64,1024]{1,0:T(8,128)S(1)} %get-tuple-element.184) | copy-start | bytes 786436
  72.8 6.2 %collective-permute-start.16 = (bf16[64,1024]{1,0:T(8,128)(2,1)S(1)}, bf16[64,1024]{1,0:T(8,128)(2,1)S(1)}, u32[]{:S(2)}, u32[]{:S(2)}) collective-permute-start(bf16[64,1024]{1,0:T(8,128)(2,1)S(1)} %multiply_convert_fusion.refs_0_), channel_id=1, source_target_pairs={{0,8},{1,17},{8,0},{9,25},{16,24},{17,1},{24,16},{25,9},{2,10},{3,... | collective-permute-start | bytes 393224 | tf_op jit(solution)/shard_map/ppermute | solution.py:55
  75.6 7.3 %collective-permute-start.25 = (bf16[2,64,1024]{2,1,0:T(8,128)(2,1)S(1)}, bf16[2,64,1024]{2,1,0:T(8,128)(2,1)S(1)}, u32[]{:S(2)}, u32[]{:S(2)}) collective-permute-start(bf16[2,64,1024]{2,1,0:T(8,128)(2,1)S(1)} %shard_map.247.refs_2_), channel_id=1, source_target_pairs={{0,1},{1,0},{2,3},{3,2},{4,5},{5,4},{6,7},{7,6},{8,9},{9,8},{10,11... | collective-permute-start | bytes 786440 | tf_op jit(solution)/shard_map/ppermute | solution.py:38
  79.0 6.9 %collective-permute-start.26 = (bf16[2,64,1024]{2,1,0:T(8,128)(2,1)S(1)}, bf16[2,64,1024]{2,1,0:T(8,128)(2,1)S(1)}, u32[]{:S(2)}, u32[]{:S(2)}) collective-permute-start(bf16[2,64,1024]{2,1,0:T(8,128)(2,1)S(1)} %collective-permute-done.24.refs_3_), channel_id=1, source_target_pairs={{0,1},{1,0},{2,3},{3,2},{4,5},{5,4},{6,7},{7,6},{8,9},{9,8},{10,11... | collective-permute-start | bytes 786440 | tf_op jit(solution)/shard_map/ppermute | solution.py:38
  80.0 6.0 %collective-permute-start.17 = (bf16[64,1024]{1,0:T(8,128)(2,1)S(1)}, bf16[64,1024]{1,0:T(8,128)(2,1)S(1)}, u32[]{:S(2)}, u32[]{:S(2)}) collective-permute-start(bf16[64,1024]{1,0:T(8,128)(2,1)S(1)} %multiply_convert_fusion.refs_0_), channel_id=1, source_target_pairs={{0,16},{1,9},{8,24},{9,1},{16,0},{17,25},{24,8},{25,17},{2,18},{3,... | collective-permute-start | bytes 393224 | tf_op jit(solution)/shard_map/ppermute | solution.py:55
  82.5 7.2 %collective-permute-start.18 = (bf16[64,1024]{1,0:T(8,128)(2,1)S(1)}, bf16[64,1024]{1,0:T(8,128)(2,1)S(1)}, u32[]{:S(2)}, u32[]{:S(2)}) collective-permute-start(bf16[64,1024]{1,0:T(8,128)(2,1)S(1)} %collective-permute-done.16.refs_1_), channel_id=1, source_target_pairs={{0,16},{1,9},{8,24},{9,1},{16,0},{17,25},{24,8},{25,17},{2,18},{3,... | collective-permute-start | bytes 393224 | tf_op jit(solution)/shard_map/ppermute | solution.py:55
  82.9 6.8 %collective-permute-start.19 = (bf16[64,1024]{1,0:T(8,128)(2,1)S(1)}, bf16[64,1024]{1,0:T(8,128)(2,1)S(1)}, u32[]{:S(2)}, u32[]{:S(2)}) collective-permute-start(bf16[64,1024]{1,0:T(8,128)(2,1)S(1)} %multiply_convert_fusion.refs_0_), channel_id=1, source_target_pairs={{0,1},{1,0},{2,3},{3,2},{4,5},{5,4},{6,7},{7,6},{8,9},{9,8},{10,11... | collective-permute-start | bytes 393224 | tf_op jit(solution)/shard_map/ppermute | solution.py:38
  85.9 3.7 %collective-permute-start.20 = (bf16[64,1024]{1,0:T(8,128)(2,1)S(1)}, bf16[64,1024]{1,0:T(8,128)(2,1)S(1)}, u32[]{:S(2)}, u32[]{:S(2)}) collective-permute-start(bf16[64,1024]{1,0:T(8,128)(2,1)S(1)} %collective-permute-done.16.refs_1_), channel_id=1, source_target_pairs={{0,1},{1,0},{2,3},{3,2},{4,5},{5,4},{6,7},{7,6},{8,9},{9,8},{10,11... | collective-permute-start | bytes 393224 | tf_op jit(solution)/shard_map/ppermute | solution.py:38
  85.9 3.7 %collective-permute-start.21 = (bf16[64,1024]{1,0:T(8,128)(2,1)S(1)}, bf16[64,1024]{1,0:T(8,128)(2,1)S(1)}, u32[]{:S(2)}, u32[]{:S(2)}) collective-permute-start(bf16[64,1024]{1,0:T(8,128)(2,1)S(1)} %collective-permute-done.17.refs_2_), channel_id=1, source_target_pairs={{0,1},{1,0},{2,3},{3,2},{4,5},{5,4},{6,7},{7,6},{8,9},{9,8},{10,11... | collective-permute-start | bytes 393224 | tf_op jit(solution)/shard_map/ppermute | solution.py:38
  89.7 1.3 collective-permute-start.27
  93.7 1.6 collective-permute-start.30
  93.9 1.8 collective-permute-start.28
  95.8 8.5 %collective-permute-start.31 = (bf16[2,64,1024]{2,1,0:T(8,128)(2,1)S(1)}, bf16[2,64,1024]{2,1,0:T(8,128)(2,1)S(1)}, u32[]{:S(2)}, u32[]{:S(2)}) collective-permute-start(bf16[2,64,1024]{2,1,0:T(8,128)(2,1)S(1)} %bitcast.137), channel_id=1, source_target_pairs={{0,16},{1,9},{8,24},{9,1},{16,0},{17,25},{24,8},{25,17},{2,18},{3,... | collective-permute-start | bytes 786440 | tf_op jit(solution)/shard_map/ppermute | solution.py:55
  104.4 6.6 %collective-permute-start.32 = (bf16[1,64,1024]{2,1,0:T(8,128)(2,1)S(1)}, bf16[1,64,1024]{2,1,0:T(8,128)(2,1)S(1)}, u32[]{:S(2)}, u32[]{:S(2)}) collective-permute-start(bf16[1,64,1024]{2,1,0:T(8,128)(2,1)S(1)} %slice.380), channel_id=1, source_target_pairs={{0,8},{1,17},{8,0},{9,25},{16,24},{17,1},{24,16},{25,9},{2,10},{3,... | collective-permute-start | bytes 393224 | tf_op jit(solution)/shard_map/ppermute | solution.py:55
  110.1 3.7 %collective-permute-start.29 = (bf16[256,1024]{1,0:T(8,128)(2,1)S(1)}, bf16[256,1024]{1,0:T(8,128)(2,1)S(1)}, u32[]{:S(2)}, u32[]{:S(2)}) collective-permute-start(bf16[256,1024]{1,0:T(8,128)(2,1)S(1)} %get-tuple-element.133), channel_id=1, source_target_pairs={{0,1},{1,0},{2,3},{3,2},{4,5},{5,4},{6,7},{7,6},{8,9},{9,8},{10,11... | collective-permute-start | bytes 1572872 | tf_op jit(solution)/shard_map/ppermute | solution.py:38
  112.1 5.2 %collective-permute-start.36 = (bf16[64,1024]{1,0:T(8,128)(2,1)S(1)}, bf16[64,1024]{1,0:T(8,128)(2,1)}, u32[]{:S(2)}, u32[]{:S(2)}) collective-permute-start(bf16[64,1024]{1,0:T(8,128)(2,1)S(1)} %get-tuple-element.181.refs_9_), channel_id=1, source_target_pairs={{0,2},{1,5},{2,0},{3,7},{4,6},{5,1},{6,4},{7,3},{8,10},{9,13},{10,... | collective-permute-start | bytes 393224 | tf_op jit(solution)/shard_map/ppermute | solution.py:55
  114.8 10.5 %collective-permute-start.33 = (bf16[2,64,1024]{2,1,0:T(8,128)(2,1)}, bf16[2,64,1024]{2,1,0:T(8,128)(2,1)}, u32[]{:S(2)}, u32[]{:S(2)}) collective-permute-start(bf16[2,64,1024]{2,1,0:T(8,128)(2,1)} %bitcast.21), channel_id=1, source_target_pairs={{0,16},{1,9},{8,24},{9,1},{16,0},{17,25},{24,8},{25,17},{2,18},{3,... | collective-permute-start | bytes 786440 | tf_op jit(solution)/shard_map/ppermute | solution.py:55
  116.9 5.0 %collective-permute-start.37 = (bf16[64,1024]{1,0:T(8,128)(2,1)S(1)}, bf16[64,1024]{1,0:T(8,128)(2,1)S(1)}, u32[]{:S(2)}, u32[]{:S(2)}) collective-permute-start(bf16[64,1024]{1,0:T(8,128)(2,1)S(1)} %get-tuple-element.181.refs_9_), channel_id=1, source_target_pairs={{0,4},{1,3},{2,6},{3,1},{4,0},{5,7},{6,2},{7,5},{8,12},{9,11},{10,... | collective-permute-start | bytes 393224 | tf_op jit(solution)/shard_map/ppermute | solution.py:55
  117.3 6.0 %collective-permute-start.38 = (bf16[64,1024]{1,0:T(8,128)(2,1)}, bf16[64,1024]{1,0:T(8,128)(2,1)S(1)}, u32[]{:S(2)}, u32[]{:S(2)}) collective-permute-start(bf16[64,1024]{1,0:T(8,128)(2,1)} %collective-permute-done.36.refs_10_), channel_id=1, source_target_pairs={{0,4},{1,3},{2,6},{3,1},{4,0},{5,7},{6,2},{7,5},{8,12},{9,11},{10,... | collective-permute-start | bytes 393224 | tf_op jit(solution)/shard_map/ppermute | solution.py:55
  120.0 6.5 %collective-permute-start.39 = (bf16[64,1024]{1,0:T(8,128)(2,1)S(1)}, bf16[64,1024]{1,0:T(8,128)(2,1)S(1)}, u32[]{:S(2)}, u32[]{:S(2)}) collective-permute-start(bf16[64,1024]{1,0:T(8,128)(2,1)S(1)} %get-tuple-element.181.refs_9_), channel_id=1, source_target_pairs={{0,1},{1,0},{2,3},{3,2},{4,5},{5,4},{6,7},{7,6},{8,9},{9,8},{10,11... | collective-permute-start | bytes 393224 | tf_op jit(solution)/shard_map/ppermute | solution.py:38
  120.0 7.0 %collective-permute-start.40 = (bf16[64,1024]{1,0:T(8,128)(2,1)}, bf16[64,1024]{1,0:T(8,128)(2,1)S(1)}, u32[]{:S(2)}, u32[]{:S(2)}) collective-permute-start(bf16[64,1024]{1,0:T(8,128)(2,1)} %collective-permute-done.36.refs_10_), channel_id=1, source_target_pairs={{0,1},{1,0},{2,3},{3,2},{4,5},{5,4},{6,7},{7,6},{8,9},{9,8},{10,11... | collective-permute-start | bytes 393224 | tf_op jit(solution)/shard_map/ppermute | solution.py:38
  121.8 7.1 %collective-permute-start.41 = (bf16[64,1024]{1,0:T(8,128)(2,1)S(1)}, bf16[64,1024]{1,0:T(8,128)(2,1)S(1)}, u32[]{:S(2)}, u32[]{:S(2)}) collective-permute-start(bf16[64,1024]{1,0:T(8,128)(2,1)S(1)} %collective-permute-done.37.refs_11_), channel_id=1, source_target_pairs={{0,1},{1,0},{2,3},{3,2},{4,5},{5,4},{6,7},{7,6},{8,9},{9,8},{10,11... | collective-permute-start | bytes 393224 | tf_op jit(solution)/shard_map/ppermute | solution.py:38
  123.2 16.7 %collective-permute-start.50 = (bf16[2,4,64,384]{3,2,1,0:T(8,128)(2,1)}, bf16[2,4,64,384]{3,2,1,0:T(8,128)(2,1)S(1)}, u32[]{:S(2)}, u32[]{:S(2)}) collective-permute-start(bf16[2,4,64,384]{3,2,1,0:T(8,128)(2,1)} %copy-done.3), channel_id=1, source_target_pairs={{0,4},{1,3},{2,6},{3,1},{4,0},{5,7},{6,2},{7,5},{8,12},{9,11},{10,... | collective-permute-start | bytes 1179656 | tf_op jit(solution)/shard_map/ppermute | solution.py:55
  125.2 3.7 %collective-permute-start.42 = (bf16[64,1024]{1,0:T(8,128)(2,1)S(1)}, bf16[64,1024]{1,0:T(8,128)(2,1)S(1)}, u32[]{:S(2)}, u32[]{:S(2)}) collective-permute-start(bf16[64,1024]{1,0:T(8,128)(2,1)S(1)} %collective-permute-done.38.refs_12_), channel_id=1, source_target_pairs={{0,1},{1,0},{2,3},{3,2},{4,5},{5,4},{6,7},{7,6},{8,9},{9,8},{10,11... | collective-permute-start | bytes 393224 | tf_op jit(solution)/shard_map/ppermute | solution.py:38
  126.5 19.5 %collective-permute-start.44 = (bf16[2,4,64,768]{3,2,1,0:T(8,128)(2,1)S(1)}, bf16[2,4,64,768]{3,2,1,0:T(8,128)(2,1)S(1)}, u32[]{:S(2)}, u32[]{:S(2)}) collective-permute-start(bf16[2,4,64,768]{3,2,1,0:T(8,128)(2,1)S(1)} %copy-done.2), channel_id=1, source_target_pairs={{0,4},{1,3},{2,6},{3,1},{4,0},{5,7},{6,2},{7,5},{8,12},{9,11},{10,... | collective-permute-start | bytes 2359304 | tf_op jit(solution)/shard_map/ppermute | solution.py:55
  127.0 14.8 %collective-permute-start.34 = (bf16[1,64,1024]{2,1,0:T(8,128)(2,1)S(1)}, bf16[1,64,1024]{2,1,0:T(8,128)(2,1)S(1)}, u32[]{:S(2)}, u32[]{:S(2)}) collective-permute-start(bf16[1,64,1024]{2,1,0:T(8,128)(2,1)S(1)} %slice.379), channel_id=1, source_target_pairs={{0,8},{1,17},{8,0},{9,25},{16,24},{17,1},{24,16},{25,9},{2,10},{3,... | collective-permute-start | bytes 393224 | tf_op jit(solution)/shard_map/ppermute | solution.py:55
  137.2 8.6 %collective-permute-start.43 = (bf16[256,1024]{1,0:T(8,128)(2,1)S(1)}, bf16[256,1024]{1,0:T(8,128)(2,1)S(1)}, u32[]{:S(2)}, u32[]{:S(2)}) collective-permute-start(bf16[256,1024]{1,0:T(8,128)(2,1)S(1)} %get-tuple-element.145), channel_id=1, source_target_pairs={{0,1},{1,0},{2,3},{3,2},{4,5},{5,4},{6,7},{7,6},{8,9},{9,8},{10,11... | collective-permute-start | bytes 1572872 | tf_op jit(solution)/shard_map/ppermute | solution.py:38
  137.3 23.7 %collective-permute-start.48 = (bf16[2,264,512]{2,1,0:T(8,128)(2,1)S(1)}, bf16[2,264,512]{2,1,0:T(8,128)(2,1)S(1)}, u32[]{:S(2)}, u32[]{:S(2)}) collective-permute-start(bf16[2,264,512]{2,1,0:T(8,128)(2,1)S(1)} %get-tuple-element.151), channel_id=1, source_target_pairs={{0,16},{1,9},{8,24},{9,1},{16,0},{17,25},{24,8},{25,17},{2,18},{3,... | collective-permute-start | bytes 1622024 | tf_op jit(solution)/shard_map/ppermute | solution.py:55
  140.0 5.7 %collective-permute-start.51 = (bf16[1,4,64,384]{3,2,1,0:T(8,128)(2,1)S(1)}, bf16[1,4,64,384]{3,2,1,0:T(8,128)(2,1)S(1)}, u32[]{:S(2)}, u32[]{:S(2)}) collective-permute-start(bf16[1,4,64,384]{3,2,1,0:T(8,128)(2,1)S(1)} %slice.376), channel_id=1, source_target_pairs={{0,2},{1,5},{2,0},{3,7},{4,6},{5,1},{6,4},{7,3},{8,10},{9,13},{10,... | collective-permute-start | bytes 589832 | tf_op jit(solution)/shard_map/ppermute | solution.py:55
  141.8 23.9 %collective-permute-start.35 = (bf16[64,1024]{1,0:T(8,128)(2,1)S(1)}, bf16[64,1024]{1,0:T(8,128)(2,1)S(1)}, u32[]{:S(2)}, u32[]{:S(2)}) collective-permute-start(bf16[64,1024]{1,0:T(8,128)(2,1)S(1)} %fusion.20), channel_id=1, source_target_pairs={{0,1},{1,0},{2,3},{3,2},{4,5},{5,4},{6,7},{7,6},{8,9},{9,8},{10,11... | collective-permute-start | bytes 393224 | tf_op jit(solution)/shard_map/ppermute | solution.py:38
  146.0 9.2 %collective-permute-start.45 = (bf16[2,64,1024]{2,1,0:T(8,128)(2,1)S(1)}, bf16[2,64,1024]{2,1,0:T(8,128)(2,1)S(1)}, u32[]{:S(2)}, u32[]{:S(2)}) collective-permute-start(bf16[2,64,1024]{2,1,0:T(8,128)(2,1)S(1)} %bitcast.136), channel_id=1, source_target_pairs={{0,4},{1,3},{2,6},{3,1},{4,0},{5,7},{6,2},{7,5},{8,12},{9,11},{10,... | collective-permute-start | bytes 786440 | tf_op jit(solution)/shard_map/ppermute | solution.py:55
  147.3 10.3 %collective-permute-start.53 = (bf16[2,256,256]{2,1,0:T(8,128)(2,1)S(1)}, bf16[2,256,256]{2,1,0:T(8,128)(2,1)S(1)}, u32[]{:S(2)}, u32[]{:S(2)}) collective-permute-start(bf16[2,256,256]{2,1,0:T(8,128)(2,1)S(1)} %get-tuple-element.161), channel_id=1, source_target_pairs={{0,16},{1,9},{8,24},{9,1},{16,0},{17,25},{24,8},{25,17},{2,18},{3,... | collective-permute-start | bytes 786440 | tf_op jit(solution)/shard_map/ppermute | solution.py:55
  148.1 12.7 %collective-permute-start.49 = (bf16[1,4,64,768]{3,2,1,0:T(8,128)(2,1)S(1)}, bf16[1,4,64,768]{3,2,1,0:T(8,128)(2,1)S(1)}, u32[]{:S(2)}, u32[]{:S(2)}) collective-permute-start(bf16[1,4,64,768]{3,2,1,0:T(8,128)(2,1)S(1)} %slice.374), channel_id=1, source_target_pairs={{0,2},{1,5},{2,0},{3,7},{4,6},{5,1},{6,4},{7,3},{8,10},{9,13},{10,... | collective-permute-start | bytes 1179656 | tf_op jit(solution)/shard_map/ppermute | solution.py:55
  155.3 5.0 %collective-permute-start.46 = (bf16[1,64,1024]{2,1,0:T(8,128)(2,1)S(1)}, bf16[1,64,1024]{2,1,0:T(8,128)(2,1)S(1)}, u32[]{:S(2)}, u32[]{:S(2)}) collective-permute-start(bf16[1,64,1024]{2,1,0:T(8,128)(2,1)S(1)} %slice.378), channel_id=1, source_target_pairs={{0,2},{1,5},{2,0},{3,7},{4,6},{5,1},{6,4},{7,3},{8,10},{9,13},{10,... | collective-permute-start | bytes 393224 | tf_op jit(solution)/shard_map/ppermute | solution.py:55
  157.7 6.9 %collective-permute-start.54 = (bf16[1,256,256]{2,1,0:T(8,128)(2,1)S(1)}, bf16[1,256,256]{2,1,0:T(8,128)(2,1)S(1)}, u32[]{:S(2)}, u32[]{:S(2)}) collective-permute-start(bf16[1,256,256]{2,1,0:T(8,128)(2,1)S(1)} %slice.377), channel_id=1, source_target_pairs={{0,8},{1,17},{8,0},{9,25},{16,24},{17,1},{24,16},{25,9},{2,10},{3,... | collective-permute-start | bytes 393224 | tf_op jit(solution)/shard_map/ppermute | solution.py:55
  160.8 8.5 %collective-permute-start.47 = (bf16[64,1024]{1,0:T(8,128)(2,1)S(1)}, bf16[64,1024]{1,0:T(8,128)(2,1)S(1)}, u32[]{:S(2)}, u32[]{:S(2)}) collective-permute-start(bf16[64,1024]{1,0:T(8,128)(2,1)S(1)} %fusion.12), channel_id=1, source_target_pairs={{0,1},{1,0},{2,3},{3,2},{4,5},{5,4},{6,7},{7,6},{8,9},{9,8},{10,11... | collective-permute-start | bytes 393224 | tf_op jit(solution)/shard_map/ppermute | solution.py:38
  161.3 13.2 %collective-permute-start.52 = (bf16[1,264,512]{2,1,0:T(8,128)(2,1)S(1)}, bf16[1,264,512]{2,1,0:T(8,128)(2,1)S(1)}, u32[]{:S(2)}, u32[]{:S(2)}) collective-permute-start(bf16[1,264,512]{2,1,0:T(8,128)(2,1)S(1)} %slice.375), channel_id=1, source_target_pairs={{0,8},{1,17},{8,0},{9,25},{16,24},{17,1},{24,16},{25,9},{2,10},{3,... | collective-permute-start | bytes 811016 | tf_op jit(solution)/shard_map/ppermute | solution.py:55
  161.5 15.1 %collective-permute-start.55 = (bf16[64,1152]{1,0:T(8,128)(2,1)S(1)}, bf16[64,1152]{1,0:T(8,128)(2,1)S(1)}, u32[]{:S(2)}, u32[]{:S(2)}) collective-permute-start(bf16[64,1152]{1,0:T(8,128)(2,1)S(1)} %get-tuple-element.165), channel_id=1, source_target_pairs={{0,8},{8,0},{16,24},{24,16},{1,9},{9,1},{17,25},{25,17},{2,10},{10... | collective-permute-start | bytes 442376 | tf_op jit(solution)/shard_map/ppermute | solution.py:38
  164.6 21.4 %collective-permute-start.59 = (bf16[64,1152]{1,0:T(8,128)(2,1)S(1)}, bf16[64,1152]{1,0:T(8,128)(2,1)S(1)}, u32[]{:S(2)}, u32[]{:S(2)}) collective-permute-start(bf16[64,1152]{1,0:T(8,128)(2,1)S(1)} %get-tuple-element.174), channel_id=1, source_target_pairs={{0,16},{8,24},{16,0},{24,8},{1,17},{9,25},{17,1},{25,9},{2,18},{10... | collective-permute-start | bytes 442376 | tf_op jit(solution)/shard_map/ppermute | solution.py:38
  165.7 20.3 %collective-permute-start.60 = (bf16[64,1152]{1,0:T(8,128)(2,1)S(1)}, bf16[64,1152]{1,0:T(8,128)(2,1)S(1)}, u32[]{:S(2)}, u32[]{:S(2)}) collective-permute-start(bf16[64,1152]{1,0:T(8,128)(2,1)S(1)} %get-tuple-element.175), channel_id=1, source_target_pairs={{0,24},{8,16},{16,8},{24,0},{1,25},{9,17},{17,9},{25,1},{2,26},{10... | collective-permute-start | bytes 442376 | tf_op jit(solution)/shard_map/ppermute | solution.py:38
  176.7 4.8 %collective-permute-start.56 = (bf16[72,768]{1,0:T(8,128)(2,1)S(1)}, bf16[72,768]{1,0:T(8,128)(2,1)S(1)}, u32[]{:S(2)}, u32[]{:S(2)}) collective-permute-start(bf16[72,768]{1,0:T(8,128)(2,1)S(1)} %fusion.34), channel_id=1, source_target_pairs={{0,2},{2,0},{4,6},{6,4},{1,3},{3,1},{5,7},{7,5},{8,10},{10,8},{12,... | collective-permute-start | bytes 331784 | tf_op jit(solution)/shard_map/ppermute | solution.py:38
  178.6 4.7 %collective-permute-start.57 = (bf16[72,768]{1,0:T(8,128)(2,1)S(1)}, bf16[72,768]{1,0:T(8,128)(2,1)S(1)}, u32[]{:S(2)}, u32[]{:S(2)}) collective-permute-start(bf16[72,768]{1,0:T(8,128)(2,1)S(1)} %fusion.35), channel_id=1, source_target_pairs={{0,4},{2,6},{4,0},{6,2},{1,5},{3,7},{5,1},{7,3},{8,12},{10,14},{12... | collective-permute-start | bytes 331784 | tf_op jit(solution)/shard_map/ppermute | solution.py:38
  180.2 5.6 %collective-permute-start.58 = (bf16[72,768]{1,0:T(8,128)(2,1)S(1)}, bf16[72,768]{1,0:T(8,128)(2,1)S(1)}, u32[]{:S(2)}, u32[]{:S(2)}) collective-permute-start(bf16[72,768]{1,0:T(8,128)(2,1)S(1)} %fusion.36), channel_id=1, source_target_pairs={{0,6},{2,4},{4,2},{6,0},{1,7},{3,5},{5,3},{7,1},{8,14},{10,12},{12... | collective-permute-start | bytes 331784 | tf_op jit(solution)/shard_map/ppermute | solution.py:38
  185.9 2.1 %collective-permute-start.61 = (f32[8,512]{1,0:T(8,128)S(1)}, f32[8,512]{1,0:T(8,128)S(1)}, u32[]{:S(2)}, u32[]{:S(2)}) collective-permute-start(f32[8,512]{1,0:T(8,128)S(1)} %shard_map.253), channel_id=1, source_target_pairs={{0,1},{1,0},{2,3},{3,2},{4,5},{5,4},{6,7},{7,6},{8,9},{9,8},{10,11... | collective-permute-start | bytes 49160 | tf_op jit(solution)/shard_map/ppermute | solution.py:38
  (18 other events, 72.8 us)
